TPU v7x, 32 devices: a whole 2x2x4 slice. The times are simulated.
32 devices in a mesh: dp: 8 (over y, x, core), tensor: 4 (over z).
Axes of the slice: x: 2, y: 2, z: 4, core: 2. Of those that a mesh axis runs over, the one named last changes fastest.
Arguments:
- tokens: bfloat16 [8192, 2048], P(('dp', 'tensor')), may hold values from -6 to 6
- cotangent: bfloat16 [8192, 2048], P(('dp', 'tensor')), may hold values from -6 to 6
- ln1_gain: bfloat16 [2048], P(('dp', 'tensor')), may hold values from 0.5 to 1.5
- ln1_bias: bfloat16 [2048], P(('dp', 'tensor')), may hold values from -3 to 3
- qkv_weight: bfloat16 [3, 2048, 2048], P(None, 'dp', 'tensor'), may hold values from -0.125 to 0.125
- qv_bias: bfloat16 [2, 2048], P(None, ('tensor', 'dp')), may hold values from -3 to 3
- out_weight: bfloat16 [2048, 2048], P('tensor', 'dp'), may hold values from -2 to 2
- out_bias: bfloat16 [2048], P(('dp', 'tensor')), may hold values from -3 to 3
- ln2_gain: bfloat16 [2048], P(('dp', 'tensor')), may hold values from 0.5 to 1.5
- ln2_bias: bfloat16 [2048], P(('dp', 'tensor')), may hold values from -3 to 3
- up_weight: bfloat16 [2048, 8192], P('dp', 'tensor'), may hold values from -0.125 to 0.125
- up_bias: bfloat16 [8192], P(('tensor', 'dp')), may hold values from -3 to 3
- down_weight: bfloat16 [8192, 2048], P('tensor', 'dp'), may hold values from -0.0625 to 0.0625
- down_bias: bfloat16 [2048], P(('dp', 'tensor')), may hold values from -3 to 3
Outputs:
- layer_out: bfloat16 [8192, 2048], P(('dp', 'tensor'))
- grad_tokens: bfloat16 [8192, 2048], P(('dp', 'tensor'))
- grad_ln1_gain: float32 [2048], P(('dp', 'tensor'))
- grad_ln1_bias: float32 [2048], P(('dp', 'tensor'))
- grad_qkv_weight: float32 [3, 2048, 2048], P(None, 'dp', 'tensor')
- grad_qv_bias: float32 [2, 2048], P(None, ('tensor', 'dp'))
- grad_out_weight: float32 [2048, 2048], P('tensor', 'dp')
- grad_out_bias: float32 [2048], P(('dp', 'tensor'))
- grad_ln2_gain: float32 [2048], P(('dp', 'tensor'))
- grad_ln2_bias: float32 [2048], P(('dp', 'tensor'))
- grad_up_weight: float32 [2048, 8192], P('dp', 'tensor')
- grad_up_bias: float32 [8192], P(('tensor', 'dp'))
- grad_down_weight: float32 [8192, 2048], P('tensor', 'dp')
- grad_down_bias: float32 [2048], P(('dp', 'tensor'))
All inputs are finite; a program needn't handle non-finite values.
Results may differ from a plain program's by a relative error of at most 0.012.
Values may be sent and summed in bfloat16 or wider, within the bound.
A program may use at most 192 MiB of HBM per device.

v0:
```python
import jax
import jax.numpy as jnp
from jax import lax
from jax.sharding import PartitionSpec as P

HD = 128
LEN = 1024
SEQS = 1


EPS = 1e-05


def layer_norm(row_block, scale_vec, shift_vec):
    row_mean = jnp.mean(row_block, axis=-1, keepdims=True)
    centred = row_block - row_mean
    variance = jnp.mean(centred * centred, axis=-1, keepdims=True)
    inverse = lax.rsqrt(variance + EPS)
    normal_rows = centred * inverse
    return (normal_rows * scale_vec + shift_vec, normal_rows, inverse)


def norm_back(grad_rows, normal_rows, inverse, scale_vec):
    scaled = grad_rows * scale_vec
    first_mean = jnp.mean(scaled, axis=-1, keepdims=True)
    second_mean = jnp.mean(scaled * normal_rows, axis=-1, keepdims=True)
    return inverse * (scaled - first_mean - normal_rows * second_mean)


def masked_scores(queries, key_rows):
    positions = jnp.arange(LEN)
    causal = positions[:, None] >= positions[None, :]
    scores = jnp.einsum(
        "qhd,khd->hqk", queries, key_rows, preferred_element_type=jnp.float32
    ) * HD ** (-0.5)
    return jnp.where(causal[None], scores, -1e30)


def attend(inputs):
    queries, key_rows, value_rows = inputs
    scores = masked_scores(queries, key_rows)
    row_top = jnp.max(scores, axis=-1, keepdims=True)
    exponent = jnp.exp(scores - row_top)
    row_total = jnp.sum(exponent, axis=-1, keepdims=True)
    attention = (exponent / row_total).astype(jnp.bfloat16)
    mixture = jnp.einsum("hqk,khd->qhd", attention, value_rows, preferred_element_type=jnp.float32)
    return (mixture.astype(jnp.bfloat16), row_top + jnp.log(row_total))


def attend_back(inputs):
    queries, key_rows, value_rows, log_total, grad_mix = inputs
    factor = HD ** (-0.5)
    attention = jnp.exp(masked_scores(queries, key_rows) - log_total)
    grad_value = jnp.einsum(
        "hqk,qhd->khd", attention.astype(jnp.bfloat16), grad_mix, preferred_element_type=jnp.float32
    )
    grad_attn = jnp.einsum("qhd,khd->hqk", grad_mix, value_rows, preferred_element_type=jnp.float32)
    inner = jnp.sum(attention * grad_attn, axis=-1, keepdims=True)
    grad_scores = (attention * (grad_attn - inner)).astype(jnp.bfloat16)
    grad_query = (
        jnp.einsum("hqk,khd->qhd", grad_scores, key_rows, preferred_element_type=jnp.float32)
        * factor
    )
    grad_key = (
        jnp.einsum("hqk,qhd->khd", grad_scores, queries, preferred_element_type=jnp.float32)
        * factor
    )
    return (
        grad_query.astype(jnp.bfloat16),
        grad_key.astype(jnp.bfloat16),
        grad_value.astype(jnp.bfloat16),
    )


def gelu_exact(preact):
    return jax.nn.gelu(preact, approximate=False)


def body(
    tokens,
    cotangent,
    ln1_gain,
    ln1_bias,
    qkv_weight,
    qv_bias,
    out_weight,
    out_bias,
    ln2_gain,
    ln2_bias,
    up_weight,
    up_bias,
    down_weight,
    down_bias,
):
    vectors = (
        lax.all_gather(ln1_gain, ("dp", "tensor"), axis=0, tiled=True),
        lax.all_gather(ln1_bias, ("dp", "tensor"), axis=0, tiled=True),
        lax.all_gather(out_bias, ("dp", "tensor"), axis=0, tiled=True),
        lax.all_gather(ln2_gain, ("dp", "tensor"), axis=0, tiled=True),
        lax.all_gather(ln2_bias, ("dp", "tensor"), axis=0, tiled=True),
        lax.all_gather(down_bias, ("dp", "tensor"), axis=0, tiled=True),
    )
    gain_one, shift_one, bias_out, gain_two, shift_two, bias_down = [
        vector.astype(jnp.float32) for vector in vectors
    ]
    w_qkv, bias_qv, w_out, w_up, bias_up, w_down = (
        lax.all_gather(qkv_weight, "dp", axis=1, tiled=True),
        lax.all_gather(qv_bias, "dp", axis=1, tiled=True),
        lax.all_gather(out_weight, "dp", axis=1, tiled=True),
        lax.all_gather(up_weight, "dp", axis=0, tiled=True),
        lax.all_gather(up_bias, "dp", axis=0, tiled=True),
        lax.all_gather(down_weight, "dp", axis=1, tiled=True),
    )
    bias_qv = bias_qv.astype(jnp.float32)
    bias_up = bias_up.astype(jnp.float32)
    rows_all = SEQS * LEN
    width_local = w_qkv.shape[2]
    head_shape = (SEQS, LEN, width_local // HD, HD)
    rows_in = tokens.astype(jnp.float32)
    normed_one, normal_one, inverse_one = layer_norm(rows_in, gain_one, shift_one)
    attn_in = lax.all_gather(normed_one.astype(jnp.bfloat16), "tensor", axis=0, tiled=True)
    projected = jnp.einsum("rd,kde->kre", attn_in, w_qkv, preferred_element_type=jnp.float32)
    queries = (projected[0] + bias_qv[0]).astype(jnp.bfloat16).reshape(head_shape)
    key_rows = projected[1].astype(jnp.bfloat16).reshape(head_shape)
    value_rows = (projected[2] + bias_qv[1]).astype(jnp.bfloat16).reshape(head_shape)
    mixture, log_totals = lax.map(attend, (queries, key_rows, value_rows))
    mixture = mixture.reshape(rows_all, width_local)
    attn_part = jnp.dot(mixture, w_out, preferred_element_type=jnp.float32)
    residual = rows_in + (
        lax.psum_scatter(attn_part, "tensor", scatter_dimension=0, tiled=True) + bias_out
    )
    normed_two, normal_two, inverse_two = layer_norm(residual, gain_two, shift_two)
    mlp_in = lax.all_gather(normed_two.astype(jnp.bfloat16), "tensor", axis=0, tiled=True)
    preact = jnp.dot(mlp_in, w_up, preferred_element_type=jnp.float32) + bias_up
    hidden = gelu_exact(preact).astype(jnp.bfloat16)
    mlp_part = jnp.dot(hidden, w_down, preferred_element_type=jnp.float32)
    layer_out = (
        residual
        + (lax.psum_scatter(mlp_part, "tensor", scatter_dimension=0, tiled=True) + bias_down)
    ).astype(jnp.bfloat16)
    grad_out = cotangent.astype(jnp.float32)
    down_cot = lax.all_gather(cotangent, "tensor", axis=0, tiled=True)
    grad_down_w = jnp.einsum("rf,rd->fd", hidden, down_cot, preferred_element_type=jnp.float32)
    grad_hidden = jnp.einsum("rd,fd->rf", down_cot, w_down, preferred_element_type=jnp.float32)
    ignored, gelu_pullback = jax.vjp(gelu_exact, preact)
    grad_pre = gelu_pullback(grad_hidden)[0].astype(jnp.bfloat16)
    grad_up_w = jnp.einsum("rd,rf->df", mlp_in, grad_pre, preferred_element_type=jnp.float32)
    grad_up_b = jnp.sum(grad_pre.astype(jnp.float32), axis=0)
    mlp_back = jnp.einsum("rf,df->rd", grad_pre, w_up, preferred_element_type=jnp.float32)
    grad_normed_two = lax.psum_scatter(mlp_back, "tensor", scatter_dimension=0, tiled=True)
    grad_resid = grad_out + norm_back(grad_normed_two, normal_two, inverse_two, gain_two)
    branch_cot = grad_resid.astype(jnp.bfloat16)
    attn_cot = lax.all_gather(branch_cot, "tensor", axis=0, tiled=True)
    grad_out_w = jnp.einsum("re,rd->ed", mixture, attn_cot, preferred_element_type=jnp.float32)
    grad_mix = jnp.einsum("rd,ed->re", attn_cot, w_out, preferred_element_type=jnp.float32).astype(
        jnp.bfloat16
    )
    grad_query, grad_key, grad_value = lax.map(
        attend_back, (queries, key_rows, value_rows, log_totals, grad_mix.reshape(head_shape))
    )
    grad_qkv = jnp.stack((grad_query, grad_key, grad_value)).reshape(3, rows_all, width_local)
    grad_qkv_w = jnp.einsum("rd,kre->kde", attn_in, grad_qkv, preferred_element_type=jnp.float32)
    grad_qv_b = jnp.sum(grad_qkv[0::2].astype(jnp.float32), axis=1)
    attn_back = jnp.einsum("kre,kde->rd", grad_qkv, w_qkv, preferred_element_type=jnp.float32)
    grad_normed_one = lax.psum_scatter(attn_back, "tensor", scatter_dimension=0, tiled=True)
    grad_tokens = (
        grad_resid + norm_back(grad_normed_one, normal_one, inverse_one, gain_one)
    ).astype(jnp.bfloat16)
    vector_grads = (
        lax.psum_scatter(
            jnp.sum(grad_normed_one * normal_one, axis=0),
            ("dp", "tensor"),
            scatter_dimension=0,
            tiled=True,
        ),
        lax.psum_scatter(
            jnp.sum(grad_normed_one, axis=0), ("dp", "tensor"), scatter_dimension=0, tiled=True
        ),
        lax.psum_scatter(
            jnp.sum(branch_cot.astype(jnp.float32), axis=0),
            ("dp", "tensor"),
            scatter_dimension=0,
            tiled=True,
        ),
        lax.psum_scatter(
            jnp.sum(grad_normed_two * normal_two, axis=0),
            ("dp", "tensor"),
            scatter_dimension=0,
            tiled=True,
        ),
        lax.psum_scatter(
            jnp.sum(grad_normed_two, axis=0), ("dp", "tensor"), scatter_dimension=0, tiled=True
        ),
        lax.psum_scatter(
            jnp.sum(grad_out, axis=0), ("dp", "tensor"), scatter_dimension=0, tiled=True
        ),
    )
    grad_qkv_w, grad_qv_b, grad_out_w, grad_up_w, grad_up_b, grad_down_w = (
        lax.psum_scatter(grad_qkv_w, "dp", scatter_dimension=1, tiled=True),
        lax.psum_scatter(grad_qv_b, "dp", scatter_dimension=1, tiled=True),
        lax.psum_scatter(grad_out_w, "dp", scatter_dimension=1, tiled=True),
        lax.psum_scatter(grad_up_w, "dp", scatter_dimension=0, tiled=True),
        lax.psum_scatter(grad_up_b, "dp", scatter_dimension=0, tiled=True),
        lax.psum_scatter(grad_down_w, "dp", scatter_dimension=1, tiled=True),
    )
    return (
        layer_out,
        grad_tokens,
        vector_grads[0],
        vector_grads[1],
        grad_qkv_w,
        grad_qv_b,
        grad_out_w,
        vector_grads[2],
        vector_grads[3],
        vector_grads[4],
        grad_up_w,
        grad_up_b,
        grad_down_w,
        vector_grads[5],
    )


def solution(mesh):
    in_specs = (
        P(("dp", "tensor"), None),
        P(("dp", "tensor"), None),
        P(("dp", "tensor")),
        P(("dp", "tensor")),
        P(None, "dp", "tensor"),
        P(None, ("tensor", "dp")),
        P("tensor", "dp"),
        P(("dp", "tensor")),
        P(("dp", "tensor")),
        P(("dp", "tensor")),
        P("dp", "tensor"),
        P(("tensor", "dp")),
        P("tensor", "dp"),
        P(("dp", "tensor")),
    )
    out_specs = (
        P(("dp", "tensor"), None),
        P(("dp", "tensor"), None),
        P(("dp", "tensor")),
        P(("dp", "tensor")),
        P(None, "dp", "tensor"),
        P(None, ("tensor", "dp")),
        P("tensor", "dp"),
        P(("dp", "tensor")),
        P(("dp", "tensor")),
        P(("dp", "tensor")),
        P("dp", "tensor"),
        P(("tensor", "dp")),
        P("tensor", "dp"),
        P(("dp", "tensor")),
    )
    return jax.shard_map(body, mesh=mesh, in_specs=in_specs, out_specs=out_specs, check_vma=False)
```

profile of v0, /device:TPU:0, one launch (start us, length us, event | category | flops | bytes accessed | tf_op | source)
XLA Modules:
  0.0 1717.2 jit_solution(16901120449746523394)
XLA Ops:
  12.4 42.6 %all-reduce.14 = (bf16[2048]{0:T(1024)(128)(2,1)S(1)}, bf16[2048]{0:T(1024)(128)(2,1)S(1)}, bf16[2048]{0:T(1024)(128)(2,1)S(1)}, bf16[2048]{0:T(1024)(128)(2,1)S...) all-reduce(bf16[2048]{0:T(1024)(128)(2,1)S(1)} %dynamic-update-slic, ...), channel_id=1, replica_groups=mesh['dp'=8,'tensor'=4] {'dp','tensor'}, use_global_device_ids=true, to_apply=%add.1 | all-reduce | flops 12288 | bytes 49152
  58.7 2.7 fusion.25
  64.7 10.1 all-gather
  74.9 67.2 %all-gather.11.cloned.1.call-done = bf16[1024,2048]{1,0:T(8,128)(2,1)} async-done(((bf16[256,2048]{1,0:T(8,128)(2,1)}), bf16[1024,2048]{1,0:T(8,128)(2,1)}) %all-gather.11.cloned.1.call-update) | async-done | bytes 4194320 | tf_op jit(solution)/shard_map/all_gather | solution.py:121
  142.1 47.5 %all-gather.13.cloned.1.call-done = bf16[3,2048,512]{1,2,0:T(8,128)(2,1)} async-done(((bf16[3,256,512]{1,2,0:T(8,128)(2,1)}), bf16[3,2048,512]{1,2,0:T(8,128)(2,1)}) %all-gather.13.cloned.1.call-update) | async-done | bytes 6291472 | tf_op jit(solution)/shard_map/all_gather | solution.py:107
  189.6 10.1 fusion.15
  201.6 3.8 copy.80
  205.5 8.7 fusion.42
  214.2 8.3 fusion
  223.1 7.6 fusion.33
  230.8 7.6 fusion.43
  239.2 144.1 %reduce-scatter.12.cloned.1.call-done = f32[256,2048]{1,0:T(8,128)} async-done(((f32[1024,2048]{1,0:T(8,128)}), f32[256,2048]{1,0:T(8,128)}) %reduce-scatter.12.cloned.1.call-update) | async-done | bytes 2097168 | tf_op jit(solution)/shard_map/reduce_scatter | solution.py:130
  390.2 9.0 all-gather.1
  399.3 40.7 %all-gather.19.cloned.1.call-done = bf16[2048,2048]{1,0:T(8,128)(2,1)} async-done(((bf16[256,2048]{1,0:T(8,128)(2,1)}), bf16[2048,2048]{1,0:T(8,128)(2,1)}) %all-gather.19.cloned.1.call-update) | async-done | bytes 8388624 | tf_op jit(solution)/shard_map/all_gather | solution.py:110
  440.0 82.8 %all-gather.17.cloned.1.call-done = bf16[1024,2048]{1,0:T(8,128)(2,1)} async-done(((bf16[256,2048]{1,0:T(8,128)(2,1)}), bf16[1024,2048]{1,0:T(8,128)(2,1)}) %all-gather.17.cloned.1.call-update) | async-done | bytes 4194320 | tf_op jit(solution)/shard_map/all_gather | solution.py:133
  522.7 14.4 fusion.44
  537.2 66.4 %all-gather.23.cloned.1.call-done = bf16[1024,2048]{1,0:T(8,128)(2,1)} async-done(((bf16[256,2048]{1,0:T(8,128)(2,1)}), bf16[1024,2048]{1,0:T(8,128)(2,1)}) %all-gather.23.cloned.1.call-update) | async-done | bytes 4194320 | tf_op jit(solution)/shard_map/all_gather | solution.py:142
  603.6 56.3 %all-gather.21.cloned.1.call-done = bf16[2048,2048]{1,0:T(8,128)(2,1)} async-done(((bf16[2048,256]{1,0:T(8,128)(2,1)}), bf16[2048,2048]{1,0:T(8,128)(2,1)}) %all-gather.21.cloned.1.call-update) | async-done | bytes 8388624 | tf_op jit(solution)/shard_map/all_gather | solution.py:112
  659.8 33.7 %convert_reduce_fusion = (f32[2048]{0:T(1024)}, bf16[1024,2048]{1,0:T(8,128)(2,1)S(1)}, f32[1024,2048]{1,0:T(8,128)}) fusion(f32[1024,2048]{1,0:T(8,128)} %fusion.44, f32[2048]{0:T(1024)S(1)} %bitcast.80, bf16[1024,2048]{1,0:T(8,128)(2,1)} %all-gather.23.cloned.1.call-done, bf16[2048,2048]{1,0:T(8,128)(2,1)} %all-gather.21.cloned.1.call-done), kind=kOutput, calls=%fused_computation.11 | convolution fusion | flops 8747218944 | bytes 33570816 | tf_op jit(solution)/shard_map/rd,fd->rf/dot_general | solution.py:144
  695.5 11.3 fusion.46
  706.9 8.0 multiply_convert_fusion.1
  717.0 13.2 fusion.45
  730.9 120.7 %reduce-scatter.16.cloned.1.call-done = f32[256,2048]{1,0:T(8,128)} async-done(((f32[1024,2048]{1,0:T(8,128)}), f32[256,2048]{1,0:T(8,128)}) %reduce-scatter.16.cloned.1.call-update) | async-done | bytes 2097168 | tf_op jit(solution)/shard_map/reduce_scatter | solution.py:150
  851.6 3.1 multiply_reduce_fusion.1
  854.7 144.3 %reduce-scatter.14.cloned.1.call-done = f32[256,2048]{1,0:T(8,128)} async-done(((f32[1024,2048]{1,0:T(8,128)}), f32[256,2048]{1,0:T(8,128)}) %reduce-scatter.14.cloned.1.call-update) | async-done | bytes 2097168 | tf_op jit(solution)/shard_map/reduce_scatter | solution.py:139
  999.0 6.4 convert_reduce_fusion.4
  1006.0 81.0 %all-gather.25.cloned.1.call-done = bf16[1024,2048]{1,0:T(8,128)(2,1)} async-done(((bf16[256,2048]{1,0:T(8,128)(2,1)}), bf16[1024,2048]{1,0:T(8,128)(2,1)}) %all-gather.25.cloned.1.call-update) | async-done | bytes 4194320 | tf_op jit(solution)/shard_map/all_gather | solution.py:153
  1087.0 5.2 convolution_convert_fusion
  1092.2 11.0 multiply_reduce_fusion
  1103.3 12.1 multiply_convert_fusion
  1115.4 4.2 copy-done
  1121.6 7.5 multiply_convert_fusion.2
  1129.1 5.2 fusion.34
  1139.7 10.8 convolution_bitcast_fusion.1
  1150.6 12.0 convolution_bitcast_fusion
  1162.7 15.2 fusion.48
  1178.2 16.0 fusion.49
  1195.4 6.5 fusion.47
  1203.8 13.8 all-reduce.11
  1219.7 99.1 %reduce-scatter.18.cloned.1.call-done = f32[256,2048]{1,0:T(8,128)} async-done(((f32[1024,2048]{1,0:T(8,128)}), f32[256,2048]{1,0:T(8,128)}) %reduce-scatter.18.cloned.1.call-update) | async-done | bytes 2097168 | tf_op jit(solution)/shard_map/reduce_scatter | solution.py:165
  1318.8 2.7 fusion.31
  1321.5 42.1 %all-reduce.13 = (f32[2048]{0:T(1024)S(1)}, f32[2048]{0:T(1024)S(1)}, f32[2048]{0:T(1024)S(1)}, f32[2048]{0:T(1024)S(1)}, f32[2048]{0:T(1024)S(1)}, /*index=5*/f32[2048]{0:T(1024)S(1)}) all-reduce(f32[2048]{0:T(1024)S(1)} %get-tuple-element.117, ...), channel_id=6, replica_groups=mesh['dp'=8,'tensor'=4] {'dp','tensor'}, use_global_device_ids=true, to_apply=%region_16.17.clone | all-reduce | flops 12288 | bytes 98304
  1367.2 3.5 fusion.30
  1370.7 44.6 %reduce-scatter.20.cloned.1.call-done = f32[3,256,512]{1,2,0:T(8,128)} async-done(((f32[3,2048,512]{1,2,0:T(8,128)}), f32[3,256,512]{1,2,0:T(8,128)}) %reduce-scatter.20.cloned.1.call-update) | async-done | bytes 1572880 | tf_op jit(solution)/shard_map/reduce_scatter | solution.py:199
  1415.3 3.0 copy.94
  1418.4 117.2 %reduce-scatter.24.cloned.1.call-done = f32[256,2048]{1,0:T(8,128)} async-done(((f32[2048,2048]{1,0:T(8,128)}), f32[256,2048]{1,0:T(8,128)}) %reduce-scatter.24.cloned.1.call-update) | async-done | bytes 2097168 | tf_op jit(solution)/shard_map/reduce_scatter | solution.py:202
  1535.6 120.0 %reduce-scatter.26.cloned.1.call-done = f32[2048,256]{1,0:T(8,128)} async-done(((f32[2048,2048]{1,0:T(8,128)}), f32[2048,256]{1,0:T(8,128)}) %reduce-scatter.26.cloned.1.call-update) | async-done | bytes 2097168 | tf_op jit(solution)/shard_map/reduce_scatter | solution.py:204
  1655.6 54.9 %reduce-scatter.22.cloned.1.call-done = f32[512,256]{1,0:T(8,128)} async-done(((f32[512,2048]{1,0:T(8,128)}), f32[512,256]{1,0:T(8,128)}) %reduce-scatter.22.cloned.1.call-update) | async-done | bytes 524304 | tf_op jit(solution)/shard_map/reduce_scatter | solution.py:201
  (198 shorter events, 43.2 us)
Async XLA Ops:
  7.2 54.3 %copy-start.15 = (bf16[3,256,512]{2,1,0:T(8,128)(2,1)S(1)}, bf16[3,256,512]{2,1,0:T(8,128)(2,1)}, u32[]{:S(2)}) copy-start(bf16[3,256,512]{2,1,0:T(8,128)(2,1)} %param.18) | copy-start | bytes 2359300
  7.2 134.9 %all-gather.11.cloned.1.call-start = ((), (), s32[]{:S(2)}) async-start(), calls=%async_computation.9 | async-start | bytes 5242880 | tf_op jit(solution)/shard_map/all_gather | solution.py:121
  61.4 128.2 %all-gather.13.cloned.1.call-start = ((), (), s32[]{:S(2)}) async-start(), calls=%async_computation.10 | async-start | bytes 7077888 | tf_op jit(solution)/shard_map/all_gather | solution.py:107
  62.7 168.1 %all-gather.15.cloned.1.call-start = ((), (), s32[]{:S(2)}) async-start(), calls=%async_computation.11 | async-start | bytes 2359296 | tf_op jit(solution)/shard_map/all_gather | solution.py:109
  63.4 320.0 %reduce-scatter.12.cloned.1.call-start = ((), (), s32[]{:S(2)}) async-start(), calls=%async_computation.12 | async-start | bytes 10485760 | tf_op jit(solution)/shard_map/reduce_scatter | solution.py:130
  74.9 130.6 %copy-start.32 = (f32[1,512]{1,0:T(1,128)}, f32[1,512]{1,0:T(1,128)S(1)}, u32[]{:S(2)}) copy-start(f32[1,512]{1,0:T(1,128)S(1)} %get-tuple-element.148) | copy-start | bytes 6148
  74.9 147.6 %copy-start.38 = (f32[1,512]{1,0:T(1,128)}, f32[1,512]{1,0:T(1,128)S(1)}, u32[]{:S(2)}) copy-start(f32[1,512]{1,0:T(1,128)S(1)} %get-tuple-element.147) | copy-start | bytes 6148
  201.5 12.7 copy-start.5
  201.6 12.5 copy-start.7
  214.1 8.9 copy-start.10
  238.4 145.0 %copy-start.3 = (bf16[256,2048]{1,0:T(8,128)(2,1)S(1)}, bf16[256,2048]{1,0:T(8,128)(2,1)}, u32[]{:S(2)}) copy-start(bf16[256,2048]{1,0:T(8,128)(2,1)} %param.14) | copy-start | bytes 3145732
  238.4 201.6 %all-gather.19.cloned.1.call-start = ((), (), s32[]{:S(2)}) async-start(), calls=%async_computation.14 | async-start | bytes 9437184 | tf_op jit(solution)/shard_map/all_gather | solution.py:110
  239.0 283.8 %all-gather.17.cloned.1.call-start = ((), (), s32[]{:S(2)}) async-start(), calls=%async_computation.13 | async-start | bytes 5242880 | tf_op jit(solution)/shard_map/all_gather | solution.py:133
  239.2 149.4 %copy-start.21 = (f32[2048]{0:T(1024)}, f32[2048]{0:T(1024)S(1)}, u32[]{:S(2)}) copy-start(f32[2048]{0:T(1024)S(1)} %convert_element_type.128) | copy-start | bytes 24580
  388.6 214.9 %all-gather.23.cloned.1.call-start = ((), (), s32[]{:S(2)}) async-start(), calls=%async_computation.17 | async-start | bytes 5242880 | tf_op jit(solution)/shard_map/all_gather | solution.py:142
  389.4 270.4 %all-gather.21.cloned.1.call-start = ((), (), s32[]{:S(2)}) async-start(), calls=%async_computation.15 | async-start | bytes 9437184 | tf_op jit(solution)/shard_map/all_gather | solution.py:112
  390.1 461.5 %reduce-scatter.16.cloned.1.call-start = ((), (), s32[]{:S(2)}) async-start(), calls=%async_computation.18 | async-start | bytes 10485760 | tf_op jit(solution)/shard_map/reduce_scatter | solution.py:150
  659.8 35.7 %copy-start.43 = (bf16[2048,2048]{1,0:T(8,128)(2,1)S(1)}, bf16[2048,2048]{1,0:T(8,128)(2,1)}, u32[]{:S(2)}) copy-start(bf16[2048,2048]{1,0:T(8,128)(2,1)} %all-gather.19.cloned.1.call-done) | copy-start | bytes 25165828
  706.8 292.2 %reduce-scatter.14.cloned.1.call-start = ((), (), s32[]{:S(2)}) async-start(), calls=%async_computation.16 | async-start | bytes 10485760 | tf_op jit(solution)/shard_map/reduce_scatter | solution.py:139
  730.2 121.4 %copy-start.2 = (f32[256,2048]{1,0:T(8,128)S(1)}, f32[256,2048]{1,0:T(8,128)}, u32[]{:S(2)}) copy-start(f32[256,2048]{1,0:T(8,128)} %copy-done.1) | copy-start | bytes 6291460
  730.2 121.4 %copy-start.22 = (f32[2048]{0:T(1024)S(1)}, f32[2048]{0:T(1024)}, u32[]{:S(2)}) copy-start(f32[2048]{0:T(1024)} %copy-done.21) | copy-start | bytes 24580
  730.2 121.4 %copy-start.31 = (f32[256]{0:T(256)S(1)}, f32[256]{0:T(256)}, u32[]{:S(2)}) copy-start(f32[256]{0:T(256)} %copy-done.30) | copy-start | bytes 3076
  730.2 121.4 %copy-start.37 = (f32[256]{0:T(256)S(1)}, f32[256]{0:T(256)}, u32[]{:S(2)}) copy-start(f32[256]{0:T(256)} %copy-done.36) | copy-start | bytes 3076
  730.2 268.8 %copy-start.13 = (bf16[256,2048]{1,0:T(8,128)(2,1)S(1)}, bf16[256,2048]{1,0:T(8,128)(2,1)}, u32[]{:S(2)}) copy-start(bf16[256,2048]{1,0:T(8,128)(2,1)} %param.15) | copy-start | bytes 3145732
  730.2 356.7 %all-gather.25.cloned.1.call-start = ((), (), s32[]{:S(2)}) async-start(), calls=%async_computation.19 | async-start | bytes 5242880 | tf_op jit(solution)/shard_map/all_gather | solution.py:153
  1005.4 212.9 %reduce-scatter.28.cloned.1.call-start = ((), (), s32[]{:S(2)}) async-start(), calls=%async_computation.25 | async-start | bytes 294912
  1005.9 97.3 %copy-start.16 = (f32[4,1024]{1,0:T(4,128)}, f32[4,1024]{1,0:T(4,128)S(1)}, u32[]{:S(2)}) copy-start(f32[4,1024]{1,0:T(4,128)S(1)} %log_add_fusion) | copy-start | bytes 49156
  1006.0 86.3 %copy-start.11 = (f32[1024,4,128]{2,0,1:T(8,128)S(1)}, f32[1024,4,128]{2,0,1:T(8,128)}, u32[]{:S(2)}) copy-start(f32[1024,4,128]{2,0,1:T(8,128)} %copy.80) | copy-start | bytes 6291460
  1006.0 86.3 %copy-start.39 = (f32[1,512]{1,0:T(1,128)S(1)}, f32[1,512]{1,0:T(1,128)}, u32[]{:S(2)}) copy-start(f32[1,512]{1,0:T(1,128)} %copy-done.38) | copy-start | bytes 6148
  1092.2 11.0 copy-start.14
  1103.2 16.4 copy-start.8
  1103.2 25.8 %slice-start = ((s8[16777216]{0:T(1024)(128)(4,1)}), s8[4194304]{0:T(1024)(128)(4,1)S(1)}, s32[]{:S(2)}) async-start(s8[16777216]{0:T(1024)(128)(4,1)} %bitcast.67), calls=%async_computation.26 | async-start | bytes 8388608
  1103.3 25.8 %slice-start.1 = ((s8[16777216]{0:T(1024)(128)(4,1)}), s8[4194304]{0:T(1024)(128)(4,1)S(1)}, s32[]{:S(2)}) async-start(s8[16777216]{0:T(1024)(128)(4,1)} %bitcast.67), calls=%async_computation.27 | async-start | bytes 8388608
  1103.3 25.8 %slice-start.2 = ((s8[16777216]{0:T(1024)(128)(4,1)}), s8[4194304]{0:T(1024)(128)(4,1)S(1)}, s32[]{:S(2)}) async-start(s8[16777216]{0:T(1024)(128)(4,1)} %bitcast.67), calls=%async_computation.28 | async-start | bytes 8388608
  1119.7 9.4 slice-start.3
  1139.5 179.3 %reduce-scatter.18.cloned.1.call-start = ((), (), s32[]{:S(2)}) async-start(), calls=%async_computation.20 | async-start | bytes 10485760 | tf_op jit(solution)/shard_map/reduce_scatter | solution.py:165
  1150.5 264.8 %reduce-scatter.20.cloned.1.call-start = ((), (), s32[]{:S(2)}) async-start(), calls=%async_computation.21 | async-start | bytes 14155776 | tf_op jit(solution)/shard_map/reduce_scatter | solution.py:199
  1162.6 372.9 %reduce-scatter.24.cloned.1.call-start = ((), (), s32[]{:S(2)}) async-start(), calls=%async_computation.23 | async-start | bytes 18874368 | tf_op jit(solution)/shard_map/reduce_scatter | solution.py:202
  1177.9 477.6 %reduce-scatter.26.cloned.1.call-start = ((), (), s32[]{:S(2)}) async-start(), calls=%async_computation.24 | async-start | bytes 18874368 | tf_op jit(solution)/shard_map/reduce_scatter | solution.py:204
  1194.2 516.2 %reduce-scatter.22.cloned.1.call-start = ((), (), s32[]{:S(2)}) async-start(), calls=%async_computation.22 | async-start | bytes 4718592 | tf_op jit(solution)/shard_map/reduce_scatter | solution.py:201
  1201.9 116.8 %copy-start.4 = (bf16[256,2048]{1,0:T(8,128)(2,1)S(1)}, bf16[256,2048]{1,0:T(8,128)(2,1)}, u32[]{:S(2)}) copy-start(bf16[256,2048]{1,0:T(8,128)(2,1)} %param.14) | copy-start | bytes 3145732
  1201.9 116.8 %copy-start.20 = (f32[2048]{0:T(1024)S(1)}, f32[2048]{0:T(1024)}, u32[]{:S(2)}) copy-start(f32[2048]{0:T(1024)} %copy-done.19) | copy-start | bytes 24580
  1202.0 116.8 %copy-start.29 = (f32[256]{0:T(256)S(1)}, f32[256]{0:T(256)}, u32[]{:S(2)}) copy-start(f32[256]{0:T(256)} %copy-done.28) | copy-start | bytes 3076
  1202.0 116.8 %copy-start.35 = (f32[256]{0:T(256)S(1)}, f32[256]{0:T(256)}, u32[]{:S(2)}) copy-start(f32[256]{0:T(256)} %copy-done.34) | copy-start | bytes 3076
  1202.0 119.5 %copy-start.25 = (f32[2048]{0:T(1024)S(1)}, f32[2048]{0:T(1024)}, u32[]{:S(2)}) copy-start(f32[2048]{0:T(1024)} %get-tuple-element.121) | copy-start | bytes 24580
  1202.0 119.5 %copy-start.26 = (f32[2048]{0:T(1024)S(1)}, f32[2048]{0:T(1024)}, u32[]{:S(2)}) copy-start(f32[2048]{0:T(1024)} %get-tuple-element.138) | copy-start | bytes 24580
  1202.0 119.5 %copy-start.27 = (f32[2048]{0:T(1024)S(1)}, f32[2048]{0:T(1024)}, u32[]{:S(2)}) copy-start(f32[2048]{0:T(1024)} %get-tuple-element.146) | copy-start | bytes 24580
  1318.8 48.4 %copy-start.9 = (f32[256,2048]{1,0:T(8,128)S(1)}, f32[256,2048]{1,0:T(8,128)}, u32[]{:S(2)}) copy-start(f32[256,2048]{1,0:T(8,128)} %reduce-scatter.18.cloned.1.call-done) | copy-start | bytes 6291460
  (22 other events, 68.7 us)
Sparse Core Ops, SparseCore 0:
  61.5 80.5 all-gather.10
  144.6 45.0 all-gather.12
  191.5 28.0 all-gather.14
  238.5 144.7 reduce-scatter.11
  385.1 54.8 all-gather.18
  442.0 80.7 all-gather.16
  524.3 79.2 all-gather.22
  605.4 54.3 all-gather.20
  707.0 144.6 reduce-scatter.15
  853.8 145.1 reduce-scatter.13
  1005.6 81.3 all-gather.24
  1139.6 32.1 reduce-scatter.27
  1174.1 144.6 reduce-scatter.17
  1322.1 93.1 reduce-scatter.19
  1419.3 116.1 reduce-scatter.23
  1539.6 115.9 reduce-scatter.25
  1659.3 51.0 reduce-scatter.21
where the time goes:
time: 1720 us
  waiting for transfers between devices  1290 us (75%)
  matrix products  197 us (11%)
  blocking collectives  118 us (7%)
  other arithmetic  55.6 us (3%)
  local copies, waits for them, and re-layouts  39.7 us (2%)
    reduce_scatter x1, waiting for transfers between devices, body(): lax.psum_scatter(mlp_part, 'tensor', scatter_dimension=0, tiled=True)  144 us
    reduce_scatter x1, waiting for transfers between devices, body(): lax.psum_scatter(attn_part, 'tensor', scatter_dimension=0, tiled=True)  144 us
    reduce_scatter x1, waiting for transfers between devices, body(): lax.psum_scatter(mlp_back, 'tensor', scatter_dimension=0, tiled=True)  121 us
    reduce_scatter x1, waiting for transfers between devices, body(): lax.psum_scatter(grad_down_w, 'dp', scatter_dimension=1, tiled=True)  120 us
    reduce_scatter x1, waiting for transfers between devices, body(): lax.psum_scatter(grad_up_w, 'dp', scatter_dimension=0, tiled=True)  117 us
    reduce_scatter x1, waiting for transfers between devices, body(): lax.psum_scatter(attn_back, 'tensor', scatter_dimension=0, tiled=True)  99.1 us
    unnamed x3, blocking collectives  98.6 us
    all_gather x1, waiting for transfers between devices, body(): lax.all_gather(normed_two.astype(jnp.bfloat16), 'tensor', axis=0, tiled=T...  82.8 us
  transfers between devices with their start and end apart: 17, of which 15 were waited for; matrix products, arithmetic and copies ran while one was open for 9% of the time, Pallas kernels for 0%

commit v1 on v0

v1 whole, which is shorter than its diff:
```python
import jax
import jax.numpy as jnp
from jax import lax
from jax.sharding import PartitionSpec as P

HD = 128
LEN = 1024
EPS = 1e-05
BF = jnp.bfloat16
F32 = jnp.float32


def norm_stats(rows):
    mean = jnp.mean(rows, axis=-1, keepdims=True)
    centred = rows - mean
    variance = jnp.mean(centred * centred, axis=-1, keepdims=True)
    inverse = lax.rsqrt(variance + EPS)
    return centred * inverse, inverse


def norm_back(grad_rows, normal_rows, inverse, gain):
    scaled = grad_rows * gain
    first = jnp.mean(scaled, axis=-1, keepdims=True)
    second = jnp.mean(scaled * normal_rows, axis=-1, keepdims=True)
    return inverse * (scaled - first - normal_rows * second)


def masked_scores(queries, key_rows, positions):
    causal = positions[:, None] >= positions[None, :]
    scores = jnp.einsum("qhd,khd->hqk", queries, key_rows, preferred_element_type=F32) * HD ** (-0.5)
    return jnp.where(causal[None], scores, -1e30)


def attend(queries, key_rows, value_rows, positions):
    scores = masked_scores(queries, key_rows, positions)
    row_top = jnp.max(scores, axis=-1, keepdims=True)
    exponent = jnp.exp(scores - row_top)
    row_total = jnp.sum(exponent, axis=-1, keepdims=True)
    attention = (exponent / row_total).astype(BF)
    mixture = jnp.einsum("hqk,khd->qhd", attention, value_rows, preferred_element_type=F32)
    return mixture.astype(BF), row_top + jnp.log(row_total)


def attend_back(queries, key_rows, value_rows, log_total, grad_mix, positions):
    factor = HD ** (-0.5)
    attention = jnp.exp(masked_scores(queries, key_rows, positions) - log_total)
    grad_value = jnp.einsum("hqk,qhd->khd", attention.astype(BF), grad_mix, preferred_element_type=F32)
    grad_attn = jnp.einsum("qhd,khd->hqk", grad_mix, value_rows, preferred_element_type=F32)
    inner = jnp.sum(attention * grad_attn, axis=-1, keepdims=True)
    grad_scores = (attention * (grad_attn - inner)).astype(BF)
    grad_query = jnp.einsum("hqk,khd->qhd", grad_scores, key_rows, preferred_element_type=F32) * factor
    grad_key = jnp.einsum("hqk,qhd->khd", grad_scores, queries, preferred_element_type=F32) * factor
    return grad_query.astype(BF), grad_key.astype(BF), grad_value.astype(BF)


def gelu_exact(preact):
    return jax.nn.gelu(preact, approximate=False)


class Line:
    def __init__(self, axis, size):
        self.axis, self.n = axis, size
        self.i = lax.axis_index(axis)
        self.first = self.i < size // 2

    def owner(self, k):
        return jnp.where(self.first, self.i + k, self.i - k + self.n) % self.n

    def gather(self, block):
        n = self.n
        down, up = [block], [block]
        for r in range(1, n):
            down.append(lax.ppermute(down[-1], self.axis, [(i, i - 1) for i in range(1, n) if i + r - 1 <= n - 1]))
            up.append(lax.ppermute(up[-1], self.axis, [(i, i + 1) for i in range(n - 1) if i - r + 1 >= 0]))
        slots = [block]
        for k in range(1, n):
            if 2 * k <= n:
                slots.append(jnp.where(self.first, down[k], up[k]))
            else:
                low = jnp.where(self.i + k <= n - 1, down[k], up[n - k])
                high = jnp.where(self.i - k >= 0, up[k], down[n - k])
                slots.append(jnp.where(self.first, low, high))
        return slots

    def scatter_sum(self, parts):
        n = self.n
        right = left = None
        for r in range(1, n):
            term = jnp.where(self.first, parts[n - r], parts[r]).astype(F32)
            term = term if right is None else term + right.astype(F32)
            right = lax.ppermute(term.astype(BF), self.axis, [(i, i + 1) for i in range(min(r, n - 1))])
            term = jnp.where(self.first, parts[r], parts[n - r]).astype(F32)
            term = term if left is None else term + left.astype(F32)
            left = lax.ppermute(term.astype(BF), self.axis, [(i, i - 1) for i in range(max(n - r, 1), n)])
        return parts[0].astype(F32) + (right.astype(F32) + left.astype(F32))


def body(tokens, cotangent, ln1_gain, ln1_bias, qkv_weight, qv_bias, out_weight, out_bias, ln2_gain, ln2_bias,
         up_weight, up_bias, down_weight, down_bias):
    tp = lax.axis_size("tensor")
    dp = lax.axis_size("dp")
    line = Line("tensor", tp)
    rows = tokens.shape[0]
    width = qkv_weight.shape[2]
    heads = width // HD
    piece = ln1_gain.shape[0]

    own = jnp.concatenate([ln1_gain, ln1_bias, out_bias, ln2_gain, ln2_bias, down_bias, qv_bias.reshape(-1), up_bias])
    over_dp = lax.all_gather(own, "dp", axis=0)
    whole = lax.all_gather(over_dp[:, : 6 * piece], "tensor", axis=0)
    whole = whole.reshape(tp, dp, 6, piece).transpose(2, 1, 0, 3).reshape(6, -1).astype(F32)
    gain_one, shift_one, bias_out, gain_two, shift_two, bias_down = [whole[j] for j in range(6)]
    qv = qv_bias.shape[1]
    bias_qv = over_dp[:, 6 * piece : 6 * piece + 2 * qv].reshape(dp, 2, qv).transpose(1, 0, 2).reshape(2, -1).astype(F32)
    bias_up = over_dp[:, 6 * piece + 2 * qv :].reshape(-1).astype(F32)

    w_qkv = lax.all_gather(qkv_weight, "dp", axis=1, tiled=True)
    w_out = lax.all_gather(out_weight, "dp", axis=1, tiled=True)
    w_up = lax.all_gather(up_weight, "dp", axis=0, tiled=True)
    w_down = lax.all_gather(down_weight, "dp", axis=1, tiled=True)

    positions = jnp.concatenate([line.owner(k) * rows + jnp.arange(rows) for k in range(tp)])

    def split(array):
        return [array[k * rows : (k + 1) * rows] for k in range(tp)]

    rows_all = jnp.concatenate(line.gather(tokens), axis=0)
    cot_all = jnp.concatenate(line.gather(cotangent), axis=0)

    normal_all, inverse_all = norm_stats(rows_all.astype(F32))
    attn_in = (normal_all * gain_one + shift_one).astype(BF)
    projected = jnp.einsum("rd,kde->kre", attn_in, w_qkv, preferred_element_type=F32)
    head_shape = (LEN, heads, HD)
    queries = (projected[0] + bias_qv[0]).astype(BF).reshape(head_shape)
    key_rows = projected[1].astype(BF).reshape(head_shape)
    value_rows = (projected[2] + bias_qv[1]).astype(BF).reshape(head_shape)
    mixture, log_totals = attend(queries, key_rows, value_rows, positions)
    mixture = mixture.reshape(LEN, width)
    attn_part = jnp.dot(mixture, w_out, preferred_element_type=F32).astype(BF)
    rows_in = tokens.astype(F32)
    residual = rows_in + (line.scatter_sum(split(attn_part)) + bias_out)

    normal_two, inverse_two = norm_stats(residual)
    mlp_own = (normal_two * gain_two + shift_two).astype(BF)
    mlp_in = jnp.concatenate(line.gather(mlp_own), axis=0)
    preact = jnp.dot(mlp_in, w_up, preferred_element_type=F32) + bias_up
    hidden, gelu_pullback = jax.vjp(gelu_exact, preact)
    hidden = hidden.astype(BF)
    grad_hidden = jnp.einsum("rd,fd->rf", cot_all, w_down, preferred_element_type=F32)
    grad_pre = gelu_pullback(grad_hidden)[0].astype(BF)
    mlp_back = jnp.einsum("rf,df->rd", grad_pre, w_up, preferred_element_type=F32).astype(BF)
    grad_normed_two = line.scatter_sum(split(mlp_back))
    mlp_part = jnp.dot(hidden, w_down, preferred_element_type=F32).astype(BF)
    layer_out = (residual + (line.scatter_sum(split(mlp_part)) + bias_down)).astype(BF)

    grad_out = cotangent.astype(F32)
    grad_resid = grad_out + norm_back(grad_normed_two, normal_two, inverse_two, gain_two)
    branch_cot = grad_resid.astype(BF)
    attn_cot = jnp.concatenate(line.gather(branch_cot), axis=0)
    grad_mix = jnp.einsum("rd,ed->re", attn_cot, w_out, preferred_element_type=F32).astype(BF)
    grad_query, grad_key, grad_value = attend_back(
        queries, key_rows, value_rows, log_totals, grad_mix.reshape(head_shape), positions)
    grad_qkv = jnp.stack((grad_query, grad_key, grad_value)).reshape(3, LEN, width)
    attn_back = jnp.einsum("kre,kde->rd", grad_qkv, w_qkv, preferred_element_type=F32)
    grad_gain_one = jnp.sum(attn_back * normal_all, axis=0)
    grad_shift_one = jnp.sum(attn_back, axis=0)
    grad_normed_one = line.scatter_sum(split(attn_back.astype(BF)))
    grad_tokens = (grad_resid + norm_back(grad_normed_one, normal_all[:rows], inverse_all[:rows], gain_one)).astype(BF)

    grad_down_w = jnp.einsum("rf,rd->fd", hidden, cot_all, preferred_element_type=F32).astype(BF)
    grad_up_w = jnp.einsum("rd,rf->df", mlp_in, grad_pre, preferred_element_type=F32).astype(BF)
    grad_out_w = jnp.einsum("re,rd->ed", mixture, attn_cot, preferred_element_type=F32).astype(BF)
    grad_qkv_w = jnp.einsum("rd,kre->kde", attn_in, grad_qkv, preferred_element_type=F32).astype(BF)
    grad_down_w = lax.psum_scatter(grad_down_w, "dp", scatter_dimension=1, tiled=True).astype(F32)
    grad_up_w = lax.psum_scatter(grad_up_w, "dp", scatter_dimension=0, tiled=True).astype(F32)
    grad_out_w = lax.psum_scatter(grad_out_w, "dp", scatter_dimension=1, tiled=True).astype(F32)
    grad_qkv_w = lax.psum_scatter(grad_qkv_w, "dp", scatter_dimension=1, tiled=True).astype(F32)

    vectors = jnp.stack([
        grad_gain_one,
        grad_shift_one,
        jnp.sum(branch_cot.astype(F32), axis=0),
        jnp.sum(grad_normed_two * normal_two, axis=0),
        jnp.sum(grad_normed_two, axis=0),
        jnp.sum(grad_out, axis=0),
    ])
    vectors = vectors.reshape(6, dp, tp, piece).transpose(1, 2, 0, 3).reshape(dp, tp * 6 * piece)
    grad_qv_b = jnp.sum(grad_qkv[0::2].astype(F32), axis=1).reshape(2, dp, qv).transpose(1, 0, 2).reshape(dp, 2 * qv)
    grad_up_b = jnp.sum(grad_pre.astype(F32), axis=0).reshape(dp, -1)
    packed = jnp.concatenate([vectors, grad_qv_b, grad_up_b], axis=1)
    packed = jnp.sum(lax.all_to_all(packed, "dp", 0, 0), axis=0)
    grad_up_b = packed[tp * 6 * piece + 2 * qv :]
    grad_qv_b = packed[tp * 6 * piece : tp * 6 * piece + 2 * qv].reshape(2, qv)
    vectors = packed[: tp * 6 * piece].reshape(tp, 6 * piece)
    vectors = jnp.sum(lax.all_to_all(vectors, "tensor", 0, 0), axis=0).reshape(6, piece)
    return (layer_out, grad_tokens, vectors[0], vectors[1], grad_qkv_w, grad_qv_b, grad_out_w, vectors[2],
            vectors[3], vectors[4], grad_up_w, grad_up_b, grad_down_w, vectors[5])


def solution(mesh):
    vector, matrix = P(("dp", "tensor")), P(("dp", "tensor"), None)
    in_specs = (matrix, matrix, vector, vector, P(None, "dp", "tensor"), P(None, ("tensor", "dp")), P("tensor", "dp"),
                vector, vector, vector, P("dp", "tensor"), P(("tensor", "dp")), P("tensor", "dp"), vector)
    out_specs = (matrix, matrix, vector, vector, P(None, "dp", "tensor"), P(None, ("tensor", "dp")),
                 P("tensor", "dp"), vector, vector, vector, P("dp", "tensor"), P(("tensor", "dp")), P("tensor", "dp"),
                 vector)
    return jax.shard_map(body, mesh=mesh, in_specs=in_specs, out_specs=out_specs, check_vma=False)
```

time: 1720 us -> 1010 us (0.59)
  waiting for transfers between devices: 1290 us -> 409 us
  starting transfers between devices: 1.65 us -> 213 us
  blocking collectives: 118 us -> 35.8 us
  other arithmetic: 55.6 us -> 79.9 us
    reduce_scatter x4 -> x0, waiting for transfers between devices: 508 us -> none  [the longest x1 144 us: body(): lax.psum_scatter(mlp_part, 'tensor', scatter_dimension=0, tiled=True)]
    all_gather x8 -> x4, waiting for transfers between devices: 442 us -> 0.06 us  [the longest x1 0.02 us: body(): w_qkv = lax.all_gather(qkv_weight, 'dp', axis=1, tiled=True)]
    ppermute x0 -> x48, waiting for transfers between devices: none -> 396 us  [the longest x12 212 us: gather(): lax.ppermute(down[-1], self.axis, [(i, i - 1) for i in range(1, n) if i +...]
    ppermute x0 -> x48, starting transfers between devices: none -> 175 us  [the longest x12 77.8 us: gather(): lax.ppermute(up[-1], self.axis, [(i, i + 1) for i in range(n - 1) if i -...]
    reduce_scatter x1, waiting for transfers between devices: 120 us -> 0.01 us  [body(): lax.psum_scatter(grad_down_w, 'dp', scatter_dimension=1, tiled=True)]
    reduce_scatter x1, waiting for transfers between devices: 117 us -> 0.01 us  [body(): lax.psum_scatter(grad_up_w, 'dp', scatter_dimension=0, tiled=True)]
    unnamed x3 -> x0, blocking collectives: 98.6 us -> none
    reduce_scatter x1, waiting for transfers between devices: 54.9 us -> 0.01 us  [body(): lax.psum_scatter(grad_out_w, 'dp', scatter_dimension=1, tiled=True)]
  transfers between devices with their start and end apart: 17 -> 57, of which waited for: 15 -> 24; matrix products, arithmetic and copies ran while one was open for 9% -> 29% of each run, Pallas kernels for 0% -> 0%
where the time goes in v1:
time: 1010 us; the launch traced here: 1000 us
  waiting for transfers between devices  409 us (40%)
  starting transfers between devices  213 us (21%)
  matrix products  209 us (21%)
  other arithmetic  79.9 us (8%)
  local copies, waits for them, and re-layouts  38.7 us (4%)
  blocking collectives  35.8 us (4%)
  between operations  16.2 us (2%)
    ppermute x12, waiting for transfers between devices, gather(): lax.ppermute(down[-1], self.axis, [(i, i - 1) for i in range(1, n) if i +...  212 us
    ppermute x12, waiting for transfers between devices, scatter_sum(): lax.ppermute(term.astype(BF), self.axis, [(i, i + 1) for i in range(min(r...  126 us
    ppermute x12, starting transfers between devices, gather(): lax.ppermute(up[-1], self.axis, [(i, i + 1) for i in range(n - 1) if i -...  77.8 us
    ppermute x12, starting transfers between devices, scatter_sum(): lax.ppermute(term.astype(BF), self.axis, [(i, i + 1) for i in range(min(r...  69.8 us
    ppermute x12, waiting for transfers between devices, scatter_sum(): lax.ppermute(term.astype(BF), self.axis, [(i, i - 1) for i in range(max(n...  46.9 us
    all_to_all x1, starting transfers between devices, body(): lax.all_to_all(vectors, 'tensor', 0, 0)  37 us
    dot_general x1, matrix products, body(): preact = jnp.dot(mlp_in, w_up, preferred_element_type=F32) + bias_up  35.1 us
    dot_general x1, matrix products, body(): jnp.einsum('rd,fd->rf', cot_all, w_down, preferred_element_type=F32)  21.4 us
  transfers between devices with their start and end apart: 57, of which 24 were waited for; matrix products, arithmetic and copies ran while one was open for 29% of the time, Pallas kernels for 0%

profile of v1, /device:TPU:0, one launch (start us, length us, event | category | flops | bytes accessed | tf_op | source)
XLA Modules:
  0.0 1002.1 jit_solution(5798718638237805836)
XLA Ops:
  17.3 21.4 %collective-permute-done = bf16[256,2048]{1,0:T(8,128)(2,1)S(1)} collective-permute-done((bf16[256,2048]{1,0:T(8,128)(2,1)}, bf16[256,2048]{1,0:T(8,128)(2,1)S(1)}, u32[]{:S(2)}, u32[]{:S(2)}) %collective-permute-start) | collective-permute-done | bytes 1048608 | tf_op jit(solution)/shard_map/ppermute | solution.py:73
  47.2 9.6 all-gather.2
  56.9 17.5 %all-gather.1 = bf16[32,384]{1,0:T(8,128)(2,1)S(1)} all-gather(bf16[8,384]{1,0:T(8,128)(2,1)S(1)} %slice.203), channel_id=3, replica_groups=mesh['dp'=8,'tensor'=4] {'tensor'}, dimensions={0}, use_global_device_ids=true | all-gather | bytes 30720 | tf_op jit(solution)/shard_map/all_gather | solution.py:110
  80.4 18.4 %collective-permute-done.4 = bf16[256,2048]{1,0:T(8,128)(2,1)} collective-permute-done((bf16[256,2048]{1,0:T(8,128)(2,1)S(1)}, bf16[256,2048]{1,0:T(8,128)(2,1)}, u32[]{:S(2)}, u32[]{:S(2)}) %collective-permute-start.4) | collective-permute-done | bytes 1048608 | tf_op jit(solution)/shard_map/ppermute | solution.py:73
  105.9 10.1 %convolution_bitcast_fusion = f32[3,1024,512]{1,2,0:T(8,128)S(1)} fusion(bf16[3,2048,512]{1,2,0:T(8,128)(2,1)} %all-gather.8.cloned.1.call-done, f32[2048]{0:T(1024)S(1)} %add.265, f32[2048]{0:T(1024)S(1)} %mul.161, f32[1024]{0:T(1024)S(1)} %add_rsqrt_fusion, f32[1024]{0:T(1024)S(1)} %broadcast_multiply_fusion, bf16[256,2048]{1,0:T(8,128)(2,1)} %copy-done.19, ...), kind=kOutput, calls=%fused_computation.53 | convolution fusion | flops 6469713920 | bytes 16801792 | tf_op jit(solution)/shard_map/rd,kde->kre/dot_general | solution.py:132
  121.9 9.1 fusion.50
  131.1 8.3 fusion
  140.0 7.8 fusion.25
  153.6 18.8 %collective-permute-done.6 = bf16[256,2048]{1,0:T(8,128)(2,1)S(1)} collective-permute-done((bf16[256,2048]{1,0:T(8,128)(2,1)S(1)}, bf16[256,2048]{1,0:T(8,128)(2,1)S(1)}, u32[]{:S(2)}, u32[]{:S(2)}) %collective-permute-start.6) | collective-permute-done | bytes 1048608 | tf_op jit(solution)/shard_map/ppermute | solution.py:91
  177.3 17.9 %collective-permute-done.7 = bf16[256,2048]{1,0:T(8,128)(2,1)S(1)} collective-permute-done((bf16[256,2048]{1,0:T(8,128)(2,1)S(1)}, bf16[256,2048]{1,0:T(8,128)(2,1)S(1)}, u32[]{:S(2)}, u32[]{:S(2)}) %collective-permute-start.7) | collective-permute-done | bytes 1048608 | tf_op jit(solution)/shard_map/ppermute | solution.py:91
  209.8 40.6 %collective-permute-start.25 = (bf16[256,2048]{1,0:T(8,128)(2,1)S(1)}, bf16[256,2048]{1,0:T(8,128)(2,1)}, u32[]{:S(2)}, u32[]{:S(2)}) collective-permute-start(bf16[256,2048]{1,0:T(8,128)(2,1)S(1)} %copy-done.27), channel_id=1, source_target_pairs={{0,1},{1,2},{2,3},{4,5},{5,6},{6,7},{8,9},{9,10},{10,11},{12,13},{... | collective-permute-start | bytes 3145736 | tf_op jit(solution)/shard_map/ppermute | solution.py:74
  250.7 19.0 %collective-permute-done.11 = bf16[256,2048]{1,0:T(8,128)(2,1)} collective-permute-done((bf16[256,2048]{1,0:T(8,128)(2,1)S(1)}, bf16[256,2048]{1,0:T(8,128)(2,1)}, u32[]{:S(2)}, u32[]{:S(2)}) %collective-permute-start.11) | collective-permute-done | bytes 1048608 | tf_op jit(solution)/shard_map/ppermute | solution.py:94
  279.2 12.9 %collective-permute-done.24 = bf16[256,2048]{1,0:T(8,128)(2,1)} collective-permute-done((bf16[256,2048]{1,0:T(8,128)(2,1)S(1)}, bf16[256,2048]{1,0:T(8,128)(2,1)}, u32[]{:S(2)}, u32[]{:S(2)}) %collective-permute-start.24) | collective-permute-done | bytes 1048608 | tf_op jit(solution)/shard_map/ppermute | solution.py:73
  294.9 19.6 %collective-permute-done.12 = bf16[256,2048]{1,0:T(8,128)(2,1)S(1)} collective-permute-done((bf16[256,2048]{1,0:T(8,128)(2,1)S(1)}, bf16[256,2048]{1,0:T(8,128)(2,1)S(1)}, u32[]{:S(2)}, u32[]{:S(2)}) %collective-permute-start.12) | collective-permute-done | bytes 1048608 | tf_op jit(solution)/shard_map/ppermute | solution.py:73
  315.8 21.2 %collective-permute-done.26 = bf16[256,2048]{1,0:T(8,128)(2,1)S(1)} collective-permute-done((bf16[256,2048]{1,0:T(8,128)(2,1)}, bf16[256,2048]{1,0:T(8,128)(2,1)S(1)}, u32[]{:S(2)}, u32[]{:S(2)}) %collective-permute-start.26) | collective-permute-done | bytes 1048608 | tf_op jit(solution)/shard_map/ppermute | solution.py:73
  340.1 19.3 %collective-permute-done.14 = bf16[256,2048]{1,0:T(8,128)(2,1)S(1)} collective-permute-done((bf16[256,2048]{1,0:T(8,128)(2,1)S(1)}, bf16[256,2048]{1,0:T(8,128)(2,1)S(1)}, u32[]{:S(2)}, u32[]{:S(2)}) %collective-permute-start.14) | collective-permute-done | bytes 1048608 | tf_op jit(solution)/shard_map/ppermute | solution.py:73
  360.7 21.2 %collective-permute-done.28 = bf16[256,2048]{1,0:T(8,128)(2,1)S(1)} collective-permute-done((bf16[256,2048]{1,0:T(8,128)(2,1)S(1)}, bf16[256,2048]{1,0:T(8,128)(2,1)S(1)}, u32[]{:S(2)}, u32[]{:S(2)}) %collective-permute-start.28) | collective-permute-done | bytes 1048608 | tf_op jit(solution)/shard_map/ppermute | solution.py:73
  385.3 11.0 %collective-permute-done.16 = bf16[256,2048]{1,0:T(8,128)(2,1)S(1)} collective-permute-done((bf16[256,2048]{1,0:T(8,128)(2,1)S(1)}, bf16[256,2048]{1,0:T(8,128)(2,1)S(1)}, u32[]{:S(2)}, u32[]{:S(2)}) %collective-permute-start.16) | collective-permute-done | bytes 1048608 | tf_op jit(solution)/shard_map/ppermute | solution.py:73
  397.9 35.1 %multiply_convert_fusion.1 = (bf16[1024,2048]{1,0:T(8,128)(2,1)}, f32[1024,2048]{1,0:T(8,128)}, f32[1024,2048]{1,0:T(8,128)}) fusion(f32[2048]{0:T(1024)S(1)} %bitcast.89, bf16[2048,2048]{1,0:T(8,128)(2,1)} %all-gather.12.cloned.1.call-done, bf16[256,2048]{1,0:T(8,128)(2,1)} %get-tuple-element.118, bf16[256,2048]{1,0:T(8,128)(2,1)S(1)} %broadcast_select_fusion.10, ...), kind=kOutput, calls=%fused_computation.23 | convolution fusion | flops 8745123840 | bytes 33562624 | tf_op jit(solution)/shard_map/dot_general | solution.py:146
  432.9 12.5 %convolution_convert_fusion.3 = bf16[1024,2048]{1,0:T(8,128)(2,1)S(1)} fusion(bf16[1024,2048]{1,0:T(8,128)(2,1)} %get-tuple-element.103, bf16[2048,2048]{1,0:T(8,128)(2,1)} %all-gather.14.cloned.1.call-done), kind=kOutput, calls=%fused_computation.49 | convolution fusion | flops 8592031744 | bytes 16777216 | tf_op jit(solution)/shard_map/dot_general | solution.py:153
  450.3 21.4 %convert_reduce_fusion.1 = (f32[2048]{0:T(1024)}, bf16[1024,2048]{1,0:T(8,128)(2,1)}) fusion(f32[1024,2048]{1,0:T(8,128)} %get-tuple-element.104, bf16[2048,2048]{1,0:T(8,128)(2,1)} %all-gather.14.cloned.1.call-done, bf16[256,2048]{1,0:T(8,128)(2,1)} %get-tuple-element.116, bf16[256,2048]{1,0:T(8,128)(2,1)S(1)} %broadcast_select_fusion.6, ...), kind=kOutput, calls=%fused_computation.20 | convolution fusion | flops 8642361344 | bytes 33570816 | tf_op jit(solution)/shard_map/rd,fd->rf/dot_general | solution.py:149
  471.6 12.7 %convolution_convert_fusion.2 = bf16[1024,2048]{1,0:T(8,128)(2,1)S(1)} fusion(bf16[1024,2048]{1,0:T(8,128)(2,1)} %get-tuple-element.138, bf16[2048,2048]{1,0:T(8,128)(2,1)} %all-gather.12.cloned.1.call-done), kind=kOutput, calls=%fused_computation.48 | convolution fusion | flops 8592031744 | bytes 16777216 | tf_op jit(solution)/shard_map/rf,df->rd/dot_general | solution.py:151
  487.6 21.7 %collective-permute-done.30 = bf16[256,2048]{1,0:T(8,128)(2,1)S(1)} collective-permute-done((bf16[256,2048]{1,0:T(8,128)(2,1)S(1)}, bf16[256,2048]{1,0:T(8,128)(2,1)S(1)}, u32[]{:S(2)}, u32[]{:S(2)}) %collective-permute-start.30) | collective-permute-done | bytes 1048608 | tf_op jit(solution)/shard_map/ppermute | solution.py:91
  514.6 17.2 %collective-permute-done.19 = bf16[256,2048]{1,0:T(8,128)(2,1)S(1)} collective-permute-done((bf16[256,2048]{1,0:T(8,128)(2,1)S(1)}, bf16[256,2048]{1,0:T(8,128)(2,1)S(1)}, u32[]{:S(2)}, u32[]{:S(2)}) %collective-permute-start.19) | collective-permute-done | bytes 1048608 | tf_op jit(solution)/shard_map/ppermute | solution.py:91
  531.8 13.7 %collective-permute-done.31 = bf16[256,2048]{1,0:T(8,128)(2,1)S(1)} collective-permute-done((bf16[256,2048]{1,0:T(8,128)(2,1)S(1)}, bf16[256,2048]{1,0:T(8,128)(2,1)S(1)}, u32[]{:S(2)}, u32[]{:S(2)}) %collective-permute-start.31) | collective-permute-done | bytes 1048608 | tf_op jit(solution)/shard_map/ppermute | solution.py:91
  552.0 5.7 collective-permute-start.32
  560.6 32.3 %collective-permute-start.20 = (bf16[256,2048]{1,0:T(8,128)(2,1)}, bf16[256,2048]{1,0:T(8,128)(2,1)}, u32[]{:S(2)}, u32[]{:S(2)}) collective-permute-start(bf16[256,2048]{1,0:T(8,128)(2,1)} %get-tuple-element.142), channel_id=1, source_target_pairs={{0,1},{1,2},{2,3},{4,5},{5,6},{6,7},{8,9},{9,10},{10,11},{12,13},{... | collective-permute-start | bytes 3145736 | tf_op jit(solution)/shard_map/ppermute | solution.py:91
  595.8 13.1 %collective-permute-done.35 = bf16[256,2048]{1,0:T(8,128)(2,1)} collective-permute-done((bf16[256,2048]{1,0:T(8,128)(2,1)}, bf16[256,2048]{1,0:T(8,128)(2,1)}, u32[]{:S(2)}, u32[]{:S(2)}) %collective-permute-start.35) | collective-permute-done | bytes 1048608 | tf_op jit(solution)/shard_map/ppermute | solution.py:94
  611.7 14.8 %collective-permute-done.23 = bf16[256,2048]{1,0:T(8,128)(2,1)} collective-permute-done((bf16[256,2048]{1,0:T(8,128)(2,1)}, bf16[256,2048]{1,0:T(8,128)(2,1)}, u32[]{:S(2)}, u32[]{:S(2)}) %collective-permute-start.23) | collective-permute-done | bytes 1048608 | tf_op jit(solution)/shard_map/ppermute | solution.py:94
  631.5 19.2 %collective-permute-start.37 = (bf16[256,2048]{1,0:T(8,128)(2,1)S(1)}, bf16[256,2048]{1,0:T(8,128)(2,1)S(1)}, u32[]{:S(2)}, u32[]{:S(2)}) collective-permute-start(bf16[256,2048]{1,0:T(8,128)(2,1)S(1)} %get-tuple-element.95), channel_id=1, source_target_pairs={{0,1},{1,2},{2,3},{4,5},{5,6},{6,7},{8,9},{9,10},{10,11},{12,13},{... | collective-permute-start | bytes 3145736 | tf_op jit(solution)/shard_map/ppermute | solution.py:74
  651.9 10.9 %collective-permute-done.37 = bf16[256,2048]{1,0:T(8,128)(2,1)S(1)} collective-permute-done((bf16[256,2048]{1,0:T(8,128)(2,1)S(1)}, bf16[256,2048]{1,0:T(8,128)(2,1)S(1)}, u32[]{:S(2)}, u32[]{:S(2)}) %collective-permute-start.37) | collective-permute-done | bytes 1048608 | tf_op jit(solution)/shard_map/ppermute | solution.py:74
  663.6 28.2 %collective-permute-done.36 = bf16[256,2048]{1,0:T(8,128)(2,1)S(1)} collective-permute-done((bf16[256,2048]{1,0:T(8,128)(2,1)S(1)}, bf16[256,2048]{1,0:T(8,128)(2,1)S(1)}, u32[]{:S(2)}, u32[]{:S(2)}) %collective-permute-start.36) | collective-permute-done | bytes 1048608 | tf_op jit(solution)/shard_map/ppermute | solution.py:73
  693.8 23.6 %collective-permute-done.38 = bf16[256,2048]{1,0:T(8,128)(2,1)S(1)} collective-permute-done((bf16[256,2048]{1,0:T(8,128)(2,1)S(1)}, bf16[256,2048]{1,0:T(8,128)(2,1)S(1)}, u32[]{:S(2)}, u32[]{:S(2)}) %collective-permute-start.38) | collective-permute-done | bytes 1048608 | tf_op jit(solution)/shard_map/ppermute | solution.py:73
  718.9 15.3 %collective-permute-done.40 = bf16[256,2048]{1,0:T(8,128)(2,1)S(1)} collective-permute-done((bf16[256,2048]{1,0:T(8,128)(2,1)S(1)}, bf16[256,2048]{1,0:T(8,128)(2,1)S(1)}, u32[]{:S(2)}, u32[]{:S(2)}) %collective-permute-start.40) | collective-permute-done | bytes 1048608 | tf_op jit(solution)/shard_map/ppermute | solution.py:73
  739.5 13.6 %convolution_convert_fusion = bf16[2048,2048]{1,0:T(8,128)(2,1)} fusion(bf16[1024,2048]{1,0:T(8,128)(2,1)} %get-tuple-element.103, bf16[256,2048]{1,0:T(8,128)(2,1)} %get-tuple-element.116, bf16[256,2048]{1,0:T(8,128)(2,1)S(1)} %copy-done.33, bf16[256,2048]{1,0:T(8,128)(2,1)S(1)} %copy-done.40, bf16[256,2048]{1,0:T(8,128)(2,1)S(1)} %copy-done.29), kind=kOutput, calls=%fused_computation.39 | convolution fusion | flops 8610906112 | bytes 16777216 | tf_op jit(solution)/shard_map/rf,rd->fd/dot_general | solution.py:170
  754.9 13.5 %convolution_convert_fusion.1 = bf16[2048,2048]{1,0:T(8,128)(2,1)} fusion(bf16[1024,2048]{1,0:T(8,128)(2,1)} %get-tuple-element.138, bf16[256,2048]{1,0:T(8,128)(2,1)} %get-tuple-element.118, bf16[256,2048]{1,0:T(8,128)(2,1)S(1)} %copy-done.35, bf16[256,2048]{1,0:T(8,128)(2,1)S(1)} %copy-done.41, bf16[256,2048]{1,0:T(8,128)(2,1)S(1)} %copy-done.39), kind=kOutput, calls=%fused_computation.40 | convolution fusion | flops 8610906112 | bytes 16777216 | tf_op jit(solution)/shard_map/rd,rf->df/dot_general | solution.py:171
  774.8 9.9 fusion.26
  787.2 15.5 %multiply_reduce_fusion = (f32[4,1024]{1,0:T(4,128)S(1)}, f32[4,1024,1024]{1,2,0:T(8,128)}) fusion(f32[4,1024,1024]{1,2,0:T(8,128)} %get-tuple-element.135, f32[4,1024]{1,0:T(4,128)S(1)} %log_add_fusion, bf16[1024,4,128]{0,2,1:T(8,128)(2,1)S(1)} %bitcast.79, f32[1024,4,128]{2,0,1:T(8,128)S(1)} %copy-done.22, f32[4,128]{1,0:T(4,128)S(1)} %copy-done.64), kind=kOutput, calls=%fused_computation.1 | convolution fusion | flops 1087369216 | bytes 36734976 | tf_op jit(solution)/shard_map/qhd,khd->hqk/dot_general | solution.py:48
  802.7 12.8 %multiply_convert_fusion = bf16[4,1024,1024]{1,2,0:T(8,128)(2,1)S(1)} fusion(f32[4,1024,1024]{1,2,0:T(8,128)} %get-tuple-element.140, f32[4,1024,1024]{1,2,0:T(8,128)} %get-tuple-element.135, f32[4,1024]{1,0:T(4,128)S(1)} %get-tuple-element.139, f32[4,1024]{1,0:T(4,128)S(1)} %log_add_fusion), kind=kLoop, calls=%fused_computation | loop fusion | flops 16777216 | bytes 41975808 | tf_op jit(solution)/shard_map/convert_element_type | solution.py:50
  820.6 7.5 multiply_convert_fusion.2
  830.6 11.5 %convert_bitcast_fusion = bf16[3,2048,512]{1,2,0:T(8,128)(2,1)} fusion(f32[2048]{0:T(1024)S(1)} %copy-done.66, f32[2048]{0:T(1024)S(1)} %copy-done.51, bf16[1,1024,512]{2,1,0:T(8,128)(2,1)} %copy.133, bf16[1,1024,512]{2,1,0:T(8,128)(2,1)S(1)} %copy.132, bf16[1,1024,512]{2,1,0:T(8,128)(2,1)} %copy.131, f32[1024]{0:T(1024)S(1)} %copy-done.69, ...), kind=kOutput, calls=%fused_computation.41 | convolution fusion | flops 6476005376 | bytes 13656064 | tf_op jit(solution)/shard_map/rd,kre->kde/dot_general | solution.py:173
  843.6 15.5 %bitcast_reduce_fusion = (f32[2048]{0:T(1024)S(1)}, f32[2048]{0:T(1024)S(1)}, f32[1024,2048]{1,0:T(8,128)}, bf16[1024,2048,1]{1,0,2:T(8,128)(2,1)S(1)}) fusion(f32[1024]{0:T(1024)S(1)} %copy-done.69, f32[1024]{0:T(1024)S(1)} %copy-done.62, bf16[256,2048]{1,0:T(8,128)(2,1)} %copy-done.19, bf16[256,2048]{1,0:T(8,128)(2,1)S(1)} %copy-done.13, ...), kind=kOutput, calls=%fused_computation.16 | convolution fusion | flops 6474952704 | bytes 26238976 | tf_op jit(solution)/shard_map/kre,kde->rd/dot_general | solution.py:164
  860.6 16.9 %collective-permute-done.42 = bf16[256,2048]{1,0:T(8,128)(2,1)S(1)} collective-permute-done((bf16[256,2048]{1,0:T(8,128)(2,1)S(1)}, bf16[256,2048]{1,0:T(8,128)(2,1)S(1)}, u32[]{:S(2)}, u32[]{:S(2)}) %collective-permute-start.42) | collective-permute-done | bytes 1048608 | tf_op jit(solution)/shard_map/ppermute | solution.py:91
  882.3 20.0 %collective-permute-done.43 = bf16[256,2048]{1,0:T(8,128)(2,1)S(1)} collective-permute-done((bf16[256,2048]{1,0:T(8,128)(2,1)S(1)}, bf16[256,2048]{1,0:T(8,128)(2,1)S(1)}, u32[]{:S(2)}, u32[]{:S(2)}) %collective-permute-start.43) | collective-permute-done | bytes 1048608 | tf_op jit(solution)/shard_map/ppermute | solution.py:91
  905.9 6.0 collective-permute-start.44
  916.4 8.6 all_to_all.15
  925.7 37.0 %all-to-all-start.1 = ((f32[4,1,384]{2,1,0:T(1,128)}), f32[4,1,384]{2,1,0:T(1,128)S(1)}, u32[]{:S(2)}, u32[]{:S(2)}) async-start(f32[4,1,384]{2,1,0:T(1,128)} %slice.194), calls=%async_computation.1 | async-start | bytes 12288 | tf_op jit(solution)/shard_map/all_to_all | solution.py:195
  984.4 7.8 reduce-scatter.5.cloned.1.call-done
  (354 shorter events, 189.0 us)
Async XLA Ops:
  7.2 98.7 %all-gather.8.cloned.1.call-start = ((), (), s32[]{:S(2)}) async-start(), calls=%async_computation.6 | async-start | bytes 7077888 | tf_op jit(solution)/shard_map/all_gather | solution.py:117
  9.5 138.3 %all-gather.10.cloned.1.call-start = ((), (), s32[]{:S(2)}) async-start(), calls=%async_computation.7 | async-start | bytes 2359296 | tf_op jit(solution)/shard_map/all_gather | solution.py:118
  10.3 387.6 %all-gather.12.cloned.1.call-start = ((), (), s32[]{:S(2)}) async-start(), calls=%async_computation.8 | async-start | bytes 9437184 | tf_op jit(solution)/shard_map/all_gather | solution.py:119
  10.3 28.3 %collective-permute-start = (bf16[256,2048]{1,0:T(8,128)(2,1)}, bf16[256,2048]{1,0:T(8,128)(2,1)S(1)}, u32[]{:S(2)}, u32[]{:S(2)}) collective-permute-start(bf16[256,2048]{1,0:T(8,128)(2,1)} %param.14), channel_id=1, source_target_pairs={{1,0},{2,1},{3,2},{5,4},{6,5},{7,6},{9,8},{10,9},{11,10},{13,12},{... | collective-permute-start | bytes 3145736 | tf_op jit(solution)/shard_map/ppermute | solution.py:73
  11.6 28.3 %collective-permute-start.1 = (bf16[256,2048]{1,0:T(8,128)(2,1)}, bf16[256,2048]{1,0:T(8,128)(2,1)S(1)}, u32[]{:S(2)}, u32[]{:S(2)}) collective-permute-start(bf16[256,2048]{1,0:T(8,128)(2,1)} %param.14), channel_id=1, source_target_pairs={{0,1},{1,2},{2,3},{4,5},{5,6},{6,7},{8,9},{9,10},{10,11},{12,13},{... | collective-permute-start | bytes 3145736 | tf_op jit(solution)/shard_map/ppermute | solution.py:74
  38.7 36.6 %collective-permute-start.2 = (bf16[256,2048]{1,0:T(8,128)(2,1)S(1)}, bf16[256,2048]{1,0:T(8,128)(2,1)S(1)}, u32[]{:S(2)}, u32[]{:S(2)}) collective-permute-start(bf16[256,2048]{1,0:T(8,128)(2,1)S(1)} %collective-permute-done), channel_id=1, source_target_pairs={{1,0},{2,1},{5,4},{6,5},{9,8},{10,9},{13,12},{14,13},{17,16},{18,1... | collective-permute-start | bytes 3145736 | tf_op jit(solution)/shard_map/ppermute | solution.py:73
  40.0 36.6 %collective-permute-start.3 = (bf16[256,2048]{1,0:T(8,128)(2,1)S(1)}, bf16[256,2048]{1,0:T(8,128)(2,1)}, u32[]{:S(2)}, u32[]{:S(2)}) collective-permute-start(bf16[256,2048]{1,0:T(8,128)(2,1)S(1)} %collective-permute-done.1), channel_id=1, source_target_pairs={{1,2},{2,3},{5,6},{6,7},{9,10},{10,11},{13,14},{14,15},{17,18},{18... | collective-permute-start | bytes 3145736 | tf_op jit(solution)/shard_map/ppermute | solution.py:74
  41.6 391.3 %all-gather.14.cloned.1.call-start = ((), (), s32[]{:S(2)}) async-start(), calls=%async_computation.9 | async-start | bytes 9437184 | tf_op jit(solution)/shard_map/all_gather | solution.py:120
  75.3 23.5 %collective-permute-start.4 = (bf16[256,2048]{1,0:T(8,128)(2,1)S(1)}, bf16[256,2048]{1,0:T(8,128)(2,1)}, u32[]{:S(2)}, u32[]{:S(2)}) collective-permute-start(bf16[256,2048]{1,0:T(8,128)(2,1)S(1)} %collective-permute-done.2), channel_id=1, source_target_pairs={{1,0},{5,4},{9,8},{13,12},{17,16},{21,20},{25,24},{29,28}} | collective-permute-start | bytes 3145736 | tf_op jit(solution)/shard_map/ppermute | solution.py:73
  76.6 22.2 %collective-permute-start.5 = (bf16[256,2048]{1,0:T(8,128)(2,1)}, bf16[256,2048]{1,0:T(8,128)(2,1)}, u32[]{:S(2)}, u32[]{:S(2)}) collective-permute-start(bf16[256,2048]{1,0:T(8,128)(2,1)} %collective-permute-done.3), channel_id=1, source_target_pairs={{2,3},{6,7},{10,11},{14,15},{18,19},{22,23},{26,27},{30,31}} | collective-permute-start | bytes 3145736 | tf_op jit(solution)/shard_map/ppermute | solution.py:74
  152.3 20.2 %collective-permute-start.6 = (bf16[256,2048]{1,0:T(8,128)(2,1)S(1)}, bf16[256,2048]{1,0:T(8,128)(2,1)S(1)}, u32[]{:S(2)}, u32[]{:S(2)}) collective-permute-start(bf16[256,2048]{1,0:T(8,128)(2,1)S(1)} %broadcast_select_fusion.12), channel_id=1, source_target_pairs={{0,1},{4,5},{8,9},{12,13},{16,17},{20,21},{24,25},{28,29}} | collective-permute-start | bytes 3145736 | tf_op jit(solution)/shard_map/ppermute | solution.py:91
  172.8 22.4 %collective-permute-start.7 = (bf16[256,2048]{1,0:T(8,128)(2,1)S(1)}, bf16[256,2048]{1,0:T(8,128)(2,1)S(1)}, u32[]{:S(2)}, u32[]{:S(2)}) collective-permute-start(bf16[256,2048]{1,0:T(8,128)(2,1)S(1)} %fusion.17), channel_id=1, source_target_pairs={{0,1},{1,2},{4,5},{5,6},{8,9},{9,10},{12,13},{13,14},{16,17},{17,1... | collective-permute-start | bytes 3145736 | tf_op jit(solution)/shard_map/ppermute | solution.py:91
  199.8 769.1 %reduce-scatter.7.cloned.1.call-start = ((), (), s32[]{:S(2)}) async-start(), calls=%async_computation.11 | async-start | bytes 2359296 | tf_op jit(solution)/shard_map/reduce_scatter | solution.py:176
  199.8 50.8 %collective-permute-start.8 = (bf16[256,2048]{1,0:T(8,128)(2,1)}, bf16[256,2048]{1,0:T(8,128)(2,1)}, u32[]{:S(2)}, u32[]{:S(2)}) collective-permute-start(bf16[256,2048]{1,0:T(8,128)(2,1)} %get-tuple-element.107), channel_id=1, source_target_pairs={{0,1},{1,2},{2,3},{4,5},{5,6},{6,7},{8,9},{9,10},{10,11},{12,13},{... | collective-permute-start | bytes 3145736 | tf_op jit(solution)/shard_map/ppermute | solution.py:91
  207.2 62.4 %collective-permute-start.11 = (bf16[256,2048]{1,0:T(8,128)(2,1)S(1)}, bf16[256,2048]{1,0:T(8,128)(2,1)}, u32[]{:S(2)}, u32[]{:S(2)}) collective-permute-start(bf16[256,2048]{1,0:T(8,128)(2,1)S(1)} %add_convert_fusion.11), channel_id=1, source_target_pairs={{1,0},{2,1},{3,2},{5,4},{6,5},{7,6},{9,8},{10,9},{11,10},{13,12},{... | collective-permute-start | bytes 3145736 | tf_op jit(solution)/shard_map/ppermute | solution.py:94
  208.5 83.6 %collective-permute-start.24 = (bf16[256,2048]{1,0:T(8,128)(2,1)S(1)}, bf16[256,2048]{1,0:T(8,128)(2,1)}, u32[]{:S(2)}, u32[]{:S(2)}) collective-permute-start(bf16[256,2048]{1,0:T(8,128)(2,1)S(1)} %copy-done.27), channel_id=1, source_target_pairs={{1,0},{2,1},{3,2},{5,4},{6,5},{7,6},{9,8},{10,9},{11,10},{13,12},{... | collective-permute-start | bytes 3145736 | tf_op jit(solution)/shard_map/ppermute | solution.py:73
  209.8 83.6 %collective-permute-start.25 = (bf16[256,2048]{1,0:T(8,128)(2,1)S(1)}, bf16[256,2048]{1,0:T(8,128)(2,1)}, u32[]{:S(2)}, u32[]{:S(2)}) collective-permute-start(bf16[256,2048]{1,0:T(8,128)(2,1)S(1)} %copy-done.27), channel_id=1, source_target_pairs={{0,1},{1,2},{2,3},{4,5},{5,6},{6,7},{8,9},{9,10},{10,11},{12,13},{... | collective-permute-start | bytes 3145736 | tf_op jit(solution)/shard_map/ppermute | solution.py:74
  273.1 21.1 %collective-permute-start.13 = (bf16[256,2048]{1,0:T(8,128)(2,1)S(1)}, bf16[256,2048]{1,0:T(8,128)(2,1)S(1)}, u32[]{:S(2)}, u32[]{:S(2)}) collective-permute-start(bf16[256,2048]{1,0:T(8,128)(2,1)S(1)} %add_convert_fusion.10), channel_id=1, source_target_pairs={{0,1},{1,2},{2,3},{4,5},{5,6},{6,7},{8,9},{9,10},{10,11},{12,13},{... | collective-permute-start | bytes 3145736 | tf_op jit(solution)/shard_map/ppermute | solution.py:74
  277.9 36.6 %collective-permute-start.12 = (bf16[256,2048]{1,0:T(8,128)(2,1)S(1)}, bf16[256,2048]{1,0:T(8,128)(2,1)S(1)}, u32[]{:S(2)}, u32[]{:S(2)}) collective-permute-start(bf16[256,2048]{1,0:T(8,128)(2,1)S(1)} %add_convert_fusion.10), channel_id=1, source_target_pairs={{1,0},{2,1},{3,2},{5,4},{6,5},{7,6},{9,8},{10,9},{11,10},{13,12},{... | collective-permute-start | bytes 3145736 | tf_op jit(solution)/shard_map/ppermute | solution.py:73
  292.1 44.8 %collective-permute-start.26 = (bf16[256,2048]{1,0:T(8,128)(2,1)}, bf16[256,2048]{1,0:T(8,128)(2,1)S(1)}, u32[]{:S(2)}, u32[]{:S(2)}) collective-permute-start(bf16[256,2048]{1,0:T(8,128)(2,1)} %collective-permute-done.24), channel_id=1, source_target_pairs={{1,0},{2,1},{5,4},{6,5},{9,8},{10,9},{13,12},{14,13},{17,16},{18,1... | collective-permute-start | bytes 3145736 | tf_op jit(solution)/shard_map/ppermute | solution.py:73
  293.4 45.0 %collective-permute-start.27 = (bf16[256,2048]{1,0:T(8,128)(2,1)}, bf16[256,2048]{1,0:T(8,128)(2,1)S(1)}, u32[]{:S(2)}, u32[]{:S(2)}) collective-permute-start(bf16[256,2048]{1,0:T(8,128)(2,1)} %collective-permute-done.25), channel_id=1, source_target_pairs={{1,2},{2,3},{5,6},{6,7},{9,10},{10,11},{13,14},{14,15},{17,18},{18... | collective-permute-start | bytes 3145736 | tf_op jit(solution)/shard_map/ppermute | solution.py:74
  294.2 45.2 %collective-permute-start.15 = (bf16[256,2048]{1,0:T(8,128)(2,1)S(1)}, bf16[256,2048]{1,0:T(8,128)(2,1)S(1)}, u32[]{:S(2)}, u32[]{:S(2)}) collective-permute-start(bf16[256,2048]{1,0:T(8,128)(2,1)S(1)} %collective-permute-done.13), channel_id=1, source_target_pairs={{1,2},{2,3},{5,6},{6,7},{9,10},{10,11},{13,14},{14,15},{17,18},{18... | collective-permute-start | bytes 3145736 | tf_op jit(solution)/shard_map/ppermute | solution.py:74
  314.5 44.9 %collective-permute-start.14 = (bf16[256,2048]{1,0:T(8,128)(2,1)S(1)}, bf16[256,2048]{1,0:T(8,128)(2,1)S(1)}, u32[]{:S(2)}, u32[]{:S(2)}) collective-permute-start(bf16[256,2048]{1,0:T(8,128)(2,1)S(1)} %collective-permute-done.12), channel_id=1, source_target_pairs={{1,0},{2,1},{5,4},{6,5},{9,8},{10,9},{13,12},{14,13},{17,16},{18,1... | collective-permute-start | bytes 3145736 | tf_op jit(solution)/shard_map/ppermute | solution.py:73
  337.0 44.9 %collective-permute-start.28 = (bf16[256,2048]{1,0:T(8,128)(2,1)S(1)}, bf16[256,2048]{1,0:T(8,128)(2,1)S(1)}, u32[]{:S(2)}, u32[]{:S(2)}) collective-permute-start(bf16[256,2048]{1,0:T(8,128)(2,1)S(1)} %collective-permute-done.26), channel_id=1, source_target_pairs={{1,0},{5,4},{9,8},{13,12},{17,16},{21,20},{25,24},{29,28}} | collective-permute-start | bytes 3145736 | tf_op jit(solution)/shard_map/ppermute | solution.py:73
  338.4 43.5 %collective-permute-start.29 = (bf16[256,2048]{1,0:T(8,128)(2,1)S(1)}, bf16[256,2048]{1,0:T(8,128)(2,1)S(1)}, u32[]{:S(2)}, u32[]{:S(2)}) collective-permute-start(bf16[256,2048]{1,0:T(8,128)(2,1)S(1)} %collective-permute-done.27), channel_id=1, source_target_pairs={{2,3},{6,7},{10,11},{14,15},{18,19},{22,23},{26,27},{30,31}} | collective-permute-start | bytes 3145736 | tf_op jit(solution)/shard_map/ppermute | solution.py:74
  339.3 45.9 %collective-permute-start.17 = (bf16[256,2048]{1,0:T(8,128)(2,1)S(1)}, bf16[256,2048]{1,0:T(8,128)(2,1)S(1)}, u32[]{:S(2)}, u32[]{:S(2)}) collective-permute-start(bf16[256,2048]{1,0:T(8,128)(2,1)S(1)} %collective-permute-done.15), channel_id=1, source_target_pairs={{2,3},{6,7},{10,11},{14,15},{18,19},{22,23},{26,27},{30,31}} | collective-permute-start | bytes 3145736 | tf_op jit(solution)/shard_map/ppermute | solution.py:74
  359.4 36.9 %collective-permute-start.16 = (bf16[256,2048]{1,0:T(8,128)(2,1)S(1)}, bf16[256,2048]{1,0:T(8,128)(2,1)S(1)}, u32[]{:S(2)}, u32[]{:S(2)}) collective-permute-start(bf16[256,2048]{1,0:T(8,128)(2,1)S(1)} %collective-permute-done.14), channel_id=1, source_target_pairs={{1,0},{5,4},{9,8},{13,12},{17,16},{21,20},{25,24},{29,28}} | collective-permute-start | bytes 3145736 | tf_op jit(solution)/shard_map/ppermute | solution.py:73
  448.5 37.3 %collective-permute-start.18 = (bf16[256,2048]{1,0:T(8,128)(2,1)}, bf16[256,2048]{1,0:T(8,128)(2,1)S(1)}, u32[]{:S(2)}, u32[]{:S(2)}) collective-permute-start(bf16[256,2048]{1,0:T(8,128)(2,1)} %broadcast_select_fusion.8), channel_id=1, source_target_pairs={{0,1},{4,5},{8,9},{12,13},{16,17},{20,21},{24,25},{28,29}} | collective-permute-start | bytes 3145736 | tf_op jit(solution)/shard_map/ppermute | solution.py:91
  484.5 24.8 %collective-permute-start.30 = (bf16[256,2048]{1,0:T(8,128)(2,1)S(1)}, bf16[256,2048]{1,0:T(8,128)(2,1)S(1)}, u32[]{:S(2)}, u32[]{:S(2)}) collective-permute-start(bf16[256,2048]{1,0:T(8,128)(2,1)S(1)} %broadcast_select_fusion.4), channel_id=1, source_target_pairs={{0,1},{4,5},{8,9},{12,13},{16,17},{20,21},{24,25},{28,29}} | collective-permute-start | bytes 3145736 | tf_op jit(solution)/shard_map/ppermute | solution.py:91
  486.3 45.5 %collective-permute-start.19 = (bf16[256,2048]{1,0:T(8,128)(2,1)S(1)}, bf16[256,2048]{1,0:T(8,128)(2,1)S(1)}, u32[]{:S(2)}, u32[]{:S(2)}) collective-permute-start(bf16[256,2048]{1,0:T(8,128)(2,1)S(1)} %fusion.19), channel_id=1, source_target_pairs={{0,1},{1,2},{4,5},{5,6},{8,9},{9,10},{12,13},{13,14},{16,17},{17,1... | collective-permute-start | bytes 3145736 | tf_op jit(solution)/shard_map/ppermute | solution.py:91
  509.7 35.7 %collective-permute-start.31 = (bf16[256,2048]{1,0:T(8,128)(2,1)S(1)}, bf16[256,2048]{1,0:T(8,128)(2,1)S(1)}, u32[]{:S(2)}, u32[]{:S(2)}) collective-permute-start(bf16[256,2048]{1,0:T(8,128)(2,1)S(1)} %fusion.21), channel_id=1, source_target_pairs={{0,1},{1,2},{4,5},{5,6},{8,9},{9,10},{12,13},{13,14},{16,17},{17,1... | collective-permute-start | bytes 3145736 | tf_op jit(solution)/shard_map/ppermute | solution.py:91
  551.2 41.6 %collective-permute-start.22 = (bf16[256,2048]{1,0:T(8,128)(2,1)S(1)}, bf16[256,2048]{1,0:T(8,128)(2,1)S(1)}, u32[]{:S(2)}, u32[]{:S(2)}) collective-permute-start(bf16[256,2048]{1,0:T(8,128)(2,1)S(1)} %fusion.20), channel_id=1, source_target_pairs={{2,1},{3,2},{6,5},{7,6},{10,9},{11,10},{14,13},{15,14},{18,17},{19... | collective-permute-start | bytes 3145736 | tf_op jit(solution)/shard_map/ppermute | solution.py:94
  552.0 43.8 %collective-permute-start.32 = (bf16[256,2048]{1,0:T(8,128)(2,1)}, bf16[256,2048]{1,0:T(8,128)(2,1)S(1)}, u32[]{:S(2)}, u32[]{:S(2)}) collective-permute-start(bf16[256,2048]{1,0:T(8,128)(2,1)} %get-tuple-element.99), channel_id=1, source_target_pairs={{0,1},{1,2},{2,3},{4,5},{5,6},{6,7},{8,9},{9,10},{10,11},{12,13},{... | collective-permute-start | bytes 3145736 | tf_op jit(solution)/shard_map/ppermute | solution.py:91
  559.3 49.6 %collective-permute-start.35 = (bf16[256,2048]{1,0:T(8,128)(2,1)}, bf16[256,2048]{1,0:T(8,128)(2,1)}, u32[]{:S(2)}, u32[]{:S(2)}) collective-permute-start(bf16[256,2048]{1,0:T(8,128)(2,1)} %add_convert_fusion.5), channel_id=1, source_target_pairs={{1,0},{2,1},{3,2},{5,4},{6,5},{7,6},{9,8},{10,9},{11,10},{13,12},{... | collective-permute-start | bytes 3145736 | tf_op jit(solution)/shard_map/ppermute | solution.py:94
  560.6 51.1 %collective-permute-start.20 = (bf16[256,2048]{1,0:T(8,128)(2,1)}, bf16[256,2048]{1,0:T(8,128)(2,1)}, u32[]{:S(2)}, u32[]{:S(2)}) collective-permute-start(bf16[256,2048]{1,0:T(8,128)(2,1)} %get-tuple-element.142), channel_id=1, source_target_pairs={{0,1},{1,2},{2,3},{4,5},{5,6},{6,7},{8,9},{9,10},{10,11},{12,13},{... | collective-permute-start | bytes 3145736 | tf_op jit(solution)/shard_map/ppermute | solution.py:91
  594.4 32.0 %collective-permute-start.23 = (bf16[256,2048]{1,0:T(8,128)(2,1)}, bf16[256,2048]{1,0:T(8,128)(2,1)}, u32[]{:S(2)}, u32[]{:S(2)}) collective-permute-start(bf16[256,2048]{1,0:T(8,128)(2,1)} %add_convert_fusion.8), channel_id=1, source_target_pairs={{1,0},{2,1},{3,2},{5,4},{6,5},{7,6},{9,8},{10,9},{11,10},{13,12},{... | collective-permute-start | bytes 3145736 | tf_op jit(solution)/shard_map/ppermute | solution.py:94
  631.5 31.4 %collective-permute-start.37 = (bf16[256,2048]{1,0:T(8,128)(2,1)S(1)}, bf16[256,2048]{1,0:T(8,128)(2,1)S(1)}, u32[]{:S(2)}, u32[]{:S(2)}) collective-permute-start(bf16[256,2048]{1,0:T(8,128)(2,1)S(1)} %get-tuple-element.95), channel_id=1, source_target_pairs={{0,1},{1,2},{2,3},{4,5},{5,6},{6,7},{8,9},{9,10},{10,11},{12,13},{... | collective-permute-start | bytes 3145736 | tf_op jit(solution)/shard_map/ppermute | solution.py:74
  650.6 41.1 %collective-permute-start.36 = (bf16[256,2048]{1,0:T(8,128)(2,1)S(1)}, bf16[256,2048]{1,0:T(8,128)(2,1)S(1)}, u32[]{:S(2)}, u32[]{:S(2)}) collective-permute-start(bf16[256,2048]{1,0:T(8,128)(2,1)S(1)} %get-tuple-element.95), channel_id=1, source_target_pairs={{1,0},{2,1},{3,2},{5,4},{6,5},{7,6},{9,8},{10,9},{11,10},{13,12},{... | collective-permute-start | bytes 3145736 | tf_op jit(solution)/shard_map/ppermute | solution.py:73
  662.9 30.2 %collective-permute-start.39 = (bf16[256,2048]{1,0:T(8,128)(2,1)S(1)}, bf16[256,2048]{1,0:T(8,128)(2,1)S(1)}, u32[]{:S(2)}, u32[]{:S(2)}) collective-permute-start(bf16[256,2048]{1,0:T(8,128)(2,1)S(1)} %collective-permute-done.37), channel_id=1, source_target_pairs={{1,2},{2,3},{5,6},{6,7},{9,10},{10,11},{13,14},{14,15},{17,18},{18... | collective-permute-start | bytes 3145736 | tf_op jit(solution)/shard_map/ppermute | solution.py:74
  691.8 25.6 %collective-permute-start.38 = (bf16[256,2048]{1,0:T(8,128)(2,1)S(1)}, bf16[256,2048]{1,0:T(8,128)(2,1)S(1)}, u32[]{:S(2)}, u32[]{:S(2)}) collective-permute-start(bf16[256,2048]{1,0:T(8,128)(2,1)S(1)} %collective-permute-done.36), channel_id=1, source_target_pairs={{1,0},{2,1},{5,4},{6,5},{9,8},{10,9},{13,12},{14,13},{17,16},{18,1... | collective-permute-start | bytes 3145736 | tf_op jit(solution)/shard_map/ppermute | solution.py:73
  693.1 25.8 %collective-permute-start.41 = (bf16[256,2048]{1,0:T(8,128)(2,1)S(1)}, bf16[256,2048]{1,0:T(8,128)(2,1)S(1)}, u32[]{:S(2)}, u32[]{:S(2)}) collective-permute-start(bf16[256,2048]{1,0:T(8,128)(2,1)S(1)} %collective-permute-done.39), channel_id=1, source_target_pairs={{2,3},{6,7},{10,11},{14,15},{18,19},{22,23},{26,27},{30,31}} | collective-permute-start | bytes 3145736 | tf_op jit(solution)/shard_map/ppermute | solution.py:74
  739.2 231.5 %reduce-scatter.11.cloned.1.call-start = ((), (), s32[]{:S(2)}) async-start(), calls=%async_computation.13 | async-start | bytes 9437184 | tf_op jit(solution)/shard_map/reduce_scatter | solution.py:174
  753.1 220.3 %reduce-scatter.9.cloned.1.call-start = ((), (), s32[]{:S(2)}) async-start(), calls=%async_computation.12 | async-start | bytes 9437184 | tf_op jit(solution)/shard_map/reduce_scatter | solution.py:175
  768.5 223.8 %reduce-scatter.5.cloned.1.call-start = ((), (), s32[]{:S(2)}) async-start(), calls=%async_computation.10 | async-start | bytes 7077888 | tf_op jit(solution)/shard_map/reduce_scatter | solution.py:177
  877.9 24.5 %collective-permute-start.43 = (bf16[256,2048]{1,0:T(8,128)(2,1)S(1)}, bf16[256,2048]{1,0:T(8,128)(2,1)S(1)}, u32[]{:S(2)}, u32[]{:S(2)}) collective-permute-start(bf16[256,2048]{1,0:T(8,128)(2,1)S(1)} %fusion.23), channel_id=1, source_target_pairs={{0,1},{1,2},{4,5},{5,6},{8,9},{9,10},{12,13},{13,14},{16,17},{17,1... | collective-permute-start | bytes 3145736 | tf_op jit(solution)/shard_map/ppermute | solution.py:91
  905.9 70.5 %collective-permute-start.44 = (bf16[256,2048]{1,0:T(8,128)(2,1)}, bf16[256,2048]{1,0:T(8,128)(2,1)}, u32[]{:S(2)}, u32[]{:S(2)}) collective-permute-start(bf16[256,2048]{1,0:T(8,128)(2,1)} %get-tuple-element.97), channel_id=1, source_target_pairs={{0,1},{1,2},{2,3},{4,5},{5,6},{6,7},{8,9},{9,10},{10,11},{12,13},{... | collective-permute-start | bytes 3145736 | tf_op jit(solution)/shard_map/ppermute | solution.py:91
  913.4 63.0 %collective-permute-start.47 = (bf16[256,2048]{1,0:T(8,128)(2,1)}, bf16[256,2048]{1,0:T(8,128)(2,1)}, u32[]{:S(2)}, u32[]{:S(2)}) collective-permute-start(bf16[256,2048]{1,0:T(8,128)(2,1)} %add_convert_fusion.3), channel_id=1, source_target_pairs={{1,0},{2,1},{3,2},{5,4},{6,5},{7,6},{9,8},{10,9},{11,10},{13,12},{... | collective-permute-start | bytes 3145736 | tf_op jit(solution)/shard_map/ppermute | solution.py:94
  925.7 42.6 %all-to-all-start.1 = ((f32[4,1,384]{2,1,0:T(1,128)}), f32[4,1,384]{2,1,0:T(1,128)S(1)}, u32[]{:S(2)}, u32[]{:S(2)}) async-start(f32[4,1,384]{2,1,0:T(1,128)} %slice.194), calls=%async_computation.1 | async-start | bytes 12288 | tf_op jit(solution)/shard_map/all_to_all | solution.py:195
  (82 other events, 1937.9 us)
Sparse Core Ops, SparseCore 0:
  10.4 49.3 all-gather.7
  61.7 28.0 all-gather.9
  91.7 54.2 all-gather.11
  199.9 80.3 all-gather.13
  739.3 38.1 reduce-scatter.6
  780.8 71.2 reduce-scatter.10
  855.6 72.1 reduce-scatter.8
  931.2 61.0 reduce-scatter.4

commit v2 on v1

v2 whole, which is shorter than its diff:
```python
import functools

import jax
import jax.numpy as jnp
from jax import lax
from jax.experimental import pallas as pl
from jax.experimental.pallas import tpu as pltpu
from jax.sharding import PartitionSpec as P

HD = 128
LEN = 1024
LANES = 128
EPS = 1e-05
BF = jnp.bfloat16
F32 = jnp.float32
MESH = pl.DeviceIdType.MESH
ANY = pl.BlockSpec(memory_space=pl.ANY)
VM = pl.BlockSpec(memory_space=pltpu.VMEM)
NT = (((1,), (1,)), ((), ()))
TN = (((0,), (0,)), ((), ()))
BIG = 64 * 1024 * 1024 - 65536
RB = 32


def norm_stats(rows):
    mean = jnp.mean(rows, axis=-1, keepdims=True)
    centred = rows - mean
    variance = jnp.mean(centred * centred, axis=-1, keepdims=True)
    inverse = lax.rsqrt(variance + EPS)
    return centred * inverse, inverse


def norm_back(grad_rows, normal_rows, inverse, gain):
    scaled = grad_rows * gain
    first = jnp.mean(scaled, axis=-1, keepdims=True)
    second = jnp.mean(scaled * normal_rows, axis=-1, keepdims=True)
    return inverse * (scaled - first - normal_rows * second)


def loop(count, step):
    def run(i, carry):
        step(i)
        return carry

    lax.fori_loop(0, count, run, 0)


def rows_at(j, size):
    return pl.ds(pl.multiple_of(j * size, size), size)


def remote(src, dst, send, recv, target):
    return pltpu.make_async_remote_copy(src_ref=src, dst_ref=dst, send_sem=send, recv_sem=recv,
                                        device_id={"tensor": target}, device_id_type=MESH)


def greet_neighbours(i, n):
    barrier = pltpu.get_barrier_semaphore()

    @pl.when(i > 0)
    def _():
        pl.semaphore_signal(barrier, inc=1, device_id={"tensor": i - 1}, device_id_type=MESH)

    @pl.when(i < n - 1)
    def _():
        pl.semaphore_signal(barrier, inc=1, device_id={"tensor": i + 1}, device_id_type=MESH)

    pl.semaphore_wait(barrier, jnp.minimum(i, 1) + jnp.minimum(n - 1 - i, 1))


class LineGather:
    def __init__(self, i, n, own, buf, send, recv):
        self.i, self.n, self.own, self.buf, self.send, self.recv = i, n, own, buf, send, recv

    def copy(self, src, j, side, target):
        return remote(src, self.buf.at[j], self.send.at[side, j], self.recv.at[j], target)

    def start(self):
        i, n = self.i, self.n

        @pl.when(i < n - 1)
        def _():
            self.copy(self.own, i, 0, i + 1).start()

        @pl.when(i > 0)
        def _():
            self.copy(self.own, i, 1, i - 1).start()

    def step(self, r):
        i, n = self.i, self.n

        @pl.when(i - r >= 0)
        def _():
            self.copy(self.own, i - r, 0, i).wait_recv()

            @pl.when(i < n - 1)
            def _():
                self.copy(self.buf.at[i - r], i - r, 0, i + 1).start()

        @pl.when(i + r <= n - 1)
        def _():
            self.copy(self.own, i + r, 1, i).wait_recv()

            @pl.when(i > 0)
            def _():
                self.copy(self.buf.at[i + r], i + r, 1, i - 1).start()

    def finish(self):
        i, n = self.i, self.n

        def one(j):
            @pl.when(jnp.logical_and(i < n - 1, j <= i))
            def _():
                self.copy(self.own, j, 0, i + 1).wait_send()

            @pl.when(jnp.logical_and(i > 0, j >= i))
            def _():
                self.copy(self.own, j, 1, i - 1).wait_send()

        loop(n, one)


class LineSum:
    def __init__(self, i, n, part, land, send, recv, pieces):
        self.i, self.n, self.part, self.land, self.send, self.recv = i, n, part, land, send, recv
        self.pieces = pieces
        self.size = part.shape[1] // pieces

    def copy(self, src, d, right, s):
        i, n = self.i, self.n
        target = i + 1 if right else i - 1
        slot = d if right else jnp.where(d == target, n, d)
        here = rows_at(s, self.size)
        return remote(src.at[d, here], self.land.at[slot, here], self.send.at[d, s], self.recv.at[slot, s], target)

    def arrived(self, slot, s):
        here = rows_at(s, self.size)
        remote(self.part.at[0, here], self.land.at[slot, here], self.send.at[0, s], self.recv.at[slot, s],
               self.i).wait_recv()

    def launch(self, d):
        i, n = self.i, self.n

        @pl.when(jnp.logical_and(i == 0, d > 0))
        def _():
            loop(self.pieces, lambda s: self.copy(self.part, d, True, s).start())

        @pl.when(jnp.logical_and(i == n - 1, d < n - 1))
        def _():
            loop(self.pieces, lambda s: self.copy(self.part, d, False, s).start())

    def relay(self, d, right):
        def one(s):
            self.arrived(d, s)
            here = rows_at(s, self.size)
            total = self.land[d, here, :].astype(F32) + self.part[d, here, :].astype(F32)
            self.land[d, here, :] = total.astype(BF)
            self.copy(self.land, d, right, s).start()

        loop(self.pieces, one)

    def own(self):
        i, n = self.i, self.n

        @pl.when(i > 0)
        def _():
            loop(self.pieces, lambda s: self.arrived(i, s))

        @pl.when(i < n - 1)
        def _():
            loop(self.pieces, lambda s: self.arrived(n, s))

    def add(self, here, out):
        i, n = self.i, self.n
        out[...] = self.part[i, here, :].astype(F32)

        @pl.when(i > 0)
        def _():
            out[...] += self.land[i, here, :].astype(F32)

        @pl.when(i < n - 1)
        def _():
            out[...] += self.land[n, here, :].astype(F32)

    def finish(self):
        i, n = self.i, self.n

        def one(d):
            @pl.when(jnp.logical_and(i < n - 1, d > i))
            def _():
                loop(self.pieces, lambda s: self.copy(self.part, d, True, s).wait_send())

            @pl.when(jnp.logical_and(i > 0, d < i))
            def _():
                loop(self.pieces, lambda s: self.copy(self.part, d, False, s).wait_send())

        loop(n, one)


def project_kernel(n, m, pieces, pack_ref, x_ref, w_hbm, a_ref, qkv_ref, vec_ref, buf, w, affine, bias, w_sem, own_sem,
                   send, recv, v_send, v_recv):
    i, row = lax.axis_index("tensor"), lax.axis_index("dp")
    me, total = row * n + i, m * n
    size, width = x_ref.shape[0], w.shape[2]
    barrier = pltpu.get_barrier_semaphore()

    def greet(s):
        other = (me + s + 1) % total
        pl.semaphore_signal(barrier, inc=1, device_id={"dp": other // n, "tensor": other % n}, device_id_type=MESH)

    loop(total - 1, greet)
    pl.semaphore_wait(barrier, total - 1)

    line = LineGather(i, n, x_ref, buf, send, recv)
    line.start()

    def vector(src, other):
        return pltpu.make_async_remote_copy(
            src_ref=pack_ref, dst_ref=vec_ref.at[src], send_sem=v_send.at[other], recv_sem=v_recv.at[src],
            device_id={"dp": other // n, "tensor": other % n}, device_id_type=MESH)

    loop(total - 1, lambda s: vector(me, (me + s + 1) % total).start())
    own_copy = pltpu.make_async_copy(x_ref, buf.at[i], own_sem)
    own_copy.start()
    weights = pltpu.make_async_copy(w_hbm, w, w_sem)
    weights.start()
    vec_ref[me] = pack_ref[...]
    loop(total - 1, lambda s: vector((me + s + 1) % total, me).wait_recv())

    piece, qv_piece = pieces
    depth = affine.shape[1]
    group = LANES // piece
    for tile in range(depth // LANES):
        value = vec_ref[tile * group, 0:2, :]
        for g in range(1, group):
            value = value + vec_ref[tile * group + g, 0:2, :]
        affine[0:2, tile * LANES : (tile + 1) * LANES] = value
    group = LANES // qv_piece
    for tile in range(width // LANES):
        value = vec_ref[tile * group * n + i, 6:8, :]
        for g in range(1, group):
            value = value + vec_ref[(tile * group + g) * n + i, 6:8, :]
        bias[0:2, tile * LANES : (tile + 1) * LANES] = value
    own_copy.wait()
    weights.wait()

    def compute(j):
        def norm(b):
            normal, _ = norm_stats(buf[j, rows_at(b, RB), :].astype(F32))
            here = pl.ds(pl.multiple_of(j * size + b * RB, RB), RB)
            a_ref[here, :] = (normal * affine[0:1, :] + affine[1:2, :]).astype(BF)

        loop(size // RB, norm)
        here = rows_at(j, size)
        for t in range(3):
            value = jnp.dot(a_ref[here, :], w[t], preferred_element_type=F32)
            if t != 1:
                value = value + bias[t // 2 : t // 2 + 1, :]
            qkv_ref[t, here, :] = value.astype(BF)

    def round_of(r):
        @pl.when(r > 0)
        def _():
            line.step(r)

        def side(s):
            j = jnp.where(s == 0, i - r, i + r)

            @pl.when(jnp.logical_and(jnp.logical_and(j >= 0, j <= n - 1), s * r == s * jnp.maximum(r, 1)))
            def _():
                compute(j)

        loop(2, side)

    loop(n, round_of)
    line.finish()
    loop(total - 1, lambda s: vector(me, (me + s + 1) % total).wait_send())


def attend_kernel(n, pieces, qkv_ref, w_ref, x_ref, cot_ref, out_bias, gain, shift, o_ref, h_ref, c_ref, cot_all,
                  part, land, send, recv, s_send, s_recv, own_sem):
    i = lax.axis_index("tensor")
    size = x_ref.shape[0]
    heads = qkv_ref.shape[2] // HD
    depth = w_ref.shape[1]
    greet_neighbours(i, n)
    line = LineGather(i, n, cot_ref, cot_all, send, recv)
    line.start()
    own_copy = pltpu.make_async_copy(cot_ref, cot_all.at[i], own_sem)
    own_copy.start()

    block = 256

    def head(t):
        cols = pl.ds(pl.multiple_of(t * HD, HD), HD)
        for b in range(LEN // block):
            here, keys = slice(b * block, (b + 1) * block), (b + 1) * block
            s = lax.dot_general(qkv_ref[0, here, cols], qkv_ref[1, 0:keys, cols], NT,
                                preferred_element_type=F32) * HD ** (-0.5)
            query = lax.broadcasted_iota(jnp.int32, s.shape, 0) + b * block
            s = jnp.where(query >= lax.broadcasted_iota(jnp.int32, s.shape, 1), s, -1e30)
            e = jnp.exp(s - jnp.max(s, axis=-1, keepdims=True))
            prob = (e / jnp.sum(e, axis=-1, keepdims=True)).astype(BF)
            o_ref[here, cols] = jnp.dot(prob, qkv_ref[2, 0:keys, cols], preferred_element_type=F32).astype(BF)

    loop(heads, head)
    sums = LineSum(i, n, part, land, s_send, s_recv, pieces)
    tile = 512

    def project(t):
        d = jnp.where(i < n // 2, n - 1 - t, t)

        def columns(k):
            cols = rows_at(k, tile)
            part[d, :, cols] = jnp.dot(o_ref[rows_at(d, size), :], w_ref[:, cols], preferred_element_type=F32).astype(BF)

        loop(depth // tile, columns)
        sums.launch(d)

    loop(n, project)

    def round_of(r):
        line.step(r + 1)
        right, left = n - 1 + i - (r + 1), r + 1 - (n - 1 - i)

        @pl.when(jnp.logical_and(i > 0, jnp.logical_and(right > i, right <= n - 1)))
        def _():
            sums.relay(right, True)

        @pl.when(jnp.logical_and(i < n - 1, jnp.logical_and(left >= 0, left < i)))
        def _():
            sums.relay(left, False)

    loop(n - 1, round_of)
    sums.own()

    def norm(b):
        here = rows_at(b, RB)
        sums.add(here, h_ref.at[here, :])
        rows = h_ref[here, :] + (x_ref[here, :].astype(F32) + out_bias[...])
        h_ref[here, :] = rows
        normal, _ = norm_stats(rows)
        c_ref[here, :] = (normal * gain[...] + shift[...]).astype(BF)

    loop(size // RB, norm)
    own_copy.wait()
    line.finish()
    sums.finish()


def hidden_kernel(n, pieces, c_ref, h_ref, cot_hbm, up_hbm, down_hbm, up_bias, gain, c_hbm, g_hbm, du_hbm, dh_ref,
                  db_ref, vec_ref, upb_ref, c_all, g_all, du_all, cot_all, up, down, part, land, send, recv, s_send,
                  s_recv, w_sem, cot_sem, own_sem, c_sem, g_sem, du_sem):
    i = lax.axis_index("tensor")
    size, depth = c_ref.shape
    units = up.shape[1]
    greet_neighbours(i, n)
    line = LineGather(i, n, c_ref, c_all, send, recv)
    line.start()
    own_copy = pltpu.make_async_copy(c_ref, c_all.at[i], own_sem)
    own_copy.start()
    up_copy = pltpu.make_async_copy(up_hbm, up, w_sem.at[0])
    up_copy.start()
    down_copy = pltpu.make_async_copy(down_hbm, down, w_sem.at[1])
    down_copy.start()
    cot_copy = pltpu.make_async_copy(cot_hbm, cot_all, cot_sem)
    cot_copy.start()
    upb_ref[...] = jnp.zeros_like(upb_ref)
    vec_ref[...] = jnp.zeros_like(vec_ref)
    own_copy.wait()
    up_copy.wait()
    down_copy.wait()
    cot_copy.wait()
    sums = LineSum(i, n, part, land, s_send, s_recv, pieces)
    tile = 256

    def out_copy(src, dst, sem, j):
        return pltpu.make_async_copy(src.at[j], dst.at[j], sem.at[j])

    def compute(j):
        def unit(k):
            cols = rows_at(k, tile)
            u = jnp.dot(c_all[j], up[:, cols], preferred_element_type=F32) + up_bias[0:1, cols]
            dg = lax.dot_general(cot_all[j], down[cols, :], NT, preferred_element_type=F32)
            half = 0.5 + 0.5 * lax.erf(u * (0.5 ** 0.5))
            g_all[j, :, cols] = (u * half).astype(BF)
            slope = half + u * (jnp.exp(u * u * -0.5) * 0.3989422804014327)
            du = (slope * dg).astype(BF)
            du_all[j, :, cols] = du
            upb_ref[0:1, cols] += jnp.sum(du.astype(F32), axis=0, keepdims=True)

        loop(units // tile, unit)

        def back(k):
            cols = rows_at(k, tile)
            part[j, :, cols] = lax.dot_general(du_all[j], up[cols, :], NT, preferred_element_type=F32).astype(BF)

        loop(depth // tile, back)
        sums.launch(j)
        out_copy(g_all, g_hbm, g_sem, j).start()
        out_copy(du_all, du_hbm, du_sem, j).start()
        out_copy(c_all, c_hbm, c_sem, j).start()

    def round_of(r):
        @pl.when(r > 0)
        def _():
            line.step(r)

        def side(s):
            j = jnp.where(s == 0, i - r, i + r)

            @pl.when(jnp.logical_and(jnp.logical_and(j >= 0, j <= n - 1), s * r == s * jnp.maximum(r, 1)))
            def _():
                compute(j)

        loop(2, side)

    loop(n, round_of)

    def relay(t):
        right, left = t + 2 - i, 2 * n - 4 - i - t

        @pl.when(jnp.logical_and(i > 0, jnp.logical_and(right > i, right <= n - 1)))
        def _():
            sums.relay(right, True)

        @pl.when(jnp.logical_and(i < n - 1, jnp.logical_and(left >= 0, left < i)))
        def _():
            sums.relay(left, False)

    loop(2 * n - 3, relay)
    sums.own()

    def norm(b):
        here = rows_at(b, RB)
        sums.add(here, dh_ref.at[here, :])
        grad = dh_ref[here, :]
        normal, inverse = norm_stats(h_ref[here, :])
        vec_ref[0:1, :] += jnp.sum(grad * normal, axis=0, keepdims=True)
        vec_ref[1:2, :] += jnp.sum(grad, axis=0, keepdims=True)
        cot = cot_all[i, here, :].astype(F32)
        dh = cot + norm_back(grad, normal, inverse, gain[...])
        dh_ref[here, :] = dh
        db = dh.astype(BF)
        db_ref[here, :] = db
        vec_ref[2:3, :] += jnp.sum(db.astype(F32), axis=0, keepdims=True)
        vec_ref[3:4, :] += jnp.sum(cot, axis=0, keepdims=True)

    loop(size // RB, norm)

    def done(j):
        out_copy(g_all, g_hbm, g_sem, j).wait()
        out_copy(du_all, du_hbm, du_sem, j).wait()
        out_copy(c_all, c_hbm, c_sem, j).wait()

    loop(n, done)
    line.finish()
    sums.finish()


def attend_back_kernel(qkv_ref, do_ref, out_ref, dk, dv):
    heads = qkv_ref.shape[2] // HD
    block = 256
    factor = HD ** (-0.5)

    def head(t):
        cols = pl.ds(pl.multiple_of(t * HD, HD), HD)
        dk[...] = jnp.zeros_like(dk)
        dv[...] = jnp.zeros_like(dv)
        for b in range(LEN // block):
            here, keys = slice(b * block, (b + 1) * block), (b + 1) * block
            q, k, v = qkv_ref[0, here, cols], qkv_ref[1, 0:keys, cols], qkv_ref[2, 0:keys, cols]
            do = do_ref[here, cols]
            s = lax.dot_general(q, k, NT, preferred_element_type=F32) * factor
            query = lax.broadcasted_iota(jnp.int32, s.shape, 0) + b * block
            s = jnp.where(query >= lax.broadcasted_iota(jnp.int32, s.shape, 1), s, -1e30)
            e = jnp.exp(s - jnp.max(s, axis=-1, keepdims=True))
            prob = e / jnp.sum(e, axis=-1, keepdims=True)
            dv[0:keys, :] += lax.dot_general(prob.astype(BF), do, TN, preferred_element_type=F32)
            dp = lax.dot_general(do, v, NT, preferred_element_type=F32)
            ds = (prob * (dp - jnp.sum(prob * dp, axis=-1, keepdims=True))).astype(BF)
            out_ref[0, here, cols] = (jnp.dot(ds, k, preferred_element_type=F32) * factor).astype(BF)
            dk[0:keys, :] += lax.dot_general(ds, q, TN, preferred_element_type=F32)
        out_ref[1, :, cols] = (dk[...] * factor).astype(BF)
        out_ref[2, :, cols] = dv[...].astype(BF)

    loop(heads, head)


def params(collective=None):
    if collective is None:
        return pltpu.CompilerParams(vmem_limit_bytes=BIG)
    return pltpu.CompilerParams(vmem_limit_bytes=BIG, collective_id=collective, has_side_effects=True)


def shape(dims, dtype):
    return jax.ShapeDtypeStruct(dims, dtype)


class Line:
    def __init__(self, axis, size):
        self.axis, self.n = axis, size
        self.i = lax.axis_index(axis)
        self.first = self.i < size // 2

    def owner(self, k):
        return jnp.where(self.first, self.i + k, self.i - k + self.n) % self.n

    def gather(self, block):
        n = self.n
        down, up = [block], [block]
        for r in range(1, n):
            down.append(lax.ppermute(down[-1], self.axis, [(i, i - 1) for i in range(1, n) if i + r - 1 <= n - 1]))
            up.append(lax.ppermute(up[-1], self.axis, [(i, i + 1) for i in range(n - 1) if i - r + 1 >= 0]))
        slots = [block]
        for k in range(1, n):
            if 2 * k <= n:
                slots.append(jnp.where(self.first, down[k], up[k]))
            else:
                low = jnp.where(self.i + k <= n - 1, down[k], up[n - k])
                high = jnp.where(self.i - k >= 0, up[k], down[n - k])
                slots.append(jnp.where(self.first, low, high))
        return slots

    def scatter_sum(self, parts):
        n = self.n
        right = left = None

        def pick(owner):
            return lax.dynamic_index_in_dim(parts, owner % n, 0, keepdims=False).astype(F32)

        for r in range(1, n):
            term = pick(self.i + n - r)
            term = term if right is None else term + right.astype(F32)
            right = lax.ppermute(term.astype(BF), self.axis, [(i, i + 1) for i in range(min(r, n - 1))])
            term = pick(self.i + r)
            term = term if left is None else term + left.astype(F32)
            left = lax.ppermute(term.astype(BF), self.axis, [(i, i - 1) for i in range(max(n - r, 1), n)])
        return pick(self.i) + (right.astype(F32) + left.astype(F32))


def body(tokens, cotangent, ln1_gain, ln1_bias, qkv_weight, qv_bias, out_weight, out_bias, ln2_gain, ln2_bias,
         up_weight, up_bias, down_weight, down_bias):
    n = lax.axis_size("tensor")
    m = lax.axis_size("dp")
    i, row = lax.axis_index("tensor"), lax.axis_index("dp")
    line = Line("tensor", n)
    size, depth = tokens.shape
    width = qkv_weight.shape[2]
    units = up_weight.shape[1]
    piece, qv_piece, up_piece = ln1_gain.shape[0], qv_bias.shape[1], up_bias.shape[0]
    total = m * n

    def lane_rows(value, index):
        count = value.shape[-1]
        if count >= LANES:
            return value.reshape(-1, LANES)
        places = LANES // count
        spread = jnp.tile(value.reshape(-1, count), (1, places))
        return jnp.where((jnp.arange(LANES) // count)[None] == index % places, spread, 0)

    me = row * n + i
    whole = jnp.stack([ln1_gain, ln1_bias, out_bias, ln2_gain, ln2_bias, down_bias])
    pack = jnp.concatenate([lane_rows(whole, me), lane_rows(qv_bias, row), lane_rows(up_bias, row)])
    pack = jnp.pad(pack.astype(F32), ((0, -pack.shape[0] % 8), (0, 0)))
    lanes_up = 8 + max(up_piece // LANES, 1)

    w_qkv = lax.all_gather(qkv_weight, "dp", axis=1, tiled=True)
    w_out = lax.all_gather(out_weight, "dp", axis=1, tiled=True)
    w_up = lax.all_gather(up_weight, "dp", axis=0, tiled=True)
    w_down = lax.all_gather(down_weight, "dp", axis=1, tiled=True)

    dma = pltpu.SemaphoreType.DMA
    attn_in, qkv, vecs = pl.pallas_call(
        functools.partial(project_kernel, n, m, (piece, qv_piece)),
        out_shape=(shape((LEN, depth), BF), shape((3, LEN, width), BF), shape((total,) + pack.shape, F32)),
        in_specs=[VM, VM, ANY], out_specs=(VM, VM, VM),
        scratch_shapes=[pltpu.VMEM((n, size, depth), BF), pltpu.VMEM((3, depth, width), BF), pltpu.VMEM((8, depth), F32),
                        pltpu.VMEM((8, width), F32), dma, dma, dma((2, n)), dma((n,)), dma((total,)), dma((total,))],
        compiler_params=params(0), name="project",
    )(pack, tokens, w_qkv)
    vectors = vecs.reshape(depth // LANES, LANES // piece, -1, LANES).sum(axis=1)
    vectors = vectors[:, 2:6].transpose(1, 0, 2).reshape(4, 1, depth)
    bias_out, gain_two, shift_two, bias_down = [vectors[j] for j in range(4)]
    ups = lax.dynamic_index_in_dim(vecs.reshape(m, n, -1, LANES), i, 1, keepdims=False)[:, 8:lanes_up]
    if up_piece < LANES:
        ups = ups.reshape(units // LANES, LANES // up_piece, LANES).sum(axis=1)
    bias_up = ups.reshape(1, units)

    pieces = 2
    sums = [pltpu.VMEM((n, size, depth), BF), pltpu.VMEM((n + 1, size, depth), BF)]
    mixture, residual, mlp_own, cot_all = pl.pallas_call(
        functools.partial(attend_kernel, n, pieces),
        out_shape=(shape((LEN, width), BF), shape((size, depth), F32), shape((size, depth), BF),
                   shape((n, size, depth), BF)),
        in_specs=[VM] * 7, out_specs=(VM,) * 4,
        scratch_shapes=sums + [dma((2, n)), dma((n,)), dma((n, pieces)), dma((n + 1, pieces)), dma],
        compiler_params=params(1), name="attend",
    )(qkv, w_out, tokens, cotangent, bias_out, gain_two, shift_two)

    pieces = 4
    mlp_in, hidden, grad_pre, grad_resid, branch_cot, vec_two, grad_up_b = pl.pallas_call(
        functools.partial(hidden_kernel, n, pieces),
        out_shape=(shape((n, size, depth), BF), shape((n, size, units), BF), shape((n, size, units), BF),
                   shape((size, depth), F32), shape((size, depth), BF), shape((8, depth), F32), shape((8, units), F32)),
        in_specs=[VM, VM, ANY, ANY, ANY, VM, VM], out_specs=(ANY, ANY, ANY, VM, VM, VM, VM),
        scratch_shapes=[pltpu.VMEM((n, size, depth), BF), pltpu.VMEM((n, size, units), BF),
                        pltpu.VMEM((n, size, units), BF), pltpu.VMEM((n, size, depth), BF),
                        pltpu.VMEM((depth, units), BF), pltpu.VMEM((units, depth), BF)] + sums +
                       [dma((2, n)), dma((n,)), dma((n, pieces)), dma((n + 1, pieces)), dma((2,)), dma, dma,
                        dma((n,)), dma((n,)), dma((n,))],
        compiler_params=params(2), name="hidden",
    )(mlp_own, residual, cot_all, w_up, w_down, bias_up, gain_two)
    mlp_in, hidden, grad_pre = [v.reshape(LEN, -1) for v in (mlp_in, hidden, grad_pre)]
    cot_rows = cot_all.reshape(LEN, depth)

    mlp_part = jnp.dot(hidden, w_down, preferred_element_type=F32).astype(BF)
    layer_out = (residual + (line.scatter_sum(mlp_part.reshape(n, size, depth)) + bias_down)).astype(BF)
    grad_down_w = jnp.einsum("rf,rd->fd", hidden, cot_rows, preferred_element_type=F32).astype(BF)
    grad_up_w = jnp.einsum("rd,rf->df", mlp_in, grad_pre, preferred_element_type=F32).astype(BF)

    slots = line.gather(branch_cot)
    attn_cot = jnp.zeros((LEN, depth), BF)
    for k in range(n):
        attn_cot = lax.dynamic_update_slice(attn_cot, slots[k], (line.owner(k) * size, 0))
    grad_mix = jnp.einsum("rd,ed->re", attn_cot, w_out, preferred_element_type=F32).astype(BF)
    grad_qkv = pl.pallas_call(
        attend_back_kernel, out_shape=shape((3, LEN, width), BF), in_specs=[VM, VM], out_specs=VM,
        scratch_shapes=[pltpu.VMEM((LEN, HD), F32), pltpu.VMEM((LEN, HD), F32)],
        compiler_params=params(), name="attend_back",
        cost_estimate=pl.CostEstimate(flops=14 * LEN * LEN * width // 2, bytes_accessed=14 * LEN * width,
                                      transcendentals=LEN * LEN * width // HD),
    )(qkv, grad_mix)
    attn_back = jnp.einsum("kre,kde->rd", grad_qkv, w_qkv, preferred_element_type=F32).astype(BF)
    grad_normed_one = line.scatter_sum(attn_back.reshape(n, size, depth))
    normal_one, inverse_one = norm_stats(tokens.astype(F32))
    gain_one = vecs.reshape(depth // LANES, LANES // piece, -1, LANES).sum(axis=1)[:, 0].reshape(1, depth)
    grad_tokens = (grad_resid + norm_back(grad_normed_one, normal_one, inverse_one, gain_one)).astype(BF)

    grad_out_w = jnp.einsum("re,rd->ed", mixture, attn_cot, preferred_element_type=F32).astype(BF)
    grad_qkv_w = jnp.einsum("rd,kre->kde", attn_in, grad_qkv, preferred_element_type=F32).astype(BF)
    grad_down_w = lax.psum_scatter(grad_down_w, "dp", scatter_dimension=1, tiled=True).astype(F32)
    grad_up_w = lax.psum_scatter(grad_up_w, "dp", scatter_dimension=0, tiled=True).astype(F32)
    grad_out_w = lax.psum_scatter(grad_out_w, "dp", scatter_dimension=1, tiled=True).astype(F32)
    grad_qkv_w = lax.psum_scatter(grad_qkv_w, "dp", scatter_dimension=1, tiled=True).astype(F32)

    vectors = jnp.stack([
        jnp.sum(grad_normed_one * normal_one, axis=0),
        jnp.sum(grad_normed_one, axis=0),
        vec_two[2], vec_two[0], vec_two[1], vec_two[3],
    ])
    vectors = vectors.reshape(6, m, n, piece).transpose(1, 2, 0, 3).reshape(m, n * 6 * piece)
    grad_qv_b = jnp.sum(grad_qkv[0::2].astype(F32), axis=1).reshape(2, m, qv_piece).transpose(1, 0, 2)
    packed = jnp.concatenate([vectors, grad_qv_b.reshape(m, -1), grad_up_b[0].reshape(m, -1)], axis=1)
    packed = jnp.sum(lax.all_to_all(packed, "dp", 0, 0), axis=0)
    grad_up_b = packed[n * 6 * piece + 2 * qv_piece :]
    grad_qv_b = packed[n * 6 * piece : n * 6 * piece + 2 * qv_piece].reshape(2, qv_piece)
    vectors = packed[: n * 6 * piece].reshape(n, 6 * piece)
    vectors = jnp.sum(lax.all_to_all(vectors, "tensor", 0, 0), axis=0).reshape(6, piece)
    return (layer_out, grad_tokens, vectors[0], vectors[1], grad_qkv_w, grad_qv_b, grad_out_w, vectors[2],
            vectors[3], vectors[4], grad_up_w, grad_up_b, grad_down_w, vectors[5])


def solution(mesh):
    vector, matrix = P(("dp", "tensor")), P(("dp", "tensor"), None)
    in_specs = (matrix, matrix, vector, vector, P(None, "dp", "tensor"), P(None, ("tensor", "dp")), P("tensor", "dp"),
                vector, vector, vector, P("dp", "tensor"), P(("tensor", "dp")), P("tensor", "dp"), vector)
    out_specs = (matrix, matrix, vector, vector, P(None, "dp", "tensor"), P(None, ("tensor", "dp")),
                 P("tensor", "dp"), vector, vector, vector, P("dp", "tensor"), P(("tensor", "dp")), P("tensor", "dp"),
                 vector)
    return jax.shard_map(body, mesh=mesh, in_specs=in_specs, out_specs=out_specs, check_vma=False)
```

time: 1010 us -> 769 us (0.76)
  Pallas kernels: 0 us -> 346 us
  waiting for transfers between devices: 409 us -> 185 us
  matrix products: 209 us -> 67.9 us
  starting transfers between devices: 213 us -> 87.1 us
  other arithmetic: 79.9 us -> 37.4 us
  blocking collectives: 35.8 us -> 0 us
  local copies, waits for them, and re-layouts: 38.7 us -> 21 us
    pallas_call x0 -> x4, Pallas kernels: none -> 346 us  [the longest x1 128 us: body(): pl.pallas_call(functools.partial(hidden_kernel, n, pieces), out_shape=(sh...]
    ppermute x12 -> x3, waiting for transfers between devices: 212 us -> 46.5 us  [gather(): lax.ppermute(down[-1], self.axis, [(i, i - 1) for i in range(1, n) if i +...]
    dot_general x12 -> x1, matrix products: 148 us -> 14.1 us  [body(): jnp.einsum('rf,rd->fd', hidden, cot_rows, preferred_element_type=F32)]
    ppermute x12 -> x6, waiting for transfers between devices: 126 us -> 45.4 us  [scatter_sum(): lax.ppermute(term.astype(BF), self.axis, [(i, i + 1) for i in range(min(r...]
    ppermute x12 -> x3, starting transfers between devices: 77.8 us -> 3.86 us  [gather(): lax.ppermute(up[-1], self.axis, [(i, i + 1) for i in range(n - 1) if i -...]
    all_gather x1, waiting for transfers between devices: 0.02 us -> 47.1 us  [body(): w_qkv = lax.all_gather(qkv_weight, 'dp', axis=1, tiled=True)]
    all_gather x2 -> x0, blocking collectives: 27.1 us -> none  [the longest x1 17.5 us: body(): whole = lax.all_gather(over_dp[:, :6 * piece], 'tensor', axis=0)]
    ppermute x12 -> x6, starting transfers between devices: 69.8 us -> 42.8 us  [scatter_sum(): lax.ppermute(term.astype(BF), self.axis, [(i, i + 1) for i in range(min(r...]
  transfers between devices with their start and end apart: 57 -> 28, of which waited for: 24 -> 12; matrix products, arithmetic and copies ran while one was open for 29% -> 15% of each run, Pallas kernels for 0% -> 29%
where the time goes in v2:
time: 769 us; the launch traced here: 760 us
  Pallas kernels  346 us (45%)
  waiting for transfers between devices  185 us (24%)
  starting transfers between devices  87.1 us (11%)
  matrix products  67.9 us (9%)
  other arithmetic  37.4 us (5%)
  local copies, waits for them, and re-layouts  21 us (3%)
  between operations  15.3 us (2%)
    pallas_call x1, Pallas kernels, body(): pl.pallas_call(functools.partial(hidden_kernel, n, pieces), out_shape=(sh...  128 us
    pallas_call x1, Pallas kernels, body(): pl.pallas_call(functools.partial(attend_kernel, n, pieces), out_shape=(sh...  101 us
    pallas_call x1, Pallas kernels, body(): pl.pallas_call(functools.partial(project_kernel, n, m, (piece, qv_piece))...  96 us
    all_gather x1, waiting for transfers between devices, body(): w_qkv = lax.all_gather(qkv_weight, 'dp', axis=1, tiled=True)  47.1 us
    ppermute x3, waiting for transfers between devices, gather(): lax.ppermute(down[-1], self.axis, [(i, i - 1) for i in range(1, n) if i +...  46.5 us
    ppermute x6, waiting for transfers between devices, scatter_sum(): lax.ppermute(term.astype(BF), self.axis, [(i, i + 1) for i in range(min(r...  45.4 us
    ppermute x6, starting transfers between devices, scatter_sum(): lax.ppermute(term.astype(BF), self.axis, [(i, i + 1) for i in range(min(r...  42.8 us
    all_to_all x1, starting transfers between devices, body(): lax.all_to_all(vectors, 'tensor', 0, 0)  26.4 us
  transfers between devices with their start and end apart: 28, of which 12 were waited for; matrix products, arithmetic and copies ran while one was open for 15% of the time, Pallas kernels for 29%

profile of v2, /device:TPU:0, one launch (start us, length us, event | category | flops | bytes accessed | tf_op | source)
XLA Modules:
  0.0 760.0 jit_solution(1102469243158090272)
XLA Ops:
  11.0 47.1 %all-gather.5.cloned.1.call-done.w_hbm = bf16[3,2048,512]{2,1,0:T(8,128)(2,1)} async-done(((bf16[3,256,512]{2,1,0:T(8,128)(2,1)}), bf16[3,2048,512]{2,1,0:T(8,128)(2,1)}) %all-gather.5.cloned.1.call-update) | async-done | bytes 6291472 | tf_op jit(solution)/shard_map/all_gather | solution.py:568
  58.1 96.0 %project.1 = (bf16[1024,2048]{1,0:T(8,128)(2,1)}, bf16[3,1024,512]{2,1,0:T(8,128)(2,1)}, f32[32,16,128]{2,1,0:T(8,128)}) custom-call(f32[16,128]{1,0:T(8,128)} %fusion.25.pack_ref, bf16[256,2048]{1,0:T(8,128)(2,1)} %x_ref.3, bf16[3,2048,512]{2,1,0:T(8,128)(2,1)} %all-gather.5.cloned.1.call-done.w_hbm), custom_call_target="tpu_custom_call" | custom-call | tf_op jit(solution)/shard_map/project/pallas_call | solution.py:574
  157.9 100.7 %attend.1 = (bf16[1024,512]{1,0:T(8,128)(2,1)}, f32[256,2048]{1,0:T(8,128)}, bf16[256,2048]{1,0:T(8,128)(2,1)}, bf16[4,256,2048]{2,1,0:T(8,128)(2,1)}) custom-call(bf16[3,1024,512]{2,1,0:T(8,128)(2,1)} %get-tuple-element.28.qkv_ref, bf16[512,2048]{1,0:T(8,128)(2,1)} %all-gather.7.cloned.1.call-done.w_ref, bf16[256,2048]{1,0:T(8,128)(2,1)} %x_ref.3, ...), custom_call_target="tpu_custom_call" | custom-call | tf_op jit(solution)/shard_map/attend/pallas_call | solution.py:592
  258.7 127.5 %hidden.1 = (bf16[4,256,2048]{2,1,0:T(8,128)(2,1)}, bf16[4,256,2048]{2,1,0:T(8,128)(2,1)}, bf16[4,256,2048]{2,1,0:T(8,128)(2,1)}, f32[256,2048]{1,0:T(8,128)}, b...) custom-call(bf16[256,2048]{1,0:T(8,128)(2,1)} %get-tuple-element.31.c_ref, ...), custom_call_target="tpu_custom_call" | custom-call | tf_op jit(solution)/shard_map/hidden/pallas_call | solution.py:602
  386.2 1.5 collective-permute-start.7
  389.0 17.3 %collective-permute-done.7 = bf16[256,2048]{1,0:T(8,128)(2,1)S(1)} collective-permute-done((bf16[256,2048]{1,0:T(8,128)(2,1)}, bf16[256,2048]{1,0:T(8,128)(2,1)S(1)}, u32[]{:S(2)}, u32[]{:S(2)}) %collective-permute-start.7) | collective-permute-done | bytes 1048608 | tf_op jit(solution)/shard_map/ppermute | solution.py:514
  406.3 1.6 collective-permute-start.9
  407.9 2.4 collective-permute-done.6
  413.1 25.1 %collective-permute-done.8 = bf16[256,2048]{1,0:T(8,128)(2,1)} collective-permute-done((bf16[256,2048]{1,0:T(8,128)(2,1)S(1)}, bf16[256,2048]{1,0:T(8,128)(2,1)}, u32[]{:S(2)}, u32[]{:S(2)}) %collective-permute-start.8) | collective-permute-done | bytes 1048608 | tf_op jit(solution)/shard_map/ppermute | solution.py:513
  439.9 1.6 select_dynamic-update-slice_fusion.1
  441.6 19.0 %collective-permute-done.10 = bf16[256,2048]{1,0:T(8,128)(2,1)S(1)} collective-permute-done((bf16[256,2048]{1,0:T(8,128)(2,1)}, bf16[256,2048]{1,0:T(8,128)(2,1)S(1)}, u32[]{:S(2)}, u32[]{:S(2)}) %collective-permute-start.10) | collective-permute-done | bytes 1048608 | tf_op jit(solution)/shard_map/ppermute | solution.py:513
  461.3 2.1 copy-done.6
  463.3 3.7 convolution_convert_fusion.1
  467.3 14.1 %bitcast_convert_fusion.1 = bf16[2048,2048]{1,0:T(8,128)(2,1)} fusion(bf16[4,256,2048]{2,1,0:T(8,128)(2,1)} %get-tuple-element.40, bf16[4,256,2048]{2,1,0:T(8,128)(2,1)} %get-tuple-element.41), kind=kOutput, calls=%fused_computation.1 | convolution fusion | flops 8594128896 | bytes 16777216 | tf_op jit(solution)/shard_map/rd,rf->df/dot_general | solution.py:620
  481.5 14.1 %bitcast_convert_fusion = bf16[2048,2048]{1,0:T(8,128)(2,1)} fusion(bf16[4,256,2048]{2,1,0:T(8,128)(2,1)} %get-tuple-element.33, bf16[4,256,2048]{2,1,0:T(8,128)(2,1)} %get-tuple-element.32.cot_hbm), kind=kOutput, calls=%fused_computation | convolution fusion | flops 8594128896 | bytes 16777216 | tf_op jit(solution)/shard_map/rf,rd->fd/dot_general | solution.py:619
  495.6 12.6 %convolution_convert_fusion = bf16[1024,2048]{1,0:T(8,128)(2,1)S(1)} fusion(bf16[1024,2048]{1,0:T(8,128)(2,1)} %bitcast.115, bf16[2048,2048]{1,0:T(8,128)(2,1)} %all-gather.11.cloned.1.call-done.down_hbm), kind=kOutput, calls=%fused_computation.6 | convolution fusion | flops 8592031744 | bytes 16777216 | tf_op jit(solution)/shard_map/dot_general | solution.py:617
  508.3 2.0 copy-done.1
  511.3 2.8 collective-permute-start
  514.1 3.3 convolution_convert_fusion.2.do_ref
  517.5 21.8 %attend_back.1 = bf16[3,1024,512]{2,1,0:T(8,128)(2,1)} custom-call(bf16[3,1024,512]{2,1,0:T(8,128)(2,1)} %get-tuple-element.28.qkv_ref, bf16[1024,512]{1,0:T(8,128)(2,1)} %convolution_convert_fusion.2.do_ref), custom_call_target="tpu_custom_call" | custom-call | flops 3758096384 | bytes 7340032 | tf_op jit(solution)/shard_map/attend_back/pallas_call | solution.py:627
  539.3 11.2 %convert_bitcast_fusion = bf16[3,2048,512]{1,2,0:T(8,128)(2,1)} fusion(bf16[3,1024,512]{2,1,0:T(8,128)(2,1)} %attend_back.1, bf16[1024,2048]{1,0:T(8,128)(2,1)} %get-tuple-element.38), kind=kOutput, calls=%fused_computation.3 | convolution fusion | flops 6445596672 | bytes 13631488 | tf_op jit(solution)/shard_map/rd,kre->kde/dot_general | solution.py:641
  550.6 1.9 copy-done.9
  552.5 8.9 %bitcast_convert_fusion.2 = bf16[1024,2048]{1,0:T(8,128)(2,1)S(1)} fusion(bf16[3,1024,512]{2,1,0:T(8,128)(2,1)S(1)} %copy-done.9, bf16[3,2048,512]{2,1,0:T(8,128)(2,1)} %all-gather.5.cloned.1.call-done.w_hbm), kind=kOutput, calls=%fused_computation.2 | convolution fusion | flops 6444548096 | bytes 13631488 | tf_op jit(solution)/shard_map/kre,kde->rd/dot_general | solution.py:634
  561.4 2.0 copy-done.3
  563.5 2.3 collective-permute-start.12
  565.8 3.4 fusion.13
  569.1 1.6 collective-permute-start.1
  570.7 17.6 %collective-permute-done.12 = bf16[256,2048]{1,0:T(8,128)(2,1)} collective-permute-done((bf16[256,2048]{1,0:T(8,128)(2,1)S(1)}, bf16[256,2048]{1,0:T(8,128)(2,1)}, u32[]{:S(2)}, u32[]{:S(2)}) %collective-permute-start.12) | collective-permute-done | bytes 1048608 | tf_op jit(solution)/shard_map/ppermute | solution.py:535
  588.3 1.9 fusion.15
  590.3 4.7 collective-permute-start.13
  595.0 15.9 %collective-permute-done.1 = bf16[256,2048]{1,0:T(8,128)(2,1)S(1)} collective-permute-done((bf16[256,2048]{1,0:T(8,128)(2,1)}, bf16[256,2048]{1,0:T(8,128)(2,1)S(1)}, u32[]{:S(2)}, u32[]{:S(2)}) %collective-permute-start.1) | collective-permute-done | bytes 1048608 | tf_op jit(solution)/shard_map/ppermute | solution.py:535
  610.9 2.6 add_convert_fusion.3
  614.4 11.9 %collective-permute-done.13 = bf16[256,2048]{1,0:T(8,128)(2,1)S(1)} collective-permute-done((bf16[256,2048]{1,0:T(8,128)(2,1)S(1)}, bf16[256,2048]{1,0:T(8,128)(2,1)S(1)}, u32[]{:S(2)}, u32[]{:S(2)}) %collective-permute-start.13) | collective-permute-done | bytes 1048608 | tf_op jit(solution)/shard_map/ppermute | solution.py:535
  631.5 6.7 collective-permute-start.2
  640.9 24.7 %collective-permute-start.14 = (bf16[256,2048]{1,0:T(8,128)(2,1)}, bf16[256,2048]{1,0:T(8,128)(2,1)}, u32[]{:S(2)}, u32[]{:S(2)}) collective-permute-start(bf16[256,2048]{1,0:T(8,128)(2,1)} %get-tuple-element.119), channel_id=1, source_target_pairs={{0,1},{1,2},{2,3},{4,5},{5,6},{6,7},{8,9},{9,10},{10,11},{12,13},{... | collective-permute-start | bytes 3145736 | tf_op jit(solution)/shard_map/ppermute | solution.py:535
  670.4 2.3 convert_reduce_fusion
  672.8 7.9 %collective-permute-done.5 = bf16[256,2048]{1,0:T(8,128)(2,1)} collective-permute-done((bf16[256,2048]{1,0:T(8,128)(2,1)}, bf16[256,2048]{1,0:T(8,128)(2,1)}, u32[]{:S(2)}, u32[]{:S(2)}) %collective-permute-start.5) | collective-permute-done | bytes 1048608 | tf_op jit(solution)/shard_map/ppermute | solution.py:538
  680.8 3.5 fusion.19
  684.3 1.8 convert_element_type.204
  686.1 12.2 %collective-permute-done.17 = bf16[256,2048]{1,0:T(8,128)(2,1)} collective-permute-done((bf16[256,2048]{1,0:T(8,128)(2,1)}, bf16[256,2048]{1,0:T(8,128)(2,1)}, u32[]{:S(2)}, u32[]{:S(2)}) %collective-permute-start.17) | collective-permute-done | bytes 1048608 | tf_op jit(solution)/shard_map/ppermute | solution.py:538
  698.3 3.1 fusion.11
  702.5 4.0 all-to-all-start
  706.5 5.0 all-to-all-done
  712.1 26.4 %all-to-all-start.1 = ((f32[4,1,384]{2,1,0:T(1,128)}), f32[4,1,384]{2,1,0:T(1,128)S(1)}, u32[]{:S(2)}, u32[]{:S(2)}) async-start(f32[4,1,384]{2,1,0:T(1,128)} %slice.106), calls=%async_computation.1 | async-start | bytes 12288 | tf_op jit(solution)/shard_map/all_to_all | solution.py:659
  738.5 3.4 fusion.10
  744.7 2.8 convert_element_type.206
  747.5 2.7 convert_element_type.208
  750.2 2.6 copy.67
  (140 shorter events, 33.5 us)
Async XLA Ops:
  7.2 2.9 copy-start.22
  7.2 3.0 copy-start.14
  7.2 3.0 copy-start.15
  7.2 3.0 copy-start.16
  7.2 3.0 copy-start.17
  7.2 3.0 copy-start.18
  7.2 3.0 copy-start.19
  7.3 3.2 copy-start.20
  7.3 50.9 %all-gather.5.cloned.1.call-start = ((), (), s32[]{:S(2)}) async-start(), calls=%async_computation.6 | async-start | bytes 7077888 | tf_op jit(solution)/shard_map/all_gather | solution.py:568
  8.0 149.9 %all-gather.7.cloned.1.call-start = ((), (), s32[]{:S(2)}) async-start(), calls=%async_computation.7 | async-start | bytes 2359296 | tf_op jit(solution)/shard_map/all_gather | solution.py:569
  8.7 249.9 %all-gather.9.cloned.1.call-start = ((), (), s32[]{:S(2)}) async-start(), calls=%async_computation.8 | async-start | bytes 9437184 | tf_op jit(solution)/shard_map/all_gather | solution.py:570
  9.5 249.2 %all-gather.11.cloned.1.call-start = ((), (), s32[]{:S(2)}) async-start(), calls=%async_computation.9 | async-start | bytes 9437184 | tf_op jit(solution)/shard_map/all_gather | solution.py:571
  10.1 674.2 %reduce-scatter.7.cloned.1.call-start = ((), (), s32[]{:S(2)}) async-start(), calls=%async_computation.11 | async-start | bytes 2359296 | tf_op jit(solution)/shard_map/reduce_scatter | solution.py:644
  386.2 26.0 %copy-start.10 = (bf16[256,2048]{1,0:T(8,128)(2,1)S(1)}, bf16[256,2048]{1,0:T(8,128)(2,1)}, u32[]{:S(2)}) copy-start(bf16[256,2048]{1,0:T(8,128)(2,1)} %get-tuple-element.35) | copy-start | bytes 3145732
  386.2 20.1 %collective-permute-start.7 = (bf16[256,2048]{1,0:T(8,128)(2,1)}, bf16[256,2048]{1,0:T(8,128)(2,1)S(1)}, u32[]{:S(2)}, u32[]{:S(2)}) collective-permute-start(bf16[256,2048]{1,0:T(8,128)(2,1)} %get-tuple-element.35), channel_id=1, source_target_pairs={{0,1},{1,2},{2,3},{4,5},{5,6},{6,7},{8,9},{9,10},{10,11},{12,13},{... | collective-permute-start | bytes 3145736 | tf_op jit(solution)/shard_map/ppermute | solution.py:514
  387.7 22.6 %collective-permute-start.6 = (bf16[256,2048]{1,0:T(8,128)(2,1)}, bf16[256,2048]{1,0:T(8,128)(2,1)S(1)}, u32[]{:S(2)}, u32[]{:S(2)}) collective-permute-start(bf16[256,2048]{1,0:T(8,128)(2,1)} %get-tuple-element.35), channel_id=1, source_target_pairs={{1,0},{2,1},{3,2},{5,4},{6,5},{7,6},{9,8},{10,9},{11,10},{13,12},{... | collective-permute-start | bytes 3145736 | tf_op jit(solution)/shard_map/ppermute | solution.py:513
  406.3 6.1 collective-permute-start.9
  410.4 27.9 %collective-permute-start.8 = (bf16[256,2048]{1,0:T(8,128)(2,1)S(1)}, bf16[256,2048]{1,0:T(8,128)(2,1)}, u32[]{:S(2)}, u32[]{:S(2)}) collective-permute-start(bf16[256,2048]{1,0:T(8,128)(2,1)S(1)} %collective-permute-done.6), channel_id=1, source_target_pairs={{1,0},{2,1},{5,4},{6,5},{9,8},{10,9},{13,12},{14,13},{17,16},{18,1... | collective-permute-start | bytes 3145736 | tf_op jit(solution)/shard_map/ppermute | solution.py:513
  412.4 29.2 %collective-permute-start.11 = (bf16[256,2048]{1,0:T(8,128)(2,1)}, bf16[256,2048]{1,0:T(8,128)(2,1)S(1)}, u32[]{:S(2)}, u32[]{:S(2)}) collective-permute-start(bf16[256,2048]{1,0:T(8,128)(2,1)} %collective-permute-done.9), channel_id=1, source_target_pairs={{2,3},{6,7},{10,11},{14,15},{18,19},{22,23},{26,27},{30,31}} | collective-permute-start | bytes 3145736 | tf_op jit(solution)/shard_map/ppermute | solution.py:514
  438.2 22.3 %collective-permute-start.10 = (bf16[256,2048]{1,0:T(8,128)(2,1)}, bf16[256,2048]{1,0:T(8,128)(2,1)S(1)}, u32[]{:S(2)}, u32[]{:S(2)}) collective-permute-start(bf16[256,2048]{1,0:T(8,128)(2,1)} %collective-permute-done.8), channel_id=1, source_target_pairs={{1,0},{5,4},{9,8},{13,12},{17,16},{21,20},{25,24},{29,28}} | collective-permute-start | bytes 3145736 | tf_op jit(solution)/shard_map/ppermute | solution.py:513
  441.6 21.8 %copy-start.21 = (bf16[1024,512]{1,0:T(8,128)(2,1)S(1)}, bf16[1024,512]{1,0:T(8,128)(2,1)}, u32[]{:S(2)}) copy-start(bf16[1024,512]{1,0:T(8,128)(2,1)} %get-tuple-element.39) | copy-start | bytes 3145732
  461.3 2.1 copy-start.6
  467.1 277.6 %reduce-scatter.9.cloned.1.call-start = ((), (), s32[]{:S(2)}) async-start(), calls=%async_computation.12 | async-start | bytes 9437184 | tf_op jit(solution)/shard_map/reduce_scatter | solution.py:643
  481.4 266.1 %reduce-scatter.11.cloned.1.call-start = ((), (), s32[]{:S(2)}) async-start(), calls=%async_computation.13 | async-start | bytes 9437184 | tf_op jit(solution)/shard_map/reduce_scatter | solution.py:642
  495.5 254.6 %reduce-scatter.5.cloned.1.call-start = ((), (), s32[]{:S(2)}) async-start(), calls=%async_computation.10 | async-start | bytes 7077888 | tf_op jit(solution)/shard_map/reduce_scatter | solution.py:645
  495.6 18.5 %copy-start.7 = (bf16[1024,2048]{1,0:T(8,128)(2,1)S(1)}, bf16[1024,2048]{1,0:T(8,128)(2,1)}, u32[]{:S(2)}) copy-start(bf16[1024,2048]{1,0:T(8,128)(2,1)} %copy-done.6) | copy-start | bytes 12582916
  495.6 18.5 %copy-start.8 = (bf16[512,2048]{1,0:T(8,128)(2,1)S(1)}, bf16[512,2048]{1,0:T(8,128)(2,1)}, u32[]{:S(2)}) copy-start(bf16[512,2048]{1,0:T(8,128)(2,1)} %all-gather.7.cloned.1.call-done.w_ref) | copy-start | bytes 6291460
  511.3 54.5 %collective-permute-start = (bf16[256,2048]{1,0:T(8,128)(2,1)}, bf16[256,2048]{1,0:T(8,128)(2,1)}, u32[]{:S(2)}, u32[]{:S(2)}) collective-permute-start(bf16[256,2048]{1,0:T(8,128)(2,1)} %dynamic-slice_bitcast_fusion.2), channel_id=1, source_target_pairs={{0,1},{4,5},{8,9},{12,13},{16,17},{20,21},{24,25},{28,29}} | collective-permute-start | bytes 3145736 | tf_op jit(solution)/shard_map/ppermute | solution.py:535
  561.4 2.1 copy-start.3
  563.5 24.8 %collective-permute-start.12 = (bf16[256,2048]{1,0:T(8,128)(2,1)S(1)}, bf16[256,2048]{1,0:T(8,128)(2,1)}, u32[]{:S(2)}, u32[]{:S(2)}) collective-permute-start(bf16[256,2048]{1,0:T(8,128)(2,1)S(1)} %dynamic-slice_bitcast_fusion), channel_id=1, source_target_pairs={{0,1},{4,5},{8,9},{12,13},{16,17},{20,21},{24,25},{28,29}} | collective-permute-start | bytes 3145736 | tf_op jit(solution)/shard_map/ppermute | solution.py:535
  569.1 41.8 %collective-permute-start.1 = (bf16[256,2048]{1,0:T(8,128)(2,1)}, bf16[256,2048]{1,0:T(8,128)(2,1)S(1)}, u32[]{:S(2)}, u32[]{:S(2)}) collective-permute-start(bf16[256,2048]{1,0:T(8,128)(2,1)} %fusion.13), channel_id=1, source_target_pairs={{0,1},{1,2},{4,5},{5,6},{8,9},{9,10},{12,13},{13,14},{16,17},{17,1... | collective-permute-start | bytes 3145736 | tf_op jit(solution)/shard_map/ppermute | solution.py:535
  590.3 36.0 %collective-permute-start.13 = (bf16[256,2048]{1,0:T(8,128)(2,1)S(1)}, bf16[256,2048]{1,0:T(8,128)(2,1)S(1)}, u32[]{:S(2)}, u32[]{:S(2)}) collective-permute-start(bf16[256,2048]{1,0:T(8,128)(2,1)S(1)} %fusion.15), channel_id=1, source_target_pairs={{0,1},{1,2},{4,5},{5,6},{8,9},{9,10},{12,13},{13,14},{16,17},{17,1... | collective-permute-start | bytes 3145736 | tf_op jit(solution)/shard_map/ppermute | solution.py:535
  595.0 31.3 %copy-start.4 = (bf16[1024,2048]{1,0:T(8,128)(2,1)S(1)}, bf16[1024,2048]{1,0:T(8,128)(2,1)}, u32[]{:S(2)}) copy-start(bf16[1024,2048]{1,0:T(8,128)(2,1)} %copy-done.3) | copy-start | bytes 12582916
  613.5 15.0 %copy-start.2 = (bf16[1024,2048]{1,0:T(8,128)(2,1)S(1)}, bf16[1024,2048]{1,0:T(8,128)(2,1)}, u32[]{:S(2)}) copy-start(bf16[1024,2048]{1,0:T(8,128)(2,1)} %copy-done.1) | copy-start | bytes 12582916
  613.5 15.0 %collective-permute-start.3 = (bf16[256,2048]{1,0:T(8,128)(2,1)S(1)}, bf16[256,2048]{1,0:T(8,128)(2,1)S(1)}, u32[]{:S(2)}, u32[]{:S(2)}) collective-permute-start(bf16[256,2048]{1,0:T(8,128)(2,1)S(1)} %get-tuple-element.122), channel_id=1, source_target_pairs={{3,2},{7,6},{11,10},{15,14},{19,18},{23,22},{27,26},{31,30}} | collective-permute-start | bytes 3145736 | tf_op jit(solution)/shard_map/ppermute | solution.py:538
  627.6 3.2 copy-start
  627.6 2.0 collective-permute-start.15
  628.9 9.2 %collective-permute-start.4 = (bf16[256,2048]{1,0:T(8,128)(2,1)S(1)}, bf16[256,2048]{1,0:T(8,128)(2,1)S(1)}, u32[]{:S(2)}, u32[]{:S(2)}) collective-permute-start(bf16[256,2048]{1,0:T(8,128)(2,1)S(1)} %fusion.14), channel_id=1, source_target_pairs={{2,1},{3,2},{6,5},{7,6},{10,9},{11,10},{14,13},{15,14},{18,17},{19... | collective-permute-start | bytes 3145736 | tf_op jit(solution)/shard_map/ppermute | solution.py:538
  630.1 35.6 %collective-permute-start.16 = (bf16[256,2048]{1,0:T(8,128)(2,1)S(1)}, bf16[256,2048]{1,0:T(8,128)(2,1)S(1)}, u32[]{:S(2)}, u32[]{:S(2)}) collective-permute-start(bf16[256,2048]{1,0:T(8,128)(2,1)S(1)} %fusion.16), channel_id=1, source_target_pairs={{2,1},{3,2},{6,5},{7,6},{10,9},{11,10},{14,13},{15,14},{18,17},{19... | collective-permute-start | bytes 3145736 | tf_op jit(solution)/shard_map/ppermute | solution.py:538
  631.5 37.7 %copy-start.13 = (f32[8,2048]{1,0:T(8,128)S(1)}, f32[8,2048]{1,0:T(8,128)}, u32[]{:S(2)}) copy-start(f32[8,2048]{1,0:T(8,128)} %get-tuple-element.36) | copy-start | bytes 196612
  631.5 41.4 %collective-permute-start.2 = (bf16[256,2048]{1,0:T(8,128)(2,1)}, bf16[256,2048]{1,0:T(8,128)(2,1)}, u32[]{:S(2)}, u32[]{:S(2)}) collective-permute-start(bf16[256,2048]{1,0:T(8,128)(2,1)} %get-tuple-element.121), channel_id=1, source_target_pairs={{0,1},{1,2},{2,3},{4,5},{5,6},{6,7},{8,9},{9,10},{10,11},{12,13},{... | collective-permute-start | bytes 3145736 | tf_op jit(solution)/shard_map/ppermute | solution.py:535
  639.5 41.3 %copy-start.5 = (f32[256,2048]{1,0:T(8,128)S(1)}, f32[256,2048]{1,0:T(8,128)}, u32[]{:S(2)}) copy-start(f32[256,2048]{1,0:T(8,128)} %get-tuple-element.30.h_ref) | copy-start | bytes 6291460
  639.5 41.3 %copy-start.12 = (f32[1,16,128]{2,0,1:T(1,128)S(1)}, f32[1,16,128]{2,0,1:T(1,128)}, u32[]{:S(2)}) copy-start(f32[1,16,128]{2,0,1:T(1,128)} %get-tuple-element.123) | copy-start | bytes 24580
  639.5 41.3 %collective-permute-start.5 = (bf16[256,2048]{1,0:T(8,128)(2,1)}, bf16[256,2048]{1,0:T(8,128)(2,1)}, u32[]{:S(2)}, u32[]{:S(2)}) collective-permute-start(bf16[256,2048]{1,0:T(8,128)(2,1)} %add_convert_fusion.2), channel_id=1, source_target_pairs={{1,0},{2,1},{3,2},{5,4},{6,5},{7,6},{9,8},{10,9},{11,10},{13,12},{... | collective-permute-start | bytes 3145736 | tf_op jit(solution)/shard_map/ppermute | solution.py:538
  640.9 45.2 %collective-permute-start.14 = (bf16[256,2048]{1,0:T(8,128)(2,1)}, bf16[256,2048]{1,0:T(8,128)(2,1)}, u32[]{:S(2)}, u32[]{:S(2)}) collective-permute-start(bf16[256,2048]{1,0:T(8,128)(2,1)} %get-tuple-element.119), channel_id=1, source_target_pairs={{0,1},{1,2},{2,3},{4,5},{5,6},{6,7},{8,9},{9,10},{10,11},{12,13},{... | collective-permute-start | bytes 3145736 | tf_op jit(solution)/shard_map/ppermute | solution.py:535
  667.0 31.3 %collective-permute-start.17 = (bf16[256,2048]{1,0:T(8,128)(2,1)}, bf16[256,2048]{1,0:T(8,128)(2,1)}, u32[]{:S(2)}, u32[]{:S(2)}) collective-permute-start(bf16[256,2048]{1,0:T(8,128)(2,1)} %add_convert_fusion), channel_id=1, source_target_pairs={{1,0},{2,1},{3,2},{5,4},{6,5},{7,6},{9,8},{10,9},{11,10},{13,12},{... | collective-permute-start | bytes 3145736 | tf_op jit(solution)/shard_map/ppermute | solution.py:538
  702.5 9.0 %all-to-all-start = ((f32[8,1,1920]{2,1,0:T(1,128)}), f32[8,1,1920]{2,1,0:T(1,128)S(1)}, u32[]{:S(2)}, u32[]{:S(2)}) async-start(f32[8,1,1920]{2,1,0:T(1,128)} %copy.62), calls=%async_computation | async-start | bytes 122880 | tf_op jit(solution)/shard_map/all_to_all | solution.py:655
  712.1 31.9 %all-to-all-start.1 = ((f32[4,1,384]{2,1,0:T(1,128)}), f32[4,1,384]{2,1,0:T(1,128)S(1)}, u32[]{:S(2)}, u32[]{:S(2)}) async-start(f32[4,1,384]{2,1,0:T(1,128)} %slice.106), calls=%async_computation.1 | async-start | bytes 12288 | tf_op jit(solution)/shard_map/all_to_all | solution.py:659
  (3 other events, 4.6 us)
Sparse Core Ops, SparseCore 0:
  10.0 48.1 all-gather.4
  60.0 28.0 all-gather.6
  90.0 54.4 all-gather.8
  146.2 56.0 all-gather.10
  467.2 39.5 reduce-scatter.6
  510.1 71.4 reduce-scatter.8
  585.1 71.2 reduce-scatter.10
  659.8 61.5 reduce-scatter.4

commit v3 on v2

--- a/solution.py
+++ b/solution.py
@@ -68,6 +68,35 @@
     pl.semaphore_wait(barrier, jnp.minimum(i, 1) + jnp.minimum(n - 1 - i, 1))
 
 
+def greet_all(me, n, total):
+    barrier = pltpu.get_barrier_semaphore()
+
+    def greet(s):
+        other = (me + s + 1) % total
+        pl.semaphore_signal(barrier, inc=1, device_id={"dp": other // n, "tensor": other % n}, device_id_type=MESH)
+
+    loop(total - 1, greet)
+    pl.semaphore_wait(barrier, total - 1)
+
+
+def rounds(i, n, line, compute):
+    def round_of(r):
+        @pl.when(r > 0)
+        def _():
+            line.step(r)
+
+        def side(s):
+            j = jnp.where(s == 0, i - r, i + r)
+
+            @pl.when(jnp.logical_and(jnp.logical_and(j >= 0, j <= n - 1), s * r == s * jnp.maximum(r, 1)))
+            def _():
+                compute(j)
+
+        loop(2, side)
+
+    loop(n, round_of)
+
+
 class LineGather:
     def __init__(self, i, n, own, buf, send, recv):
         self.i, self.n, self.own, self.buf, self.send, self.recv = i, n, own, buf, send, recv
@@ -197,20 +226,11 @@
         loop(n, one)
 
 
-def project_kernel(n, m, pieces, pack_ref, x_ref, w_hbm, a_ref, qkv_ref, vec_ref, buf, w, affine, bias, w_sem, own_sem,
-                   send, recv, v_send, v_recv):
+def tokens_kernel(n, m, piece, pack_ref, x_ref, a_ref, vec_ref, buf, affine, own_sem, send, recv, v_send, v_recv):
     i, row = lax.axis_index("tensor"), lax.axis_index("dp")
     me, total = row * n + i, m * n
-    size, width = x_ref.shape[0], w.shape[2]
-    barrier = pltpu.get_barrier_semaphore()
-
-    def greet(s):
-        other = (me + s + 1) % total
-        pl.semaphore_signal(barrier, inc=1, device_id={"dp": other // n, "tensor": other % n}, device_id_type=MESH)
-
-    loop(total - 1, greet)
-    pl.semaphore_wait(barrier, total - 1)
-
+    size = x_ref.shape[0]
+    greet_all(me, n, total)
     line = LineGather(i, n, x_ref, buf, send, recv)
     line.start()
 
@@ -222,12 +242,8 @@
     loop(total - 1, lambda s: vector(me, (me + s + 1) % total).start())
     own_copy = pltpu.make_async_copy(x_ref, buf.at[i], own_sem)
     own_copy.start()
-    weights = pltpu.make_async_copy(w_hbm, w, w_sem)
-    weights.start()
     vec_ref[me] = pack_ref[...]
     loop(total - 1, lambda s: vector((me + s + 1) % total, me).wait_recv())
-
-    piece, qv_piece = pieces
     depth = affine.shape[1]
     group = LANES // piece
     for tile in range(depth // LANES):
@@ -235,14 +251,7 @@
         for g in range(1, group):
             value = value + vec_ref[tile * group + g, 0:2, :]
         affine[0:2, tile * LANES : (tile + 1) * LANES] = value
-    group = LANES // qv_piece
-    for tile in range(width // LANES):
-        value = vec_ref[tile * group * n + i, 6:8, :]
-        for g in range(1, group):
-            value = value + vec_ref[(tile * group + g) * n + i, 6:8, :]
-        bias[0:2, tile * LANES : (tile + 1) * LANES] = value
     own_copy.wait()
-    weights.wait()
 
     def compute(j):
         def norm(b):
@@ -251,36 +260,21 @@
             a_ref[here, :] = (normal * affine[0:1, :] + affine[1:2, :]).astype(BF)
 
         loop(size // RB, norm)
-        here = rows_at(j, size)
-        for t in range(3):
-            value = jnp.dot(a_ref[here, :], w[t], preferred_element_type=F32)
-            if t != 1:
-                value = value + bias[t // 2 : t // 2 + 1, :]
-            qkv_ref[t, here, :] = value.astype(BF)
-
-    def round_of(r):
-        @pl.when(r > 0)
-        def _():
-            line.step(r)
-
-        def side(s):
-            j = jnp.where(s == 0, i - r, i + r)
-
-            @pl.when(jnp.logical_and(jnp.logical_and(j >= 0, j <= n - 1), s * r == s * jnp.maximum(r, 1)))
-            def _():
-                compute(j)
-
-        loop(2, side)
-
-    loop(n, round_of)
+
+    rounds(i, n, line, compute)
     line.finish()
     loop(total - 1, lambda s: vector(me, (me + s + 1) % total).wait_send())
 
 
-def attend_kernel(n, pieces, qkv_ref, w_ref, x_ref, cot_ref, out_bias, gain, shift, o_ref, h_ref, c_ref, cot_all,
-                  part, land, send, recv, s_send, s_recv, own_sem):
+def attend_kernel(n, pieces, a_hbm, wq_hbm, wo_hbm, x_ref, cot_ref, bias, out_bias, gain, shift, qkv_ref, o_ref, h_ref,
+                  c_ref, cot_all, a_ref, wq_ref, w_ref, part, land, send, recv, s_send, s_recv, own_sem, a_sem, w_sem):
     i = lax.axis_index("tensor")
     size = x_ref.shape[0]
+    loads = [pltpu.make_async_copy(a_hbm, a_ref, a_sem)]
+    loads += [pltpu.make_async_copy(wq_hbm.at[t], wq_ref.at[t], w_sem.at[t]) for t in range(3)]
+    loads += [pltpu.make_async_copy(wo_hbm, w_ref, w_sem.at[3])]
+    for load in loads:
+        load.start()
     heads = qkv_ref.shape[2] // HD
     depth = w_ref.shape[1]
     greet_neighbours(i, n)
@@ -289,7 +283,19 @@
     own_copy = pltpu.make_async_copy(cot_ref, cot_all.at[i], own_sem)
     own_copy.start()
 
+    loads[0].wait()
     block = 256
+    for t in range(3):
+        loads[1 + t].wait()
+
+        def project(b):
+            here = rows_at(b, block)
+            value = jnp.dot(a_ref[here, :], wq_ref[t], preferred_element_type=F32)
+            if t != 1:
+                value = value + bias[t // 2 : t // 2 + 1, :]
+            qkv_ref[t, here, :] = value.astype(BF)
+
+        loop(LEN // block, project)
 
     def head(t):
         cols = pl.ds(pl.multiple_of(t * HD, HD), HD)
@@ -304,6 +310,7 @@
             o_ref[here, cols] = jnp.dot(prob, qkv_ref[2, 0:keys, cols], preferred_element_type=F32).astype(BF)
 
     loop(heads, head)
+    loads[4].wait()
     sums = LineSum(i, n, part, land, s_send, s_recv, pieces)
     tile = 512
 
@@ -401,21 +408,7 @@
         out_copy(du_all, du_hbm, du_sem, j).start()
         out_copy(c_all, c_hbm, c_sem, j).start()
 
-    def round_of(r):
-        @pl.when(r > 0)
-        def _():
-            line.step(r)
-
-        def side(s):
-            j = jnp.where(s == 0, i - r, i + r)
-
-            @pl.when(jnp.logical_and(jnp.logical_and(j >= 0, j <= n - 1), s * r == s * jnp.maximum(r, 1)))
-            def _():
-                compute(j)
-
-        loop(2, side)
-
-    loop(n, round_of)
+    rounds(i, n, line, compute)
 
     def relay(t):
         right, left = t + 2 - i, 2 * n - 4 - i - t
@@ -487,6 +480,31 @@
     loop(heads, head)
 
 
+def share_kernel(n, m, load_ref, every_ref, column_ref, land, send, recv):
+    i, row = lax.axis_index("tensor"), lax.axis_index("dp")
+    me, total = row * n + i, m * n
+    greet_all(me, n, total)
+
+    def copy(src, other):
+        return pltpu.make_async_remote_copy(
+            src_ref=load_ref.at[other], dst_ref=land.at[src], send_sem=send.at[other], recv_sem=recv.at[src],
+            device_id={"dp": other // n, "tensor": other % n}, device_id_type=MESH)
+
+    loop(total - 1, lambda s: copy(me, (me + s + 1) % total).start())
+    land[me] = load_ref[me]
+    every_ref[...] = jnp.zeros_like(every_ref)
+    column_ref[...] = jnp.zeros_like(column_ref)
+    loop(total - 1, lambda s: copy((me + s + 1) % total, me).wait_recv())
+
+    def add(d):
+        for t in range(n):
+            every_ref[...] += land[d * n + t]
+        column_ref[...] += land[d * n + i]
+
+    loop(m, add)
+    loop(total - 1, lambda s: copy(me, (me + s + 1) % total).wait_send())
+
+
 def params(collective=None):
     if collective is None:
         return pltpu.CompilerParams(vmem_limit_bytes=BIG)
@@ -506,12 +524,15 @@
     def owner(self, k):
         return jnp.where(self.first, self.i + k, self.i - k + self.n) % self.n
 
-    def gather(self, block):
+    def hop(self, block, step, r):
         n = self.n
-        down, up = [block], [block]
-        for r in range(1, n):
-            down.append(lax.ppermute(down[-1], self.axis, [(i, i - 1) for i in range(1, n) if i + r - 1 <= n - 1]))
-            up.append(lax.ppermute(up[-1], self.axis, [(i, i + 1) for i in range(n - 1) if i - r + 1 >= 0]))
+        if step < 0:
+            return lax.ppermute(block, self.axis, [(i, i - 1) for i in range(1, n) if i + r - 1 <= n - 1])
+        return lax.ppermute(block, self.axis, [(i, i + 1) for i in range(n - 1) if i - r + 1 >= 0])
+
+    def slots(self, block, down, up):
+        n = self.n
+        down, up = [block] + down, [block] + up
         slots = [block]
         for k in range(1, n):
             if 2 * k <= n:
@@ -522,9 +543,10 @@
                 slots.append(jnp.where(self.first, low, high))
         return slots
 
-    def scatter_sum(self, parts):
+    def scatter_sum(self, parts, work=None):
         n = self.n
         right = left = None
+        done = []
 
         def pick(owner):
             return lax.dynamic_index_in_dim(parts, owner % n, 0, keepdims=False).astype(F32)
@@ -536,7 +558,11 @@
             term = pick(self.i + r)
             term = term if left is None else term + left.astype(F32)
             left = lax.ppermute(term.astype(BF), self.axis, [(i, i - 1) for i in range(max(n - r, 1), n)])
-        return pick(self.i) + (right.astype(F32) + left.astype(F32))
+            if work and r <= len(work):
+                right, left, value = lax.optimization_barrier((right, left, work[r - 1]()))
+                done.append(value)
+        total = pick(self.i) + (right.astype(F32) + left.astype(F32))
+        return (total, done) if work else total
 
 
 def body(tokens, cotangent, ln1_gain, ln1_bias, qkv_weight, qv_bias, out_weight, out_bias, ln2_gain, ln2_bias,
@@ -571,32 +597,37 @@
     w_down = lax.all_gather(down_weight, "dp", axis=1, tiled=True)
 
     dma = pltpu.SemaphoreType.DMA
-    attn_in, qkv, vecs = pl.pallas_call(
-        functools.partial(project_kernel, n, m, (piece, qv_piece)),
-        out_shape=(shape((LEN, depth), BF), shape((3, LEN, width), BF), shape((total,) + pack.shape, F32)),
-        in_specs=[VM, VM, ANY], out_specs=(VM, VM, VM),
-        scratch_shapes=[pltpu.VMEM((n, size, depth), BF), pltpu.VMEM((3, depth, width), BF), pltpu.VMEM((8, depth), F32),
-                        pltpu.VMEM((8, width), F32), dma, dma, dma((2, n)), dma((n,)), dma((total,)), dma((total,))],
-        compiler_params=params(0), name="project",
-    )(pack, tokens, w_qkv)
-    vectors = vecs.reshape(depth // LANES, LANES // piece, -1, LANES).sum(axis=1)
-    vectors = vectors[:, 2:6].transpose(1, 0, 2).reshape(4, 1, depth)
-    bias_out, gain_two, shift_two, bias_down = [vectors[j] for j in range(4)]
-    ups = lax.dynamic_index_in_dim(vecs.reshape(m, n, -1, LANES), i, 1, keepdims=False)[:, 8:lanes_up]
-    if up_piece < LANES:
-        ups = ups.reshape(units // LANES, LANES // up_piece, LANES).sum(axis=1)
-    bias_up = ups.reshape(1, units)
+    attn_in, vecs = pl.pallas_call(
+        functools.partial(tokens_kernel, n, m, piece),
+        out_shape=(shape((LEN, depth), BF), shape((total,) + pack.shape, F32)),
+        in_specs=[VM, VM], out_specs=(VM, VM),
+        scratch_shapes=[pltpu.VMEM((n, size, depth), BF), pltpu.VMEM((8, depth), F32), dma, dma((2, n)), dma((n,)),
+                        dma((total,)), dma((total,))],
+        compiler_params=params(0), name="gather_tokens",
+    )(pack, tokens)
+
+    def whole_rows(block, count):
+        if count < LANES:
+            block = block.reshape(-1, LANES // count, *block.shape[1:]).sum(axis=1)
+        return block
+
+    vectors = whole_rows(vecs[:, 0:6], piece).transpose(1, 0, 2).reshape(6, 1, depth)
+    gain_one, shift_one, bias_out, gain_two, shift_two, bias_down = [vectors[j] for j in range(6)]
+    mine = lax.dynamic_index_in_dim(vecs.reshape(m, n, -1, LANES), i, 1, keepdims=False)
+    bias_qv = whole_rows(mine[:, 6:8], qv_piece).transpose(1, 0, 2).reshape(2, width)
+    bias_up = whole_rows(mine[:, 8:lanes_up], up_piece).reshape(1, units)
 
     pieces = 2
     sums = [pltpu.VMEM((n, size, depth), BF), pltpu.VMEM((n + 1, size, depth), BF)]
-    mixture, residual, mlp_own, cot_all = pl.pallas_call(
+    qkv, mixture, residual, mlp_own, cot_all = pl.pallas_call(
         functools.partial(attend_kernel, n, pieces),
-        out_shape=(shape((LEN, width), BF), shape((size, depth), F32), shape((size, depth), BF),
-                   shape((n, size, depth), BF)),
-        in_specs=[VM] * 7, out_specs=(VM,) * 4,
-        scratch_shapes=sums + [dma((2, n)), dma((n,)), dma((n, pieces)), dma((n + 1, pieces)), dma],
+        out_shape=(shape((3, LEN, width), BF), shape((LEN, width), BF), shape((size, depth), F32),
+                   shape((size, depth), BF), shape((n, size, depth), BF)),
+        in_specs=[ANY] * 3 + [VM] * 6, out_specs=(VM, VM, VM, VM, ANY),
+        scratch_shapes=[pltpu.VMEM((LEN, depth), BF), pltpu.VMEM((3, depth, width), BF), pltpu.VMEM((width, depth), BF)] +
+                       sums + [dma((2, n)), dma((n,)), dma((n, pieces)), dma((n + 1, pieces)), dma, dma, dma((4,))],
         compiler_params=params(1), name="attend",
-    )(qkv, w_out, tokens, cotangent, bias_out, gain_two, shift_two)
+    )(attn_in, w_qkv, w_out, tokens, cotangent, bias_qv, bias_out, gain_two, shift_two)
 
     pieces = 4
     mlp_in, hidden, grad_pre, grad_resid, branch_cot, vec_two, grad_up_b = pl.pallas_call(
@@ -614,15 +645,31 @@
     mlp_in, hidden, grad_pre = [v.reshape(LEN, -1) for v in (mlp_in, hidden, grad_pre)]
     cot_rows = cot_all.reshape(LEN, depth)
 
-    mlp_part = jnp.dot(hidden, w_down, preferred_element_type=F32).astype(BF)
-    layer_out = (residual + (line.scatter_sum(mlp_part.reshape(n, size, depth)) + bias_down)).astype(BF)
-    grad_down_w = jnp.einsum("rf,rd->fd", hidden, cot_rows, preferred_element_type=F32).astype(BF)
-    grad_up_w = jnp.einsum("rd,rf->df", mlp_in, grad_pre, preferred_element_type=F32).astype(BF)
-
-    slots = line.gather(branch_cot)
+    hold = lax.optimization_barrier
+    down, up = line.hop(branch_cot, -1, 1), line.hop(branch_cot, 1, 1)
+    downs, ups = [down], [up]
+    work = [
+        lambda: jnp.einsum("rf,rd->fd", hidden, cot_rows, preferred_element_type=F32).astype(BF),
+        lambda: jnp.dot(hidden, w_down, preferred_element_type=F32).astype(BF),
+        lambda: jnp.einsum("rd,rf->df", mlp_in, grad_pre, preferred_element_type=F32).astype(BF),
+    ]
+    done = []
+    for r in range(1, n):
+        if r - 1 < len(work):
+            value = work[r - 1]()
+            down, up, value = hold((down, up, value))
+            done.append(value)
+            downs[-1], ups[-1] = down, up
+        if r < n - 1:
+            down, up = line.hop(down, -1, r + 1), line.hop(up, 1, r + 1)
+            downs.append(down)
+            ups.append(up)
+    grad_down_w, mlp_part, grad_up_w = done
+    slots = line.slots(branch_cot, downs, ups)
     attn_cot = jnp.zeros((LEN, depth), BF)
     for k in range(n):
         attn_cot = lax.dynamic_update_slice(attn_cot, slots[k], (line.owner(k) * size, 0))
+    layer_out = (residual + (line.scatter_sum(mlp_part.reshape(n, size, depth)) + bias_down)).astype(BF)
     grad_mix = jnp.einsum("rd,ed->re", attn_cot, w_out, preferred_element_type=F32).astype(BF)
     grad_qkv = pl.pallas_call(
         attend_back_kernel, out_shape=shape((3, LEN, width), BF), in_specs=[VM, VM], out_specs=VM,
@@ -631,32 +678,43 @@
         cost_estimate=pl.CostEstimate(flops=14 * LEN * LEN * width // 2, bytes_accessed=14 * LEN * width,
                                       transcendentals=LEN * LEN * width // HD),
     )(qkv, grad_mix)
+    grad_qkv, layer_out = hold((grad_qkv, layer_out))
     attn_back = jnp.einsum("kre,kde->rd", grad_qkv, w_qkv, preferred_element_type=F32).astype(BF)
-    grad_normed_one = line.scatter_sum(attn_back.reshape(n, size, depth))
+    work = [
+        lambda: jnp.einsum("rd,kre->kde", attn_in, grad_qkv, preferred_element_type=F32).astype(BF),
+        lambda: jnp.einsum("re,rd->ed", mixture, attn_cot, preferred_element_type=F32).astype(BF),
+    ]
+    grad_normed_one, (grad_qkv_w, grad_out_w) = line.scatter_sum(attn_back.reshape(n, size, depth), work)
     normal_one, inverse_one = norm_stats(tokens.astype(F32))
-    gain_one = vecs.reshape(depth // LANES, LANES // piece, -1, LANES).sum(axis=1)[:, 0].reshape(1, depth)
     grad_tokens = (grad_resid + norm_back(grad_normed_one, normal_one, inverse_one, gain_one)).astype(BF)
 
-    grad_out_w = jnp.einsum("re,rd->ed", mixture, attn_cot, preferred_element_type=F32).astype(BF)
-    grad_qkv_w = jnp.einsum("rd,kre->kde", attn_in, grad_qkv, preferred_element_type=F32).astype(BF)
     grad_down_w = lax.psum_scatter(grad_down_w, "dp", scatter_dimension=1, tiled=True).astype(F32)
     grad_up_w = lax.psum_scatter(grad_up_w, "dp", scatter_dimension=0, tiled=True).astype(F32)
+    grad_qkv_w = lax.psum_scatter(grad_qkv_w, "dp", scatter_dimension=1, tiled=True).astype(F32)
     grad_out_w = lax.psum_scatter(grad_out_w, "dp", scatter_dimension=1, tiled=True).astype(F32)
-    grad_qkv_w = lax.psum_scatter(grad_qkv_w, "dp", scatter_dimension=1, tiled=True).astype(F32)
 
     vectors = jnp.stack([
         jnp.sum(grad_normed_one * normal_one, axis=0),
         jnp.sum(grad_normed_one, axis=0),
         vec_two[2], vec_two[0], vec_two[1], vec_two[3],
     ])
-    vectors = vectors.reshape(6, m, n, piece).transpose(1, 2, 0, 3).reshape(m, n * 6 * piece)
-    grad_qv_b = jnp.sum(grad_qkv[0::2].astype(F32), axis=1).reshape(2, m, qv_piece).transpose(1, 0, 2)
-    packed = jnp.concatenate([vectors, grad_qv_b.reshape(m, -1), grad_up_b[0].reshape(m, -1)], axis=1)
-    packed = jnp.sum(lax.all_to_all(packed, "dp", 0, 0), axis=0)
-    grad_up_b = packed[n * 6 * piece + 2 * qv_piece :]
-    grad_qv_b = packed[n * 6 * piece : n * 6 * piece + 2 * qv_piece].reshape(2, qv_piece)
-    vectors = packed[: n * 6 * piece].reshape(n, 6 * piece)
-    vectors = jnp.sum(lax.all_to_all(vectors, "tensor", 0, 0), axis=0).reshape(6, piece)
+    vectors = vectors.reshape(6, total, piece).transpose(1, 0, 2).reshape(total, 6 * piece)
+    local = jnp.concatenate([
+        jnp.sum(grad_qkv[0::2].astype(F32), axis=1).reshape(2, m, qv_piece).transpose(1, 0, 2).reshape(m, -1),
+        grad_up_b[0].reshape(m, -1)], axis=1)
+    local = jnp.broadcast_to(local[:, None], (m, n, local.shape[1])).reshape(total, -1)
+    load = jnp.concatenate([vectors, local], axis=1)
+    load = jnp.pad(load, ((0, 0), (0, -load.shape[1] % 1024))).reshape(total, -1, LANES)
+    everyone, column = pl.pallas_call(
+        functools.partial(share_kernel, n, m),
+        out_shape=(shape(load.shape[1:], F32),) * 2, in_specs=[VM], out_specs=(VM, VM),
+        scratch_shapes=[pltpu.VMEM(load.shape, F32), dma((total,)), dma((total,))],
+        compiler_params=params(3), name="share",
+    )(load)
+    vectors = everyone.reshape(-1)[: 6 * piece].reshape(6, piece)
+    local = column.reshape(-1)[6 * piece :]
+    grad_qv_b = local[: 2 * qv_piece].reshape(2, qv_piece)
+    grad_up_b = local[2 * qv_piece : 2 * qv_piece + up_piece]
     return (layer_out, grad_tokens, vectors[0], vectors[1], grad_qkv_w, grad_qv_b, grad_out_w, vectors[2],
             vectors[3], vectors[4], grad_up_w, grad_up_b, grad_down_w, vectors[5])
 

time: 769 us -> 846 us (1.10)
  waiting for transfers between devices: 185 us -> 282 us
  starting transfers between devices: 87.1 us -> 59.6 us
  Pallas kernels: 346 us -> 355 us
    reduce_scatter x1, waiting for transfers between devices: 0.01 us -> 72.3 us  [body(): lax.psum_scatter(grad_up_w, 'dp', scatter_dimension=0, tiled=True)]
    reduce_scatter x1, waiting for transfers between devices: 0.01 us -> 62.2 us  [body(): lax.psum_scatter(grad_qkv_w, 'dp', scatter_dimension=1, tiled=True)]
    reduce_scatter x1, waiting for transfers between devices: 0.01 us -> 60 us  [body(): lax.psum_scatter(grad_down_w, 'dp', scatter_dimension=1, tiled=True)]
    all_gather x1, waiting for transfers between devices: 47.1 us -> 0.01 us  [body(): w_qkv = lax.all_gather(qkv_weight, 'dp', axis=1, tiled=True)]
    ppermute x6, waiting for transfers between devices: 63.8 us -> 27 us  [the longest x3 25.8 us: hop(): lax.ppermute(block, self.axis, [(i, i - 1) for i in range(1, n) if i + r...]
    all_to_all x2 -> x0, starting transfers between devices: 30.3 us -> none  [the longest x1 26.4 us: body(): lax.all_to_all(vectors, 'tensor', 0, 0)]
    ppermute x6, waiting for transfers between devices: 20.2 us -> 5.54 us  [scatter_sum(): lax.ppermute(term.astype(BF), self.axis, [(i, i - 1) for i in range(max(n...]
    pallas_call x1 -> x2, Pallas kernels: 96 us -> 105 us  [the longest x1 93.5 us: body(): pl.pallas_call(functools.partial(tokens_kernel, n, m, piece), out_shape=(...]
  transfers between devices with their start and end apart: 28 -> 26, of which waited for: 12 -> 13; matrix products, arithmetic and copies ran while one was open for 15% -> 11% of each run, Pallas kernels for 29% -> 27%
where the time goes in v3:
time: 846 us; the launch traced here: 836 us
  Pallas kernels  355 us (42%)
  waiting for transfers between devices  282 us (33%)
  matrix products  64.8 us (8%)
  starting transfers between devices  59.6 us (7%)
  other arithmetic  44 us (5%)
  between operations  15.3 us (2%)
  local copies, waits for them, and re-layouts  15.1 us (2%)
    pallas_call x1, Pallas kernels, body(): pl.pallas_call(functools.partial(hidden_kernel, n, pieces), out_shape=(sh...  130 us
    pallas_call x1, Pallas kernels, body(): pl.pallas_call(functools.partial(attend_kernel, n, pieces), out_shape=(sh...  99.7 us
    pallas_call x1, Pallas kernels, body(): pl.pallas_call(functools.partial(tokens_kernel, n, m, piece), out_shape=(...  93.5 us
    reduce_scatter x1, waiting for transfers between devices, body(): lax.psum_scatter(grad_up_w, 'dp', scatter_dimension=0, tiled=True)  72.3 us
    reduce_scatter x1, waiting for transfers between devices, body(): lax.psum_scatter(grad_qkv_w, 'dp', scatter_dimension=1, tiled=True)  62.2 us
    reduce_scatter x1, waiting for transfers between devices, body(): lax.psum_scatter(grad_down_w, 'dp', scatter_dimension=1, tiled=True)  60 us
    ppermute x6, waiting for transfers between devices, scatter_sum(): lax.ppermute(term.astype(BF), self.axis, [(i, i + 1) for i in range(min(r...  50.3 us
    ppermute x6, starting transfers between devices, scatter_sum(): lax.ppermute(term.astype(BF), self.axis, [(i, i + 1) for i in range(min(r...  41.2 us
  transfers between devices with their start and end apart: 26, of which 13 were waited for; matrix products, arithmetic and copies ran while one was open for 11% of the time, Pallas kernels for 27%

profile of v3, /device:TPU:0, one launch (start us, length us, event | category | flops | bytes accessed | tf_op | source)
XLA Modules:
  0.0 835.9 jit_solution(242435974139824755)
XLA Ops:
  11.1 93.5 %gather_tokens.1 = (bf16[1024,2048]{1,0:T(8,128)(2,1)}, f32[32,16,128]{2,1,0:T(8,128)}) custom-call(f32[16,128]{1,0:T(8,128)} %fusion.26.pack_ref, bf16[256,2048]{1,0:T(8,128)(2,1)} %x_ref.3), custom_call_target="tpu_custom_call" | custom-call | tf_op jit(solution)/shard_map/gather_tokens/pallas_call | solution.py:600
  108.2 99.7 %attend.1 = (bf16[3,1024,512]{2,1,0:T(8,128)(2,1)}, bf16[1024,512]{1,0:T(8,128)(2,1)}, f32[256,2048]{1,0:T(8,128)}, bf16[256,2048]{1,0:T(8,128)(2,1)}, bf16[4,256,2048]{2,1,0:T(8,128)(2,1)}) custom-call(bf16[1024,2048]{1,0:T(8,128)(2,1)} %get-tuple-element.47.a_hbm, bf16[3,2048,512]{2,1,0:T(8,128)(2,1)} %all-gather.5.cloned.1.call-done.wq_hbm, ...), custom_call_target="tpu_custom_call" | custom-call | tf_op jit(solution)/shard_map/attend/pallas_call | solution.py:622
  208.0 129.9 %hidden.1 = (bf16[4,256,2048]{2,1,0:T(8,128)(2,1)}, bf16[4,256,2048]{2,1,0:T(8,128)(2,1)}, bf16[4,256,2048]{2,1,0:T(8,128)(2,1)}, f32[256,2048]{1,0:T(8,128)}, b...) custom-call(bf16[256,2048]{1,0:T(8,128)(2,1)} %get-tuple-element.50.c_ref, ...), custom_call_target="tpu_custom_call" | custom-call | tf_op jit(solution)/shard_map/hidden/pallas_call | solution.py:633
  339.2 4.6 collective-permute-start.1
  343.8 14.1 %bitcast_convert_fusion.1 = bf16[2048,2048]{1,0:T(8,128)(2,1)} fusion(bf16[4,256,2048]{2,1,0:T(8,128)(2,1)} %get-tuple-element.54, bf16[4,256,2048]{2,1,0:T(8,128)(2,1)} %get-tuple-element.52.cot_hbm), kind=kOutput, calls=%fused_computation.1 | convolution fusion | flops 8594128896 | bytes 16777216 | tf_op jit(solution)/shard_map/rf,rd->fd/dot_general | solution.py:652
  357.9 3.5 collective-permute-done
  364.9 12.5 %convolution_convert_fusion = bf16[1024,2048]{1,0:T(8,128)(2,1)S(1)} fusion(bf16[1024,2048]{1,0:T(8,128)(2,1)} %bitcast.129, bf16[2048,2048]{1,0:T(8,128)(2,1)} %all-gather.11.cloned.1.call-done.down_hbm), kind=kOutput, calls=%fused_computation.6 | convolution fusion | flops 8592031744 | bytes 16777216 | tf_op jit(solution)/shard_map/dot_general | solution.py:653
  377.4 8.1 collective-permute-done.2
  386.8 5.7 collective-permute-start.6
  392.5 15.7 %collective-permute-done.6 = bf16[256,2048]{1,0:T(8,128)(2,1)} collective-permute-done((bf16[256,2048]{1,0:T(8,128)(2,1)S(1)}, bf16[256,2048]{1,0:T(8,128)(2,1)}, u32[]{:S(2)}, u32[]{:S(2)}) %collective-permute-start.6) | collective-permute-done | bytes 1048608 | tf_op jit(solution)/shard_map/ppermute | solution.py:557
  408.2 2.9 fusion.13
  411.1 4.5 collective-permute-start.7
  415.8 16.0 %collective-permute-done.7 = bf16[256,2048]{1,0:T(8,128)(2,1)S(1)} collective-permute-done((bf16[256,2048]{1,0:T(8,128)(2,1)}, bf16[256,2048]{1,0:T(8,128)(2,1)S(1)}, u32[]{:S(2)}, u32[]{:S(2)}) %collective-permute-start.7) | collective-permute-done | bytes 1048608 | tf_op jit(solution)/shard_map/ppermute | solution.py:557
  431.7 3.0 add_convert_fusion.3
  434.7 1.6 collective-permute-start.9
  436.3 13.4 %bitcast_convert_fusion = bf16[2048,2048]{1,0:T(8,128)(2,1)} fusion(bf16[4,256,2048]{2,1,0:T(8,128)(2,1)S(1)} %copy-done.27, bf16[4,256,2048]{2,1,0:T(8,128)(2,1)} %get-tuple-element.60), kind=kOutput, calls=%fused_computation | convolution fusion | flops 8594128896 | bytes 16777216 | tf_op jit(solution)/shard_map/rd,rf->df/dot_general | solution.py:654
  451.3 1.4 collective-permute-start.4
  453.5 1.6 fusion.14
  456.6 14.1 %collective-permute-done.4 = bf16[256,2048]{1,0:T(8,128)(2,1)S(1)} collective-permute-done((bf16[256,2048]{1,0:T(8,128)(2,1)S(1)}, bf16[256,2048]{1,0:T(8,128)(2,1)S(1)}, u32[]{:S(2)}, u32[]{:S(2)}) %collective-permute-start.4) | collective-permute-done | bytes 1048608 | tf_op jit(solution)/shard_map/ppermute | solution.py:530
  470.8 2.4 collective-permute-start.8
  474.6 1.6 collective-permute-start.11
  477.0 3.3 convolution_convert_fusion.2.do_ref
  480.3 21.0 %attend_back.1 = bf16[3,1024,512]{2,1,0:T(8,128)(2,1)} custom-call(bf16[3,1024,512]{2,1,0:T(8,128)(2,1)} %get-tuple-element.49.qkv_ref, bf16[1024,512]{1,0:T(8,128)(2,1)} %convolution_convert_fusion.2.do_ref), custom_call_target="tpu_custom_call" | custom-call | flops 3758096384 | bytes 7340032 | tf_op jit(solution)/shard_map/attend_back/pallas_call | solution.py:674
  501.3 4.2 fusion.19
  505.5 8.8 %bitcast_convert_fusion.2 = bf16[1024,2048]{1,0:T(8,128)(2,1)S(1)} fusion(bf16[3,1024,512]{2,1,0:T(8,128)(2,1)S(1)} %copy-done.8, bf16[3,2048,512]{2,1,0:T(8,128)(2,1)} %all-gather.5.cloned.1.call-done.wq_hbm), kind=kOutput, calls=%fused_computation.2 | convolution fusion | flops 6444548096 | bytes 13631488 | tf_op jit(solution)/shard_map/kre,kde->rd/dot_general | solution.py:682
  514.5 11.0 %collective-permute-start.12 = (bf16[256,2048]{1,0:T(8,128)(2,1)S(1)}, bf16[256,2048]{1,0:T(8,128)(2,1)S(1)}, u32[]{:S(2)}, u32[]{:S(2)}) collective-permute-start(bf16[256,2048]{1,0:T(8,128)(2,1)S(1)} %get-tuple-element.148), channel_id=1, source_target_pairs={{0,1},{4,5},{8,9},{12,13},{16,17},{20,21},{24,25},{28,29}} | collective-permute-start | bytes 3145736 | tf_op jit(solution)/shard_map/ppermute | solution.py:557
  525.5 1.9 collective-permute-start.13
  527.3 8.8 %convert_bitcast_fusion = bf16[3,2048,512]{1,2,0:T(8,128)(2,1)} fusion(bf16[3,1024,512]{2,1,0:T(8,128)(2,1)S(1)} %copy-done.8, bf16[1024,2048]{1,0:T(8,128)(2,1)S(1)} %copy-done.3), kind=kOutput, calls=%fused_computation.3 | convolution fusion | flops 6445596672 | bytes 13631488 | tf_op jit(solution)/shard_map/rd,kre->kde/dot_general | solution.py:684
  536.2 5.2 collective-permute-done.12
  541.4 3.5 fusion.16
  544.9 5.4 collective-permute-start.14
  551.1 3.8 convolution_convert_fusion.1
  554.8 7.4 collective-permute-done.14
  565.4 2.7 add_convert_fusion.1
  568.1 12.2 %collective-permute-start.16 = (bf16[256,2048]{1,0:T(8,128)(2,1)}, bf16[256,2048]{1,0:T(8,128)(2,1)}, u32[]{:S(2)}, u32[]{:S(2)}) collective-permute-start(bf16[256,2048]{1,0:T(8,128)(2,1)} %add_convert_fusion.1), channel_id=1, source_target_pairs={{0,1},{1,2},{2,3},{4,5},{5,6},{6,7},{8,9},{9,10},{10,11},{12,13},{... | collective-permute-start | bytes 3145736 | tf_op jit(solution)/shard_map/ppermute | solution.py:557
  583.7 1.9 convert_reduce_fusion
  585.8 6.0 collective-permute-done.16
  591.9 5.5 collective-permute-done.17
  597.4 4.6 fusion.11
  603.1 11.2 %share.1 = (f32[8,128]{1,0:T(8,128)}, f32[8,128]{1,0:T(8,128)}) custom-call(f32[32,8,128]{2,1,0:T(8,128)} %bitcast.111), custom_call_target="tpu_custom_call" | custom-call | tf_op jit(solution)/shard_map/share/pallas_call | solution.py:708
  619.6 4.8 fusion.10
  624.3 1.8 convert_element_type.208
  626.2 60.0 %reduce-scatter.11.cloned.1.call-done = bf16[2048,256]{1,0:T(8,128)(2,1)} async-done(((bf16[2048,2048]{1,0:T(8,128)(2,1)}), bf16[2048,256]{1,0:T(8,128)(2,1)}) %reduce-scatter.11.cloned.1.call-update) | async-done | bytes 1048592 | tf_op jit(solution)/shard_map/reduce_scatter | solution.py:691
  686.1 2.7 convert_element_type.210
  688.8 72.3 %reduce-scatter.9.cloned.1.call-done = bf16[256,2048]{1,0:T(8,128)(2,1)} async-done(((bf16[2048,2048]{1,0:T(8,128)(2,1)}), bf16[256,2048]{1,0:T(8,128)(2,1)}) %reduce-scatter.9.cloned.1.call-update) | async-done | bytes 1048592 | tf_op jit(solution)/shard_map/reduce_scatter | solution.py:692
  761.1 2.8 convert_element_type.209
  763.9 62.2 %reduce-scatter.5.cloned.1.call-done = bf16[3,256,512]{1,2,0:T(8,128)(2,1)} async-done(((bf16[3,2048,512]{1,2,0:T(8,128)(2,1)}), bf16[3,256,512]{1,2,0:T(8,128)(2,1)}) %reduce-scatter.5.cloned.1.call-update) | async-done | bytes 786448 | tf_op jit(solution)/shard_map/reduce_scatter | solution.py:693
  826.1 2.6 copy.55
  (152 shorter events, 33.1 us)
Async XLA Ops:
  7.2 3.0 copy-start.20
  7.2 3.0 copy-start.21
  7.2 3.0 copy-start.22
  7.2 3.0 copy-start.23
  7.2 3.0 copy-start.24
  7.2 3.1 copy-start.29
  7.3 3.2 copy-start.26
  7.3 100.9 %all-gather.7.cloned.1.call-start = ((), (), s32[]{:S(2)}) async-start(), calls=%async_computation.5 | async-start | bytes 2359296 | tf_op jit(solution)/shard_map/all_gather | solution.py:595
  8.0 100.2 %all-gather.5.cloned.1.call-start = ((), (), s32[]{:S(2)}) async-start(), calls=%async_computation.4 | async-start | bytes 7077888 | tf_op jit(solution)/shard_map/all_gather | solution.py:594
  8.7 199.2 %all-gather.11.cloned.1.call-start = ((), (), s32[]{:S(2)}) async-start(), calls=%async_computation.7 | async-start | bytes 9437184 | tf_op jit(solution)/shard_map/all_gather | solution.py:597
  9.5 198.5 %all-gather.9.cloned.1.call-start = ((), (), s32[]{:S(2)}) async-start(), calls=%async_computation.6 | async-start | bytes 9437184 | tf_op jit(solution)/shard_map/all_gather | solution.py:596
  10.1 614.3 %reduce-scatter.7.cloned.1.call-start = ((), (), s32[]{:S(2)}) async-start(), calls=%async_computation.9 | async-start | bytes 2359296 | tf_op jit(solution)/shard_map/reduce_scatter | solution.py:694
  337.9 23.5 %collective-permute-start = (bf16[256,2048]{1,0:T(8,128)(2,1)}, bf16[256,2048]{1,0:T(8,128)(2,1)S(1)}, u32[]{:S(2)}, u32[]{:S(2)}) collective-permute-start(bf16[256,2048]{1,0:T(8,128)(2,1)} %get-tuple-element.53), channel_id=1, source_target_pairs={{1,0},{2,1},{3,2},{5,4},{6,5},{7,6},{9,8},{10,9},{11,10},{13,12},{... | collective-permute-start | bytes 3145736 | tf_op jit(solution)/shard_map/ppermute | solution.py:530
  339.2 23.5 %collective-permute-start.1 = (bf16[256,2048]{1,0:T(8,128)(2,1)}, bf16[256,2048]{1,0:T(8,128)(2,1)S(1)}, u32[]{:S(2)}, u32[]{:S(2)}) collective-permute-start(bf16[256,2048]{1,0:T(8,128)(2,1)} %get-tuple-element.53), channel_id=1, source_target_pairs={{0,1},{1,2},{2,3},{4,5},{5,6},{6,7},{8,9},{9,10},{10,11},{12,13},{... | collective-permute-start | bytes 3145736 | tf_op jit(solution)/shard_map/ppermute | solution.py:531
  362.7 22.8 %collective-permute-start.2 = (bf16[256,2048]{1,0:T(8,128)(2,1)S(1)}, bf16[256,2048]{1,0:T(8,128)(2,1)S(1)}, u32[]{:S(2)}, u32[]{:S(2)}) collective-permute-start(bf16[256,2048]{1,0:T(8,128)(2,1)S(1)} %collective-permute-done), channel_id=1, source_target_pairs={{1,0},{2,1},{5,4},{6,5},{9,8},{10,9},{13,12},{14,13},{17,16},{18,1... | collective-permute-start | bytes 3145736 | tf_op jit(solution)/shard_map/ppermute | solution.py:530
  364.0 21.5 %collective-permute-start.3 = (bf16[256,2048]{1,0:T(8,128)(2,1)S(1)}, bf16[256,2048]{1,0:T(8,128)(2,1)S(1)}, u32[]{:S(2)}, u32[]{:S(2)}) collective-permute-start(bf16[256,2048]{1,0:T(8,128)(2,1)S(1)} %collective-permute-done.1), channel_id=1, source_target_pairs={{1,2},{2,3},{5,6},{6,7},{9,10},{10,11},{13,14},{14,15},{17,18},{18... | collective-permute-start | bytes 3145736 | tf_op jit(solution)/shard_map/ppermute | solution.py:531
  377.4 8.1 copy-start.1
  386.8 21.4 %collective-permute-start.6 = (bf16[256,2048]{1,0:T(8,128)(2,1)S(1)}, bf16[256,2048]{1,0:T(8,128)(2,1)}, u32[]{:S(2)}, u32[]{:S(2)}) collective-permute-start(bf16[256,2048]{1,0:T(8,128)(2,1)S(1)} %dynamic-slice_bitcast_fusion.2), channel_id=1, source_target_pairs={{0,1},{4,5},{8,9},{12,13},{16,17},{20,21},{24,25},{28,29}} | collective-permute-start | bytes 3145736 | tf_op jit(solution)/shard_map/ppermute | solution.py:557
  411.1 20.6 %collective-permute-start.7 = (bf16[256,2048]{1,0:T(8,128)(2,1)}, bf16[256,2048]{1,0:T(8,128)(2,1)S(1)}, u32[]{:S(2)}, u32[]{:S(2)}) collective-permute-start(bf16[256,2048]{1,0:T(8,128)(2,1)} %fusion.13), channel_id=1, source_target_pairs={{0,1},{1,2},{4,5},{5,6},{8,9},{9,10},{12,13},{13,14},{16,17},{17,1... | collective-permute-start | bytes 3145736 | tf_op jit(solution)/shard_map/ppermute | solution.py:557
  415.7 20.6 %copy-start.27 = (bf16[4,256,2048]{2,1,0:T(8,128)(2,1)S(1)}, bf16[4,256,2048]{2,1,0:T(8,128)(2,1)}, u32[]{:S(2)}) copy-start(bf16[4,256,2048]{2,1,0:T(8,128)(2,1)} %get-tuple-element.59) | copy-start | bytes 12582916
  434.7 18.7 %collective-permute-start.9 = (bf16[256,2048]{1,0:T(8,128)(2,1)}, bf16[256,2048]{1,0:T(8,128)(2,1)}, u32[]{:S(2)}, u32[]{:S(2)}) collective-permute-start(bf16[256,2048]{1,0:T(8,128)(2,1)} %get-tuple-element.144), channel_id=1, source_target_pairs={{3,2},{7,6},{11,10},{15,14},{19,18},{23,22},{27,26},{31,30}} | collective-permute-start | bytes 3145736 | tf_op jit(solution)/shard_map/ppermute | solution.py:560
  449.7 3.7 copy-start.2
  451.3 4.9 copy-start.15
  451.3 19.5 %collective-permute-start.4 = (bf16[256,2048]{1,0:T(8,128)(2,1)S(1)}, bf16[256,2048]{1,0:T(8,128)(2,1)S(1)}, u32[]{:S(2)}, u32[]{:S(2)}) collective-permute-start(bf16[256,2048]{1,0:T(8,128)(2,1)S(1)} %copy-done.13), channel_id=1, source_target_pairs={{1,0},{5,4},{9,8},{13,12},{17,16},{21,20},{25,24},{29,28}} | collective-permute-start | bytes 3145736 | tf_op jit(solution)/shard_map/ppermute | solution.py:530
  452.7 18.1 %collective-permute-start.5 = (bf16[256,2048]{1,0:T(8,128)(2,1)}, bf16[256,2048]{1,0:T(8,128)(2,1)S(1)}, u32[]{:S(2)}, u32[]{:S(2)}) collective-permute-start(bf16[256,2048]{1,0:T(8,128)(2,1)} %copy-done.14), channel_id=1, source_target_pairs={{2,3},{6,7},{10,11},{14,15},{18,19},{22,23},{26,27},{30,31}} | collective-permute-start | bytes 3145736 | tf_op jit(solution)/shard_map/ppermute | solution.py:531
  455.1 18.1 %collective-permute-start.10 = (bf16[256,2048]{1,0:T(8,128)(2,1)S(1)}, bf16[256,2048]{1,0:T(8,128)(2,1)S(1)}, u32[]{:S(2)}, u32[]{:S(2)}) collective-permute-start(bf16[256,2048]{1,0:T(8,128)(2,1)S(1)} %fusion.14), channel_id=1, source_target_pairs={{2,1},{3,2},{6,5},{7,6},{10,9},{11,10},{14,13},{15,14},{18,17},{19... | collective-permute-start | bytes 3145736 | tf_op jit(solution)/shard_map/ppermute | solution.py:560
  470.8 30.5 %collective-permute-start.8 = (bf16[256,2048]{1,0:T(8,128)(2,1)}, bf16[256,2048]{1,0:T(8,128)(2,1)}, u32[]{:S(2)}, u32[]{:S(2)}) collective-permute-start(bf16[256,2048]{1,0:T(8,128)(2,1)} %get-tuple-element.143), channel_id=1, source_target_pairs={{0,1},{1,2},{2,3},{4,5},{5,6},{6,7},{8,9},{9,10},{10,11},{12,13},{... | collective-permute-start | bytes 3145736 | tf_op jit(solution)/shard_map/ppermute | solution.py:557
  474.6 26.7 %collective-permute-start.11 = (bf16[256,2048]{1,0:T(8,128)(2,1)}, bf16[256,2048]{1,0:T(8,128)(2,1)}, u32[]{:S(2)}, u32[]{:S(2)}) collective-permute-start(bf16[256,2048]{1,0:T(8,128)(2,1)} %add_convert_fusion.2), channel_id=1, source_target_pairs={{1,0},{2,1},{3,2},{5,4},{6,5},{7,6},{9,8},{10,9},{11,10},{13,12},{... | collective-permute-start | bytes 3145736 | tf_op jit(solution)/shard_map/ppermute | solution.py:560
  477.0 3.3 copy-start.4
  501.3 4.2 copy-start.8
  514.3 11.2 %copy-start.6 = (bf16[1024,2048]{1,0:T(8,128)(2,1)}, bf16[1024,2048]{1,0:T(8,128)(2,1)S(1)}, u32[]{:S(2)}) copy-start(bf16[1024,2048]{1,0:T(8,128)(2,1)S(1)} %bitcast_convert_fusion.2) | copy-start | bytes 12582916
  514.3 13.0 %copy-start.3 = (bf16[1024,2048]{1,0:T(8,128)(2,1)S(1)}, bf16[1024,2048]{1,0:T(8,128)(2,1)}, u32[]{:S(2)}) copy-start(bf16[1024,2048]{1,0:T(8,128)(2,1)} %get-tuple-element.47.a_hbm) | copy-start | bytes 12582916
  514.5 26.9 %collective-permute-start.12 = (bf16[256,2048]{1,0:T(8,128)(2,1)S(1)}, bf16[256,2048]{1,0:T(8,128)(2,1)S(1)}, u32[]{:S(2)}, u32[]{:S(2)}) collective-permute-start(bf16[256,2048]{1,0:T(8,128)(2,1)S(1)} %get-tuple-element.148), channel_id=1, source_target_pairs={{0,1},{4,5},{8,9},{12,13},{16,17},{20,21},{24,25},{28,29}} | collective-permute-start | bytes 3145736 | tf_op jit(solution)/shard_map/ppermute | solution.py:557
  525.5 15.9 %collective-permute-start.13 = (bf16[256,2048]{1,0:T(8,128)(2,1)S(1)}, bf16[256,2048]{1,0:T(8,128)(2,1)}, u32[]{:S(2)}, u32[]{:S(2)}) collective-permute-start(bf16[256,2048]{1,0:T(8,128)(2,1)S(1)} %get-tuple-element.147), channel_id=1, source_target_pairs={{3,2},{7,6},{11,10},{15,14},{19,18},{23,22},{27,26},{31,30}} | collective-permute-start | bytes 3145736 | tf_op jit(solution)/shard_map/ppermute | solution.py:560
  536.2 14.9 %copy-start.5 = (bf16[1024,2048]{1,0:T(8,128)(2,1)S(1)}, bf16[1024,2048]{1,0:T(8,128)(2,1)}, u32[]{:S(2)}) copy-start(bf16[1024,2048]{1,0:T(8,128)(2,1)} %copy-done.4) | copy-start | bytes 12582916
  536.2 14.9 %copy-start.28 = (bf16[1024,512]{1,0:T(8,128)(2,1)S(1)}, bf16[1024,512]{1,0:T(8,128)(2,1)}, u32[]{:S(2)}) copy-start(bf16[1024,512]{1,0:T(8,128)(2,1)} %get-tuple-element.69) | copy-start | bytes 3145732
  544.9 17.3 %collective-permute-start.14 = (bf16[256,2048]{1,0:T(8,128)(2,1)}, bf16[256,2048]{1,0:T(8,128)(2,1)}, u32[]{:S(2)}, u32[]{:S(2)}) collective-permute-start(bf16[256,2048]{1,0:T(8,128)(2,1)} %get-tuple-element.146), channel_id=1, source_target_pairs={{0,1},{1,2},{4,5},{5,6},{8,9},{9,10},{12,13},{13,14},{16,17},{17,1... | collective-permute-start | bytes 3145736 | tf_op jit(solution)/shard_map/ppermute | solution.py:557
  550.3 11.9 %collective-permute-start.15 = (bf16[256,2048]{1,0:T(8,128)(2,1)}, bf16[256,2048]{1,0:T(8,128)(2,1)S(1)}, u32[]{:S(2)}, u32[]{:S(2)}) collective-permute-start(bf16[256,2048]{1,0:T(8,128)(2,1)} %get-tuple-element.145), channel_id=1, source_target_pairs={{2,1},{3,2},{6,5},{7,6},{10,9},{11,10},{14,13},{15,14},{18,17},{19... | collective-permute-start | bytes 3145736 | tf_op jit(solution)/shard_map/ppermute | solution.py:560
  562.3 123.9 %reduce-scatter.11.cloned.1.call-start = ((), (), s32[]{:S(2)}) async-start(), calls=%async_computation.11 | async-start | bytes 9437184 | tf_op jit(solution)/shard_map/reduce_scatter | solution.py:691
  563.2 197.9 %reduce-scatter.9.cloned.1.call-start = ((), (), s32[]{:S(2)}) async-start(), calls=%async_computation.10 | async-start | bytes 9437184 | tf_op jit(solution)/shard_map/reduce_scatter | solution.py:692
  564.0 262.1 %reduce-scatter.5.cloned.1.call-start = ((), (), s32[]{:S(2)}) async-start(), calls=%async_computation.8 | async-start | bytes 7077888 | tf_op jit(solution)/shard_map/reduce_scatter | solution.py:693
  565.2 15.1 %copy-start.10 = (bf16[256,2048]{1,0:T(8,128)(2,1)S(1)}, bf16[256,2048]{1,0:T(8,128)(2,1)}, u32[]{:S(2)}) copy-start(bf16[256,2048]{1,0:T(8,128)(2,1)} %copy-done.9) | copy-start | bytes 3145732
  565.4 17.0 %copy-start.17 = (f32[8,2048]{1,0:T(8,128)S(1)}, f32[8,2048]{1,0:T(8,128)}, u32[]{:S(2)}) copy-start(f32[8,2048]{1,0:T(8,128)} %get-tuple-element.72) | copy-start | bytes 196612
  568.1 29.3 %copy-start.16 = (f32[1,16,128]{2,0,1:T(1,128)S(1)}, f32[1,16,128]{2,0,1:T(1,128)}, u32[]{:S(2)}) copy-start(f32[1,16,128]{2,0,1:T(1,128)} %get-tuple-element.149) | copy-start | bytes 24580
  568.1 23.8 %collective-permute-start.16 = (bf16[256,2048]{1,0:T(8,128)(2,1)}, bf16[256,2048]{1,0:T(8,128)(2,1)}, u32[]{:S(2)}, u32[]{:S(2)}) collective-permute-start(bf16[256,2048]{1,0:T(8,128)(2,1)} %add_convert_fusion.1), channel_id=1, source_target_pairs={{0,1},{1,2},{2,3},{4,5},{5,6},{6,7},{8,9},{9,10},{10,11},{12,13},{... | collective-permute-start | bytes 3145736 | tf_op jit(solution)/shard_map/ppermute | solution.py:557
  580.7 16.7 %collective-permute-start.17 = (bf16[256,2048]{1,0:T(8,128)(2,1)S(1)}, bf16[256,2048]{1,0:T(8,128)(2,1)S(1)}, u32[]{:S(2)}, u32[]{:S(2)}) collective-permute-start(bf16[256,2048]{1,0:T(8,128)(2,1)S(1)} %add_convert_fusion), channel_id=1, source_target_pairs={{1,0},{2,1},{3,2},{5,4},{6,5},{7,6},{9,8},{10,9},{11,10},{13,12},{... | collective-permute-start | bytes 3145736 | tf_op jit(solution)/shard_map/ppermute | solution.py:560
  582.0 20.0 %copy-start.18 = (f32[256]{0:T(256)}, f32[256]{0:T(256)S(1)}, u32[]{:S(2)}) copy-start(f32[256]{0:T(256)S(1)} %broadcast_multiply_fusion.2) | copy-start | bytes 3076
  582.4 19.6 %copy-start.19 = (f32[256]{0:T(256)}, f32[256]{0:T(256)S(1)}, u32[]{:S(2)}) copy-start(f32[256]{0:T(256)S(1)} %add_rsqrt_fusion) | copy-start | bytes 3076
  (8 other events, 12.6 us)
Sparse Core Ops, SparseCore 0:
  9.9 30.8 all-gather.6
  42.7 45.4 all-gather.4
  90.1 55.8 all-gather.10
  147.7 54.2 all-gather.8
  562.4 48.3 reduce-scatter.6
  614.1 72.0 reduce-scatter.10
  689.6 71.4 reduce-scatter.8
  764.5 61.5 reduce-scatter.4

commit v4 on v3

--- a/solution.py
+++ b/solution.py
@@ -232,7 +232,6 @@
     size = x_ref.shape[0]
     greet_all(me, n, total)
     line = LineGather(i, n, x_ref, buf, send, recv)
-    line.start()
 
     def vector(src, other):
         return pltpu.make_async_remote_copy(
@@ -240,6 +239,7 @@
             device_id={"dp": other // n, "tensor": other % n}, device_id_type=MESH)
 
     loop(total - 1, lambda s: vector(me, (me + s + 1) % total).start())
+    line.start()
     own_copy = pltpu.make_async_copy(x_ref, buf.at[i], own_sem)
     own_copy.start()
     vec_ref[me] = pack_ref[...]
@@ -247,9 +247,9 @@
     depth = affine.shape[1]
     group = LANES // piece
     for tile in range(depth // LANES):
-        value = vec_ref[tile * group, 0:2, :]
+        value = vec_ref[tile * group, 0:2, :].astype(F32)
         for g in range(1, group):
-            value = value + vec_ref[tile * group + g, 0:2, :]
+            value = value + vec_ref[tile * group + g, 0:2, :].astype(F32)
         affine[0:2, tile * LANES : (tile + 1) * LANES] = value
     own_copy.wait()
 
@@ -355,9 +355,9 @@
     sums.finish()
 
 
-def hidden_kernel(n, pieces, c_ref, h_ref, cot_hbm, up_hbm, down_hbm, up_bias, gain, c_hbm, g_hbm, du_hbm, dh_ref,
+def hidden_kernel(n, pieces, c_ref, h_ref, cot_hbm, up_hbm, down_hbm, up_bias, gain, c_hbm, g_hbm, du_hbm, mlp_hbm, dh_ref,
                   db_ref, vec_ref, upb_ref, c_all, g_all, du_all, cot_all, up, down, part, land, send, recv, s_send,
-                  s_recv, w_sem, cot_sem, own_sem, c_sem, g_sem, du_sem):
+                  s_recv, w_sem, cot_sem, own_sem, c_sem, g_sem, du_sem, mlp, mlp_sem):
     i = lax.axis_index("tensor")
     size, depth = c_ref.shape
     units = up.shape[1]
@@ -410,6 +410,16 @@
 
     rounds(i, n, line, compute)
 
+    def forward(j):
+        def columns(k):
+            cols = rows_at(k, tile)
+            mlp[j, :, cols] = jnp.dot(g_all[j], down[:, cols], preferred_element_type=F32).astype(BF)
+
+        loop(depth // tile, columns)
+        out_copy(mlp, mlp_hbm, mlp_sem, j).start()
+
+    loop(n, forward)
+
     def relay(t):
         right, left = t + 2 - i, 2 * n - 4 - i - t
 
@@ -445,6 +455,7 @@
         out_copy(g_all, g_hbm, g_sem, j).wait()
         out_copy(du_all, du_hbm, du_sem, j).wait()
         out_copy(c_all, c_hbm, c_sem, j).wait()
+        out_copy(mlp, mlp_hbm, mlp_sem, j).wait()
 
     loop(n, done)
     line.finish()
@@ -480,6 +491,305 @@
     loop(heads, head)
 
 
+def partner(row, bit):
+    return row + bit * (1 - 2 * ((row // bit) % 2))
+
+
+class PlaneSum:
+    def __init__(self, row, m, terms, land, halves, send, recv, h_send, h_recv):
+        self.row, self.m, self.terms, self.land, self.halves = row, m, terms, land, halves
+        self.send, self.recv, self.h_send, self.h_recv = send, recv, h_send, h_recv
+        bits = [1 << k for k in range(1, m.bit_length() - 1)]
+        self.plan = []
+        for order in (bits, bits[::-1]):
+            left, at, stages = [e for e in range(m) if e % 2 == 0], 0, []
+            for bit in order:
+                out = [e for e in left if e & bit]
+                stages.append((bit, [(e, e ^ bit, at + k) for k, e in enumerate(out)]))
+                left, at = [e for e in left if not e & bit], at + len(out)
+            self.plan.append(stages)
+        self.stages = len(bits)
+
+    def owner(self, e):
+        d = self.row
+        for k in range(self.m.bit_length() - 1):
+            if e & (1 << k):
+                d = d + (partner(self.row, 1 << k) - self.row)
+        return d
+
+    def whole(self, e):
+        return pltpu.make_async_remote_copy(
+            src_ref=self.terms.at[e], dst_ref=self.land.at[e // 2], send_sem=self.send.at[e // 2],
+            recv_sem=self.recv.at[e // 2], device_id={"dp": partner(self.row, 1)}, device_id_type=MESH)
+
+    def half(self, h, bit, e, at):
+        size = self.halves.shape[2]
+        return pltpu.make_async_remote_copy(
+            src_ref=self.terms.at[e, pl.ds(h * size, size)], dst_ref=self.halves.at[h, at],
+            send_sem=self.h_send.at[h, at], recv_sem=self.h_recv.at[h, at],
+            device_id={"dp": partner(self.row, bit)}, device_id_type=MESH)
+
+    def merge(self):
+        for e in range(0, self.m, 2):
+            self.whole(e + 1).wait_recv()
+
+            def add(b):
+                here = rows_at(b, RB)
+                total = self.terms[e, here, :].astype(F32) + self.land[e // 2, here, :].astype(F32)
+                self.terms[e, here, :] = total.astype(BF)
+
+            loop(self.terms.shape[1] // RB, add)
+
+    def push(self, stage):
+        for h in range(2):
+            bit, moves = self.plan[h][stage]
+            for e, _, at in moves:
+                self.half(h, bit, e, at).start()
+
+    def take(self, stage, out=None):
+        size = self.halves.shape[2]
+        for h in range(2):
+            bit, moves = self.plan[h][stage]
+            for e, into, at in moves:
+                self.half(h, bit, e, at).wait_recv()
+
+                def add(b):
+                    here, there = rows_at(b, RB), pl.ds(pl.multiple_of(h * size + b * RB, RB), RB)
+                    total = self.terms[into, there, :].astype(F32) + self.halves[h, at, here, :].astype(F32)
+                    if out is None:
+                        self.terms[into, there, :] = total.astype(BF)
+                    else:
+                        out(there, total)
+
+                loop(size // RB, add)
+
+    def finish(self):
+        for e in range(1, self.m, 2):
+            self.whole(e).wait_send()
+        for h in range(2):
+            for bit, moves in self.plan[h]:
+                for e, _, at in moves:
+                    self.half(h, bit, e, at).wait_send()
+
+
+def greet_cross(i, n, row, m):
+    barrier = pltpu.get_barrier_semaphore()
+
+    @pl.when(i > 0)
+    def _():
+        pl.semaphore_signal(barrier, inc=1, device_id={"tensor": i - 1}, device_id_type=MESH)
+
+    @pl.when(i < n - 1)
+    def _():
+        pl.semaphore_signal(barrier, inc=1, device_id={"tensor": i + 1}, device_id_type=MESH)
+
+    bits = [1 << k for k in range(m.bit_length() - 1)]
+    for bit in bits:
+        pl.semaphore_signal(barrier, inc=1, device_id={"dp": partner(row, bit)}, device_id_type=MESH)
+    pl.semaphore_wait(barrier, jnp.minimum(i, 1) + jnp.minimum(n - 1 - i, 1) + len(bits))
+
+
+def relays(sums, i, n, r):
+    right, left = n - 1 + i - r, r - (n - 1 - i)
+
+    @pl.when(jnp.logical_and(i > 0, jnp.logical_and(right > i, right <= n - 1)))
+    def _():
+        sums.relay(right, True)
+
+    @pl.when(jnp.logical_and(i < n - 1, jnp.logical_and(left >= 0, left < i)))
+    def _():
+        sums.relay(left, False)
+
+
+def block_terms(plane, e, pairs):
+    size = plane.terms.shape[1]
+    cols = rows_at(plane.owner(e), size)
+    for lhs, rhs, first in pairs:
+        width = rhs.shape[1]
+        tile = min(512, width)
+
+        def columns(k):
+            there = pl.ds(pl.multiple_of(first + k * tile, tile), tile)
+            plane.terms[e, :, there] = lax.dot_general(
+                lhs[:, cols], rhs[:, rows_at(k, tile)], TN, preferred_element_type=F32).astype(BF)
+
+        loop(width // tile, columns)
+
+
+def branch_kernel(n, m, pieces, db_ref, h_ref, down_bias, mlp_hbm, g_hbm, cot_hbm, c_hbm, du_hbm, db_all, lo_ref,
+                  down_ref, up_ref, lhs, rhs, part, land, terms_a, land_a, half_a, terms_b, land_b, half_b, acc, send,
+                  recv, s_send, s_recv, own_sem, part_sem, in_sem, p_send, p_recv, h_send, h_recv):
+    i, row = lax.axis_index("tensor"), lax.axis_index("dp")
+    size = db_ref.shape[0]
+    greet_cross(i, n, row, m)
+    line = LineGather(i, n, db_ref, db_all, send, recv)
+    line.start()
+    part_copy = pltpu.make_async_copy(mlp_hbm, part, part_sem)
+    part_copy.start()
+    own_copy = pltpu.make_async_copy(db_ref, db_all.at[i], own_sem)
+    own_copy.start()
+
+    def load(left, right):
+        return [pltpu.make_async_copy(left, lhs, in_sem.at[0]), pltpu.make_async_copy(right, rhs, in_sem.at[1])]
+
+    loads = load(cot_hbm, g_hbm)
+    for copy in loads:
+        copy.start()
+    sums = LineSum(i, n, part, land, s_send, s_recv, pieces)
+    part_copy.wait()
+    loop(n, lambda t: sums.launch(jnp.where(i < n // 2, n - 1 - t, t)))
+    planes = [PlaneSum(row, m, terms_a, land_a, half_a, p_send.at[0], p_recv.at[0], h_send.at[0], h_recv.at[0]),
+              PlaneSum(row, m, terms_b, land_b, half_b, p_send.at[1], p_recv.at[1], h_send.at[1], h_recv.at[1])]
+
+    def line_round(r):
+        line.step(r)
+        relays(sums, i, n, r)
+
+    first, second = planes
+    for copy in loads:
+        copy.wait()
+    for e in range(1, m, 2):
+        block_terms(first, e, [(lhs, rhs, 0)])
+        first.whole(e).start()
+    for e in range(m - 2, -1, -2):
+        block_terms(first, e, [(lhs, rhs, 0)])
+    loads = load(c_hbm, du_hbm)
+    for copy in loads:
+        copy.start()
+    first.merge()
+    first.push(0)
+    for copy in loads:
+        copy.wait()
+    for e in range(1, m, 2):
+        block_terms(second, e, [(lhs, rhs, 0)])
+        second.whole(e).start()
+    line_round(1)
+    for e in range(m - 2, -1, -2):
+        block_terms(second, e, [(lhs, rhs, 0)])
+    second.merge()
+    second.push(0)
+
+    def keep(ref):
+        def out(here, total):
+            ref[here, :] = total
+
+        return out
+
+    def advance(plane, stage, ref):
+        if stage < plane.stages - 1:
+            plane.take(stage)
+            plane.push(stage + 1)
+        else:
+            plane.take(stage, keep(ref))
+
+    advance(first, 0, down_ref)
+    line_round(2)
+    advance(second, 0, up_ref)
+    for r in range(3, n):
+        line_round(r)
+    for stage in range(1, first.stages):
+        advance(first, stage, down_ref)
+        advance(second, stage, up_ref)
+    sums.own()
+
+    def output(b):
+        here = rows_at(b, RB)
+        sums.add(here, acc)
+        lo_ref[here, :] = (h_ref[here, :] + (acc[...] + down_bias[...])).astype(BF)
+
+    loop(size // RB, output)
+    own_copy.wait()
+    line.finish()
+    sums.finish()
+    for plane in planes:
+        plane.finish()
+
+
+def input_kernel(n, m, pieces, dqkv_ref, wq_hbm, x_ref, dh_ref, gain, a_hbm, db_hbm, o_hbm, gt_ref, gqkv_ref, gout_ref,
+                 vec_ref, qv_ref, wq, a_ref, db_ref, o_ref, part, land, terms, land_p, half_p, acc, s_send, s_recv,
+                 in_sem, p_send, p_recv, h_send, h_recv):
+    i, row = lax.axis_index("tensor"), lax.axis_index("dp")
+    size = x_ref.shape[0]
+    width = dqkv_ref.shape[2]
+    depth = part.shape[2]
+    loads = [pltpu.make_async_copy(wq_hbm, wq, in_sem.at[0]), pltpu.make_async_copy(a_hbm, a_ref, in_sem.at[1]),
+             pltpu.make_async_copy(db_hbm, db_ref, in_sem.at[2]), pltpu.make_async_copy(o_hbm, o_ref, in_sem.at[3])]
+    for copy in loads:
+        copy.start()
+    greet_cross(i, n, row, m)
+    sums = LineSum(i, n, part, land, s_send, s_recv, pieces)
+    vec_ref[...] = jnp.zeros_like(vec_ref)
+    qv_ref[...] = jnp.zeros_like(qv_ref)
+    loads[0].wait()
+    tile = 512
+
+    def term(t):
+        d = jnp.where(i < n // 2, n - 1 - t, t)
+        here = rows_at(d, size)
+
+        def columns(k):
+            cols = rows_at(k, tile)
+            total = lax.dot_general(dqkv_ref[0, here, :], wq[0, cols, :], NT, preferred_element_type=F32)
+            for p in range(1, 3):
+                total += lax.dot_general(dqkv_ref[p, here, :], wq[p, cols, :], NT, preferred_element_type=F32)
+            part[d, :, cols] = total.astype(BF)
+
+        loop(depth // tile, columns)
+        sums.launch(d)
+        for p in range(2):
+            qv_ref[p : p + 1, :] += jnp.sum(dqkv_ref[2 * p, here, :].astype(F32), axis=0, keepdims=True)
+
+    loop(n, term)
+    for copy in loads[1:]:
+        copy.wait()
+    plane = PlaneSum(row, m, terms, land_p, half_p, p_send, p_recv, h_send, h_recv)
+    pairs = [(a_ref, dqkv_ref.at[p], p * width) for p in range(3)] + [(db_ref, o_ref, 3 * width)]
+    for e in range(1, m, 2):
+        block_terms(plane, e, pairs)
+        plane.whole(e).start()
+    for e in range(m - 2, -1, -2):
+        block_terms(plane, e, pairs)
+    plane.merge()
+    plane.push(0)
+
+    def out(here, total):
+        for p in range(3):
+            gqkv_ref[p, here, :] = total[:, p * width : (p + 1) * width]
+        gout_ref[here, :] = total[:, 3 * width :]
+
+    stage = 0
+    for r in range(1, n):
+        relays(sums, i, n, r)
+        if r > 1 and stage < plane.stages:
+            if stage < plane.stages - 1:
+                plane.take(stage)
+                plane.push(stage + 1)
+            else:
+                plane.take(stage, out)
+            stage += 1
+    sums.own()
+
+    def norm(b):
+        here = rows_at(b, RB)
+        sums.add(here, acc)
+        grad = acc[...]
+        normal, inverse = norm_stats(x_ref[here, :].astype(F32))
+        vec_ref[0:1, :] += jnp.sum(grad * normal, axis=0, keepdims=True)
+        vec_ref[1:2, :] += jnp.sum(grad, axis=0, keepdims=True)
+        gt_ref[here, :] = (dh_ref[here, :] + norm_back(grad, normal, inverse, gain[...])).astype(BF)
+
+    loop(size // RB, norm)
+    while stage < plane.stages:
+        if stage < plane.stages - 1:
+            plane.take(stage)
+            plane.push(stage + 1)
+        else:
+            plane.take(stage, out)
+        stage += 1
+    sums.finish()
+    plane.finish()
+
+
 def share_kernel(n, m, load_ref, every_ref, column_ref, land, send, recv):
     i, row = lax.axis_index("tensor"), lax.axis_index("dp")
     me, total = row * n + i, m * n
@@ -515,62 +825,11 @@
     return jax.ShapeDtypeStruct(dims, dtype)
 
 
-class Line:
-    def __init__(self, axis, size):
-        self.axis, self.n = axis, size
-        self.i = lax.axis_index(axis)
-        self.first = self.i < size // 2
-
-    def owner(self, k):
-        return jnp.where(self.first, self.i + k, self.i - k + self.n) % self.n
-
-    def hop(self, block, step, r):
-        n = self.n
-        if step < 0:
-            return lax.ppermute(block, self.axis, [(i, i - 1) for i in range(1, n) if i + r - 1 <= n - 1])
-        return lax.ppermute(block, self.axis, [(i, i + 1) for i in range(n - 1) if i - r + 1 >= 0])
-
-    def slots(self, block, down, up):
-        n = self.n
-        down, up = [block] + down, [block] + up
-        slots = [block]
-        for k in range(1, n):
-            if 2 * k <= n:
-                slots.append(jnp.where(self.first, down[k], up[k]))
-            else:
-                low = jnp.where(self.i + k <= n - 1, down[k], up[n - k])
-                high = jnp.where(self.i - k >= 0, up[k], down[n - k])
-                slots.append(jnp.where(self.first, low, high))
-        return slots
-
-    def scatter_sum(self, parts, work=None):
-        n = self.n
-        right = left = None
-        done = []
-
-        def pick(owner):
-            return lax.dynamic_index_in_dim(parts, owner % n, 0, keepdims=False).astype(F32)
-
-        for r in range(1, n):
-            term = pick(self.i + n - r)
-            term = term if right is None else term + right.astype(F32)
-            right = lax.ppermute(term.astype(BF), self.axis, [(i, i + 1) for i in range(min(r, n - 1))])
-            term = pick(self.i + r)
-            term = term if left is None else term + left.astype(F32)
-            left = lax.ppermute(term.astype(BF), self.axis, [(i, i - 1) for i in range(max(n - r, 1), n)])
-            if work and r <= len(work):
-                right, left, value = lax.optimization_barrier((right, left, work[r - 1]()))
-                done.append(value)
-        total = pick(self.i) + (right.astype(F32) + left.astype(F32))
-        return (total, done) if work else total
-
-
 def body(tokens, cotangent, ln1_gain, ln1_bias, qkv_weight, qv_bias, out_weight, out_bias, ln2_gain, ln2_bias,
          up_weight, up_bias, down_weight, down_bias):
     n = lax.axis_size("tensor")
     m = lax.axis_size("dp")
     i, row = lax.axis_index("tensor"), lax.axis_index("dp")
-    line = Line("tensor", n)
     size, depth = tokens.shape
     width = qkv_weight.shape[2]
     units = up_weight.shape[1]
@@ -588,7 +847,7 @@
     me = row * n + i
     whole = jnp.stack([ln1_gain, ln1_bias, out_bias, ln2_gain, ln2_bias, down_bias])
     pack = jnp.concatenate([lane_rows(whole, me), lane_rows(qv_bias, row), lane_rows(up_bias, row)])
-    pack = jnp.pad(pack.astype(F32), ((0, -pack.shape[0] % 8), (0, 0)))
+    pack = jnp.pad(pack, ((0, -pack.shape[0] % 16), (0, 0)))
     lanes_up = 8 + max(up_piece // LANES, 1)
 
     w_qkv = lax.all_gather(qkv_weight, "dp", axis=1, tiled=True)
@@ -599,12 +858,13 @@
     dma = pltpu.SemaphoreType.DMA
     attn_in, vecs = pl.pallas_call(
         functools.partial(tokens_kernel, n, m, piece),
-        out_shape=(shape((LEN, depth), BF), shape((total,) + pack.shape, F32)),
+        out_shape=(shape((LEN, depth), BF), shape((total,) + pack.shape, BF)),
         in_specs=[VM, VM], out_specs=(VM, VM),
         scratch_shapes=[pltpu.VMEM((n, size, depth), BF), pltpu.VMEM((8, depth), F32), dma, dma((2, n)), dma((n,)),
                         dma((total,)), dma((total,))],
         compiler_params=params(0), name="gather_tokens",
     )(pack, tokens)
+    vecs = vecs.astype(F32)
 
     def whole_rows(block, count):
         if count < LANES:
@@ -630,77 +890,65 @@
     )(attn_in, w_qkv, w_out, tokens, cotangent, bias_qv, bias_out, gain_two, shift_two)
 
     pieces = 4
-    mlp_in, hidden, grad_pre, grad_resid, branch_cot, vec_two, grad_up_b = pl.pallas_call(
+    mlp_in, hidden, grad_pre, mlp_part, grad_resid, branch_cot, vec_two, grad_up_b = pl.pallas_call(
         functools.partial(hidden_kernel, n, pieces),
         out_shape=(shape((n, size, depth), BF), shape((n, size, units), BF), shape((n, size, units), BF),
-                   shape((size, depth), F32), shape((size, depth), BF), shape((8, depth), F32), shape((8, units), F32)),
-        in_specs=[VM, VM, ANY, ANY, ANY, VM, VM], out_specs=(ANY, ANY, ANY, VM, VM, VM, VM),
+                   shape((n, size, depth), BF), shape((size, depth), F32), shape((size, depth), BF),
+                   shape((8, depth), F32), shape((8, units), F32)),
+        in_specs=[VM, VM, ANY, ANY, ANY, VM, VM], out_specs=(ANY, ANY, ANY, ANY, VM, VM, VM, VM),
         scratch_shapes=[pltpu.VMEM((n, size, depth), BF), pltpu.VMEM((n, size, units), BF),
                         pltpu.VMEM((n, size, units), BF), pltpu.VMEM((n, size, depth), BF),
                         pltpu.VMEM((depth, units), BF), pltpu.VMEM((units, depth), BF)] + sums +
                        [dma((2, n)), dma((n,)), dma((n, pieces)), dma((n + 1, pieces)), dma((2,)), dma, dma,
-                        dma((n,)), dma((n,)), dma((n,))],
+                        dma((n,)), dma((n,)), dma((n,)), pltpu.VMEM((n, size, depth), BF), dma((n,))],
         compiler_params=params(2), name="hidden",
     )(mlp_own, residual, cot_all, w_up, w_down, bias_up, gain_two)
-    mlp_in, hidden, grad_pre = [v.reshape(LEN, -1) for v in (mlp_in, hidden, grad_pre)]
-    cot_rows = cot_all.reshape(LEN, depth)
-
-    hold = lax.optimization_barrier
-    down, up = line.hop(branch_cot, -1, 1), line.hop(branch_cot, 1, 1)
-    downs, ups = [down], [up]
-    work = [
-        lambda: jnp.einsum("rf,rd->fd", hidden, cot_rows, preferred_element_type=F32).astype(BF),
-        lambda: jnp.dot(hidden, w_down, preferred_element_type=F32).astype(BF),
-        lambda: jnp.einsum("rd,rf->df", mlp_in, grad_pre, preferred_element_type=F32).astype(BF),
-    ]
-    done = []
-    for r in range(1, n):
-        if r - 1 < len(work):
-            value = work[r - 1]()
-            down, up, value = hold((down, up, value))
-            done.append(value)
-            downs[-1], ups[-1] = down, up
-        if r < n - 1:
-            down, up = line.hop(down, -1, r + 1), line.hop(up, 1, r + 1)
-            downs.append(down)
-            ups.append(up)
-    grad_down_w, mlp_part, grad_up_w = done
-    slots = line.slots(branch_cot, downs, ups)
-    attn_cot = jnp.zeros((LEN, depth), BF)
-    for k in range(n):
-        attn_cot = lax.dynamic_update_slice(attn_cot, slots[k], (line.owner(k) * size, 0))
-    layer_out = (residual + (line.scatter_sum(mlp_part.reshape(n, size, depth)) + bias_down)).astype(BF)
+    mlp_in, hidden, grad_pre, cot_rows = [v.reshape(LEN, -1) for v in (mlp_in, hidden, grad_pre, cot_all)]
+
+    def plane_scratch(columns):
+        rows = depth // m
+        return [pltpu.VMEM((m, rows, columns), BF), pltpu.VMEM((m // 2, rows, columns), BF),
+                pltpu.VMEM((2, m // 2 - 1, rows // 2, columns), BF)]
+
+    pieces = 2
+    sum_sems = [dma((n, pieces)), dma((n + 1, pieces))]
+    attn_cot, layer_out, grad_down_w, grad_up_w = pl.pallas_call(
+        functools.partial(branch_kernel, n, m, pieces),
+        out_shape=(shape((n, size, depth), BF), shape((size, depth), BF), shape((depth // m, units), F32),
+                   shape((depth // m, units), F32)),
+        in_specs=[VM] * 3 + [ANY] * 5, out_specs=(ANY, VM, VM, VM),
+        scratch_shapes=[pltpu.VMEM((LEN, depth), BF), pltpu.VMEM((LEN, units), BF)] + sums + plane_scratch(units) * 2 +
+                       [pltpu.VMEM((RB, depth), F32), dma((2, n)), dma((n,))] + sum_sems +
+                       [dma, dma, dma((2,)), dma((2, m // 2)), dma((2, m // 2)), dma((2, 2, m // 2 - 1)),
+                        dma((2, 2, m // 2 - 1))],
+        compiler_params=params(4), name="branch",
+    )(branch_cot, residual, bias_down, mlp_part, hidden, cot_rows, mlp_in, grad_pre)
+    attn_cot = attn_cot.reshape(LEN, depth)
     grad_mix = jnp.einsum("rd,ed->re", attn_cot, w_out, preferred_element_type=F32).astype(BF)
     grad_qkv = pl.pallas_call(
         attend_back_kernel, out_shape=shape((3, LEN, width), BF), in_specs=[VM, VM], out_specs=VM,
         scratch_shapes=[pltpu.VMEM((LEN, HD), F32), pltpu.VMEM((LEN, HD), F32)],
         compiler_params=params(), name="attend_back",
-        cost_estimate=pl.CostEstimate(flops=14 * LEN * LEN * width // 2, bytes_accessed=14 * LEN * width,
-                                      transcendentals=LEN * LEN * width // HD),
     )(qkv, grad_mix)
-    grad_qkv, layer_out = hold((grad_qkv, layer_out))
-    attn_back = jnp.einsum("kre,kde->rd", grad_qkv, w_qkv, preferred_element_type=F32).astype(BF)
-    work = [
-        lambda: jnp.einsum("rd,kre->kde", attn_in, grad_qkv, preferred_element_type=F32).astype(BF),
-        lambda: jnp.einsum("re,rd->ed", mixture, attn_cot, preferred_element_type=F32).astype(BF),
-    ]
-    grad_normed_one, (grad_qkv_w, grad_out_w) = line.scatter_sum(attn_back.reshape(n, size, depth), work)
-    normal_one, inverse_one = norm_stats(tokens.astype(F32))
-    grad_tokens = (grad_resid + norm_back(grad_normed_one, normal_one, inverse_one, gain_one)).astype(BF)
-
-    grad_down_w = lax.psum_scatter(grad_down_w, "dp", scatter_dimension=1, tiled=True).astype(F32)
-    grad_up_w = lax.psum_scatter(grad_up_w, "dp", scatter_dimension=0, tiled=True).astype(F32)
-    grad_qkv_w = lax.psum_scatter(grad_qkv_w, "dp", scatter_dimension=1, tiled=True).astype(F32)
-    grad_out_w = lax.psum_scatter(grad_out_w, "dp", scatter_dimension=1, tiled=True).astype(F32)
+    grad_tokens, grad_qkv_w, grad_out_w, vec_one, grad_qv_b = pl.pallas_call(
+        functools.partial(input_kernel, n, m, pieces),
+        out_shape=(shape((size, depth), BF), shape((3, depth // m, width), F32), shape((depth // m, width), F32),
+                   shape((8, depth), F32), shape((8, width), F32)),
+        in_specs=[VM, ANY, VM, VM, VM, ANY, ANY, ANY], out_specs=(VM,) * 5,
+        scratch_shapes=[pltpu.VMEM((3, depth, width), BF), pltpu.VMEM((LEN, depth), BF), pltpu.VMEM((LEN, depth), BF),
+                        pltpu.VMEM((LEN, width), BF)] + sums + plane_scratch(4 * width) +
+                       [pltpu.VMEM((RB, depth), F32)] + sum_sems +
+                       [dma((4,)), dma((m // 2,)), dma((m // 2,)), dma((2, m // 2 - 1)), dma((2, m // 2 - 1))],
+        compiler_params=params(5), name="input",
+    )(grad_qkv, w_qkv, tokens, grad_resid, gain_one, attn_in, attn_cot, mixture)
+    grad_down_w, grad_out_w = grad_down_w.T, grad_out_w.T
 
     vectors = jnp.stack([
-        jnp.sum(grad_normed_one * normal_one, axis=0),
-        jnp.sum(grad_normed_one, axis=0),
-        vec_two[2], vec_two[0], vec_two[1], vec_two[3],
+        vec_one[0], vec_one[1], vec_two[2], vec_two[0], vec_two[1], vec_two[3],
     ])
     vectors = vectors.reshape(6, total, piece).transpose(1, 0, 2).reshape(total, 6 * piece)
     local = jnp.concatenate([
-        jnp.sum(grad_qkv[0::2].astype(F32), axis=1).reshape(2, m, qv_piece).transpose(1, 0, 2).reshape(m, -1),
+        grad_qv_b[:2].reshape(2, m, qv_piece).transpose(1, 0, 2).reshape(m, -1),
         grad_up_b[0].reshape(m, -1)], axis=1)
     local = jnp.broadcast_to(local[:, None], (m, n, local.shape[1])).reshape(total, -1)
     load = jnp.concatenate([vectors, local], axis=1)

time: 846 us -> 593 us (0.70); the launches traced: 836 us -> 592 us
  waiting for transfers between devices: 282 us -> 4.52 us
  Pallas kernels: 355 us -> 546 us
  starting transfers between devices: 59.6 us -> 0.15 us
  matrix products: 64.8 us -> 6.2 us
  other arithmetic: 44 us -> 2.23 us
    reduce_scatter x4 -> x0, waiting for transfers between devices: 194 us -> none  [the longest x1 72.3 us: body(): lax.psum_scatter(grad_up_w, 'dp', scatter_dimension=0, tiled=True)]
    pallas_call x0 -> x2, Pallas kernels: none -> 188 us  [the longest x1 108 us: body(): pl.pallas_call(functools.partial(branch_kernel, n, m, pieces), out_shape=...]
    ppermute x18 -> x0, waiting for transfers between devices: 82.9 us -> none  [the longest x6 50.3 us: scatter_sum(): lax.ppermute(term.astype(BF), self.axis, [(i, i + 1) for i in range(min(r...]
    dot_general x6 -> x0, matrix products: 61.4 us -> none  [the longest x1 14.1 us: body(): jnp.einsum('rf,rd->fd', hidden, cot_rows, preferred_element_type=F32)]
    ppermute x18 -> x0, starting transfers between devices: 59.3 us -> none  [the longest x6 41.2 us: scatter_sum(): lax.ppermute(term.astype(BF), self.axis, [(i, i + 1) for i in range(min(r...]
    convert_element_type x12 -> x1, other arithmetic: 31.8 us -> 0.94 us  [body(): vecs = vecs.astype(F32)]
  transfers between devices with their start and end apart: 26 -> 4, of which waited for: 13 -> 1; matrix products, arithmetic and copies ran while one was open for 11% -> 1% of each run, Pallas kernels for 27% -> 32%
where the time goes in v4:
time: 593 us; the launch traced here: 592 us
  Pallas kernels  546 us (92%)
  local copies, waits for them, and re-layouts  19.4 us (3%)
  between operations  14.1 us (2%)
  matrix products  6.2 us (1%)
    pallas_call x1, Pallas kernels, body(): pl.pallas_call(functools.partial(hidden_kernel, n, pieces), out_shape=(sh...  137 us
    pallas_call x1, Pallas kernels, body(): pl.pallas_call(functools.partial(branch_kernel, n, m, pieces), out_shape=...  108 us
    pallas_call x1, Pallas kernels, body(): pl.pallas_call(functools.partial(attend_kernel, n, pieces), out_shape=(sh...  99.4 us
    pallas_call x1, Pallas kernels, body(): pl.pallas_call(functools.partial(tokens_kernel, n, m, piece), out_shape=(...  87.2 us
    pallas_call x1, Pallas kernels, body(): pl.pallas_call(functools.partial(input_kernel, n, m, pieces), out_shape=(...  79.8 us
    pallas_call x1, Pallas kernels, body(): pl.pallas_call(attend_back_kernel, out_shape=shape((3, LEN, width), BF),...  21 us
    pallas_call x1, Pallas kernels, body(): pl.pallas_call(functools.partial(share_kernel, n, m), out_shape=(shape(lo...  12.6 us
  transfers between devices with their start and end apart: 4, of which 1 were waited for; matrix products, arithmetic and copies ran while one was open for 1% of the time, Pallas kernels for 32%

profile of v4, /device:TPU:0, one launch (start us, length us, event | category | flops | bytes accessed | tf_op | source)
XLA Modules:
  0.0 592.3 jit_solution(14969207516037868794)
XLA Ops:
  7.3 0.0 all-gather.7.cloned.1.call-start
  7.3 0.7 all-gather.7.cloned.1.call-update
  8.0 0.0 all-gather.5.cloned.1.call-start
  8.0 0.7 all-gather.5.cloned.1.call-update
  8.7 0.0 all-gather.9.cloned.1.call-start
  8.8 0.7 all-gather.9.cloned.1.call-update
  9.5 0.0 all-gather.11.cloned.1.call-start
  9.5 0.5 all-gather.11.cloned.1.call-update
  10.1 0.1 tile.21
  10.3 0.1 tile.9
  10.4 0.6 fusion.5.pack_ref
  11.0 87.2 %gather_tokens.1 = (bf16[1024,2048]{1,0:T(8,128)(2,1)}, bf16[32,16,128]{2,1,0:T(8,128)(2,1)}) custom-call(bf16[16,128]{1,0:T(8,128)(2,1)} %fusion.5.pack_ref, bf16[256,2048]{1,0:T(8,128)(2,1)} %x_ref.5), custom_call_target="tpu_custom_call" | custom-call | tf_op jit(solution)/shard_map/gather_tokens/pallas_call | solution.py:859
  98.2 0.9 convert_element_type.14
  99.2 0.6 slice.116
  99.8 0.6 bitcast_reduce_fusion.1
  100.4 0.6 slice_bitcast_fusion
  101.1 99.4 %attend.1 = (bf16[3,1024,512]{2,1,0:T(8,128)(2,1)}, bf16[1024,512]{1,0:T(8,128)(2,1)}, f32[256,2048]{1,0:T(8,128)}, bf16[256,2048]{1,0:T(8,128)(2,1)}, bf16[4,256,2048]{2,1,0:T(8,128)(2,1)}) custom-call(bf16[1024,2048]{1,0:T(8,128)(2,1)} %get-tuple-element.40.a_hbm, bf16[3,2048,512]{2,1,0:T(8,128)(2,1)} %all-gather.5.cloned.1.call-done.wq_hbm, ...), custom_call_target="tpu_custom_call" | custom-call | tf_op jit(solution)/shard_map/attend/pallas_call | solution.py:882
  200.4 0.0 all-gather.9.cloned.1.call-done.up_hbm
  200.5 1.9 all-gather.11.cloned.1.call-done.down_hbm
  202.4 137.3 %hidden.1 = (bf16[4,256,2048]{2,1,0:T(8,128)(2,1)}, bf16[4,256,2048]{2,1,0:T(8,128)(2,1)}, bf16[4,256,2048]{2,1,0:T(8,128)(2,1)}, bf16[4,256,2048]{2,1,0:T(8,128...) custom-call(bf16[256,2048]{1,0:T(8,128)(2,1)} %get-tuple-element.42.c_ref, ...), custom_call_target="tpu_custom_call" | custom-call | tf_op jit(solution)/shard_map/hidden/pallas_call | solution.py:893
  339.7 108.5 %branch.1 = (bf16[4,256,2048]{2,1,0:T(8,128)(2,1)}, bf16[256,2048]{1,0:T(8,128)(2,1)}, f32[256,2048]{1,0:T(8,128)}, f32[256,2048]{1,0:T(8,128)}) custom-call(bf16[256,2048]{1,0:T(8,128)(2,1)} %get-tuple-element.45.db_ref, f32[256,2048]{1,0:T(8,128)} %get-tuple-element.43.h_ref, f32[1,2048]{1,0:T(1,128)} %get-tuple-element.111.down_bias, ...), custom_call_target="tpu_custom_call" | custom-call | tf_op jit(solution)/shard_map/branch/pallas_call | solution.py:915
  448.2 6.2 %convolution_convert_fusion.do_ref = bf16[1024,512]{1,0:T(8,128)(2,1)} fusion(bf16[1024,2048]{1,0:T(8,128)(2,1)} %bitcast.62, bf16[512,2048]{1,0:T(8,128)(2,1)} %all-gather.7.cloned.1.call-done.wo_hbm), kind=kOutput, calls=%fused_computation | convolution fusion | flops 2148007936 | bytes 7340032 | tf_op jit(solution)/shard_map/rd,ed->re/dot_general | solution.py:927
  454.4 21.0 %attend_back.1.dqkv_ref = bf16[3,1024,512]{2,1,0:T(8,128)(2,1)} custom-call(bf16[3,1024,512]{2,1,0:T(8,128)(2,1)} %get-tuple-element.51.qkv_ref, bf16[1024,512]{1,0:T(8,128)(2,1)} %convolution_convert_fusion.do_ref), custom_call_target="tpu_custom_call" | custom-call | tf_op jit(solution)/shard_map/attend_back/pallas_call | solution.py:928
  475.4 79.8 %input.1 = (bf16[256,2048]{1,0:T(8,128)(2,1)}, f32[3,256,512]{2,1,0:T(8,128)}, f32[256,512]{1,0:T(8,128)}, f32[8,2048]{1,0:T(8,128)}, f32[8,512]{1,0:T(8,128)}) custom-call(bf16[3,1024,512]{2,1,0:T(8,128)(2,1)} %attend_back.1.dqkv_ref, bf16[3,2048,512]{2,1,0:T(8,128)(2,1)} %all-gather.5.cloned.1.call-done.wq_hbm, bf16[256,2048]{1,0:T(8,128)(2,1)} %x_ref.5, ...), custom_call_target="tpu_custom_call" | custom-call | tf_op jit(solution)/shard_map/input/pallas_call | solution.py:933
  555.2 0.7 slice.99
  555.9 0.1 reshape.145
  556.0 0.1 reshape.146
  556.0 0.8 slice.95
  556.9 0.8 slice.97
  557.7 0.9 fusion.6
  558.7 0.1 reshape.143
  558.8 0.1 copy.42
  558.9 0.1 reshape.144
  559.0 0.7 copy.39
  559.7 12.6 %share.1 = (f32[8,128]{1,0:T(8,128)}, f32[8,128]{1,0:T(8,128)}) custom-call(f32[32,8,128]{2,1,0:T(8,128)} %bitcast.71), custom_call_target="tpu_custom_call" | custom-call | tf_op jit(solution)/shard_map/share/pallas_call | solution.py:956
  572.3 0.8 slice_reduce_fusion.1
  573.1 1.2 slice_bitcast_fusion.5
  574.4 0.7 slice.101
  575.0 0.6 reshape.150
  575.7 0.1 reshape.149
  575.7 0.5 slice_bitcast_fusion.6
  576.3 2.0 copy.37
  578.3 3.0 copy.38
  581.3 1.0 copy.48
  582.3 1.0 copy.49
  583.2 1.1 copy.50
  584.4 0.0 copy-done
  584.4 1.3 copy.51
  (41 shorter events, 0.2 us)
Async XLA Ops:
  7.2 2.9 copy-start.11
  7.2 3.0 copy-start.10
  7.2 3.0 copy-start.9
  7.2 3.0 copy-start.8
  7.2 3.0 copy-start.7
  7.2 3.0 copy-start.6
  7.2 3.0 copy-start.5
  7.3 3.1 copy-start.4
  7.3 93.8 %all-gather.7.cloned.1.call-start = ((), (), s32[]{:S(2)}) async-start(), calls=%async_computation.1 | async-start | bytes 2359296 | tf_op jit(solution)/shard_map/all_gather | solution.py:854
  8.0 93.1 %all-gather.5.cloned.1.call-start = ((), (), s32[]{:S(2)}) async-start(), calls=%async_computation | async-start | bytes 7077888 | tf_op jit(solution)/shard_map/all_gather | solution.py:853
  8.7 191.7 %all-gather.9.cloned.1.call-start = ((), (), s32[]{:S(2)}) async-start(), calls=%async_computation.2 | async-start | bytes 9437184 | tf_op jit(solution)/shard_map/all_gather | solution.py:855
  9.5 192.9 %all-gather.11.cloned.1.call-start = ((), (), s32[]{:S(2)}) async-start(), calls=%async_computation.3 | async-start | bytes 9437184 | tf_op jit(solution)/shard_map/all_gather | solution.py:856
  572.3 9.0 %copy-start.2 = (bf16[256,2048]{1,0:T(8,128)(2,1)S(1)}, bf16[256,2048]{1,0:T(8,128)(2,1)}, u32[]{:S(2)}) copy-start(bf16[256,2048]{1,0:T(8,128)(2,1)} %get-tuple-element.136) | copy-start | bytes 3145732
  578.3 3.9 copy-start.3
  581.3 2.0 copy-start.1
  582.3 2.1 copy-start
Sparse Core Ops, SparseCore 0:
  9.9 31.0 all-gather.6
  42.9 45.4 all-gather.4
  90.3 54.2 all-gather.8
  146.4 55.9 all-gather.10

commit v5 on v4

--- a/solution.py
+++ b/solution.py
@@ -462,31 +462,28 @@
     sums.finish()
 
 
-def attend_back_kernel(qkv_ref, do_ref, out_ref, dk, dv):
-    heads = qkv_ref.shape[2] // HD
+def attend_back(q_of, k_of, v_of, do_of, heads, put, dk, dv):
     block = 256
     factor = HD ** (-0.5)
 
     def head(t):
-        cols = pl.ds(pl.multiple_of(t * HD, HD), HD)
         dk[...] = jnp.zeros_like(dk)
         dv[...] = jnp.zeros_like(dv)
         for b in range(LEN // block):
-            here, keys = slice(b * block, (b + 1) * block), (b + 1) * block
-            q, k, v = qkv_ref[0, here, cols], qkv_ref[1, 0:keys, cols], qkv_ref[2, 0:keys, cols]
-            do = do_ref[here, cols]
+            here, keys = slice(b * block, (b + 1) * block), slice(0, (b + 1) * block)
+            q, k, v, do = q_of(here, t), k_of(keys, t), v_of(keys, t), do_of(here, t)
             s = lax.dot_general(q, k, NT, preferred_element_type=F32) * factor
             query = lax.broadcasted_iota(jnp.int32, s.shape, 0) + b * block
             s = jnp.where(query >= lax.broadcasted_iota(jnp.int32, s.shape, 1), s, -1e30)
             e = jnp.exp(s - jnp.max(s, axis=-1, keepdims=True))
             prob = e / jnp.sum(e, axis=-1, keepdims=True)
-            dv[0:keys, :] += lax.dot_general(prob.astype(BF), do, TN, preferred_element_type=F32)
+            dv[keys, :] += lax.dot_general(prob.astype(BF), do, TN, preferred_element_type=F32)
             dp = lax.dot_general(do, v, NT, preferred_element_type=F32)
             ds = (prob * (dp - jnp.sum(prob * dp, axis=-1, keepdims=True))).astype(BF)
-            out_ref[0, here, cols] = (jnp.dot(ds, k, preferred_element_type=F32) * factor).astype(BF)
-            dk[0:keys, :] += lax.dot_general(ds, q, TN, preferred_element_type=F32)
-        out_ref[1, :, cols] = (dk[...] * factor).astype(BF)
-        out_ref[2, :, cols] = dv[...].astype(BF)
+            put(0, here, t, (jnp.dot(ds, k, preferred_element_type=F32) * factor).astype(BF))
+            dk[keys, :] += lax.dot_general(ds, q, TN, preferred_element_type=F32)
+        put(1, slice(0, LEN), t, (dk[...] * factor).astype(BF))
+        put(2, slice(0, LEN), t, dv[...].astype(BF))
 
     loop(heads, head)
 
@@ -496,8 +493,8 @@
 
 
 class PlaneSum:
-    def __init__(self, row, m, terms, land, halves, send, recv, h_send, h_recv):
-        self.row, self.m, self.terms, self.land, self.halves = row, m, terms, land, halves
+    def __init__(self, row, m, out, terms, land, halves, send, recv, h_send, h_recv):
+        self.row, self.m, self.out, self.terms, self.land, self.halves = row, m, out, terms, land, halves
         self.send, self.recv, self.h_send, self.h_recv = send, recv, h_send, h_recv
         bits = [1 << k for k in range(1, m.bit_length() - 1)]
         self.plan = []
@@ -519,13 +516,13 @@
 
     def whole(self, e):
         return pltpu.make_async_remote_copy(
-            src_ref=self.terms.at[e], dst_ref=self.land.at[e // 2], send_sem=self.send.at[e // 2],
+            src_ref=self.out.at[e // 2], dst_ref=self.land.at[e // 2], send_sem=self.send.at[e // 2],
             recv_sem=self.recv.at[e // 2], device_id={"dp": partner(self.row, 1)}, device_id_type=MESH)
 
     def half(self, h, bit, e, at):
         size = self.halves.shape[2]
         return pltpu.make_async_remote_copy(
-            src_ref=self.terms.at[e, pl.ds(h * size, size)], dst_ref=self.halves.at[h, at],
+            src_ref=self.terms.at[e // 2, pl.ds(h * size, size)], dst_ref=self.halves.at[h, at],
             send_sem=self.h_send.at[h, at], recv_sem=self.h_recv.at[h, at],
             device_id={"dp": partner(self.row, bit)}, device_id_type=MESH)
 
@@ -535,8 +532,8 @@
 
             def add(b):
                 here = rows_at(b, RB)
-                total = self.terms[e, here, :].astype(F32) + self.land[e // 2, here, :].astype(F32)
-                self.terms[e, here, :] = total.astype(BF)
+                total = self.terms[e // 2, here, :].astype(F32) + self.land[e // 2, here, :].astype(F32)
+                self.terms[e // 2, here, :] = total.astype(BF)
 
             loop(self.terms.shape[1] // RB, add)
 
@@ -555,21 +552,52 @@
 
                 def add(b):
                     here, there = rows_at(b, RB), pl.ds(pl.multiple_of(h * size + b * RB, RB), RB)
-                    total = self.terms[into, there, :].astype(F32) + self.halves[h, at, here, :].astype(F32)
+                    total = self.terms[into // 2, there, :].astype(F32) + self.halves[h, at, here, :].astype(F32)
                     if out is None:
-                        self.terms[into, there, :] = total.astype(BF)
+                        self.terms[into // 2, there, :] = total.astype(BF)
                     else:
                         out(there, total)
 
                 loop(size // RB, add)
 
-    def finish(self):
+    def sent(self):
         for e in range(1, self.m, 2):
             self.whole(e).wait_send()
+
+    def finish(self):
         for h in range(2):
             for bit, moves in self.plan[h]:
                 for e, _, at in moves:
                     self.half(h, bit, e, at).wait_send()
+
+
+class VectorSum:
+    def __init__(self, me, count, device, vectors, piece, land, out, send, recv):
+        self.me, self.count, self.device, self.vectors, self.piece = me, count, device, vectors, piece
+        self.land, self.out, self.send, self.recv = land, out, send, recv
+
+    def lanes(self, owner):
+        size = self.land.shape[2]
+        return pl.ds(pl.multiple_of(owner * self.piece // size * size, size), size)
+
+    def copy(self, src, other):
+        return pltpu.make_async_remote_copy(
+            src_ref=self.vectors.at[:, self.lanes(other)], dst_ref=self.land.at[src], send_sem=self.send.at[other],
+            recv_sem=self.recv.at[src], device_id=self.device(other), device_id_type=MESH)
+
+    def start(self):
+        loop(self.count - 1, lambda s: self.copy(self.me, (self.me + s + 1) % self.count).start())
+
+    def finish(self):
+        self.out[...] = self.vectors[:, self.lanes(self.me)]
+
+        def take(s):
+            src = (self.me + s + 1) % self.count
+            self.copy(src, self.me).wait_recv()
+            self.out[...] += self.land[src]
+
+        loop(self.count - 1, take)
+        loop(self.count - 1, lambda s: self.copy(self.me, (self.me + s + 1) % self.count).wait_send())
 
 
 def greet_cross(i, n, row, m):
@@ -610,17 +638,19 @@
 
         def columns(k):
             there = pl.ds(pl.multiple_of(first + k * tile, tile), tile)
-            plane.terms[e, :, there] = lax.dot_general(
+            (plane.out if e % 2 else plane.terms)[e // 2, :, there] = lax.dot_general(
                 lhs[:, cols], rhs[:, rows_at(k, tile)], TN, preferred_element_type=F32).astype(BF)
 
         loop(width // tile, columns)
 
 
-def branch_kernel(n, m, pieces, db_ref, h_ref, down_bias, mlp_hbm, g_hbm, cot_hbm, c_hbm, du_hbm, db_all, lo_ref,
-                  down_ref, up_ref, lhs, rhs, part, land, terms_a, land_a, half_a, terms_b, land_b, half_b, acc, send,
-                  recv, s_send, s_recv, own_sem, part_sem, in_sem, p_send, p_recv, h_send, h_recv):
+def branch_kernel(n, m, pieces, db_ref, h_ref, down_bias, mlp_hbm, g_hbm, cot_hbm, c_hbm, du_hbm, qkv_hbm, wo_hbm,
+                  db_all, lo_ref, down_ref, up_ref, dqkv_ref, lhs, rhs, wo, dk, dv, part, land, out, terms_a, land_a,
+                  half_a, terms_b, land_b, half_b, acc, send, recv, s_send, s_recv, own_sem, part_sem, in_sem, qkv_sem,
+                  db_sem, p_send, p_recv, h_send, h_recv):
     i, row = lax.axis_index("tensor"), lax.axis_index("dp")
     size = db_ref.shape[0]
+    width = wo.shape[0]
     greet_cross(i, n, row, m)
     line = LineGather(i, n, db_ref, db_all, send, recv)
     line.start()
@@ -635,45 +665,73 @@
     loads = load(cot_hbm, g_hbm)
     for copy in loads:
         copy.start()
+    wo_copy = pltpu.make_async_copy(wo_hbm, wo, in_sem.at[2])
+    wo_copy.start()
     sums = LineSum(i, n, part, land, s_send, s_recv, pieces)
     part_copy.wait()
     loop(n, lambda t: sums.launch(jnp.where(i < n // 2, n - 1 - t, t)))
-    planes = [PlaneSum(row, m, terms_a, land_a, half_a, p_send.at[0], p_recv.at[0], h_send.at[0], h_recv.at[0]),
-              PlaneSum(row, m, terms_b, land_b, half_b, p_send.at[1], p_recv.at[1], h_send.at[1], h_recv.at[1])]
-
-    def line_round(r):
-        line.step(r)
-        relays(sums, i, n, r)
-
+    planes = [PlaneSum(row, m, out, terms_a, land_a, half_a, p_send.at[0], p_recv.at[0], h_send.at[0], h_recv.at[0]),
+              PlaneSum(row, m, out, terms_b, land_b, half_b, p_send.at[1], p_recv.at[1], h_send.at[1], h_recv.at[1])]
     first, second = planes
     for copy in loads:
         copy.wait()
+    left, right = lhs.at[:, 0 : lhs.shape[1]], rhs.at[:, 0 : down_ref.shape[1]]
     for e in range(1, m, 2):
-        block_terms(first, e, [(lhs, rhs, 0)])
+        block_terms(first, e, [(left, right, 0)])
         first.whole(e).start()
     for e in range(m - 2, -1, -2):
-        block_terms(first, e, [(lhs, rhs, 0)])
+        block_terms(first, e, [(left, right, 0)])
     loads = load(c_hbm, du_hbm)
     for copy in loads:
         copy.start()
     first.merge()
     first.push(0)
+    first.sent()
     for copy in loads:
         copy.wait()
     for e in range(1, m, 2):
-        block_terms(second, e, [(lhs, rhs, 0)])
+        block_terms(second, e, [(left, right, 0)])
         second.whole(e).start()
+
+    def line_round(r):
+        line.step(r)
+        relays(sums, i, n, r)
+
     line_round(1)
     for e in range(m - 2, -1, -2):
-        block_terms(second, e, [(lhs, rhs, 0)])
+        block_terms(second, e, [(left, right, 0)])
+    qkv_copies = [pltpu.make_async_copy(qkv_hbm.at[p], rhs.at[:, p * width : (p + 1) * width], qkv_sem.at[p])
+                  for p in range(3)]
+    for copy in qkv_copies:
+        copy.start()
     second.merge()
     second.push(0)
+    own_copy.wait()
+    wo_copy.wait()
+
+    def mixture_back(j):
+        here = rows_at(j, size)
+        copy = pltpu.make_async_copy(db_all.at[j], lhs.at[here], db_sem.at[j])
+        copy.start()
+        copy.wait()
+        rhs[here, 3 * width : 4 * width] = lax.dot_general(
+            lhs[here, :], wo[...], NT, preferred_element_type=F32).astype(BF)
+
+    def round_back(r):
+        def side(s):
+            j = jnp.where(s == 0, i - r, i + r)
+
+            @pl.when(jnp.logical_and(j >= 0, j <= n - 1))
+            def _():
+                mixture_back(j)
+
+        loop(2, side)
 
     def keep(ref):
-        def out(here, total):
+        def put(here, total):
             ref[here, :] = total
 
-        return out
+        return put
 
     def advance(plane, stage, ref):
         if stage < plane.stages - 1:
@@ -682,11 +740,32 @@
         else:
             plane.take(stage, keep(ref))
 
+    mixture_back(i)
+    round_back(1)
     advance(first, 0, down_ref)
     line_round(2)
+    round_back(2)
     advance(second, 0, up_ref)
+
+    def rest(r):
+        line_round(r)
+        round_back(r)
+
     for r in range(3, n):
-        line_round(r)
+        rest(r)
+    for copy in qkv_copies:
+        copy.wait()
+
+    def column(p):
+        def get(here, t):
+            return rhs[here, pl.ds(pl.multiple_of(p * width + t * HD, HD), HD)]
+
+        return get
+
+    def put(p, here, t, value):
+        dqkv_ref[p, here, pl.ds(pl.multiple_of(t * HD, HD), HD)] = value
+
+    attend_back(column(0), column(1), column(2), column(3), width // HD, put, dk, dv)
     for stage in range(1, first.stages):
         advance(first, stage, down_ref)
         advance(second, stage, up_ref)
@@ -698,25 +777,37 @@
         lo_ref[here, :] = (h_ref[here, :] + (acc[...] + down_bias[...])).astype(BF)
 
     loop(size // RB, output)
-    own_copy.wait()
     line.finish()
     sums.finish()
+    second.sent()
     for plane in planes:
         plane.finish()
 
 
-def input_kernel(n, m, pieces, dqkv_ref, wq_hbm, x_ref, dh_ref, gain, a_hbm, db_hbm, o_hbm, gt_ref, gqkv_ref, gout_ref,
-                 vec_ref, qv_ref, wq, a_ref, db_ref, o_ref, part, land, terms, land_p, half_p, acc, s_send, s_recv,
-                 in_sem, p_send, p_recv, h_send, h_recv):
+def input_kernel(n, m, pieces, widths, dqkv_ref, wq_hbm, x_ref, dh_ref, gain, early_ref, up_ref, a_hbm, db_hbm, o_hbm,
+                 gt_ref, gqkv_ref, gout_ref, early_out, late_out, up_out, qv_out, vec_ref, qv_ref, wq, a_ref, db_ref,
+                 o_ref, part, land, out_p, terms, land_p, half_p, acc, early_land, late_land, up_land, qv_land, s_send,
+                 s_recv, in_sem, p_send, p_recv, h_send, h_recv, e_send, e_recv, l_send, l_recv, u_send, u_recv, q_send,
+                 q_recv):
     i, row = lax.axis_index("tensor"), lax.axis_index("dp")
+    me, total_devices = row * n + i, m * n
     size = x_ref.shape[0]
     width = dqkv_ref.shape[2]
+    piece, up_piece, qv_piece = widths
     depth = part.shape[2]
     loads = [pltpu.make_async_copy(wq_hbm, wq, in_sem.at[0]), pltpu.make_async_copy(a_hbm, a_ref, in_sem.at[1]),
              pltpu.make_async_copy(db_hbm, db_ref, in_sem.at[2]), pltpu.make_async_copy(o_hbm, o_ref, in_sem.at[3])]
     for copy in loads:
         copy.start()
-    greet_cross(i, n, row, m)
+    greet_all(me, n, total_devices)
+    every = [VectorSum(me, total_devices, lambda g: {"dp": g // n, "tensor": g % n}, early_ref, piece, early_land, early_out,
+                       e_send, e_recv),
+             VectorSum(me, total_devices, lambda g: {"dp": g // n, "tensor": g % n}, vec_ref, piece, late_land, late_out,
+                       l_send, l_recv)]
+    column = [VectorSum(row, m, lambda g: {"dp": g}, up_ref, up_piece, up_land, up_out, u_send, u_recv),
+              VectorSum(row, m, lambda g: {"dp": g}, qv_ref, qv_piece, qv_land, qv_out, q_send, q_recv)]
+    every[0].start()
+    column[0].start()
     sums = LineSum(i, n, part, land, s_send, s_recv, pieces)
     vec_ref[...] = jnp.zeros_like(vec_ref)
     qv_ref[...] = jnp.zeros_like(qv_ref)
@@ -740,9 +831,10 @@
             qv_ref[p : p + 1, :] += jnp.sum(dqkv_ref[2 * p, here, :].astype(F32), axis=0, keepdims=True)
 
     loop(n, term)
+    column[1].start()
     for copy in loads[1:]:
         copy.wait()
-    plane = PlaneSum(row, m, terms, land_p, half_p, p_send, p_recv, h_send, h_recv)
+    plane = PlaneSum(row, m, out_p, terms, land_p, half_p, p_send, p_recv, h_send, h_recv)
     pairs = [(a_ref, dqkv_ref.at[p], p * width) for p in range(3)] + [(db_ref, o_ref, 3 * width)]
     for e in range(1, m, 2):
         block_terms(plane, e, pairs)
@@ -779,6 +871,7 @@
         gt_ref[here, :] = (dh_ref[here, :] + norm_back(grad, normal, inverse, gain[...])).astype(BF)
 
     loop(size // RB, norm)
+    every[1].start()
     while stage < plane.stages:
         if stage < plane.stages - 1:
             plane.take(stage)
@@ -787,32 +880,10 @@
             plane.take(stage, out)
         stage += 1
     sums.finish()
+    plane.sent()
     plane.finish()
-
-
-def share_kernel(n, m, load_ref, every_ref, column_ref, land, send, recv):
-    i, row = lax.axis_index("tensor"), lax.axis_index("dp")
-    me, total = row * n + i, m * n
-    greet_all(me, n, total)
-
-    def copy(src, other):
-        return pltpu.make_async_remote_copy(
-            src_ref=load_ref.at[other], dst_ref=land.at[src], send_sem=send.at[other], recv_sem=recv.at[src],
-            device_id={"dp": other // n, "tensor": other % n}, device_id_type=MESH)
-
-    loop(total - 1, lambda s: copy(me, (me + s + 1) % total).start())
-    land[me] = load_ref[me]
-    every_ref[...] = jnp.zeros_like(every_ref)
-    column_ref[...] = jnp.zeros_like(column_ref)
-    loop(total - 1, lambda s: copy((me + s + 1) % total, me).wait_recv())
-
-    def add(d):
-        for t in range(n):
-            every_ref[...] += land[d * n + t]
-        column_ref[...] += land[d * n + i]
-
-    loop(m, add)
-    loop(total - 1, lambda s: copy(me, (me + s + 1) % total).wait_send())
+    for group in (every[0], column[0], column[1], every[1]):
+        group.finish()
 
 
 def params(collective=None):
@@ -907,62 +978,53 @@
 
     def plane_scratch(columns):
         rows = depth // m
-        return [pltpu.VMEM((m, rows, columns), BF), pltpu.VMEM((m // 2, rows, columns), BF),
+        return [pltpu.VMEM((m // 2, rows, columns), BF), pltpu.VMEM((m // 2, rows, columns), BF),
                 pltpu.VMEM((2, m // 2 - 1, rows // 2, columns), BF)]
 
     pieces = 2
     sum_sems = [dma((n, pieces)), dma((n + 1, pieces))]
-    attn_cot, layer_out, grad_down_w, grad_up_w = pl.pallas_call(
+    attn_cot, layer_out, grad_down_w, grad_up_w, grad_qkv = pl.pallas_call(
         functools.partial(branch_kernel, n, m, pieces),
         out_shape=(shape((n, size, depth), BF), shape((size, depth), BF), shape((depth // m, units), F32),
-                   shape((depth // m, units), F32)),
-        in_specs=[VM] * 3 + [ANY] * 5, out_specs=(ANY, VM, VM, VM),
-        scratch_shapes=[pltpu.VMEM((LEN, depth), BF), pltpu.VMEM((LEN, units), BF)] + sums + plane_scratch(units) * 2 +
+                   shape((depth // m, units), F32), shape((3, LEN, width), BF)),
+        in_specs=[VM] * 3 + [ANY] * 7, out_specs=(ANY, VM, VM, VM, VM),
+        scratch_shapes=[pltpu.VMEM((LEN, depth), BF), pltpu.VMEM((LEN, units), BF), pltpu.VMEM((width, depth), BF),
+                        pltpu.VMEM((LEN, HD), F32), pltpu.VMEM((LEN, HD), F32)] + sums +
+                       [pltpu.VMEM((m // 2, depth // m, units), BF)] + plane_scratch(units) * 2 +
                        [pltpu.VMEM((RB, depth), F32), dma((2, n)), dma((n,))] + sum_sems +
-                       [dma, dma, dma((2,)), dma((2, m // 2)), dma((2, m // 2)), dma((2, 2, m // 2 - 1)),
-                        dma((2, 2, m // 2 - 1))],
+                       [dma, dma, dma((3,)), dma((3,)), dma((n,)), dma((2, m // 2)), dma((2, m // 2)),
+                        dma((2, 2, m // 2 - 1)), dma((2, 2, m // 2 - 1))],
         compiler_params=params(4), name="branch",
-    )(branch_cot, residual, bias_down, mlp_part, hidden, cot_rows, mlp_in, grad_pre)
+    )(branch_cot, residual, bias_down, mlp_part, hidden, cot_rows, mlp_in, grad_pre, qkv, w_out)
     attn_cot = attn_cot.reshape(LEN, depth)
-    grad_mix = jnp.einsum("rd,ed->re", attn_cot, w_out, preferred_element_type=F32).astype(BF)
-    grad_qkv = pl.pallas_call(
-        attend_back_kernel, out_shape=shape((3, LEN, width), BF), in_specs=[VM, VM], out_specs=VM,
-        scratch_shapes=[pltpu.VMEM((LEN, HD), F32), pltpu.VMEM((LEN, HD), F32)],
-        compiler_params=params(), name="attend_back",
-    )(qkv, grad_mix)
-    grad_tokens, grad_qkv_w, grad_out_w, vec_one, grad_qv_b = pl.pallas_call(
-        functools.partial(input_kernel, n, m, pieces),
+
+    tiles = [max(v, LANES) for v in (piece, up_piece, qv_piece)]
+    grad_tokens, grad_qkv_w, grad_out_w, early, late, grad_up_b, grad_qv_b = pl.pallas_call(
+        functools.partial(input_kernel, n, m, pieces, (piece, up_piece, qv_piece)),
         out_shape=(shape((size, depth), BF), shape((3, depth // m, width), F32), shape((depth // m, width), F32),
-                   shape((8, depth), F32), shape((8, width), F32)),
-        in_specs=[VM, ANY, VM, VM, VM, ANY, ANY, ANY], out_specs=(VM,) * 5,
-        scratch_shapes=[pltpu.VMEM((3, depth, width), BF), pltpu.VMEM((LEN, depth), BF), pltpu.VMEM((LEN, depth), BF),
-                        pltpu.VMEM((LEN, width), BF)] + sums + plane_scratch(4 * width) +
-                       [pltpu.VMEM((RB, depth), F32)] + sum_sems +
-                       [dma((4,)), dma((m // 2,)), dma((m // 2,)), dma((2, m // 2 - 1)), dma((2, m // 2 - 1))],
+                   shape((8, tiles[0]), F32), shape((8, tiles[0]), F32), shape((8, tiles[1]), F32),
+                   shape((8, tiles[2]), F32)),
+        in_specs=[VM, ANY, VM, VM, VM, VM, VM, ANY, ANY, ANY], out_specs=(VM,) * 7,
+        scratch_shapes=[pltpu.VMEM((8, depth), F32), pltpu.VMEM((8, width), F32),
+                        pltpu.VMEM((3, depth, width), BF), pltpu.VMEM((LEN, depth), BF), pltpu.VMEM((LEN, depth), BF),
+                        pltpu.VMEM((LEN, width), BF)] + sums + [pltpu.VMEM((m // 2, depth // m, 4 * width), BF)] +
+                       plane_scratch(4 * width) +
+                       [pltpu.VMEM((RB, depth), F32), pltpu.VMEM((total, 8, tiles[0]), F32),
+                        pltpu.VMEM((total, 8, tiles[0]), F32), pltpu.VMEM((m, 8, tiles[1]), F32),
+                        pltpu.VMEM((m, 8, tiles[2]), F32)] + sum_sems +
+                       [dma((4,)), dma((m // 2,)), dma((m // 2,)), dma((2, m // 2 - 1)), dma((2, m // 2 - 1))] +
+                       [dma((total,))] * 4 + [dma((m,))] * 4,
         compiler_params=params(5), name="input",
-    )(grad_qkv, w_qkv, tokens, grad_resid, gain_one, attn_in, attn_cot, mixture)
+    )(grad_qkv, w_qkv, tokens, grad_resid, gain_one, vec_two, grad_up_b, attn_in, attn_cot, mixture)
     grad_down_w, grad_out_w = grad_down_w.T, grad_out_w.T
 
-    vectors = jnp.stack([
-        vec_one[0], vec_one[1], vec_two[2], vec_two[0], vec_two[1], vec_two[3],
-    ])
-    vectors = vectors.reshape(6, total, piece).transpose(1, 0, 2).reshape(total, 6 * piece)
-    local = jnp.concatenate([
-        grad_qv_b[:2].reshape(2, m, qv_piece).transpose(1, 0, 2).reshape(m, -1),
-        grad_up_b[0].reshape(m, -1)], axis=1)
-    local = jnp.broadcast_to(local[:, None], (m, n, local.shape[1])).reshape(total, -1)
-    load = jnp.concatenate([vectors, local], axis=1)
-    load = jnp.pad(load, ((0, 0), (0, -load.shape[1] % 1024))).reshape(total, -1, LANES)
-    everyone, column = pl.pallas_call(
-        functools.partial(share_kernel, n, m),
-        out_shape=(shape(load.shape[1:], F32),) * 2, in_specs=[VM], out_specs=(VM, VM),
-        scratch_shapes=[pltpu.VMEM(load.shape, F32), dma((total,)), dma((total,))],
-        compiler_params=params(3), name="share",
-    )(load)
-    vectors = everyone.reshape(-1)[: 6 * piece].reshape(6, piece)
-    local = column.reshape(-1)[6 * piece :]
-    grad_qv_b = local[: 2 * qv_piece].reshape(2, qv_piece)
-    grad_up_b = local[2 * qv_piece : 2 * qv_piece + up_piece]
+    def own_lanes(block, index, count):
+        return lax.dynamic_slice_in_dim(block, index * count % block.shape[1], count, axis=1)
+
+    early, late = own_lanes(early, me, piece), own_lanes(late, me, piece)
+    vectors = [late[0], late[1], early[2], early[0], early[1], early[3]]
+    grad_qv_b = own_lanes(grad_qv_b, row, qv_piece)[:2]
+    grad_up_b = own_lanes(grad_up_b, row, up_piece)[0]
     return (layer_out, grad_tokens, vectors[0], vectors[1], grad_qkv_w, grad_qv_b, grad_out_w, vectors[2],
             vectors[3], vectors[4], grad_up_w, grad_up_b, grad_down_w, vectors[5])
 

time: 593 us -> 568 us (0.958)
  Pallas kernels: 546 us -> 531 us
  matrix products: 6.2 us -> 0 us
    pallas_call x3 -> x1, Pallas kernels: 113 us -> 90.3 us  [body(): pl.pallas_call(functools.partial(input_kernel, n, m, pieces, (piece, up_p...]
    pallas_call x1, Pallas kernels: 108 us -> 117 us  [body(): pl.pallas_call(functools.partial(branch_kernel, n, m, pieces), out_shape=...]
    dot_general x1 -> x0, matrix products: 6.2 us -> none  [body(): jnp.einsum('rd,ed->re', attn_cot, w_out, preferred_element_type=F32)]
  transfers between devices with their start and end apart: 4 -> 4, of which waited for: 1 -> 1; matrix products, arithmetic and copies ran while one was open for 1% -> 1% of each run, Pallas kernels for 32% -> 33%
where the time goes in v5:
time: 568 us
  Pallas kernels  531 us (93%)
  local copies, waits for them, and re-layouts  16.1 us (3%)
  between operations  14 us (2%)
    pallas_call x1, Pallas kernels, body(): pl.pallas_call(functools.partial(hidden_kernel, n, pieces), out_shape=(sh...  137 us
    pallas_call x1, Pallas kernels, body(): pl.pallas_call(functools.partial(branch_kernel, n, m, pieces), out_shape=...  117 us
    pallas_call x1, Pallas kernels, body(): pl.pallas_call(functools.partial(attend_kernel, n, pieces), out_shape=(sh...  99.3 us
    pallas_call x1, Pallas kernels, body(): pl.pallas_call(functools.partial(input_kernel, n, m, pieces, (piece, up_p...  90.3 us
    pallas_call x1, Pallas kernels, body(): pl.pallas_call(functools.partial(tokens_kernel, n, m, piece), out_shape=(...  87.2 us
  transfers between devices with their start and end apart: 4, of which 1 were waited for; matrix products, arithmetic and copies ran while one was open for 1% of the time, Pallas kernels for 33%

profile of v5, /device:TPU:0, one launch (start us, length us, event | category | flops | bytes accessed | tf_op | source)
XLA Modules:
  0.0 567.8 jit_solution(14361898963285436342)
XLA Ops:
  7.2 0.0 copy-start.11
  7.2 0.0 copy-start.10
  7.2 0.0 copy-start.9
  7.2 0.0 copy-start.8
  7.2 0.0 copy-start.7
  7.2 0.0 copy-start.6
  7.2 0.0 copy-start.5
  7.3 0.0 copy-start.4
  7.3 0.0 all-gather.7.cloned.1.call-start
  7.3 0.7 all-gather.7.cloned.1.call-update
  8.0 0.0 all-gather.5.cloned.1.call-start
  8.0 0.7 all-gather.5.cloned.1.call-update
  8.7 0.0 all-gather.9.cloned.1.call-start
  8.8 0.7 all-gather.9.cloned.1.call-update
  9.5 0.0 all-gather.11.cloned.1.call-start
  9.5 0.5 all-gather.11.cloned.1.call-update
  10.1 0.0 copy-done.11
  10.1 0.1 tile.21
  10.2 0.0 copy-done.10
  10.2 0.0 copy-done.9
  10.2 0.0 copy-done.8
  10.3 0.1 tile.9
  10.4 0.6 fusion.4.pack_ref
  11.0 87.2 %gather_tokens.1 = (bf16[1024,2048]{1,0:T(8,128)(2,1)}, bf16[32,16,128]{2,1,0:T(8,128)(2,1)}) custom-call(bf16[16,128]{1,0:T(8,128)(2,1)} %fusion.4.pack_ref, bf16[256,2048]{1,0:T(8,128)(2,1)} %x_ref.5), custom_call_target="tpu_custom_call" | custom-call | tf_op jit(solution)/shard_map/gather_tokens/pallas_call | solution.py:930
  98.3 0.9 convert_element_type.9
  99.2 0.6 slice.74
  99.8 0.6 bitcast_reduce_fusion.1
  100.4 0.6 slice_bitcast_fusion
  101.1 99.3 %attend.1 = (bf16[3,1024,512]{2,1,0:T(8,128)(2,1)}, bf16[1024,512]{1,0:T(8,128)(2,1)}, f32[256,2048]{1,0:T(8,128)}, bf16[256,2048]{1,0:T(8,128)(2,1)}, bf16[4,256,2048]{2,1,0:T(8,128)(2,1)}) custom-call(bf16[1024,2048]{1,0:T(8,128)(2,1)} %get-tuple-element.41.a_hbm, bf16[3,2048,512]{2,1,0:T(8,128)(2,1)} %all-gather.5.cloned.1.call-done.wq_hbm, ...), custom_call_target="tpu_custom_call" | custom-call | tf_op jit(solution)/shard_map/attend/pallas_call | solution.py:953
  200.4 0.0 all-gather.9.cloned.1.call-done.up_hbm
  200.4 2.0 all-gather.11.cloned.1.call-done.down_hbm
  202.4 137.3 %hidden.1 = (bf16[4,256,2048]{2,1,0:T(8,128)(2,1)}, bf16[4,256,2048]{2,1,0:T(8,128)(2,1)}, bf16[4,256,2048]{2,1,0:T(8,128)(2,1)}, bf16[4,256,2048]{2,1,0:T(8,128...) custom-call(bf16[256,2048]{1,0:T(8,128)(2,1)} %get-tuple-element.43.c_ref, ...), custom_call_target="tpu_custom_call" | custom-call | tf_op jit(solution)/shard_map/hidden/pallas_call | solution.py:964
  339.7 116.6 %branch.1 = (bf16[4,256,2048]{2,1,0:T(8,128)(2,1)}, bf16[256,2048]{1,0:T(8,128)(2,1)}, f32[256,2048]{1,0:T(8,128)}, f32[256,2048]{1,0:T(8,128)}, bf16[3,1024,512]{2,1,0:T(8,128)(2,1)}) custom-call(bf16[256,2048]{1,0:T(8,128)(2,1)} %get-tuple-element.46.db_ref, f32[256,2048]{1,0:T(8,128)} %get-tuple-element.44.h_ref, f32[1,2048]{1,0:T(1,128)} %get-tuple-element.97.down_bias, ...), custom_call_target="tpu_custom_call" | custom-call | tf_op jit(solution)/shard_map/branch/pallas_call | solution.py:986
  456.3 90.3 %input.1 = (bf16[256,2048]{1,0:T(8,128)(2,1)}, f32[3,256,512]{2,1,0:T(8,128)}, f32[256,512]{1,0:T(8,128)}, f32[8,128]{1,0:T(8,128)}, f32[8,128]{1,0:T(8,128)}, /*index=5*/f32[8,256]{1,0:T(8,128)}, f32[8,128]{1,0:T(8,128)}) custom-call(bf16[3,1024,512]{2,1,0:T(8,128)(2,1)} %get-tuple-element.53.dqkv_ref, ...), custom_call_target="tpu_custom_call" | custom-call | tf_op jit(solution)/shard_map/input/pallas_call | solution.py:1002
  546.6 1.3 slice.67
  548.0 0.8 constant_dynamic-slice_fusion.1
  548.7 0.6 slice.63
  549.3 0.7 constant_dynamic-slice_fusion.2
  550.1 0.5 slice_bitcast_fusion.9
  550.6 0.7 constant_dynamic-slice_fusion
  551.3 0.5 slice_bitcast_fusion.5
  551.8 2.0 copy.30
  553.9 3.0 copy.31
  556.9 1.0 copy.36
  557.8 1.0 copy.37
  558.8 1.1 copy.38
  559.9 0.0 copy-done
  560.0 1.3 copy.39
  (21 shorter events, 0.1 us)
Async XLA Ops:
  7.2 2.9 copy-start.11
  7.2 3.0 copy-start.10
  7.2 3.0 copy-start.9
  7.2 3.0 copy-start.8
  7.2 3.0 copy-start.7
  7.2 3.0 copy-start.6
  7.2 3.0 copy-start.5
  7.3 3.1 copy-start.4
  7.3 93.8 %all-gather.7.cloned.1.call-start = ((), (), s32[]{:S(2)}) async-start(), calls=%async_computation.1 | async-start | bytes 2359296 | tf_op jit(solution)/shard_map/all_gather | solution.py:925
  8.0 93.1 %all-gather.5.cloned.1.call-start = ((), (), s32[]{:S(2)}) async-start(), calls=%async_computation | async-start | bytes 7077888 | tf_op jit(solution)/shard_map/all_gather | solution.py:924
  8.7 191.7 %all-gather.9.cloned.1.call-start = ((), (), s32[]{:S(2)}) async-start(), calls=%async_computation.2 | async-start | bytes 9437184 | tf_op jit(solution)/shard_map/all_gather | solution.py:926
  9.5 192.9 %all-gather.11.cloned.1.call-start = ((), (), s32[]{:S(2)}) async-start(), calls=%async_computation.3 | async-start | bytes 9437184 | tf_op jit(solution)/shard_map/all_gather | solution.py:927
  546.6 10.2 %copy-start.2 = (bf16[256,2048]{1,0:T(8,128)(2,1)S(1)}, bf16[256,2048]{1,0:T(8,128)(2,1)}, u32[]{:S(2)}) copy-start(bf16[256,2048]{1,0:T(8,128)(2,1)} %get-tuple-element.123) | copy-start | bytes 3145732
  553.9 3.9 copy-start.3
  556.9 2.0 copy-start.1
  557.8 2.1 copy-start
Sparse Core Ops, SparseCore 0:
  9.9 31.0 all-gather.6
  42.9 45.4 all-gather.4
  90.3 54.3 all-gather.8
  146.4 55.9 all-gather.10

commit v6 on v5

--- a/solution.py
+++ b/solution.py
@@ -98,53 +98,58 @@
 
 
 class LineGather:
+    PIECES = 2
+
     def __init__(self, i, n, own, buf, send, recv):
         self.i, self.n, self.own, self.buf, self.send, self.recv = i, n, own, buf, send, recv
-
-    def copy(self, src, j, side, target):
-        return remote(src, self.buf.at[j], self.send.at[side, j], self.recv.at[j], target)
+        self.size = own.shape[0] // self.PIECES
+
+    def copy(self, src, j, side, s, target):
+        here = pl.ds(s * self.size, self.size)
+        return remote(src.at[here], self.buf.at[j, here], self.send.at[side, j, s], self.recv.at[j, s], target)
 
     def start(self):
         i, n = self.i, self.n
-
-        @pl.when(i < n - 1)
-        def _():
-            self.copy(self.own, i, 0, i + 1).start()
-
-        @pl.when(i > 0)
-        def _():
-            self.copy(self.own, i, 1, i - 1).start()
+        for s in range(self.PIECES):
+            @pl.when(i < n - 1)
+            def _():
+                self.copy(self.own, i, 0, s, i + 1).start()
+
+            @pl.when(i > 0)
+            def _():
+                self.copy(self.own, i, 1, s, i - 1).start()
 
     def step(self, r):
         i, n = self.i, self.n
-
-        @pl.when(i - r >= 0)
-        def _():
-            self.copy(self.own, i - r, 0, i).wait_recv()
-
-            @pl.when(i < n - 1)
-            def _():
-                self.copy(self.buf.at[i - r], i - r, 0, i + 1).start()
-
-        @pl.when(i + r <= n - 1)
-        def _():
-            self.copy(self.own, i + r, 1, i).wait_recv()
-
-            @pl.when(i > 0)
-            def _():
-                self.copy(self.buf.at[i + r], i + r, 1, i - 1).start()
+        for s in range(self.PIECES):
+            @pl.when(i - r >= 0)
+            def _():
+                self.copy(self.own, i - r, 0, s, i).wait_recv()
+
+                @pl.when(i < n - 1)
+                def _():
+                    self.copy(self.buf.at[i - r], i - r, 0, s, i + 1).start()
+
+            @pl.when(i + r <= n - 1)
+            def _():
+                self.copy(self.own, i + r, 1, s, i).wait_recv()
+
+                @pl.when(i > 0)
+                def _():
+                    self.copy(self.buf.at[i + r], i + r, 1, s, i - 1).start()
 
     def finish(self):
         i, n = self.i, self.n
 
         def one(j):
-            @pl.when(jnp.logical_and(i < n - 1, j <= i))
-            def _():
-                self.copy(self.own, j, 0, i + 1).wait_send()
-
-            @pl.when(jnp.logical_and(i > 0, j >= i))
-            def _():
-                self.copy(self.own, j, 1, i - 1).wait_send()
+            for s in range(self.PIECES):
+                @pl.when(jnp.logical_and(i < n - 1, j <= i))
+                def _():
+                    self.copy(self.own, j, 0, s, i + 1).wait_send()
+
+                @pl.when(jnp.logical_and(i > 0, j >= i))
+                def _():
+                    self.copy(self.own, j, 1, s, i - 1).wait_send()
 
         loop(n, one)
 
@@ -178,26 +183,42 @@
         def _():
             loop(self.pieces, lambda s: self.copy(self.part, d, False, s).start())
 
-    def relay(self, d, right):
-        def one(s):
+    def relay(self, right, left):
+        i, n = self.i, self.n
+
+        def move(d, to_right, s):
             self.arrived(d, s)
             here = rows_at(s, self.size)
             total = self.land[d, here, :].astype(F32) + self.part[d, here, :].astype(F32)
             self.land[d, here, :] = total.astype(BF)
-            self.copy(self.land, d, right, s).start()
+            self.copy(self.land, d, to_right, s).start()
+
+        def one(s):
+            @pl.when(jnp.logical_and(i > 0, jnp.logical_and(right > i, right <= n - 1)))
+            def _():
+                move(right, True, s)
+
+            @pl.when(jnp.logical_and(i < n - 1, jnp.logical_and(left >= 0, left < i)))
+            def _():
+                move(left, False, s)
 
         loop(self.pieces, one)
 
-    def own(self):
+    def own(self, step):
         i, n = self.i, self.n
 
-        @pl.when(i > 0)
-        def _():
-            loop(self.pieces, lambda s: self.arrived(i, s))
-
-        @pl.when(i < n - 1)
-        def _():
-            loop(self.pieces, lambda s: self.arrived(n, s))
+        def one(s):
+            @pl.when(i > 0)
+            def _():
+                self.arrived(i, s)
+
+            @pl.when(i < n - 1)
+            def _():
+                self.arrived(n, s)
+
+            loop(self.size // RB, lambda b: step(s * (self.size // RB) + b))
+
+        loop(self.pieces, one)
 
     def add(self, here, out):
         i, n = self.i, self.n
@@ -226,7 +247,7 @@
         loop(n, one)
 
 
-def tokens_kernel(n, m, piece, pack_ref, x_ref, a_ref, vec_ref, buf, affine, own_sem, send, recv, v_send, v_recv):
+def tokens_kernel(n, m, piece, pack_ref, x_ref, a_ref, n_ref, vec_ref, buf, affine, own_sem, send, recv, v_send, v_recv):
     i, row = lax.axis_index("tensor"), lax.axis_index("dp")
     me, total = row * n + i, m * n
     size = x_ref.shape[0]
@@ -257,6 +278,7 @@
         def norm(b):
             normal, _ = norm_stats(buf[j, rows_at(b, RB), :].astype(F32))
             here = pl.ds(pl.multiple_of(j * size + b * RB, RB), RB)
+            n_ref[here, :] = normal.astype(BF)
             a_ref[here, :] = (normal * affine[0:1, :] + affine[1:2, :]).astype(BF)
 
         loop(size // RB, norm)
@@ -328,18 +350,9 @@
 
     def round_of(r):
         line.step(r + 1)
-        right, left = n - 1 + i - (r + 1), r + 1 - (n - 1 - i)
-
-        @pl.when(jnp.logical_and(i > 0, jnp.logical_and(right > i, right <= n - 1)))
-        def _():
-            sums.relay(right, True)
-
-        @pl.when(jnp.logical_and(i < n - 1, jnp.logical_and(left >= 0, left < i)))
-        def _():
-            sums.relay(left, False)
+        relays(sums, i, n, r + 1)
 
     loop(n - 1, round_of)
-    sums.own()
 
     def norm(b):
         here = rows_at(b, RB)
@@ -349,7 +362,7 @@
         normal, _ = norm_stats(rows)
         c_ref[here, :] = (normal * gain[...] + shift[...]).astype(BF)
 
-    loop(size // RB, norm)
+    sums.own(norm)
     own_copy.wait()
     line.finish()
     sums.finish()
@@ -421,18 +434,10 @@
     loop(n, forward)
 
     def relay(t):
-        right, left = t + 2 - i, 2 * n - 4 - i - t
-
-        @pl.when(jnp.logical_and(i > 0, jnp.logical_and(right > i, right <= n - 1)))
-        def _():
-            sums.relay(right, True)
-
-        @pl.when(jnp.logical_and(i < n - 1, jnp.logical_and(left >= 0, left < i)))
-        def _():
-            sums.relay(left, False)
+        early = jnp.where(i < n // 2, 1, 0)
+        sums.relay(t + 3 - early - i, 2 * n - 4 - i - t - early)
 
     loop(2 * n - 3, relay)
-    sums.own()
 
     def norm(b):
         here = rows_at(b, RB)
@@ -449,7 +454,7 @@
         vec_ref[2:3, :] += jnp.sum(db.astype(F32), axis=0, keepdims=True)
         vec_ref[3:4, :] += jnp.sum(cot, axis=0, keepdims=True)
 
-    loop(size // RB, norm)
+    sums.own(norm)
 
     def done(j):
         out_copy(g_all, g_hbm, g_sem, j).wait()
@@ -618,15 +623,7 @@
 
 
 def relays(sums, i, n, r):
-    right, left = n - 1 + i - r, r - (n - 1 - i)
-
-    @pl.when(jnp.logical_and(i > 0, jnp.logical_and(right > i, right <= n - 1)))
-    def _():
-        sums.relay(right, True)
-
-    @pl.when(jnp.logical_and(i < n - 1, jnp.logical_and(left >= 0, left < i)))
-    def _():
-        sums.relay(left, False)
+    sums.relay(n - 1 + i - r, r - (n - 1 - i))
 
 
 def block_terms(plane, e, pairs):
@@ -693,11 +690,7 @@
         block_terms(second, e, [(left, right, 0)])
         second.whole(e).start()
 
-    def line_round(r):
-        line.step(r)
-        relays(sums, i, n, r)
-
-    line_round(1)
+    line.step(1)
     for e in range(m - 2, -1, -2):
         block_terms(second, e, [(left, right, 0)])
     qkv_copies = [pltpu.make_async_copy(qkv_hbm.at[p], rhs.at[:, p * width : (p + 1) * width], qkv_sem.at[p])
@@ -743,16 +736,15 @@
     mixture_back(i)
     round_back(1)
     advance(first, 0, down_ref)
-    line_round(2)
-    round_back(2)
-    advance(second, 0, up_ref)
-
-    def rest(r):
-        line_round(r)
+    for r in range(2, n):
+        line.step(r)
+        relays(sums, i, n, r - 1)
         round_back(r)
-
-    for r in range(3, n):
-        rest(r)
+        if r == 2:
+            advance(second, 0, up_ref)
+    if n == 2:
+        advance(second, 0, up_ref)
+    relays(sums, i, n, n - 1)
     for copy in qkv_copies:
         copy.wait()
 
@@ -769,14 +761,13 @@
     for stage in range(1, first.stages):
         advance(first, stage, down_ref)
         advance(second, stage, up_ref)
-    sums.own()
 
     def output(b):
         here = rows_at(b, RB)
         sums.add(here, acc)
         lo_ref[here, :] = (h_ref[here, :] + (acc[...] + down_bias[...])).astype(BF)
 
-    loop(size // RB, output)
+    sums.own(output)
     line.finish()
     sums.finish()
     second.sent()
@@ -785,8 +776,8 @@
 
 
 def input_kernel(n, m, pieces, widths, dqkv_ref, wq_hbm, x_ref, dh_ref, gain, early_ref, up_ref, a_hbm, db_hbm, o_hbm,
-                 gt_ref, gqkv_ref, gout_ref, early_out, late_out, up_out, qv_out, vec_ref, qv_ref, wq, a_ref, db_ref,
-                 o_ref, part, land, out_p, terms, land_p, half_p, acc, early_land, late_land, up_land, qv_land, s_send,
+                 n_hbm, gt_ref, gqkv_ref, gout_ref, early_out, late_out, up_out, qv_out, vec_ref, qv_ref, wq, a_ref, db_ref,
+                 o_ref, n_ref, part, land, out_p, terms, land_p, half_p, acc, early_land, late_land, up_land, qv_land, s_send,
                  s_recv, in_sem, p_send, p_recv, h_send, h_recv, e_send, e_recv, l_send, l_recv, u_send, u_recv, q_send,
                  q_recv):
     i, row = lax.axis_index("tensor"), lax.axis_index("dp")
@@ -796,7 +787,8 @@
     piece, up_piece, qv_piece = widths
     depth = part.shape[2]
     loads = [pltpu.make_async_copy(wq_hbm, wq, in_sem.at[0]), pltpu.make_async_copy(a_hbm, a_ref, in_sem.at[1]),
-             pltpu.make_async_copy(db_hbm, db_ref, in_sem.at[2]), pltpu.make_async_copy(o_hbm, o_ref, in_sem.at[3])]
+             pltpu.make_async_copy(db_hbm, db_ref, in_sem.at[2]), pltpu.make_async_copy(o_hbm, o_ref, in_sem.at[3]),
+             pltpu.make_async_copy(n_hbm, n_ref, in_sem.at[4])]
     for copy in loads:
         copy.start()
     greet_all(me, n, total_devices)
@@ -812,6 +804,7 @@
     vec_ref[...] = jnp.zeros_like(vec_ref)
     qv_ref[...] = jnp.zeros_like(qv_ref)
     loads[0].wait()
+    loads[4].wait()
     tile = 512
 
     def term(t):
@@ -824,6 +817,8 @@
             for p in range(1, 3):
                 total += lax.dot_general(dqkv_ref[p, here, :], wq[p, cols, :], NT, preferred_element_type=F32)
             part[d, :, cols] = total.astype(BF)
+            vec_ref[0:1, cols] += jnp.sum(total * n_ref[here, cols].astype(F32), axis=0, keepdims=True)
+            vec_ref[1:2, cols] += jnp.sum(total, axis=0, keepdims=True)
 
         loop(depth // tile, columns)
         sums.launch(d)
@@ -832,7 +827,8 @@
 
     loop(n, term)
     column[1].start()
-    for copy in loads[1:]:
+    every[1].start()
+    for copy in loads[1:4]:
         copy.wait()
     plane = PlaneSum(row, m, out_p, terms, land_p, half_p, p_send, p_recv, h_send, h_recv)
     pairs = [(a_ref, dqkv_ref.at[p], p * width) for p in range(3)] + [(db_ref, o_ref, 3 * width)]
@@ -859,19 +855,14 @@
             else:
                 plane.take(stage, out)
             stage += 1
-    sums.own()
 
     def norm(b):
         here = rows_at(b, RB)
         sums.add(here, acc)
         grad = acc[...]
         normal, inverse = norm_stats(x_ref[here, :].astype(F32))
-        vec_ref[0:1, :] += jnp.sum(grad * normal, axis=0, keepdims=True)
-        vec_ref[1:2, :] += jnp.sum(grad, axis=0, keepdims=True)
         gt_ref[here, :] = (dh_ref[here, :] + norm_back(grad, normal, inverse, gain[...])).astype(BF)
 
-    loop(size // RB, norm)
-    every[1].start()
     while stage < plane.stages:
         if stage < plane.stages - 1:
             plane.take(stage)
@@ -879,11 +870,12 @@
         else:
             plane.take(stage, out)
         stage += 1
+    for group in (every[0], column[0], column[1], every[1]):
+        group.finish()
+    sums.own(norm)
     sums.finish()
     plane.sent()
     plane.finish()
-    for group in (every[0], column[0], column[1], every[1]):
-        group.finish()
 
 
 def params(collective=None):
@@ -927,11 +919,11 @@
     w_down = lax.all_gather(down_weight, "dp", axis=1, tiled=True)
 
     dma = pltpu.SemaphoreType.DMA
-    attn_in, vecs = pl.pallas_call(
+    attn_in, normal_one, vecs = pl.pallas_call(
         functools.partial(tokens_kernel, n, m, piece),
-        out_shape=(shape((LEN, depth), BF), shape((total,) + pack.shape, BF)),
-        in_specs=[VM, VM], out_specs=(VM, VM),
-        scratch_shapes=[pltpu.VMEM((n, size, depth), BF), pltpu.VMEM((8, depth), F32), dma, dma((2, n)), dma((n,)),
+        out_shape=(shape((LEN, depth), BF), shape((LEN, depth), BF), shape((total,) + pack.shape, BF)),
+        in_specs=[VM, VM], out_specs=(VM, VM, VM),
+        scratch_shapes=[pltpu.VMEM((n, size, depth), BF), pltpu.VMEM((8, depth), F32), dma, dma((2, n, LineGather.PIECES)), dma((n, LineGather.PIECES)),
                         dma((total,)), dma((total,))],
         compiler_params=params(0), name="gather_tokens",
     )(pack, tokens)
@@ -956,7 +948,7 @@
                    shape((size, depth), BF), shape((n, size, depth), BF)),
         in_specs=[ANY] * 3 + [VM] * 6, out_specs=(VM, VM, VM, VM, ANY),
         scratch_shapes=[pltpu.VMEM((LEN, depth), BF), pltpu.VMEM((3, depth, width), BF), pltpu.VMEM((width, depth), BF)] +
-                       sums + [dma((2, n)), dma((n,)), dma((n, pieces)), dma((n + 1, pieces)), dma, dma, dma((4,))],
+                       sums + [dma((2, n, LineGather.PIECES)), dma((n, LineGather.PIECES)), dma((n, pieces)), dma((n + 1, pieces)), dma, dma, dma((4,))],
         compiler_params=params(1), name="attend",
     )(attn_in, w_qkv, w_out, tokens, cotangent, bias_qv, bias_out, gain_two, shift_two)
 
@@ -970,7 +962,7 @@
         scratch_shapes=[pltpu.VMEM((n, size, depth), BF), pltpu.VMEM((n, size, units), BF),
                         pltpu.VMEM((n, size, units), BF), pltpu.VMEM((n, size, depth), BF),
                         pltpu.VMEM((depth, units), BF), pltpu.VMEM((units, depth), BF)] + sums +
-                       [dma((2, n)), dma((n,)), dma((n, pieces)), dma((n + 1, pieces)), dma((2,)), dma, dma,
+                       [dma((2, n, LineGather.PIECES)), dma((n, LineGather.PIECES)), dma((n, pieces)), dma((n + 1, pieces)), dma((2,)), dma, dma,
                         dma((n,)), dma((n,)), dma((n,)), pltpu.VMEM((n, size, depth), BF), dma((n,))],
         compiler_params=params(2), name="hidden",
     )(mlp_own, residual, cot_all, w_up, w_down, bias_up, gain_two)
@@ -991,7 +983,7 @@
         scratch_shapes=[pltpu.VMEM((LEN, depth), BF), pltpu.VMEM((LEN, units), BF), pltpu.VMEM((width, depth), BF),
                         pltpu.VMEM((LEN, HD), F32), pltpu.VMEM((LEN, HD), F32)] + sums +
                        [pltpu.VMEM((m // 2, depth // m, units), BF)] + plane_scratch(units) * 2 +
-                       [pltpu.VMEM((RB, depth), F32), dma((2, n)), dma((n,))] + sum_sems +
+                       [pltpu.VMEM((RB, depth), F32), dma((2, n, LineGather.PIECES)), dma((n, LineGather.PIECES))] + sum_sems +
                        [dma, dma, dma((3,)), dma((3,)), dma((n,)), dma((2, m // 2)), dma((2, m // 2)),
                         dma((2, 2, m // 2 - 1)), dma((2, 2, m // 2 - 1))],
         compiler_params=params(4), name="branch",
@@ -1004,18 +996,19 @@
         out_shape=(shape((size, depth), BF), shape((3, depth // m, width), F32), shape((depth // m, width), F32),
                    shape((8, tiles[0]), F32), shape((8, tiles[0]), F32), shape((8, tiles[1]), F32),
                    shape((8, tiles[2]), F32)),
-        in_specs=[VM, ANY, VM, VM, VM, VM, VM, ANY, ANY, ANY], out_specs=(VM,) * 7,
+        in_specs=[VM, ANY, VM, VM, VM, VM, VM, ANY, ANY, ANY, ANY], out_specs=(VM,) * 7,
         scratch_shapes=[pltpu.VMEM((8, depth), F32), pltpu.VMEM((8, width), F32),
                         pltpu.VMEM((3, depth, width), BF), pltpu.VMEM((LEN, depth), BF), pltpu.VMEM((LEN, depth), BF),
-                        pltpu.VMEM((LEN, width), BF)] + sums + [pltpu.VMEM((m // 2, depth // m, 4 * width), BF)] +
+                        pltpu.VMEM((LEN, width), BF), pltpu.VMEM((LEN, depth), BF)] + sums +
+                       [pltpu.VMEM((m // 2, depth // m, 4 * width), BF)] +
                        plane_scratch(4 * width) +
                        [pltpu.VMEM((RB, depth), F32), pltpu.VMEM((total, 8, tiles[0]), F32),
                         pltpu.VMEM((total, 8, tiles[0]), F32), pltpu.VMEM((m, 8, tiles[1]), F32),
                         pltpu.VMEM((m, 8, tiles[2]), F32)] + sum_sems +
-                       [dma((4,)), dma((m // 2,)), dma((m // 2,)), dma((2, m // 2 - 1)), dma((2, m // 2 - 1))] +
+                       [dma((5,)), dma((m // 2,)), dma((m // 2,)), dma((2, m // 2 - 1)), dma((2, m // 2 - 1))] +
                        [dma((total,))] * 4 + [dma((m,))] * 4,
         compiler_params=params(5), name="input",
-    )(grad_qkv, w_qkv, tokens, grad_resid, gain_one, vec_two, grad_up_b, attn_in, attn_cot, mixture)
+    )(grad_qkv, w_qkv, tokens, grad_resid, gain_one, vec_two, grad_up_b, attn_in, attn_cot, mixture, normal_one)
     grad_down_w, grad_out_w = grad_down_w.T, grad_out_w.T
 
     def own_lanes(block, index, count):

time: 568 us -> 577 us (1.016)
  Pallas kernels: 531 us -> 537 us
    pallas_call x1, Pallas kernels: 137 us -> 155 us  [body(): pl.pallas_call(functools.partial(hidden_kernel, n, pieces), out_shape=(sh...]
    pallas_call x1, Pallas kernels: 117 us -> 107 us  [body(): pl.pallas_call(functools.partial(branch_kernel, n, m, pieces), out_shape=...]
  transfers between devices with their start and end apart: 4 -> 4, of which waited for: 1 -> 1; matrix products, arithmetic and copies ran while one was open for 1% -> 1% of each run, Pallas kernels for 33% -> 32%
where the time goes in v6:
time: 577 us; the launch traced here: 576 us
  Pallas kernels  537 us (93%)
  local copies, waits for them, and re-layouts  18.9 us (3%)
  between operations  13.9 us (2%)
    pallas_call x1, Pallas kernels, body(): pl.pallas_call(functools.partial(hidden_kernel, n, pieces), out_shape=(sh...  155 us
    pallas_call x1, Pallas kernels, body(): pl.pallas_call(functools.partial(branch_kernel, n, m, pieces), out_shape=...  107 us
    pallas_call x1, Pallas kernels, body(): pl.pallas_call(functools.partial(attend_kernel, n, pieces), out_shape=(sh...  100 us
    pallas_call x1, Pallas kernels, body(): pl.pallas_call(functools.partial(input_kernel, n, m, pieces, (piece, up_p...  89.6 us
    pallas_call x1, Pallas kernels, body(): pl.pallas_call(functools.partial(tokens_kernel, n, m, piece), out_shape=(...  85.8 us
  transfers between devices with their start and end apart: 4, of which 1 were waited for; matrix products, arithmetic and copies ran while one was open for 1% of the time, Pallas kernels for 32%

profile of v6, /device:TPU:0, one launch (start us, length us, event | category | flops | bytes accessed | tf_op | source)
XLA Modules:
  0.0 576.4 jit_solution(13610124274332694749)
XLA Ops:
  7.2 0.0 all-gather.7.cloned.1.call-start
  7.2 0.7 all-gather.7.cloned.1.call-update
  7.9 0.0 all-gather.5.cloned.1.call-start
  8.0 0.7 all-gather.5.cloned.1.call-update
  8.7 0.0 all-gather.9.cloned.1.call-start
  8.7 0.7 all-gather.9.cloned.1.call-update
  9.4 0.0 all-gather.11.cloned.1.call-start
  9.4 0.5 all-gather.11.cloned.1.call-update
  10.0 0.7 tile.20
  10.7 0.1 tile.21
  10.8 0.8 stack.27
  11.5 0.1 tile.9
  11.6 1.3 fusion.4.pack_ref
  12.9 85.8 %gather_tokens.1 = (bf16[1024,2048]{1,0:T(8,128)(2,1)}, bf16[1024,2048]{1,0:T(8,128)(2,1)}, bf16[32,16,128]{2,1,0:T(8,128)(2,1)}) custom-call(bf16[16,128]{1,0:T(8,128)(2,1)} %fusion.4.pack_ref, bf16[256,2048]{1,0:T(8,128)(2,1)} %x_ref.5), custom_call_target="tpu_custom_call" | custom-call | tf_op jit(solution)/shard_map/gather_tokens/pallas_call | solution.py:922
  98.7 0.9 convert_element_type.9
  99.7 0.6 slice.74
  100.3 0.6 bitcast_reduce_fusion.1
  100.9 0.6 slice_bitcast_fusion
  101.6 0.0 all-gather.7.cloned.1.call-done.wo_hbm
  101.6 0.0 all-gather.5.cloned.1.call-done.wq_hbm
  101.6 100.2 %attend.1 = (bf16[3,1024,512]{2,1,0:T(8,128)(2,1)}, bf16[1024,512]{1,0:T(8,128)(2,1)}, f32[256,2048]{1,0:T(8,128)}, bf16[256,2048]{1,0:T(8,128)(2,1)}, bf16[4,256,2048]{2,1,0:T(8,128)(2,1)}) custom-call(bf16[1024,2048]{1,0:T(8,128)(2,1)} %get-tuple-element.42.a_hbm, bf16[3,2048,512]{2,1,0:T(8,128)(2,1)} %all-gather.5.cloned.1.call-done.wq_hbm, ...), custom_call_target="tpu_custom_call" | custom-call | tf_op jit(solution)/shard_map/attend/pallas_call | solution.py:945
  201.8 0.0 all-gather.9.cloned.1.call-done.up_hbm
  201.8 0.8 all-gather.11.cloned.1.call-done.down_hbm
  202.6 154.7 %hidden.1 = (bf16[4,256,2048]{2,1,0:T(8,128)(2,1)}, bf16[4,256,2048]{2,1,0:T(8,128)(2,1)}, bf16[4,256,2048]{2,1,0:T(8,128)(2,1)}, bf16[4,256,2048]{2,1,0:T(8,128...) custom-call(bf16[256,2048]{1,0:T(8,128)(2,1)} %get-tuple-element.44.c_ref, ...), custom_call_target="tpu_custom_call" | custom-call | tf_op jit(solution)/shard_map/hidden/pallas_call | solution.py:956
  357.4 106.9 %branch.1 = (bf16[4,256,2048]{2,1,0:T(8,128)(2,1)}, bf16[256,2048]{1,0:T(8,128)(2,1)}, f32[256,2048]{1,0:T(8,128)}, f32[256,2048]{1,0:T(8,128)}, bf16[3,1024,512]{2,1,0:T(8,128)(2,1)}) custom-call(bf16[256,2048]{1,0:T(8,128)(2,1)} %get-tuple-element.47.db_ref, f32[256,2048]{1,0:T(8,128)} %get-tuple-element.45.h_ref, f32[1,2048]{1,0:T(1,128)} %get-tuple-element.99.down_bias, ...), custom_call_target="tpu_custom_call" | custom-call | tf_op jit(solution)/shard_map/branch/pallas_call | solution.py:978
  464.3 89.6 %input.1 = (bf16[256,2048]{1,0:T(8,128)(2,1)}, f32[3,256,512]{2,1,0:T(8,128)}, f32[256,512]{1,0:T(8,128)}, f32[8,128]{1,0:T(8,128)}, f32[8,128]{1,0:T(8,128)}, /*index=5*/f32[8,256]{1,0:T(8,128)}, f32[8,128]{1,0:T(8,128)}) custom-call(bf16[3,1024,512]{2,1,0:T(8,128)(2,1)} %get-tuple-element.54.dqkv_ref, ...), custom_call_target="tpu_custom_call" | custom-call | tf_op jit(solution)/shard_map/input/pallas_call | solution.py:994
  553.8 0.0 copy-start.2
  553.9 1.3 slice.67
  555.2 0.7 constant_dynamic-slice_fusion.1
  555.9 0.6 slice.63
  556.5 0.7 constant_dynamic-slice_fusion.2
  557.3 0.5 slice_bitcast_fusion.9
  557.8 0.8 constant_dynamic-slice_fusion
  558.5 0.5 slice_bitcast_fusion.5
  559.1 2.0 copy.30
  561.1 0.0 copy-start.1
  561.1 3.0 copy.31
  564.1 0.0 copy-start
  564.1 0.0 copy-done.2
  564.1 1.0 copy.36
  565.1 2.3 copy.37
  567.4 0.0 copy-done.1
  567.4 1.1 copy.38
  568.6 0.0 copy-done
  568.6 1.3 copy.39
  (6 shorter events, 0.1 us)
Async XLA Ops:
  7.2 94.4 %all-gather.7.cloned.1.call-start = ((), (), s32[]{:S(2)}) async-start(), calls=%async_computation.1 | async-start | bytes 2359296 | tf_op jit(solution)/shard_map/all_gather | solution.py:917
  7.9 93.6 %all-gather.5.cloned.1.call-start = ((), (), s32[]{:S(2)}) async-start(), calls=%async_computation | async-start | bytes 7077888 | tf_op jit(solution)/shard_map/all_gather | solution.py:916
  8.7 193.2 %all-gather.9.cloned.1.call-start = ((), (), s32[]{:S(2)}) async-start(), calls=%async_computation.2 | async-start | bytes 9437184 | tf_op jit(solution)/shard_map/all_gather | solution.py:918
  9.4 193.3 %all-gather.11.cloned.1.call-start = ((), (), s32[]{:S(2)}) async-start(), calls=%async_computation.3 | async-start | bytes 9437184 | tf_op jit(solution)/shard_map/all_gather | solution.py:919
  553.8 10.3 %copy-start.2 = (bf16[256,2048]{1,0:T(8,128)(2,1)S(1)}, bf16[256,2048]{1,0:T(8,128)(2,1)}, u32[]{:S(2)}) copy-start(bf16[256,2048]{1,0:T(8,128)(2,1)} %get-tuple-element.125) | copy-start | bytes 3145732
  561.1 6.3 %copy-start.1 = (f32[3,256,512]{2,1,0:T(8,128)S(1)}, f32[3,256,512]{2,1,0:T(8,128)}, u32[]{:S(2)}) copy-start(f32[3,256,512]{2,1,0:T(8,128)} %get-tuple-element.129) | copy-start | bytes 4718596
  564.1 4.5 copy-start
Sparse Core Ops, SparseCore 0:
  9.9 31.5 all-gather.6
  43.3 45.3 all-gather.4
  90.7 54.2 all-gather.8
  146.7 55.8 all-gather.10

commit v7 on v6

--- a/solution.py
+++ b/solution.py
@@ -193,16 +193,20 @@
             self.land[d, here, :] = total.astype(BF)
             self.copy(self.land, d, to_right, s).start()
 
+        first = jnp.where(i < n // 2, 0, 1)
+
         def one(s):
-            @pl.when(jnp.logical_and(i > 0, jnp.logical_and(right > i, right <= n - 1)))
+            turn, s = (s + first) % 2, s // 2
+
+            @pl.when(jnp.logical_and(turn == 0, jnp.logical_and(i > 0, jnp.logical_and(right > i, right <= n - 1))))
             def _():
                 move(right, True, s)
 
-            @pl.when(jnp.logical_and(i < n - 1, jnp.logical_and(left >= 0, left < i)))
+            @pl.when(jnp.logical_and(turn == 1, jnp.logical_and(i < n - 1, jnp.logical_and(left >= 0, left < i))))
             def _():
                 move(left, False, s)
 
-        loop(self.pieces, one)
+        loop(2 * self.pieces, one)
 
     def own(self, step):
         i, n = self.i, self.n
@@ -247,7 +251,7 @@
         loop(n, one)
 
 
-def tokens_kernel(n, m, piece, pack_ref, x_ref, a_ref, n_ref, vec_ref, buf, affine, own_sem, send, recv, v_send, v_recv):
+def tokens_kernel(n, m, piece, pack_ref, x_ref, a_hbm, n_hbm, vec_ref, buf, affine, a_ref, n_ref, out_sem, own_sem, send, recv, v_send, v_recv):
     i, row = lax.axis_index("tensor"), lax.axis_index("dp")
     me, total = row * n + i, m * n
     size = x_ref.shape[0]
@@ -282,14 +286,26 @@
             a_ref[here, :] = (normal * affine[0:1, :] + affine[1:2, :]).astype(BF)
 
         loop(size // RB, norm)
+        for copy in leave(j):
+            copy.start()
+
+    def leave(j):
+        here = rows_at(j, size)
+        return [pltpu.make_async_copy(a_ref.at[here], a_hbm.at[here], out_sem.at[0, j]),
+                pltpu.make_async_copy(n_ref.at[here], n_hbm.at[here], out_sem.at[1, j])]
+
+    def left(j):
+        for copy in leave(j):
+            copy.wait()
 
     rounds(i, n, line, compute)
     line.finish()
+    loop(n, left)
     loop(total - 1, lambda s: vector(me, (me + s + 1) % total).wait_send())
 
 
-def attend_kernel(n, pieces, a_hbm, wq_hbm, wo_hbm, x_ref, cot_ref, bias, out_bias, gain, shift, qkv_ref, o_ref, h_ref,
-                  c_ref, cot_all, a_ref, wq_ref, w_ref, part, land, send, recv, s_send, s_recv, own_sem, a_sem, w_sem):
+def attend_kernel(n, pieces, a_hbm, wq_hbm, wo_hbm, x_ref, cot_ref, bias, out_bias, gain, shift, qkv_hbm, o_hbm, h_ref,
+                  c_ref, cot_all, qkv_ref, o_ref, out_sem, a_ref, wq_ref, w_ref, part, land, send, recv, s_send, s_recv, own_sem, a_sem, w_sem):
     i = lax.axis_index("tensor")
     size = x_ref.shape[0]
     loads = [pltpu.make_async_copy(a_hbm, a_ref, a_sem)]
@@ -332,6 +348,9 @@
             o_ref[here, cols] = jnp.dot(prob, qkv_ref[2, 0:keys, cols], preferred_element_type=F32).astype(BF)
 
     loop(heads, head)
+    leave = [pltpu.make_async_copy(qkv_ref, qkv_hbm, out_sem.at[0]), pltpu.make_async_copy(o_ref, o_hbm, out_sem.at[1])]
+    for copy in leave:
+        copy.start()
     loads[4].wait()
     sums = LineSum(i, n, part, land, s_send, s_recv, pieces)
     tile = 512
@@ -364,6 +383,8 @@
 
     sums.own(norm)
     own_copy.wait()
+    for copy in leave:
+        copy.wait()
     line.finish()
     sums.finish()
 
@@ -642,7 +663,7 @@
 
 
 def branch_kernel(n, m, pieces, db_ref, h_ref, down_bias, mlp_hbm, g_hbm, cot_hbm, c_hbm, du_hbm, qkv_hbm, wo_hbm,
-                  db_all, lo_ref, down_ref, up_ref, dqkv_ref, lhs, rhs, wo, dk, dv, part, land, out, terms_a, land_a,
+                  db_all, lo_ref, down_ref, up_ref, dqkv_hbm, dqkv_ref, out_sem, lhs, rhs, wo, dk, dv, part, land, out, terms_a, land_a,
                   half_a, terms_b, land_b, half_b, acc, send, recv, s_send, s_recv, own_sem, part_sem, in_sem, qkv_sem,
                   db_sem, p_send, p_recv, h_send, h_recv):
     i, row = lax.axis_index("tensor"), lax.axis_index("dp")
@@ -758,6 +779,8 @@
         dqkv_ref[p, here, pl.ds(pl.multiple_of(t * HD, HD), HD)] = value
 
     attend_back(column(0), column(1), column(2), column(3), width // HD, put, dk, dv)
+    leave = pltpu.make_async_copy(dqkv_ref, dqkv_hbm, out_sem)
+    leave.start()
     for stage in range(1, first.stages):
         advance(first, stage, down_ref)
         advance(second, stage, up_ref)
@@ -773,24 +796,24 @@
     second.sent()
     for plane in planes:
         plane.finish()
-
-
-def input_kernel(n, m, pieces, widths, dqkv_ref, wq_hbm, x_ref, dh_ref, gain, early_ref, up_ref, a_hbm, db_hbm, o_hbm,
+    leave.wait()
+
+
+def input_kernel(n, m, pieces, widths, dqkv_ref, wq_hbm, x_hbm, dh_hbm, gain, early_ref, up_ref, a_hbm, db_hbm, o_hbm,
                  n_hbm, gt_ref, gqkv_ref, gout_ref, early_out, late_out, up_out, qv_out, vec_ref, qv_ref, wq, a_ref, db_ref,
-                 o_ref, n_ref, part, land, out_p, terms, land_p, half_p, acc, early_land, late_land, up_land, qv_land, s_send,
+                 o_ref, n_ref, x_ref, dh_ref, part, land, out_p, terms, land_p, half_p, acc, early_land, late_land, up_land, qv_land, s_send,
                  s_recv, in_sem, p_send, p_recv, h_send, h_recv, e_send, e_recv, l_send, l_recv, u_send, u_recv, q_send,
                  q_recv):
     i, row = lax.axis_index("tensor"), lax.axis_index("dp")
     me, total_devices = row * n + i, m * n
-    size = x_ref.shape[0]
+    size = x_hbm.shape[0]
     width = dqkv_ref.shape[2]
     piece, up_piece, qv_piece = widths
     depth = part.shape[2]
-    loads = [pltpu.make_async_copy(wq_hbm, wq, in_sem.at[0]), pltpu.make_async_copy(a_hbm, a_ref, in_sem.at[1]),
-             pltpu.make_async_copy(db_hbm, db_ref, in_sem.at[2]), pltpu.make_async_copy(o_hbm, o_ref, in_sem.at[3]),
-             pltpu.make_async_copy(n_hbm, n_ref, in_sem.at[4])]
-    for copy in loads:
-        copy.start()
+    loads = [pltpu.make_async_copy(src, dst, in_sem.at[k]) for k, (src, dst) in enumerate(
+        [(wq_hbm, wq), (a_hbm, a_ref), (db_hbm, db_ref), (o_hbm, o_ref), (n_hbm, n_ref), (x_hbm, x_ref), (dh_hbm, dh_ref)])]
+    loads[0].start()
+    loads[4].start()
     greet_all(me, n, total_devices)
     every = [VectorSum(me, total_devices, lambda g: {"dp": g // n, "tensor": g % n}, early_ref, piece, early_land, early_out,
                        e_send, e_recv),
@@ -805,6 +828,8 @@
     qv_ref[...] = jnp.zeros_like(qv_ref)
     loads[0].wait()
     loads[4].wait()
+    for k in (1, 2, 3, 5, 6):
+        loads[k].start()
     tile = 512
 
     def term(t):
@@ -828,8 +853,8 @@
     loop(n, term)
     column[1].start()
     every[1].start()
-    for copy in loads[1:4]:
-        copy.wait()
+    for k in (1, 2, 3, 5, 6):
+        loads[k].wait()
     plane = PlaneSum(row, m, out_p, terms, land_p, half_p, p_send, p_recv, h_send, h_recv)
     pairs = [(a_ref, dqkv_ref.at[p], p * width) for p in range(3)] + [(db_ref, o_ref, 3 * width)]
     for e in range(1, m, 2):
@@ -922,8 +947,9 @@
     attn_in, normal_one, vecs = pl.pallas_call(
         functools.partial(tokens_kernel, n, m, piece),
         out_shape=(shape((LEN, depth), BF), shape((LEN, depth), BF), shape((total,) + pack.shape, BF)),
-        in_specs=[VM, VM], out_specs=(VM, VM, VM),
-        scratch_shapes=[pltpu.VMEM((n, size, depth), BF), pltpu.VMEM((8, depth), F32), dma, dma((2, n, LineGather.PIECES)), dma((n, LineGather.PIECES)),
+        in_specs=[VM, VM], out_specs=(ANY, ANY, VM),
+        scratch_shapes=[pltpu.VMEM((n, size, depth), BF), pltpu.VMEM((8, depth), F32), pltpu.VMEM((LEN, depth), BF),
+                        pltpu.VMEM((LEN, depth), BF), dma((2, n)), dma, dma((2, n, LineGather.PIECES)), dma((n, LineGather.PIECES)),
                         dma((total,)), dma((total,))],
         compiler_params=params(0), name="gather_tokens",
     )(pack, tokens)
@@ -946,8 +972,9 @@
         functools.partial(attend_kernel, n, pieces),
         out_shape=(shape((3, LEN, width), BF), shape((LEN, width), BF), shape((size, depth), F32),
                    shape((size, depth), BF), shape((n, size, depth), BF)),
-        in_specs=[ANY] * 3 + [VM] * 6, out_specs=(VM, VM, VM, VM, ANY),
-        scratch_shapes=[pltpu.VMEM((LEN, depth), BF), pltpu.VMEM((3, depth, width), BF), pltpu.VMEM((width, depth), BF)] +
+        in_specs=[ANY] * 3 + [VM] * 6, out_specs=(ANY, ANY, VM, VM, ANY),
+        scratch_shapes=[pltpu.VMEM((3, LEN, width), BF), pltpu.VMEM((LEN, width), BF), dma((2,)),
+                        pltpu.VMEM((LEN, depth), BF), pltpu.VMEM((3, depth, width), BF), pltpu.VMEM((width, depth), BF)] +
                        sums + [dma((2, n, LineGather.PIECES)), dma((n, LineGather.PIECES)), dma((n, pieces)), dma((n + 1, pieces)), dma, dma, dma((4,))],
         compiler_params=params(1), name="attend",
     )(attn_in, w_qkv, w_out, tokens, cotangent, bias_qv, bias_out, gain_two, shift_two)
@@ -979,8 +1006,8 @@
         functools.partial(branch_kernel, n, m, pieces),
         out_shape=(shape((n, size, depth), BF), shape((size, depth), BF), shape((depth // m, units), F32),
                    shape((depth // m, units), F32), shape((3, LEN, width), BF)),
-        in_specs=[VM] * 3 + [ANY] * 7, out_specs=(ANY, VM, VM, VM, VM),
-        scratch_shapes=[pltpu.VMEM((LEN, depth), BF), pltpu.VMEM((LEN, units), BF), pltpu.VMEM((width, depth), BF),
+        in_specs=[VM] * 3 + [ANY] * 7, out_specs=(ANY, VM, VM, VM, ANY),
+        scratch_shapes=[pltpu.VMEM((3, LEN, width), BF), dma, pltpu.VMEM((LEN, depth), BF), pltpu.VMEM((LEN, units), BF), pltpu.VMEM((width, depth), BF),
                         pltpu.VMEM((LEN, HD), F32), pltpu.VMEM((LEN, HD), F32)] + sums +
                        [pltpu.VMEM((m // 2, depth // m, units), BF)] + plane_scratch(units) * 2 +
                        [pltpu.VMEM((RB, depth), F32), dma((2, n, LineGather.PIECES)), dma((n, LineGather.PIECES))] + sum_sems +
@@ -996,16 +1023,17 @@
         out_shape=(shape((size, depth), BF), shape((3, depth // m, width), F32), shape((depth // m, width), F32),
                    shape((8, tiles[0]), F32), shape((8, tiles[0]), F32), shape((8, tiles[1]), F32),
                    shape((8, tiles[2]), F32)),
-        in_specs=[VM, ANY, VM, VM, VM, VM, VM, ANY, ANY, ANY, ANY], out_specs=(VM,) * 7,
+        in_specs=[VM, ANY, ANY, ANY, VM, VM, VM, ANY, ANY, ANY, ANY], out_specs=(VM,) * 7,
         scratch_shapes=[pltpu.VMEM((8, depth), F32), pltpu.VMEM((8, width), F32),
                         pltpu.VMEM((3, depth, width), BF), pltpu.VMEM((LEN, depth), BF), pltpu.VMEM((LEN, depth), BF),
-                        pltpu.VMEM((LEN, width), BF), pltpu.VMEM((LEN, depth), BF)] + sums +
+                        pltpu.VMEM((LEN, width), BF), pltpu.VMEM((LEN, depth), BF), pltpu.VMEM((size, depth), BF),
+                        pltpu.VMEM((size, depth), F32)] + sums +
                        [pltpu.VMEM((m // 2, depth // m, 4 * width), BF)] +
                        plane_scratch(4 * width) +
                        [pltpu.VMEM((RB, depth), F32), pltpu.VMEM((total, 8, tiles[0]), F32),
                         pltpu.VMEM((total, 8, tiles[0]), F32), pltpu.VMEM((m, 8, tiles[1]), F32),
                         pltpu.VMEM((m, 8, tiles[2]), F32)] + sum_sems +
-                       [dma((5,)), dma((m // 2,)), dma((m // 2,)), dma((2, m // 2 - 1)), dma((2, m // 2 - 1))] +
+                       [dma((7,)), dma((m // 2,)), dma((m // 2,)), dma((2, m // 2 - 1)), dma((2, m // 2 - 1))] +
                        [dma((total,))] * 4 + [dma((m,))] * 4,
         compiler_params=params(5), name="input",
     )(grad_qkv, w_qkv, tokens, grad_resid, gain_one, vec_two, grad_up_b, attn_in, attn_cot, mixture, normal_one)

time: 577 us -> 554 us (0.960)
  Pallas kernels: 537 us -> 511 us
    pallas_call x1, Pallas kernels: 155 us -> 133 us  [body(): pl.pallas_call(functools.partial(hidden_kernel, n, pieces), out_shape=(sh...]
  transfers between devices with their start and end apart: 4 -> 4, of which waited for: 1 -> 1; matrix products, arithmetic and copies ran while one was open for 1% -> 1% of each run, Pallas kernels for 32% -> 33%
where the time goes in v7:
time: 554 us; the launch traced here: 553 us
  Pallas kernels  511 us (92%)
  local copies, waits for them, and re-layouts  18.9 us (3%)
  between operations  13.9 us (3%)
  waiting for transfers between devices  6.1 us (1%)
    pallas_call x1, Pallas kernels, body(): pl.pallas_call(functools.partial(hidden_kernel, n, pieces), out_shape=(sh...  133 us
    pallas_call x1, Pallas kernels, body(): pl.pallas_call(functools.partial(branch_kernel, n, m, pieces), out_shape=...  106 us
    pallas_call x1, Pallas kernels, body(): pl.pallas_call(functools.partial(attend_kernel, n, pieces), out_shape=(sh...  99.2 us
    pallas_call x1, Pallas kernels, body(): pl.pallas_call(functools.partial(input_kernel, n, m, pieces, (piece, up_p...  88 us
    pallas_call x1, Pallas kernels, body(): pl.pallas_call(functools.partial(tokens_kernel, n, m, piece), out_shape=(...  84.3 us
  transfers between devices with their start and end apart: 4, of which 1 were waited for; matrix products, arithmetic and copies ran while one was open for 1% of the time, Pallas kernels for 33%

profile of v7, /device:TPU:0, one launch (start us, length us, event | category | flops | bytes accessed | tf_op | source)
XLA Modules:
  0.0 553.1 jit_solution(7692929519734755669)
XLA Ops:
  7.2 0.0 all-gather.7.cloned.1.call-start
  7.2 0.7 all-gather.7.cloned.1.call-update
  7.9 0.0 all-gather.5.cloned.1.call-start
  8.0 0.7 all-gather.5.cloned.1.call-update
  8.7 0.0 all-gather.9.cloned.1.call-start
  8.7 0.7 all-gather.9.cloned.1.call-update
  9.4 0.0 all-gather.11.cloned.1.call-start
  9.4 0.5 all-gather.11.cloned.1.call-update
  10.0 0.7 tile.20
  10.7 0.1 tile.21
  10.8 0.8 stack.27
  11.5 0.1 tile.9
  11.6 1.3 fusion.4.pack_ref
  12.9 84.3 %gather_tokens.1 = (bf16[1024,2048]{1,0:T(8,128)(2,1)}, bf16[1024,2048]{1,0:T(8,128)(2,1)}, bf16[32,16,128]{2,1,0:T(8,128)(2,1)}) custom-call(bf16[16,128]{1,0:T(8,128)(2,1)} %fusion.4.pack_ref, bf16[256,2048]{1,0:T(8,128)(2,1)} %x_hbm.1), custom_call_target="tpu_custom_call" | custom-call | tf_op jit(solution)/shard_map/gather_tokens/pallas_call | solution.py:947
  97.2 1.0 convert_element_type.9
  98.2 0.6 slice.74
  98.8 0.6 bitcast_reduce_fusion.1
  99.4 0.6 slice_bitcast_fusion
  100.0 0.0 all-gather.7.cloned.1.call-done.wo_hbm
  100.0 0.0 all-gather.5.cloned.1.call-done.wq_hbm
  100.0 99.2 %attend.1 = (bf16[3,1024,512]{2,1,0:T(8,128)(2,1)}, bf16[1024,512]{1,0:T(8,128)(2,1)}, f32[256,2048]{1,0:T(8,128)}, bf16[256,2048]{1,0:T(8,128)(2,1)}, bf16[4,256,2048]{2,1,0:T(8,128)(2,1)}) custom-call(bf16[1024,2048]{1,0:T(8,128)(2,1)} %get-tuple-element.42.a_hbm, bf16[3,2048,512]{2,1,0:T(8,128)(2,1)} %all-gather.5.cloned.1.call-done.wq_hbm, ...), custom_call_target="tpu_custom_call" | custom-call | tf_op jit(solution)/shard_map/attend/pallas_call | solution.py:971
  199.3 0.0 all-gather.9.cloned.1.call-done.up_hbm
  199.3 3.5 all-gather.11.cloned.1.call-done.down_hbm
  202.8 133.4 %hidden.1 = (bf16[4,256,2048]{2,1,0:T(8,128)(2,1)}, bf16[4,256,2048]{2,1,0:T(8,128)(2,1)}, bf16[4,256,2048]{2,1,0:T(8,128)(2,1)}, bf16[4,256,2048]{2,1,0:T(8,128...) custom-call(bf16[256,2048]{1,0:T(8,128)(2,1)} %get-tuple-element.44.c_ref, ...), custom_call_target="tpu_custom_call" | custom-call | tf_op jit(solution)/shard_map/hidden/pallas_call | solution.py:983
  336.2 106.3 %branch.1 = (bf16[4,256,2048]{2,1,0:T(8,128)(2,1)}, bf16[256,2048]{1,0:T(8,128)(2,1)}, f32[256,2048]{1,0:T(8,128)}, f32[256,2048]{1,0:T(8,128)}, bf16[3,1024,512]{2,1,0:T(8,128)(2,1)}) custom-call(bf16[256,2048]{1,0:T(8,128)(2,1)} %get-tuple-element.47.db_ref, f32[256,2048]{1,0:T(8,128)} %get-tuple-element.45.h_ref, f32[1,2048]{1,0:T(1,128)} %get-tuple-element.99.down_bias, ...), custom_call_target="tpu_custom_call" | custom-call | tf_op jit(solution)/shard_map/branch/pallas_call | solution.py:1005
  442.5 88.0 %input.1 = (bf16[256,2048]{1,0:T(8,128)(2,1)}, f32[3,256,512]{2,1,0:T(8,128)}, f32[256,512]{1,0:T(8,128)}, f32[8,128]{1,0:T(8,128)}, f32[8,128]{1,0:T(8,128)}, /*index=5*/f32[8,256]{1,0:T(8,128)}, f32[8,128]{1,0:T(8,128)}) custom-call(bf16[3,1024,512]{2,1,0:T(8,128)(2,1)} %get-tuple-element.54.dqkv_ref, ...), custom_call_target="tpu_custom_call" | custom-call | tf_op jit(solution)/shard_map/input/pallas_call | solution.py:1021
  530.5 0.0 copy-start.2
  530.5 1.3 slice.67
  531.8 0.7 constant_dynamic-slice_fusion.1
  532.6 0.6 slice.63
  533.2 0.7 constant_dynamic-slice_fusion.2
  533.9 0.5 slice_bitcast_fusion.9
  534.4 0.8 constant_dynamic-slice_fusion
  535.2 0.5 slice_bitcast_fusion.5
  535.7 2.0 copy.30
  537.7 0.0 copy-start.1
  537.7 3.0 copy.31
  540.7 0.0 copy-start
  540.7 0.0 copy-done.2
  540.7 1.0 copy.36
  541.7 2.3 copy.37
  544.1 0.0 copy-done.1
  544.1 1.1 copy.38
  545.2 0.0 copy-done
  545.2 1.3 copy.39
  (6 shorter events, 0.0 us)
Async XLA Ops:
  7.2 92.8 %all-gather.7.cloned.1.call-start = ((), (), s32[]{:S(2)}) async-start(), calls=%async_computation.1 | async-start | bytes 2359296 | tf_op jit(solution)/shard_map/all_gather | solution.py:942
  7.9 92.1 %all-gather.5.cloned.1.call-start = ((), (), s32[]{:S(2)}) async-start(), calls=%async_computation | async-start | bytes 7077888 | tf_op jit(solution)/shard_map/all_gather | solution.py:941
  8.7 190.6 %all-gather.9.cloned.1.call-start = ((), (), s32[]{:S(2)}) async-start(), calls=%async_computation.2 | async-start | bytes 9437184 | tf_op jit(solution)/shard_map/all_gather | solution.py:943
  9.4 193.4 %all-gather.11.cloned.1.call-start = ((), (), s32[]{:S(2)}) async-start(), calls=%async_computation.3 | async-start | bytes 9437184 | tf_op jit(solution)/shard_map/all_gather | solution.py:944
  530.5 10.3 %copy-start.2 = (bf16[256,2048]{1,0:T(8,128)(2,1)S(1)}, bf16[256,2048]{1,0:T(8,128)(2,1)}, u32[]{:S(2)}) copy-start(bf16[256,2048]{1,0:T(8,128)(2,1)} %get-tuple-element.125) | copy-start | bytes 3145732
  537.7 6.3 %copy-start.1 = (f32[3,256,512]{2,1,0:T(8,128)S(1)}, f32[3,256,512]{2,1,0:T(8,128)}, u32[]{:S(2)}) copy-start(f32[3,256,512]{2,1,0:T(8,128)} %get-tuple-element.129) | copy-start | bytes 4718596
  540.7 4.5 copy-start
Sparse Core Ops, SparseCore 0:
  9.9 31.5 all-gather.6
  43.3 45.3 all-gather.4
  90.7 54.2 all-gather.8
  146.7 56.0 all-gather.10

commit v8 on v7

--- a/solution.py
+++ b/solution.py
@@ -79,11 +79,14 @@
     pl.semaphore_wait(barrier, total - 1)
 
 
-def rounds(i, n, line, compute):
+def rounds(i, n, line, compute, between=None):
     def round_of(r):
         @pl.when(r > 0)
         def _():
             line.step(r)
+
+        if between is not None:
+            between(r)
 
         def side(s):
             j = jnp.where(s == 0, i - r, i + r)
@@ -251,7 +254,98 @@
         loop(n, one)
 
 
-def tokens_kernel(n, m, piece, pack_ref, x_ref, a_hbm, n_hbm, vec_ref, buf, affine, a_ref, n_ref, out_sem, own_sem, send, recv, v_send, v_recv):
+def partner(row, bit):
+    return row + bit * (1 - 2 * ((row // bit) % 2))
+
+
+class PlaneGather:
+    def __init__(self, row, m, items, send, recv, local):
+        self.row, self.m, self.items, self.send, self.recv, self.local = row, m, items, send, recv, local
+        bits = [1 << k for k in range(1, m.bit_length() - 1)]
+        self.plan = []
+        for order in (bits + [1], bits[::-1] + [1]):
+            have, at, stages = [0], 0, []
+            for bit in order:
+                stages.append((bit, [(e, at + k) for k, e in enumerate(have)]))
+                at, have = at + len(have), have + [e ^ bit for e in have]
+            self.plan.append(stages)
+        self.stages = len(bits) + 1
+
+    def owner(self, e):
+        d = self.row
+        for k in range(self.m.bit_length() - 1):
+            if e & (1 << k):
+                d = d + (partner(self.row, 1 << k) - self.row)
+        return d
+
+    def copies(self, stage):
+        for k, (own, whole, own_half, half) in enumerate(self.items):
+            for h in range(2):
+                bit, moves = self.plan[h][stage]
+                for e, at in moves:
+                    there = half(whole, self.owner(e), h)
+                    src = own_half(own, h) if e == 0 else there
+                    yield pltpu.make_async_remote_copy(
+                        src_ref=src, dst_ref=there, send_sem=self.send.at[k, h, at], recv_sem=self.recv.at[k, h, e ^ bit],
+                        device_id={"dp": partner(self.row, bit)}, device_id_type=MESH)
+
+    def landed(self, stage):
+        for k, (own, whole, own_half, half) in enumerate(self.items):
+            for h in range(2):
+                bit, moves = self.plan[h][stage]
+                for e, at in moves:
+                    there = half(whole, self.owner(e ^ bit), h)
+                    pltpu.make_async_remote_copy(
+                        src_ref=there, dst_ref=there, send_sem=self.send.at[k, h, at], recv_sem=self.recv.at[k, h, e ^ bit],
+                        device_id={"dp": partner(self.row, bit)}, device_id_type=MESH).wait_recv()
+
+    def locals(self):
+        return [pltpu.make_async_copy(own_half(own, h), half(whole, self.row, h), self.local.at[k, h])
+                for k, (own, whole, own_half, half) in enumerate(self.items) for h in range(2)]
+
+    def start(self):
+        for copy in self.copies(0):
+            copy.start()
+        for copy in self.locals():
+            copy.start()
+
+    def advance(self, stage):
+        self.landed(stage - 1)
+        for copy in self.copies(stage):
+            copy.start()
+
+    def finish(self):
+        self.landed(self.stages - 1)
+        for stage in range(self.stages):
+            for copy in self.copies(stage):
+                copy.wait_send()
+        for copy in self.locals():
+            copy.wait()
+
+
+def half_rows(own, h):
+    size = own.shape[-2] // 2
+    return own.at[..., pl.ds(h * size, size), :]
+
+
+def row_blocks(m):
+    def half(whole, d, h):
+        size = whole.shape[-2] // m // 2
+        return whole.at[..., pl.ds(pl.multiple_of((2 * d + h) * size, size), size), :]
+
+    return half
+
+
+def column_blocks(m):
+    def half(whole, d, h):
+        size, width = whole.shape[-2] // 2, whole.shape[-1] // m
+        return whole.at[pl.ds(h * size, size), pl.ds(pl.multiple_of(d * width, width), width)]
+
+    return half
+
+
+def tokens_kernel(n, m, piece, pack_ref, x_ref, wq_ref, wo_ref, a_hbm, n_hbm, vec_ref, wq_all, wo_all, buf, affine,
+                  a_ref, n_ref, out_sem, w_send, w_recv, w_local, own_sem, send, recv, v_send, v_recv):
     i, row = lax.axis_index("tensor"), lax.axis_index("dp")
     me, total = row * n + i, m * n
     size = x_ref.shape[0]
@@ -265,6 +359,9 @@
 
     loop(total - 1, lambda s: vector(me, (me + s + 1) % total).start())
     line.start()
+    weights = PlaneGather(row, m, [(wq_ref, wq_all, half_rows, row_blocks(m)), (wo_ref, wo_all, half_rows, column_blocks(m))],
+                          w_send, w_recv, w_local)
+    weights.start()
     own_copy = pltpu.make_async_copy(x_ref, buf.at[i], own_sem)
     own_copy.start()
     vec_ref[me] = pack_ref[...]
@@ -298,15 +395,22 @@
         for copy in leave(j):
             copy.wait()
 
-    rounds(i, n, line, compute)
+    def between(r):
+        for stage in range(1, weights.stages):
+            @pl.when(r == stage)
+            def _():
+                weights.advance(stage)
+
+    rounds(i, n, line, compute, between)
     line.finish()
+    weights.finish()
     loop(n, left)
     loop(total - 1, lambda s: vector(me, (me + s + 1) % total).wait_send())
 
 
-def attend_kernel(n, pieces, a_hbm, wq_hbm, wo_hbm, x_ref, cot_ref, bias, out_bias, gain, shift, qkv_hbm, o_hbm, h_ref,
-                  c_ref, cot_all, qkv_ref, o_ref, out_sem, a_ref, wq_ref, w_ref, part, land, send, recv, s_send, s_recv, own_sem, a_sem, w_sem):
-    i = lax.axis_index("tensor")
+def attend_kernel(n, m, pieces, a_hbm, wq_hbm, wo_hbm, up_ref, down_ref, x_ref, cot_ref, bias, out_bias, gain, shift,
+                  qkv_hbm, o_hbm, h_ref, c_ref, cot_all, up_all, down_all, w_send, w_recv, w_local, qkv_ref, o_ref, out_sem, a_ref, wq_ref, w_ref, part, land, send, recv, s_send, s_recv, own_sem, a_sem, w_sem):
+    i, row = lax.axis_index("tensor"), lax.axis_index("dp")
     size = x_ref.shape[0]
     loads = [pltpu.make_async_copy(a_hbm, a_ref, a_sem)]
     loads += [pltpu.make_async_copy(wq_hbm.at[t], wq_ref.at[t], w_sem.at[t]) for t in range(3)]
@@ -315,9 +419,12 @@
         load.start()
     heads = qkv_ref.shape[2] // HD
     depth = w_ref.shape[1]
-    greet_neighbours(i, n)
+    greet_cross(i, n, row, m)
     line = LineGather(i, n, cot_ref, cot_all, send, recv)
     line.start()
+    weights = PlaneGather(row, m, [(up_ref, up_all, half_rows, row_blocks(m)), (down_ref, down_all, half_rows, column_blocks(m))],
+                          w_send, w_recv, w_local)
+    weights.start()
     own_copy = pltpu.make_async_copy(cot_ref, cot_all.at[i], own_sem)
     own_copy.start()
 
@@ -366,12 +473,13 @@
         sums.launch(d)
 
     loop(n, project)
-
-    def round_of(r):
-        line.step(r + 1)
-        relays(sums, i, n, r + 1)
-
-    loop(n - 1, round_of)
+    weights.advance(1)
+    for r in range(1, n):
+        line.step(r)
+        for stage in range(2, weights.stages):
+            if r == min(2 * stage - 1, n - 1):
+                weights.advance(stage)
+        relays(sums, i, n, r)
 
     def norm(b):
         here = rows_at(b, RB)
@@ -385,6 +493,7 @@
     own_copy.wait()
     for copy in leave:
         copy.wait()
+    weights.finish()
     line.finish()
     sums.finish()
 
@@ -512,10 +621,6 @@
         put(2, slice(0, LEN), t, dv[...].astype(BF))
 
     loop(heads, head)
-
-
-def partner(row, bit):
-    return row + bit * (1 - 2 * ((row // bit) % 2))
 
 
 class PlaneSum:
@@ -846,13 +951,18 @@
             vec_ref[1:2, cols] += jnp.sum(total, axis=0, keepdims=True)
 
         loop(depth // tile, columns)
-        sums.launch(d)
+
+        @pl.when(t == 0)
+        def _():
+            sums.launch(d)
+
         for p in range(2):
             qv_ref[p : p + 1, :] += jnp.sum(dqkv_ref[2 * p, here, :].astype(F32), axis=0, keepdims=True)
 
     loop(n, term)
+    every[1].start()
     column[1].start()
-    every[1].start()
+    loop(n - 1, lambda t: sums.launch(jnp.where(i < n // 2, n - 2 - t, t + 1)))
     for k in (1, 2, 3, 5, 6):
         loads[k].wait()
     plane = PlaneSum(row, m, out_p, terms, land_p, half_p, p_send, p_recv, h_send, h_recv)
@@ -938,21 +1048,18 @@
     pack = jnp.pad(pack, ((0, -pack.shape[0] % 16), (0, 0)))
     lanes_up = 8 + max(up_piece // LANES, 1)
 
-    w_qkv = lax.all_gather(qkv_weight, "dp", axis=1, tiled=True)
-    w_out = lax.all_gather(out_weight, "dp", axis=1, tiled=True)
-    w_up = lax.all_gather(up_weight, "dp", axis=0, tiled=True)
-    w_down = lax.all_gather(down_weight, "dp", axis=1, tiled=True)
-
     dma = pltpu.SemaphoreType.DMA
-    attn_in, normal_one, vecs = pl.pallas_call(
+    weight_sems = [dma((2, 2, m - 1)), dma((2, 2, m)), dma((2, 2))]
+    attn_in, normal_one, vecs, w_qkv, w_out = pl.pallas_call(
         functools.partial(tokens_kernel, n, m, piece),
-        out_shape=(shape((LEN, depth), BF), shape((LEN, depth), BF), shape((total,) + pack.shape, BF)),
-        in_specs=[VM, VM], out_specs=(ANY, ANY, VM),
+        out_shape=(shape((LEN, depth), BF), shape((LEN, depth), BF), shape((total,) + pack.shape, BF),
+                   shape((3, depth, width), BF), shape((width, depth), BF)),
+        in_specs=[VM] * 4, out_specs=(ANY, ANY, VM, ANY, ANY),
         scratch_shapes=[pltpu.VMEM((n, size, depth), BF), pltpu.VMEM((8, depth), F32), pltpu.VMEM((LEN, depth), BF),
-                        pltpu.VMEM((LEN, depth), BF), dma((2, n)), dma, dma((2, n, LineGather.PIECES)), dma((n, LineGather.PIECES)),
+                        pltpu.VMEM((LEN, depth), BF), dma((2, n))] + weight_sems + [dma, dma((2, n, LineGather.PIECES)), dma((n, LineGather.PIECES)),
                         dma((total,)), dma((total,))],
         compiler_params=params(0), name="gather_tokens",
-    )(pack, tokens)
+    )(pack, tokens, qkv_weight, out_weight)
     vecs = vecs.astype(F32)
 
     def whole_rows(block, count):
@@ -968,18 +1075,18 @@
 
     pieces = 2
     sums = [pltpu.VMEM((n, size, depth), BF), pltpu.VMEM((n + 1, size, depth), BF)]
-    qkv, mixture, residual, mlp_own, cot_all = pl.pallas_call(
-        functools.partial(attend_kernel, n, pieces),
+    qkv, mixture, residual, mlp_own, cot_all, w_up, w_down = pl.pallas_call(
+        functools.partial(attend_kernel, n, m, pieces),
         out_shape=(shape((3, LEN, width), BF), shape((LEN, width), BF), shape((size, depth), F32),
-                   shape((size, depth), BF), shape((n, size, depth), BF)),
-        in_specs=[ANY] * 3 + [VM] * 6, out_specs=(ANY, ANY, VM, VM, ANY),
-        scratch_shapes=[pltpu.VMEM((3, LEN, width), BF), pltpu.VMEM((LEN, width), BF), dma((2,)),
+                   shape((size, depth), BF), shape((n, size, depth), BF), shape((depth, units), BF), shape((units, depth), BF)),
+        in_specs=[ANY] * 3 + [VM] * 8, out_specs=(ANY, ANY, VM, VM, ANY, ANY, ANY),
+        scratch_shapes=weight_sems + [pltpu.VMEM((3, LEN, width), BF), pltpu.VMEM((LEN, width), BF), dma((2,)),
                         pltpu.VMEM((LEN, depth), BF), pltpu.VMEM((3, depth, width), BF), pltpu.VMEM((width, depth), BF)] +
                        sums + [dma((2, n, LineGather.PIECES)), dma((n, LineGather.PIECES)), dma((n, pieces)), dma((n + 1, pieces)), dma, dma, dma((4,))],
         compiler_params=params(1), name="attend",
-    )(attn_in, w_qkv, w_out, tokens, cotangent, bias_qv, bias_out, gain_two, shift_two)
-
-    pieces = 4
+    )(attn_in, w_qkv, w_out, up_weight, down_weight, tokens, cotangent, bias_qv, bias_out, gain_two, shift_two)
+
+    pieces = size // RB
     mlp_in, hidden, grad_pre, mlp_part, grad_resid, branch_cot, vec_two, grad_up_b = pl.pallas_call(
         functools.partial(hidden_kernel, n, pieces),
         out_shape=(shape((n, size, depth), BF), shape((n, size, units), BF), shape((n, size, units), BF),

time: 554 us -> 538 us (0.971)
  between operations: 13.9 us -> 0.78 us
  waiting for transfers between devices: 6.1 us -> 0 us
    pallas_call x1, Pallas kernels: 88 us -> 82.4 us  [body(): pl.pallas_call(functools.partial(input_kernel, n, m, pieces, (piece, up_p...]
  transfers between devices with their start and end apart: 4 -> 0, of which waited for: 1 -> 0; matrix products, arithmetic and copies ran while one was open for 1% -> 0% of each run, Pallas kernels for 33% -> 0%
where the time goes in v8:
time: 538 us; the launch traced here: 537 us
  Pallas kernels  514 us (96%)
  local copies, waits for them, and re-layouts  18.9 us (4%)
    pallas_call x1, Pallas kernels, body(): pl.pallas_call(functools.partial(hidden_kernel, n, pieces), out_shape=(sh...  137 us
    pallas_call x1, Pallas kernels, body(): pl.pallas_call(functools.partial(branch_kernel, n, m, pieces), out_shape=...  108 us
    pallas_call x1, Pallas kernels, body(): pl.pallas_call(functools.partial(attend_kernel, n, m, pieces), out_shape=...  101 us
    pallas_call x1, Pallas kernels, body(): pl.pallas_call(functools.partial(tokens_kernel, n, m, piece), out_shape=(...  85.2 us
    pallas_call x1, Pallas kernels, body(): pl.pallas_call(functools.partial(input_kernel, n, m, pieces, (piece, up_p...  82.4 us
    unnamed x12, local copies, waits for them, and re-layouts  10.8 us

profile of v8, /device:TPU:0, one launch (start us, length us, event | category | flops | bytes accessed | tf_op | source)
XLA Modules:
  0.0 536.6 jit_solution(9338619571913998488)
XLA Ops:
  0.7 0.7 tile.20
  1.4 0.1 tile.21
  1.5 0.8 stack.27
  2.2 0.1 tile.9
  2.3 1.3 fusion.4.pack_ref
  3.6 85.2 %gather_tokens.1 = (bf16[1024,2048]{1,0:T(8,128)(2,1)}, bf16[1024,2048]{1,0:T(8,128)(2,1)}, bf16[32,16,128]{2,1,0:T(8,128)(2,1)}, bf16[3,2048,512]{2,1,0:T(8,128)(2,1)}, bf16[512,2048]{1,0:T(8,128)(2,1)}) custom-call(bf16[16,128]{1,0:T(8,128)(2,1)} %fusion.4.pack_ref, bf16[256,2048]{1,0:T(8,128)(2,1)} %x_hbm.1, bf16[3,256,512]{2,1,0:T(8,128)(2,1)} %wq_ref.1, ...), custom_call_target="tpu_custom_call" | custom-call | tf_op jit(solution)/shard_map/gather_tokens/pallas_call | solution.py:1053
  88.8 0.9 convert_element_type.9
  89.7 0.6 bitcast_reduce_fusion.1
  90.3 0.6 slice.74
  90.9 0.6 slice_bitcast_fusion
  91.6 101.0 %attend.1 = (bf16[3,1024,512]{2,1,0:T(8,128)(2,1)}, bf16[1024,512]{1,0:T(8,128)(2,1)}, f32[256,2048]{1,0:T(8,128)}, bf16[256,2048]{1,0:T(8,128)(2,1)}, bf16[4,25...) custom-call(bf16[1024,2048]{1,0:T(8,128)(2,1)} %get-tuple-element.46.a_hbm, ...), custom_call_target="tpu_custom_call" | custom-call | tf_op jit(solution)/shard_map/attend/pallas_call | solution.py:1078
  192.6 137.1 %hidden.1 = (bf16[4,256,2048]{2,1,0:T(8,128)(2,1)}, bf16[4,256,2048]{2,1,0:T(8,128)(2,1)}, bf16[4,256,2048]{2,1,0:T(8,128)(2,1)}, bf16[4,256,2048]{2,1,0:T(8,128...) custom-call(bf16[256,2048]{1,0:T(8,128)(2,1)} %get-tuple-element.50.c_ref, ...), custom_call_target="tpu_custom_call" | custom-call | tf_op jit(solution)/shard_map/hidden/pallas_call | solution.py:1090
  329.7 108.4 %branch.1 = (bf16[4,256,2048]{2,1,0:T(8,128)(2,1)}, bf16[256,2048]{1,0:T(8,128)(2,1)}, f32[256,2048]{1,0:T(8,128)}, f32[256,2048]{1,0:T(8,128)}, bf16[3,1024,512]{2,1,0:T(8,128)(2,1)}) custom-call(bf16[256,2048]{1,0:T(8,128)(2,1)} %get-tuple-element.55.db_ref, f32[256,2048]{1,0:T(8,128)} %get-tuple-element.51.h_ref, f32[1,2048]{1,0:T(1,128)} %get-tuple-element.107.down_bias, ...), custom_call_target="tpu_custom_call" | custom-call | tf_op jit(solution)/shard_map/branch/pallas_call | solution.py:1112
  438.1 82.4 %input.1 = (bf16[256,2048]{1,0:T(8,128)(2,1)}, f32[3,256,512]{2,1,0:T(8,128)}, f32[256,512]{1,0:T(8,128)}, f32[8,128]{1,0:T(8,128)}, f32[8,128]{1,0:T(8,128)}, /*index=5*/f32[8,256]{1,0:T(8,128)}, f32[8,128]{1,0:T(8,128)}) custom-call(bf16[3,1024,512]{2,1,0:T(8,128)(2,1)} %get-tuple-element.62.dqkv_ref, bf16[3,2048,512]{2,1,0:T(8,128)(2,1)} %get-tuple-element.47.wq_hbm, ...), custom_call_target="tpu_custom_call" | custom-call | tf_op jit(solution)/shard_map/input/pallas_call | solution.py:1128
  520.5 0.0 copy-start.2
  520.5 1.3 slice.67
  521.9 0.8 constant_dynamic-slice_fusion.1
  522.6 0.6 slice.63
  523.2 0.7 constant_dynamic-slice_fusion.2
  524.0 0.5 slice_bitcast_fusion.9
  524.5 0.8 constant_dynamic-slice_fusion
  525.2 0.5 slice_bitcast_fusion.5
  525.8 2.0 copy.30
  527.8 0.0 copy-start.1
  527.8 3.0 copy.31
  530.8 0.0 copy-done.2
  530.8 0.0 copy-start
  530.8 1.0 copy.36
  531.8 2.3 copy.37
  534.1 0.0 copy-done.1
  534.1 1.1 copy.38
  535.3 0.0 copy-done
  535.3 1.3 copy.39
  (6 shorter events, 0.1 us)
Async XLA Ops:
  520.5 10.3 %copy-start.2 = (bf16[256,2048]{1,0:T(8,128)(2,1)S(1)}, bf16[256,2048]{1,0:T(8,128)(2,1)}, u32[]{:S(2)}) copy-start(bf16[256,2048]{1,0:T(8,128)(2,1)} %get-tuple-element.133) | copy-start | bytes 3145732
  527.8 6.3 %copy-start.1 = (f32[3,256,512]{2,1,0:T(8,128)S(1)}, f32[3,256,512]{2,1,0:T(8,128)}, u32[]{:S(2)}) copy-start(f32[3,256,512]{2,1,0:T(8,128)} %get-tuple-element.137) | copy-start | bytes 4718596
  530.8 4.5 copy-start

commit v9 on v8

--- a/solution.py
+++ b/solution.py
@@ -344,8 +344,8 @@
     return half
 
 
-def tokens_kernel(n, m, piece, pack_ref, x_ref, wq_ref, wo_ref, a_hbm, n_hbm, vec_ref, wq_all, wo_all, buf, affine,
-                  a_ref, n_ref, out_sem, w_send, w_recv, w_local, own_sem, send, recv, v_send, v_recv):
+def tokens_kernel(n, m, widths, pack_ref, x_ref, wq_ref, wo_ref, a_hbm, n_hbm, affine, qv_bias, up_bias, wq_all, wo_all,
+                  vec_ref, buf, a_ref, n_ref, out_sem, w_send, w_recv, w_local, own_sem, send, recv, v_send, v_recv):
     i, row = lax.axis_index("tensor"), lax.axis_index("dp")
     me, total = row * n + i, m * n
     size = x_ref.shape[0]
@@ -366,13 +366,24 @@
     own_copy.start()
     vec_ref[me] = pack_ref[...]
     loop(total - 1, lambda s: vector((me + s + 1) % total, me).wait_recv())
-    depth = affine.shape[1]
-    group = LANES // piece
-    for tile in range(depth // LANES):
-        value = vec_ref[tile * group, 0:2, :].astype(F32)
-        for g in range(1, group):
-            value = value + vec_ref[tile * group + g, 0:2, :].astype(F32)
-        affine[0:2, tile * LANES : (tile + 1) * LANES] = value
+    piece, qv_piece, up_piece = widths
+
+    def assemble(out, piece, first, rows, device):
+        group = max(LANES // piece, 1)
+        split = max(piece // LANES, 1)
+        for tile in range(out.shape[1] // LANES):
+            if split > 1:
+                at = first + tile % split
+                value = vec_ref[device(tile // split), at : at + 1, :].astype(F32)
+            else:
+                value = vec_ref[device(tile * group), first : first + rows, :].astype(F32)
+                for g in range(1, group):
+                    value = value + vec_ref[device(tile * group + g), first : first + rows, :].astype(F32)
+            out[0:rows, tile * LANES : (tile + 1) * LANES] = value
+
+    assemble(affine, piece, 0, 6, lambda g: g)
+    assemble(qv_bias, qv_piece, 6, 2, lambda d: d * n + i)
+    assemble(up_bias, up_piece, 8, 1, lambda d: d * n + i)
     own_copy.wait()
 
     def compute(j):
@@ -408,7 +419,7 @@
     loop(total - 1, lambda s: vector(me, (me + s + 1) % total).wait_send())
 
 
-def attend_kernel(n, m, pieces, a_hbm, wq_hbm, wo_hbm, up_ref, down_ref, x_ref, cot_ref, bias, out_bias, gain, shift,
+def attend_kernel(n, m, pieces, a_hbm, wq_hbm, wo_hbm, up_ref, down_ref, x_ref, cot_ref, bias, vec,
                   qkv_hbm, o_hbm, h_ref, c_ref, cot_all, up_all, down_all, w_send, w_recv, w_local, qkv_ref, o_ref, out_sem, a_ref, wq_ref, w_ref, part, land, send, recv, s_send, s_recv, own_sem, a_sem, w_sem):
     i, row = lax.axis_index("tensor"), lax.axis_index("dp")
     size = x_ref.shape[0]
@@ -484,10 +495,10 @@
     def norm(b):
         here = rows_at(b, RB)
         sums.add(here, h_ref.at[here, :])
-        rows = h_ref[here, :] + (x_ref[here, :].astype(F32) + out_bias[...])
+        rows = h_ref[here, :] + (x_ref[here, :].astype(F32) + vec[2:3, :])
         h_ref[here, :] = rows
         normal, _ = norm_stats(rows)
-        c_ref[here, :] = (normal * gain[...] + shift[...]).astype(BF)
+        c_ref[here, :] = (normal * vec[3:4, :] + vec[4:5, :]).astype(BF)
 
     sums.own(norm)
     own_copy.wait()
@@ -498,7 +509,7 @@
     sums.finish()
 
 
-def hidden_kernel(n, pieces, c_ref, h_ref, cot_hbm, up_hbm, down_hbm, up_bias, gain, c_hbm, g_hbm, du_hbm, mlp_hbm, dh_ref,
+def hidden_kernel(n, pieces, c_ref, h_ref, cot_hbm, up_hbm, down_hbm, up_bias, vec, c_hbm, g_hbm, du_hbm, mlp_hbm, dh_ref,
                   db_ref, vec_ref, upb_ref, c_all, g_all, du_all, cot_all, up, down, part, land, send, recv, s_send,
                   s_recv, w_sem, cot_sem, own_sem, c_sem, g_sem, du_sem, mlp, mlp_sem):
     i = lax.axis_index("tensor")
@@ -561,11 +572,13 @@
         loop(depth // tile, columns)
         out_copy(mlp, mlp_hbm, mlp_sem, j).start()
 
-    loop(n, forward)
-
     def relay(t):
         early = jnp.where(i < n // 2, 1, 0)
         sums.relay(t + 3 - early - i, 2 * n - 4 - i - t - early)
+
+        @pl.when(t < n // 2)
+        def _():
+            loop(2, lambda k: forward(2 * t + k))
 
     loop(2 * n - 3, relay)
 
@@ -577,7 +590,7 @@
         vec_ref[0:1, :] += jnp.sum(grad * normal, axis=0, keepdims=True)
         vec_ref[1:2, :] += jnp.sum(grad, axis=0, keepdims=True)
         cot = cot_all[i, here, :].astype(F32)
-        dh = cot + norm_back(grad, normal, inverse, gain[...])
+        dh = cot + norm_back(grad, normal, inverse, vec[3:4, :])
         dh_ref[here, :] = dh
         db = dh.astype(BF)
         db_ref[here, :] = db
@@ -703,9 +716,9 @@
 
 
 class VectorSum:
-    def __init__(self, me, count, device, vectors, piece, land, out, send, recv):
+    def __init__(self, me, count, device, vectors, piece, land, acc, send, recv):
         self.me, self.count, self.device, self.vectors, self.piece = me, count, device, vectors, piece
-        self.land, self.out, self.send, self.recv = land, out, send, recv
+        self.land, self.acc, self.send, self.recv = land, acc, send, recv
 
     def lanes(self, owner):
         size = self.land.shape[2]
@@ -720,15 +733,20 @@
         loop(self.count - 1, lambda s: self.copy(self.me, (self.me + s + 1) % self.count).start())
 
     def finish(self):
-        self.out[...] = self.vectors[:, self.lanes(self.me)]
+        self.acc[...] = self.vectors[:, self.lanes(self.me)]
 
         def take(s):
             src = (self.me + s + 1) % self.count
             self.copy(src, self.me).wait_recv()
-            self.out[...] += self.land[src]
+            self.acc[...] += self.land[src]
 
         loop(self.count - 1, take)
         loop(self.count - 1, lambda s: self.copy(self.me, (self.me + s + 1) % self.count).wait_send())
+        places = self.land.shape[2] // self.piece
+        own = self.acc[:, 0 : self.piece]
+        for k in range(1, places):
+            own = jnp.where(self.me % places == k, self.acc[:, k * self.piece : (k + 1) * self.piece], own)
+        return own
 
 
 def greet_cross(i, n, row, m):
@@ -767,7 +785,7 @@
         loop(width // tile, columns)
 
 
-def branch_kernel(n, m, pieces, db_ref, h_ref, down_bias, mlp_hbm, g_hbm, cot_hbm, c_hbm, du_hbm, qkv_hbm, wo_hbm,
+def branch_kernel(n, m, pieces, db_ref, h_ref, vec, mlp_hbm, g_hbm, cot_hbm, c_hbm, du_hbm, qkv_hbm, wo_hbm,
                   db_all, lo_ref, down_ref, up_ref, dqkv_hbm, dqkv_ref, out_sem, lhs, rhs, wo, dk, dv, part, land, out, terms_a, land_a,
                   half_a, terms_b, land_b, half_b, acc, send, recv, s_send, s_recv, own_sem, part_sem, in_sem, qkv_sem,
                   db_sem, p_send, p_recv, h_send, h_recv):
@@ -893,7 +911,7 @@
     def output(b):
         here = rows_at(b, RB)
         sums.add(here, acc)
-        lo_ref[here, :] = (h_ref[here, :] + (acc[...] + down_bias[...])).astype(BF)
+        lo_ref[here, :] = (h_ref[here, :] + (acc[...] + vec[5:6, :])).astype(BF)
 
     sums.own(output)
     line.finish()
@@ -904,8 +922,8 @@
     leave.wait()
 
 
-def input_kernel(n, m, pieces, widths, dqkv_ref, wq_hbm, x_hbm, dh_hbm, gain, early_ref, up_ref, a_hbm, db_hbm, o_hbm,
-                 n_hbm, gt_ref, gqkv_ref, gout_ref, early_out, late_out, up_out, qv_out, vec_ref, qv_ref, wq, a_ref, db_ref,
+def input_kernel(n, m, pieces, widths, dqkv_ref, wq_hbm, x_hbm, dh_hbm, vec, early_ref, up_ref, a_hbm, db_hbm, o_hbm,
+                 n_hbm, gt_ref, gqkv_ref, gout_ref, vec_out, up_out, qv_out, early_acc, late_acc, up_acc, qv_acc, vec_ref, qv_ref, wq, a_ref, db_ref,
                  o_ref, n_ref, x_ref, dh_ref, part, land, out_p, terms, land_p, half_p, acc, early_land, late_land, up_land, qv_land, s_send,
                  s_recv, in_sem, p_send, p_recv, h_send, h_recv, e_send, e_recv, l_send, l_recv, u_send, u_recv, q_send,
                  q_recv):
@@ -920,12 +938,12 @@
     loads[0].start()
     loads[4].start()
     greet_all(me, n, total_devices)
-    every = [VectorSum(me, total_devices, lambda g: {"dp": g // n, "tensor": g % n}, early_ref, piece, early_land, early_out,
+    every = [VectorSum(me, total_devices, lambda g: {"dp": g // n, "tensor": g % n}, early_ref, piece, early_land, early_acc,
                        e_send, e_recv),
-             VectorSum(me, total_devices, lambda g: {"dp": g // n, "tensor": g % n}, vec_ref, piece, late_land, late_out,
+             VectorSum(me, total_devices, lambda g: {"dp": g // n, "tensor": g % n}, vec_ref, piece, late_land, late_acc,
                        l_send, l_recv)]
-    column = [VectorSum(row, m, lambda g: {"dp": g}, up_ref, up_piece, up_land, up_out, u_send, u_recv),
-              VectorSum(row, m, lambda g: {"dp": g}, qv_ref, qv_piece, qv_land, qv_out, q_send, q_recv)]
+    column = [VectorSum(row, m, lambda g: {"dp": g}, up_ref, up_piece, up_land, up_acc, u_send, u_recv),
+              VectorSum(row, m, lambda g: {"dp": g}, qv_ref, qv_piece, qv_land, qv_acc, q_send, q_recv)]
     every[0].start()
     column[0].start()
     sums = LineSum(i, n, part, land, s_send, s_recv, pieces)
@@ -996,7 +1014,7 @@
         sums.add(here, acc)
         grad = acc[...]
         normal, inverse = norm_stats(x_ref[here, :].astype(F32))
-        gt_ref[here, :] = (dh_ref[here, :] + norm_back(grad, normal, inverse, gain[...])).astype(BF)
+        gt_ref[here, :] = (dh_ref[here, :] + norm_back(grad, normal, inverse, vec[0:1, :])).astype(BF)
 
     while stage < plane.stages:
         if stage < plane.stages - 1:
@@ -1005,8 +1023,11 @@
         else:
             plane.take(stage, out)
         stage += 1
-    for group in (every[0], column[0], column[1], every[1]):
-        group.finish()
+    early, late = every[0].finish(), every[1].finish()
+    for k, (rows, at) in enumerate([(late, 0), (late, 1), (early, 2), (early, 0), (early, 1), (early, 3)]):
+        vec_out[k : k + 1, :] = rows[at : at + 1, :]
+    up_out[...] = column[0].finish()
+    qv_out[...] = column[1].finish()
     sums.own(norm)
     sums.finish()
     plane.sent()
@@ -1050,28 +1071,16 @@
 
     dma = pltpu.SemaphoreType.DMA
     weight_sems = [dma((2, 2, m - 1)), dma((2, 2, m)), dma((2, 2))]
-    attn_in, normal_one, vecs, w_qkv, w_out = pl.pallas_call(
-        functools.partial(tokens_kernel, n, m, piece),
-        out_shape=(shape((LEN, depth), BF), shape((LEN, depth), BF), shape((total,) + pack.shape, BF),
-                   shape((3, depth, width), BF), shape((width, depth), BF)),
-        in_specs=[VM] * 4, out_specs=(ANY, ANY, VM, ANY, ANY),
-        scratch_shapes=[pltpu.VMEM((n, size, depth), BF), pltpu.VMEM((8, depth), F32), pltpu.VMEM((LEN, depth), BF),
-                        pltpu.VMEM((LEN, depth), BF), dma((2, n))] + weight_sems + [dma, dma((2, n, LineGather.PIECES)), dma((n, LineGather.PIECES)),
-                        dma((total,)), dma((total,))],
+    attn_in, normal_one, vectors, bias_qv, bias_up, w_qkv, w_out = pl.pallas_call(
+        functools.partial(tokens_kernel, n, m, (piece, qv_piece, up_piece)),
+        out_shape=(shape((LEN, depth), BF), shape((LEN, depth), BF), shape((8, depth), F32), shape((8, width), F32),
+                   shape((8, units), F32), shape((3, depth, width), BF), shape((width, depth), BF)),
+        in_specs=[VM] * 4, out_specs=(ANY, ANY, VM, VM, VM, ANY, ANY),
+        scratch_shapes=[pltpu.VMEM((total,) + pack.shape, BF), pltpu.VMEM((n, size, depth), BF), pltpu.VMEM((LEN, depth), BF),
+                        pltpu.VMEM((LEN, depth), BF), dma((2, n))] + weight_sems +
+                       [dma, dma((2, n, LineGather.PIECES)), dma((n, LineGather.PIECES)), dma((total,)), dma((total,))],
         compiler_params=params(0), name="gather_tokens",
     )(pack, tokens, qkv_weight, out_weight)
-    vecs = vecs.astype(F32)
-
-    def whole_rows(block, count):
-        if count < LANES:
-            block = block.reshape(-1, LANES // count, *block.shape[1:]).sum(axis=1)
-        return block
-
-    vectors = whole_rows(vecs[:, 0:6], piece).transpose(1, 0, 2).reshape(6, 1, depth)
-    gain_one, shift_one, bias_out, gain_two, shift_two, bias_down = [vectors[j] for j in range(6)]
-    mine = lax.dynamic_index_in_dim(vecs.reshape(m, n, -1, LANES), i, 1, keepdims=False)
-    bias_qv = whole_rows(mine[:, 6:8], qv_piece).transpose(1, 0, 2).reshape(2, width)
-    bias_up = whole_rows(mine[:, 8:lanes_up], up_piece).reshape(1, units)
 
     pieces = 2
     sums = [pltpu.VMEM((n, size, depth), BF), pltpu.VMEM((n + 1, size, depth), BF)]
@@ -1079,14 +1088,14 @@
         functools.partial(attend_kernel, n, m, pieces),
         out_shape=(shape((3, LEN, width), BF), shape((LEN, width), BF), shape((size, depth), F32),
                    shape((size, depth), BF), shape((n, size, depth), BF), shape((depth, units), BF), shape((units, depth), BF)),
-        in_specs=[ANY] * 3 + [VM] * 8, out_specs=(ANY, ANY, VM, VM, ANY, ANY, ANY),
+        in_specs=[ANY] * 3 + [VM] * 6, out_specs=(ANY, ANY, VM, VM, ANY, ANY, ANY),
         scratch_shapes=weight_sems + [pltpu.VMEM((3, LEN, width), BF), pltpu.VMEM((LEN, width), BF), dma((2,)),
                         pltpu.VMEM((LEN, depth), BF), pltpu.VMEM((3, depth, width), BF), pltpu.VMEM((width, depth), BF)] +
                        sums + [dma((2, n, LineGather.PIECES)), dma((n, LineGather.PIECES)), dma((n, pieces)), dma((n + 1, pieces)), dma, dma, dma((4,))],
         compiler_params=params(1), name="attend",
-    )(attn_in, w_qkv, w_out, up_weight, down_weight, tokens, cotangent, bias_qv, bias_out, gain_two, shift_two)
-
-    pieces = size // RB
+    )(attn_in, w_qkv, w_out, up_weight, down_weight, tokens, cotangent, bias_qv, vectors)
+
+    pieces = min(4, size // RB)
     mlp_in, hidden, grad_pre, mlp_part, grad_resid, branch_cot, vec_two, grad_up_b = pl.pallas_call(
         functools.partial(hidden_kernel, n, pieces),
         out_shape=(shape((n, size, depth), BF), shape((n, size, units), BF), shape((n, size, units), BF),
@@ -1099,7 +1108,7 @@
                        [dma((2, n, LineGather.PIECES)), dma((n, LineGather.PIECES)), dma((n, pieces)), dma((n + 1, pieces)), dma((2,)), dma, dma,
                         dma((n,)), dma((n,)), dma((n,)), pltpu.VMEM((n, size, depth), BF), dma((n,))],
         compiler_params=params(2), name="hidden",
-    )(mlp_own, residual, cot_all, w_up, w_down, bias_up, gain_two)
+    )(mlp_own, residual, cot_all, w_up, w_down, bias_up, vectors)
     mlp_in, hidden, grad_pre, cot_rows = [v.reshape(LEN, -1) for v in (mlp_in, hidden, grad_pre, cot_all)]
 
     def plane_scratch(columns):
@@ -1121,17 +1130,17 @@
                        [dma, dma, dma((3,)), dma((3,)), dma((n,)), dma((2, m // 2)), dma((2, m // 2)),
                         dma((2, 2, m // 2 - 1)), dma((2, 2, m // 2 - 1))],
         compiler_params=params(4), name="branch",
-    )(branch_cot, residual, bias_down, mlp_part, hidden, cot_rows, mlp_in, grad_pre, qkv, w_out)
+    )(branch_cot, residual, vectors, mlp_part, hidden, cot_rows, mlp_in, grad_pre, qkv, w_out)
     attn_cot = attn_cot.reshape(LEN, depth)
 
     tiles = [max(v, LANES) for v in (piece, up_piece, qv_piece)]
-    grad_tokens, grad_qkv_w, grad_out_w, early, late, grad_up_b, grad_qv_b = pl.pallas_call(
+    grad_tokens, grad_qkv_w, grad_out_w, vector_grads, grad_up_b, grad_qv_b = pl.pallas_call(
         functools.partial(input_kernel, n, m, pieces, (piece, up_piece, qv_piece)),
         out_shape=(shape((size, depth), BF), shape((3, depth // m, width), F32), shape((depth // m, width), F32),
-                   shape((8, tiles[0]), F32), shape((8, tiles[0]), F32), shape((8, tiles[1]), F32),
-                   shape((8, tiles[2]), F32)),
-        in_specs=[VM, ANY, ANY, ANY, VM, VM, VM, ANY, ANY, ANY, ANY], out_specs=(VM,) * 7,
-        scratch_shapes=[pltpu.VMEM((8, depth), F32), pltpu.VMEM((8, width), F32),
+                   shape((8, piece), F32), shape((8, up_piece), F32), shape((8, qv_piece), F32)),
+        in_specs=[VM, ANY, ANY, ANY, VM, VM, VM, ANY, ANY, ANY, ANY], out_specs=(VM,) * 6,
+        scratch_shapes=[pltpu.VMEM((8, tiles[k]), F32) for k in (0, 0, 1, 2)] + [
+                        pltpu.VMEM((8, depth), F32), pltpu.VMEM((8, width), F32),
                         pltpu.VMEM((3, depth, width), BF), pltpu.VMEM((LEN, depth), BF), pltpu.VMEM((LEN, depth), BF),
                         pltpu.VMEM((LEN, width), BF), pltpu.VMEM((LEN, depth), BF), pltpu.VMEM((size, depth), BF),
                         pltpu.VMEM((size, depth), F32)] + sums +
@@ -1143,16 +1152,11 @@
                        [dma((7,)), dma((m // 2,)), dma((m // 2,)), dma((2, m // 2 - 1)), dma((2, m // 2 - 1))] +
                        [dma((total,))] * 4 + [dma((m,))] * 4,
         compiler_params=params(5), name="input",
-    )(grad_qkv, w_qkv, tokens, grad_resid, gain_one, vec_two, grad_up_b, attn_in, attn_cot, mixture, normal_one)
+    )(grad_qkv, w_qkv, tokens, grad_resid, vectors, vec_two, grad_up_b, attn_in, attn_cot, mixture, normal_one)
     grad_down_w, grad_out_w = grad_down_w.T, grad_out_w.T
 
-    def own_lanes(block, index, count):
-        return lax.dynamic_slice_in_dim(block, index * count % block.shape[1], count, axis=1)
-
-    early, late = own_lanes(early, me, piece), own_lanes(late, me, piece)
-    vectors = [late[0], late[1], early[2], early[0], early[1], early[3]]
-    grad_qv_b = own_lanes(grad_qv_b, row, qv_piece)[:2]
-    grad_up_b = own_lanes(grad_up_b, row, up_piece)[0]
+    vectors = [vector_grads[k] for k in range(6)]
+    grad_up_b, grad_qv_b = grad_up_b[0], grad_qv_b[:2]
     return (layer_out, grad_tokens, vectors[0], vectors[1], grad_qkv_w, grad_qv_b, grad_out_w, vectors[2],
             vectors[3], vectors[4], grad_up_w, grad_up_b, grad_down_w, vectors[5])
 

time: 538 us -> 521 us (0.968)
  Pallas kernels: 514 us -> 501 us
    pallas_call x1, Pallas kernels: 137 us -> 126 us  [body(): pl.pallas_call(functools.partial(hidden_kernel, n, pieces), out_shape=(sh...]
where the time goes in v9:
time: 521 us; the launch traced here: 519 us
  Pallas kernels  501 us (96%)
  local copies, waits for them, and re-layouts  16.4 us (3%)
    pallas_call x1, Pallas kernels, body(): pl.pallas_call(functools.partial(hidden_kernel, n, pieces), out_shape=(sh...  126 us
    pallas_call x1, Pallas kernels, body(): pl.pallas_call(functools.partial(branch_kernel, n, m, pieces), out_shape=...  106 us
    pallas_call x1, Pallas kernels, body(): pl.pallas_call(functools.partial(attend_kernel, n, m, pieces), out_shape=...  101 us
    pallas_call x1, Pallas kernels, body(): pl.pallas_call(functools.partial(tokens_kernel, n, m, (piece, qv_piece, u...  85.2 us
    pallas_call x1, Pallas kernels, body(): pl.pallas_call(functools.partial(input_kernel, n, m, pieces, (piece, up_p...  82.2 us
    unnamed x12, local copies, waits for them, and re-layouts  10.8 us

profile of v9, /device:TPU:0, one launch (start us, length us, event | category | flops | bytes accessed | tf_op | source)
XLA Modules:
  0.0 519.0 jit_solution(8017329531580188120)
XLA Ops:
  0.7 0.7 tile.20
  1.4 0.1 tile.21
  1.4 0.8 stack.27
  2.2 0.1 tile.9
  2.3 1.3 fusion.4.pack_ref
  3.6 85.2 %gather_tokens.1 = (bf16[1024,2048]{1,0:T(8,128)(2,1)}, bf16[1024,2048]{1,0:T(8,128)(2,1)}, f32[8,2048]{1,0:T(8,128)}, f32[8,512]{1,0:T(8,128)}, f32[8,2048]{1,0...) custom-call(bf16[16,128]{1,0:T(8,128)(2,1)} %fusion.4.pack_ref, bf16[256,2048]{1,0:T(8,128)(2,1)} %x_hbm.1, ...), custom_call_target="tpu_custom_call" | custom-call | tf_op jit(solution)/shard_map/gather_tokens/pallas_call | solution.py:1074
  88.8 101.0 %attend.1 = (bf16[3,1024,512]{2,1,0:T(8,128)(2,1)}, bf16[1024,512]{1,0:T(8,128)(2,1)}, f32[256,2048]{1,0:T(8,128)}, bf16[256,2048]{1,0:T(8,128)(2,1)}, bf16[4,25...) custom-call(bf16[1024,2048]{1,0:T(8,128)(2,1)} %get-tuple-element.47.a_hbm, ...), custom_call_target="tpu_custom_call" | custom-call | tf_op jit(solution)/shard_map/attend/pallas_call | solution.py:1087
  189.8 125.8 %hidden.1 = (bf16[4,256,2048]{2,1,0:T(8,128)(2,1)}, bf16[4,256,2048]{2,1,0:T(8,128)(2,1)}, bf16[4,256,2048]{2,1,0:T(8,128)(2,1)}, bf16[4,256,2048]{2,1,0:T(8,128...) custom-call(bf16[256,2048]{1,0:T(8,128)(2,1)} %get-tuple-element.52.c_ref, ...), custom_call_target="tpu_custom_call" | custom-call | tf_op jit(solution)/shard_map/hidden/pallas_call | solution.py:1099
  315.6 106.2 %branch.1 = (bf16[4,256,2048]{2,1,0:T(8,128)(2,1)}, bf16[256,2048]{1,0:T(8,128)(2,1)}, f32[256,2048]{1,0:T(8,128)}, f32[256,2048]{1,0:T(8,128)}, bf16[3,1024,512]{2,1,0:T(8,128)(2,1)}) custom-call(bf16[256,2048]{1,0:T(8,128)(2,1)} %get-tuple-element.58.db_ref, f32[256,2048]{1,0:T(8,128)} %get-tuple-element.53.h_ref, f32[8,2048]{1,0:T(8,128)} %get-tuple-element.51.vec, ...), custom_call_target="tpu_custom_call" | custom-call | tf_op jit(solution)/shard_map/branch/pallas_call | solution.py:1121
  421.9 82.2 %input.1 = (bf16[256,2048]{1,0:T(8,128)(2,1)}, f32[3,256,512]{2,1,0:T(8,128)}, f32[256,512]{1,0:T(8,128)}, f32[8,64]{1,0:T(8,128)}, f32[8,256]{1,0:T(8,128)}, /*index=5*/f32[8,64]{1,0:T(8,128)}) custom-call(bf16[3,1024,512]{2,1,0:T(8,128)(2,1)} %get-tuple-element.65.dqkv_ref, bf16[3,2048,512]{2,1,0:T(8,128)(2,1)} %get-tuple-element.48.wq_hbm, ...), custom_call_target="tpu_custom_call" | custom-call | tf_op jit(solution)/shard_map/input/pallas_call | solution.py:1137
  504.1 0.0 copy-start.2
  504.1 1.3 slice.26
  505.5 1.3 slice.30
  506.7 1.4 slice_bitcast_fusion
  508.1 2.0 copy.28
  510.2 0.0 copy-start.1
  510.2 3.0 copy.29
  513.2 0.0 copy-done.2
  513.2 0.0 copy-start
  513.2 1.0 copy.34
  514.2 2.3 copy.35
  516.5 0.0 copy-done.1
  516.5 1.1 copy.36
  517.6 0.0 copy-done
  517.6 1.3 copy.37
  (5 shorter events, 0.0 us)
Async XLA Ops:
  504.1 9.1 %copy-start.2 = (bf16[256,2048]{1,0:T(8,128)(2,1)S(1)}, bf16[256,2048]{1,0:T(8,128)(2,1)}, u32[]{:S(2)}) copy-start(bf16[256,2048]{1,0:T(8,128)(2,1)} %get-tuple-element.114) | copy-start | bytes 3145732
  510.2 6.3 %copy-start.1 = (f32[3,256,512]{2,1,0:T(8,128)S(1)}, f32[3,256,512]{2,1,0:T(8,128)}, u32[]{:S(2)}) copy-start(f32[3,256,512]{2,1,0:T(8,128)} %get-tuple-element.118) | copy-start | bytes 4718596
  513.2 4.5 copy-start

commit v10 on v9

--- a/solution.py
+++ b/solution.py
@@ -610,28 +610,22 @@
     sums.finish()
 
 
-def attend_back(q_of, k_of, v_of, do_of, heads, put, dk, dv):
-    block = 256
+def attend_back(b, block, column, heads, put, dk, dv):
     factor = HD ** (-0.5)
+    here, keys = slice(b * block, (b + 1) * block), slice(0, (b + 1) * block)
 
     def head(t):
-        dk[...] = jnp.zeros_like(dk)
-        dv[...] = jnp.zeros_like(dv)
-        for b in range(LEN // block):
-            here, keys = slice(b * block, (b + 1) * block), slice(0, (b + 1) * block)
-            q, k, v, do = q_of(here, t), k_of(keys, t), v_of(keys, t), do_of(here, t)
-            s = lax.dot_general(q, k, NT, preferred_element_type=F32) * factor
-            query = lax.broadcasted_iota(jnp.int32, s.shape, 0) + b * block
-            s = jnp.where(query >= lax.broadcasted_iota(jnp.int32, s.shape, 1), s, -1e30)
-            e = jnp.exp(s - jnp.max(s, axis=-1, keepdims=True))
-            prob = e / jnp.sum(e, axis=-1, keepdims=True)
-            dv[keys, :] += lax.dot_general(prob.astype(BF), do, TN, preferred_element_type=F32)
-            dp = lax.dot_general(do, v, NT, preferred_element_type=F32)
-            ds = (prob * (dp - jnp.sum(prob * dp, axis=-1, keepdims=True))).astype(BF)
-            put(0, here, t, (jnp.dot(ds, k, preferred_element_type=F32) * factor).astype(BF))
-            dk[keys, :] += lax.dot_general(ds, q, TN, preferred_element_type=F32)
-        put(1, slice(0, LEN), t, (dk[...] * factor).astype(BF))
-        put(2, slice(0, LEN), t, dv[...].astype(BF))
+        q, k, v, do = column(0, here, t), column(1, keys, t), column(2, keys, t), column(3, here, t)
+        s = lax.dot_general(q, k, NT, preferred_element_type=F32) * factor
+        query = lax.broadcasted_iota(jnp.int32, s.shape, 0) + b * block
+        s = jnp.where(query >= lax.broadcasted_iota(jnp.int32, s.shape, 1), s, -1e30)
+        e = jnp.exp(s - jnp.max(s, axis=-1, keepdims=True))
+        prob = e / jnp.sum(e, axis=-1, keepdims=True)
+        dv[t, keys, :] += lax.dot_general(prob.astype(BF), do, TN, preferred_element_type=F32)
+        dp = lax.dot_general(do, v, NT, preferred_element_type=F32)
+        ds = (prob * (dp - jnp.sum(prob * dp, axis=-1, keepdims=True))).astype(BF)
+        put(0, here, t, (jnp.dot(ds, k, preferred_element_type=F32) * factor).astype(BF))
+        dk[t, keys, :] += lax.dot_general(ds, q, TN, preferred_element_type=F32)
 
     loop(heads, head)
 
@@ -786,7 +780,7 @@
 
 
 def branch_kernel(n, m, pieces, db_ref, h_ref, vec, mlp_hbm, g_hbm, cot_hbm, c_hbm, du_hbm, qkv_hbm, wo_hbm,
-                  db_all, lo_ref, down_ref, up_ref, dqkv_hbm, dqkv_ref, out_sem, lhs, rhs, wo, dk, dv, part, land, out, terms_a, land_a,
+                  db_all, lo_ref, down_t, up_ref, dqkv_hbm, down_ref, out_sem, lhs, rhs, wo, dk, dv, part, land, out, terms_a, land_a,
                   half_a, terms_b, land_b, half_b, acc, send, recv, s_send, s_recv, own_sem, part_sem, in_sem, qkv_sem,
                   db_sem, p_send, p_recv, h_send, h_recv):
     i, row = lax.axis_index("tensor"), lax.axis_index("dp")
@@ -846,6 +840,17 @@
     own_copy.wait()
     wo_copy.wait()
 
+    for copy in qkv_copies:
+        copy.wait()
+    dk[...] = jnp.zeros_like(dk)
+    dv[...] = jnp.zeros_like(dv)
+
+    def column(p, here, t):
+        return rhs[here, pl.ds(pl.multiple_of(p * width + t * HD, HD), HD)]
+
+    def put(p, here, t, value):
+        rhs[here, pl.ds(pl.multiple_of(p * width + t * HD, HD), HD)] = value
+
     def mixture_back(j):
         here = rows_at(j, size)
         copy = pltpu.make_async_copy(db_all.at[j], lhs.at[here], db_sem.at[j])
@@ -853,16 +858,10 @@
         copy.wait()
         rhs[here, 3 * width : 4 * width] = lax.dot_general(
             lhs[here, :], wo[...], NT, preferred_element_type=F32).astype(BF)
-
-    def round_back(r):
-        def side(s):
-            j = jnp.where(s == 0, i - r, i + r)
-
-            @pl.when(jnp.logical_and(j >= 0, j <= n - 1))
-            def _():
-                mixture_back(j)
-
-        loop(2, side)
+        for b in range(n):
+            @pl.when(j == b)
+            def _():
+                attend_back(b, size, column, width // HD, put, dk, dv)
 
     def keep(ref):
         def put(here, total):
@@ -877,36 +876,48 @@
         else:
             plane.take(stage, keep(ref))
 
-    mixture_back(i)
-    round_back(1)
-    advance(first, 0, down_ref)
-    for r in range(2, n):
-        line.step(r)
-        relays(sums, i, n, r - 1)
-        round_back(r)
-        if r == 2:
+    def round_back(r):
+        @pl.when(r >= 2)
+        def _():
+            line.step(r)
+            relays(sums, i, n, r - 1)
+
+        def side(s):
+            j = jnp.where(s == 0, i - r, i + r)
+
+            @pl.when(jnp.logical_and(jnp.logical_and(j >= 0, j <= n - 1), s * r == s * jnp.maximum(r, 1)))
+            def _():
+                mixture_back(j)
+
+        loop(2, side)
+
+        @pl.when(r == 1)
+        def _():
+            advance(first, 0, down_ref)
+
+        @pl.when(r == min(2, n - 1))
+        def _():
             advance(second, 0, up_ref)
-    if n == 2:
-        advance(second, 0, up_ref)
+
+    loop(n, round_back)
     relays(sums, i, n, n - 1)
-    for copy in qkv_copies:
-        copy.wait()
-
-    def column(p):
-        def get(here, t):
-            return rhs[here, pl.ds(pl.multiple_of(p * width + t * HD, HD), HD)]
-
-        return get
-
-    def put(p, here, t, value):
-        dqkv_ref[p, here, pl.ds(pl.multiple_of(t * HD, HD), HD)] = value
-
-    attend_back(column(0), column(1), column(2), column(3), width // HD, put, dk, dv)
-    leave = pltpu.make_async_copy(dqkv_ref, dqkv_hbm, out_sem)
-    leave.start()
+
+    def whole(t):
+        put(1, slice(0, LEN), t, (dk[t] * HD ** (-0.5)).astype(BF))
+        put(2, slice(0, LEN), t, dv[t].astype(BF))
+
+    loop(width // HD, whole)
+    leave = [pltpu.make_async_copy(rhs.at[:, p * width : (p + 1) * width], dqkv_hbm.at[p], out_sem.at[p]) for p in range(3)]
+    for copy in leave:
+        copy.start()
     for stage in range(1, first.stages):
         advance(first, stage, down_ref)
         advance(second, stage, up_ref)
+
+    def turn(k):
+        down_t[rows_at(k, LANES), :] = down_ref[:, rows_at(k, LANES)].T
+
+    loop(down_ref.shape[1] // LANES, turn)
 
     def output(b):
         here = rows_at(b, RB)
@@ -919,11 +930,12 @@
     second.sent()
     for plane in planes:
         plane.finish()
-    leave.wait()
+    for copy in leave:
+        copy.wait()
 
 
 def input_kernel(n, m, pieces, widths, dqkv_ref, wq_hbm, x_hbm, dh_hbm, vec, early_ref, up_ref, a_hbm, db_hbm, o_hbm,
-                 n_hbm, gt_ref, gqkv_ref, gout_ref, vec_out, up_out, qv_out, early_acc, late_acc, up_acc, qv_acc, vec_ref, qv_ref, wq, a_ref, db_ref,
+                 n_hbm, gt_ref, gqkv_ref, gout_t, vec_out, up_out, qv_out, gout_ref, early_acc, late_acc, up_acc, qv_acc, vec_ref, qv_ref, wq, a_ref, db_ref,
                  o_ref, n_ref, x_ref, dh_ref, part, land, out_p, terms, land_p, half_p, acc, early_land, late_land, up_land, qv_land, s_send,
                  s_recv, in_sem, p_send, p_recv, h_send, h_recv, e_send, e_recv, l_send, l_recv, u_send, u_recv, q_send,
                  q_recv):
@@ -1023,6 +1035,7 @@
         else:
             plane.take(stage, out)
         stage += 1
+    gout_t[...] = gout_ref[...].T
     early, late = every[0].finish(), every[1].finish()
     for k, (rows, at) in enumerate([(late, 0), (late, 1), (early, 2), (early, 0), (early, 1), (early, 3)]):
         vec_out[k : k + 1, :] = rows[at : at + 1, :]
@@ -1120,11 +1133,11 @@
     sum_sems = [dma((n, pieces)), dma((n + 1, pieces))]
     attn_cot, layer_out, grad_down_w, grad_up_w, grad_qkv = pl.pallas_call(
         functools.partial(branch_kernel, n, m, pieces),
-        out_shape=(shape((n, size, depth), BF), shape((size, depth), BF), shape((depth // m, units), F32),
+        out_shape=(shape((n, size, depth), BF), shape((size, depth), BF), shape((units, depth // m), F32),
                    shape((depth // m, units), F32), shape((3, LEN, width), BF)),
         in_specs=[VM] * 3 + [ANY] * 7, out_specs=(ANY, VM, VM, VM, ANY),
-        scratch_shapes=[pltpu.VMEM((3, LEN, width), BF), dma, pltpu.VMEM((LEN, depth), BF), pltpu.VMEM((LEN, units), BF), pltpu.VMEM((width, depth), BF),
-                        pltpu.VMEM((LEN, HD), F32), pltpu.VMEM((LEN, HD), F32)] + sums +
+        scratch_shapes=[pltpu.VMEM((depth // m, units), F32), dma((3,)), pltpu.VMEM((LEN, depth), BF), pltpu.VMEM((LEN, units), BF), pltpu.VMEM((width, depth), BF),
+                        pltpu.VMEM((width // HD, LEN, HD), F32), pltpu.VMEM((width // HD, LEN, HD), F32)] + sums +
                        [pltpu.VMEM((m // 2, depth // m, units), BF)] + plane_scratch(units) * 2 +
                        [pltpu.VMEM((RB, depth), F32), dma((2, n, LineGather.PIECES)), dma((n, LineGather.PIECES))] + sum_sems +
                        [dma, dma, dma((3,)), dma((3,)), dma((n,)), dma((2, m // 2)), dma((2, m // 2)),
@@ -1136,10 +1149,10 @@
     tiles = [max(v, LANES) for v in (piece, up_piece, qv_piece)]
     grad_tokens, grad_qkv_w, grad_out_w, vector_grads, grad_up_b, grad_qv_b = pl.pallas_call(
         functools.partial(input_kernel, n, m, pieces, (piece, up_piece, qv_piece)),
-        out_shape=(shape((size, depth), BF), shape((3, depth // m, width), F32), shape((depth // m, width), F32),
+        out_shape=(shape((size, depth), BF), shape((3, depth // m, width), F32), shape((width, depth // m), F32),
                    shape((8, piece), F32), shape((8, up_piece), F32), shape((8, qv_piece), F32)),
         in_specs=[VM, ANY, ANY, ANY, VM, VM, VM, ANY, ANY, ANY, ANY], out_specs=(VM,) * 6,
-        scratch_shapes=[pltpu.VMEM((8, tiles[k]), F32) for k in (0, 0, 1, 2)] + [
+        scratch_shapes=[pltpu.VMEM((depth // m, width), F32)] + [pltpu.VMEM((8, tiles[k]), F32) for k in (0, 0, 1, 2)] + [
                         pltpu.VMEM((8, depth), F32), pltpu.VMEM((8, width), F32),
                         pltpu.VMEM((3, depth, width), BF), pltpu.VMEM((LEN, depth), BF), pltpu.VMEM((LEN, depth), BF),
                         pltpu.VMEM((LEN, width), BF), pltpu.VMEM((LEN, depth), BF), pltpu.VMEM((size, depth), BF),
@@ -1153,7 +1166,6 @@
                        [dma((total,))] * 4 + [dma((m,))] * 4,
         compiler_params=params(5), name="input",
     )(grad_qkv, w_qkv, tokens, grad_resid, vectors, vec_two, grad_up_b, attn_in, attn_cot, mixture, normal_one)
-    grad_down_w, grad_out_w = grad_down_w.T, grad_out_w.T
 
     vectors = [vector_grads[k] for k in range(6)]
     grad_up_b, grad_qv_b = grad_up_b[0], grad_qv_b[:2]

time: 521 us -> 528 us (1.013)
  Pallas kernels: 501 us -> 509 us
    pallas_call x1, Pallas kernels: 106 us -> 112 us  [body(): pl.pallas_call(functools.partial(branch_kernel, n, m, pieces), out_shape=...]
    unnamed x12 -> x14, local copies, waits for them, and re-layouts: 10.8 us -> 9.35 us
where the time goes in v10:
time: 528 us; the launch traced here: 526 us
  Pallas kernels  509 us (96%)
  local copies, waits for them, and re-layouts  15 us (3%)
    pallas_call x1, Pallas kernels, body(): pl.pallas_call(functools.partial(hidden_kernel, n, pieces), out_shape=(sh...  126 us
    pallas_call x1, Pallas kernels, body(): pl.pallas_call(functools.partial(branch_kernel, n, m, pieces), out_shape=...  112 us
    pallas_call x1, Pallas kernels, body(): pl.pallas_call(functools.partial(attend_kernel, n, m, pieces), out_shape=...  101 us
    pallas_call x1, Pallas kernels, body(): pl.pallas_call(functools.partial(input_kernel, n, m, pieces, (piece, up_p...  85.5 us
    pallas_call x1, Pallas kernels, body(): pl.pallas_call(functools.partial(tokens_kernel, n, m, (piece, qv_piece, u...  85.2 us

profile of v10, /device:TPU:0, one launch (start us, length us, event | category | flops | bytes accessed | tf_op | source)
XLA Modules:
  0.0 526.3 jit_solution(14457866883009677554)
XLA Ops:
  0.7 0.7 tile.20
  1.4 0.1 tile.21
  1.4 0.8 stack.27
  2.2 0.1 tile.9
  2.3 1.3 fusion.4.pack_ref
  3.6 85.2 %gather_tokens.1 = (bf16[1024,2048]{1,0:T(8,128)(2,1)}, bf16[1024,2048]{1,0:T(8,128)(2,1)}, f32[8,2048]{1,0:T(8,128)}, f32[8,512]{1,0:T(8,128)}, f32[8,2048]{1,0...) custom-call(bf16[16,128]{1,0:T(8,128)(2,1)} %fusion.4.pack_ref, bf16[256,2048]{1,0:T(8,128)(2,1)} %x_hbm.1, ...), custom_call_target="tpu_custom_call" | custom-call | tf_op jit(solution)/shard_map/gather_tokens/pallas_call | solution.py:1087
  88.8 101.0 %attend.1 = (bf16[3,1024,512]{2,1,0:T(8,128)(2,1)}, bf16[1024,512]{1,0:T(8,128)(2,1)}, f32[256,2048]{1,0:T(8,128)}, bf16[256,2048]{1,0:T(8,128)(2,1)}, bf16[4,25...) custom-call(bf16[1024,2048]{1,0:T(8,128)(2,1)} %get-tuple-element.47.a_hbm, ...), custom_call_target="tpu_custom_call" | custom-call | tf_op jit(solution)/shard_map/attend/pallas_call | solution.py:1100
  189.8 125.8 %hidden.1 = (bf16[4,256,2048]{2,1,0:T(8,128)(2,1)}, bf16[4,256,2048]{2,1,0:T(8,128)(2,1)}, bf16[4,256,2048]{2,1,0:T(8,128)(2,1)}, bf16[4,256,2048]{2,1,0:T(8,128...) custom-call(bf16[256,2048]{1,0:T(8,128)(2,1)} %get-tuple-element.52.c_ref, ...), custom_call_target="tpu_custom_call" | custom-call | tf_op jit(solution)/shard_map/hidden/pallas_call | solution.py:1112
  315.6 111.7 %branch.1 = (bf16[4,256,2048]{2,1,0:T(8,128)(2,1)}, bf16[256,2048]{1,0:T(8,128)(2,1)}, f32[2048,256]{1,0:T(8,128)}, f32[256,2048]{1,0:T(8,128)}, bf16[3,1024,512]{2,1,0:T(8,128)(2,1)}) custom-call(bf16[256,2048]{1,0:T(8,128)(2,1)} %get-tuple-element.58.db_ref, f32[256,2048]{1,0:T(8,128)} %get-tuple-element.53.h_ref, f32[8,2048]{1,0:T(8,128)} %get-tuple-element.51.vec, ...), custom_call_target="tpu_custom_call" | custom-call | tf_op jit(solution)/shard_map/branch/pallas_call | solution.py:1134
  427.3 85.5 %input.1 = (bf16[256,2048]{1,0:T(8,128)(2,1)}, f32[3,256,512]{2,1,0:T(8,128)}, f32[512,256]{1,0:T(8,128)}, f32[8,64]{1,0:T(8,128)}, f32[8,256]{1,0:T(8,128)}, /*index=5*/f32[8,64]{1,0:T(8,128)}) custom-call(bf16[3,1024,512]{2,1,0:T(8,128)(2,1)} %get-tuple-element.65.dqkv_ref, bf16[3,2048,512]{2,1,0:T(8,128)(2,1)} %get-tuple-element.48.wq_hbm, ...), custom_call_target="tpu_custom_call" | custom-call | tf_op jit(solution)/shard_map/input/pallas_call | solution.py:1150
  512.8 0.0 copy-start.2
  512.8 0.0 copy-start.3
  512.9 1.4 slice.26
  514.2 1.3 slice.30
  515.5 1.4 slice_bitcast_fusion
  516.9 0.0 copy-start.1
  516.9 2.5 copy.34
  519.4 2.3 copy.35
  521.7 0.0 copy-done.2
  521.7 0.0 copy-start
  521.7 1.1 copy.36
  522.8 0.0 copy-done.3
  522.8 0.8 copy.37
  523.6 0.0 copy-done.1
  523.6 1.3 copy.38
  525.0 0.0 copy-done
  525.0 1.3 copy.39
  (5 shorter events, 0.0 us)
Async XLA Ops:
  512.8 8.9 %copy-start.2 = (f32[3,256,512]{2,1,0:T(8,128)S(1)}, f32[3,256,512]{2,1,0:T(8,128)}, u32[]{:S(2)}) copy-start(f32[3,256,512]{2,1,0:T(8,128)} %get-tuple-element.104) | copy-start | bytes 4718596
  512.8 10.0 %copy-start.3 = (f32[512,256]{1,0:T(8,128)S(1)}, f32[512,256]{1,0:T(8,128)}, u32[]{:S(2)}) copy-start(f32[512,256]{1,0:T(8,128)} %get-tuple-element.106) | copy-start | bytes 1572868
  516.9 6.7 %copy-start.1 = (f32[256,2048]{1,0:T(8,128)S(1)}, f32[256,2048]{1,0:T(8,128)}, u32[]{:S(2)}) copy-start(f32[256,2048]{1,0:T(8,128)} %get-tuple-element.110) | copy-start | bytes 6291460
  521.7 3.3 copy-start

commit v11 on v10

--- a/solution.py
+++ b/solution.py
@@ -877,10 +877,10 @@
             plane.take(stage, keep(ref))
 
     def round_back(r):
-        @pl.when(r >= 2)
+        @pl.when(jnp.logical_and(r >= 1, r <= n - 2))
         def _():
-            line.step(r)
-            relays(sums, i, n, r - 1)
+            line.step(r + 1)
+            relays(sums, i, n, r)
 
         def side(s):
             j = jnp.where(s == 0, i - r, i + r)

time: 528 us -> 519 us (0.983)
  Pallas kernels: 509 us -> 500 us
    pallas_call x1, Pallas kernels: 112 us -> 105 us  [body(): pl.pallas_call(functools.partial(branch_kernel, n, m, pieces), out_shape=...]
where the time goes in v11:
time: 519 us; the launch traced here: 517 us
  Pallas kernels  500 us (96%)
  local copies, waits for them, and re-layouts  15 us (3%)
    pallas_call x1, Pallas kernels, body(): pl.pallas_call(functools.partial(hidden_kernel, n, pieces), out_shape=(sh...  126 us
    pallas_call x1, Pallas kernels, body(): pl.pallas_call(functools.partial(branch_kernel, n, m, pieces), out_shape=...  105 us
    pallas_call x1, Pallas kernels, body(): pl.pallas_call(functools.partial(attend_kernel, n, m, pieces), out_shape=...  101 us
    pallas_call x1, Pallas kernels, body(): pl.pallas_call(functools.partial(tokens_kernel, n, m, (piece, qv_piece, u...  85.2 us
    pallas_call x1, Pallas kernels, body(): pl.pallas_call(functools.partial(input_kernel, n, m, pieces, (piece, up_p...  82.6 us

profile of v11, /device:TPU:0, one launch (start us, length us, event | category | flops | bytes accessed | tf_op | source)
XLA Modules:
  0.0 517.0 jit_solution(14511827734371226079)
XLA Ops:
  0.7 0.7 tile.20
  1.4 0.1 tile.21
  1.4 0.8 stack.27
  2.2 0.1 tile.9
  2.3 1.3 fusion.4.pack_ref
  3.6 85.2 %gather_tokens.1 = (bf16[1024,2048]{1,0:T(8,128)(2,1)}, bf16[1024,2048]{1,0:T(8,128)(2,1)}, f32[8,2048]{1,0:T(8,128)}, f32[8,512]{1,0:T(8,128)}, f32[8,2048]{1,0...) custom-call(bf16[16,128]{1,0:T(8,128)(2,1)} %fusion.4.pack_ref, bf16[256,2048]{1,0:T(8,128)(2,1)} %x_hbm.1, ...), custom_call_target="tpu_custom_call" | custom-call | tf_op jit(solution)/shard_map/gather_tokens/pallas_call | solution.py:1087
  88.8 101.0 %attend.1 = (bf16[3,1024,512]{2,1,0:T(8,128)(2,1)}, bf16[1024,512]{1,0:T(8,128)(2,1)}, f32[256,2048]{1,0:T(8,128)}, bf16[256,2048]{1,0:T(8,128)(2,1)}, bf16[4,25...) custom-call(bf16[1024,2048]{1,0:T(8,128)(2,1)} %get-tuple-element.47.a_hbm, ...), custom_call_target="tpu_custom_call" | custom-call | tf_op jit(solution)/shard_map/attend/pallas_call | solution.py:1100
  189.8 125.8 %hidden.1 = (bf16[4,256,2048]{2,1,0:T(8,128)(2,1)}, bf16[4,256,2048]{2,1,0:T(8,128)(2,1)}, bf16[4,256,2048]{2,1,0:T(8,128)(2,1)}, bf16[4,256,2048]{2,1,0:T(8,128...) custom-call(bf16[256,2048]{1,0:T(8,128)(2,1)} %get-tuple-element.52.c_ref, ...), custom_call_target="tpu_custom_call" | custom-call | tf_op jit(solution)/shard_map/hidden/pallas_call | solution.py:1112
  315.6 105.3 %branch.1 = (bf16[4,256,2048]{2,1,0:T(8,128)(2,1)}, bf16[256,2048]{1,0:T(8,128)(2,1)}, f32[2048,256]{1,0:T(8,128)}, f32[256,2048]{1,0:T(8,128)}, bf16[3,1024,512]{2,1,0:T(8,128)(2,1)}) custom-call(bf16[256,2048]{1,0:T(8,128)(2,1)} %get-tuple-element.58.db_ref, f32[256,2048]{1,0:T(8,128)} %get-tuple-element.53.h_ref, f32[8,2048]{1,0:T(8,128)} %get-tuple-element.51.vec, ...), custom_call_target="tpu_custom_call" | custom-call | tf_op jit(solution)/shard_map/branch/pallas_call | solution.py:1134
  420.9 82.6 %input.1 = (bf16[256,2048]{1,0:T(8,128)(2,1)}, f32[3,256,512]{2,1,0:T(8,128)}, f32[512,256]{1,0:T(8,128)}, f32[8,64]{1,0:T(8,128)}, f32[8,256]{1,0:T(8,128)}, /*index=5*/f32[8,64]{1,0:T(8,128)}) custom-call(bf16[3,1024,512]{2,1,0:T(8,128)(2,1)} %get-tuple-element.65.dqkv_ref, bf16[3,2048,512]{2,1,0:T(8,128)(2,1)} %get-tuple-element.48.wq_hbm, ...), custom_call_target="tpu_custom_call" | custom-call | tf_op jit(solution)/shard_map/input/pallas_call | solution.py:1150
  503.5 0.0 copy-start.2
  503.6 0.0 copy-start.3
  503.6 1.4 slice.26
  505.0 1.3 slice.30
  506.2 1.4 slice_bitcast_fusion
  507.6 0.0 copy-start.1
  507.7 2.5 copy.34
  510.1 2.3 copy.35
  512.4 0.0 copy-done.2
  512.4 0.0 copy-start
  512.4 1.1 copy.36
  513.6 0.0 copy-done.3
  513.6 0.8 copy.37
  514.4 0.0 copy-done.1
  514.4 1.3 copy.38
  515.7 0.0 copy-done
  515.7 1.3 copy.39
  (5 shorter events, 0.0 us)
Async XLA Ops:
  503.5 8.9 %copy-start.2 = (f32[3,256,512]{2,1,0:T(8,128)S(1)}, f32[3,256,512]{2,1,0:T(8,128)}, u32[]{:S(2)}) copy-start(f32[3,256,512]{2,1,0:T(8,128)} %get-tuple-element.104) | copy-start | bytes 4718596
  503.6 10.0 %copy-start.3 = (f32[512,256]{1,0:T(8,128)S(1)}, f32[512,256]{1,0:T(8,128)}, u32[]{:S(2)}) copy-start(f32[512,256]{1,0:T(8,128)} %get-tuple-element.106) | copy-start | bytes 1572868
  507.6 6.7 %copy-start.1 = (f32[256,2048]{1,0:T(8,128)S(1)}, f32[256,2048]{1,0:T(8,128)}, u32[]{:S(2)}) copy-start(f32[256,2048]{1,0:T(8,128)} %get-tuple-element.110) | copy-start | bytes 6291460
  512.4 3.3 copy-start

commit v12 on v11

--- a/solution.py
+++ b/solution.py
@@ -511,7 +511,7 @@
 
 def hidden_kernel(n, pieces, c_ref, h_ref, cot_hbm, up_hbm, down_hbm, up_bias, vec, c_hbm, g_hbm, du_hbm, mlp_hbm, dh_ref,
                   db_ref, vec_ref, upb_ref, c_all, g_all, du_all, cot_all, up, down, part, land, send, recv, s_send,
-                  s_recv, w_sem, cot_sem, own_sem, c_sem, g_sem, du_sem, mlp, mlp_sem):
+                  s_recv, w_sem, cot_sem, own_sem, c_sem, g_sem, du_sem, mlp, mlp_sem, ahead):
     i = lax.axis_index("tensor")
     size, depth = c_ref.shape
     units = up.shape[1]
@@ -535,6 +535,14 @@
     sums = LineSum(i, n, part, land, s_send, s_recv, pieces)
     tile = 256
 
+    far = jnp.where(i < n // 2, n - 1, 0)
+
+    def before(k):
+        cols = rows_at(k, tile)
+        ahead[1, :, cols] = lax.dot_general(cot_all[far], down[cols, :], NT, preferred_element_type=F32)
+
+    loop(units // tile, before)
+
     def out_copy(src, dst, sem, j):
         return pltpu.make_async_copy(src.at[j], dst.at[j], sem.at[j])
 
@@ -542,7 +550,12 @@
         def unit(k):
             cols = rows_at(k, tile)
             u = jnp.dot(c_all[j], up[:, cols], preferred_element_type=F32) + up_bias[0:1, cols]
-            dg = lax.dot_general(cot_all[j], down[cols, :], NT, preferred_element_type=F32)
+
+            @pl.when(j != far)
+            def _():
+                ahead[0, :, cols] = lax.dot_general(cot_all[j], down[cols, :], NT, preferred_element_type=F32)
+
+            dg = ahead[jnp.where(j == far, 1, 0), :, cols]
             half = 0.5 + 0.5 * lax.erf(u * (0.5 ** 0.5))
             g_all[j, :, cols] = (u * half).astype(BF)
             slope = half + u * (jnp.exp(u * u * -0.5) * 0.3989422804014327)
@@ -780,7 +793,7 @@
 
 
 def branch_kernel(n, m, pieces, db_ref, h_ref, vec, mlp_hbm, g_hbm, cot_hbm, c_hbm, du_hbm, qkv_hbm, wo_hbm,
-                  db_all, lo_ref, down_t, up_ref, dqkv_hbm, down_ref, out_sem, lhs, rhs, wo, dk, dv, part, land, out, terms_a, land_a,
+                  db_all, lo_ref, down_out, up_out, dqkv_hbm, down_t, up_ref, down_ref, out_sem, lhs, rhs, wo, dk, dv, part, land, out, terms_a, land_a,
                   half_a, terms_b, land_b, half_b, acc, send, recv, s_send, s_recv, own_sem, part_sem, in_sem, qkv_sem,
                   db_sem, p_send, p_recv, h_send, h_recv):
     i, row = lax.axis_index("tensor"), lax.axis_index("dp")
@@ -918,6 +931,9 @@
         down_t[rows_at(k, LANES), :] = down_ref[:, rows_at(k, LANES)].T
 
     loop(down_ref.shape[1] // LANES, turn)
+    leave += [pltpu.make_async_copy(down_t, down_out, out_sem.at[3]), pltpu.make_async_copy(up_ref, up_out, out_sem.at[4])]
+    for copy in leave[3:]:
+        copy.start()
 
     def output(b):
         here = rows_at(b, RB)
@@ -935,7 +951,7 @@
 
 
 def input_kernel(n, m, pieces, widths, dqkv_ref, wq_hbm, x_hbm, dh_hbm, vec, early_ref, up_ref, a_hbm, db_hbm, o_hbm,
-                 n_hbm, gt_ref, gqkv_ref, gout_t, vec_out, up_out, qv_out, gout_ref, early_acc, late_acc, up_acc, qv_acc, vec_ref, qv_ref, wq, a_ref, db_ref,
+                 n_hbm, gt_ref, gqkv_out, gout_out, vec_out, up_out, qv_out, gqkv_ref, gout_t, out_sem, gout_ref, early_acc, late_acc, up_acc, qv_acc, vec_ref, qv_ref, wq, a_ref, db_ref,
                  o_ref, n_ref, x_ref, dh_ref, part, land, out_p, terms, land_p, half_p, acc, early_land, late_land, up_land, qv_land, s_send,
                  s_recv, in_sem, p_send, p_recv, h_send, h_recv, e_send, e_recv, l_send, l_recv, u_send, u_recv, q_send,
                  q_recv):
@@ -1036,12 +1052,17 @@
             plane.take(stage, out)
         stage += 1
     gout_t[...] = gout_ref[...].T
+    leave = [pltpu.make_async_copy(gqkv_ref, gqkv_out, out_sem.at[0]), pltpu.make_async_copy(gout_t, gout_out, out_sem.at[1])]
+    for copy in leave:
+        copy.start()
     early, late = every[0].finish(), every[1].finish()
     for k, (rows, at) in enumerate([(late, 0), (late, 1), (early, 2), (early, 0), (early, 1), (early, 3)]):
         vec_out[k : k + 1, :] = rows[at : at + 1, :]
     up_out[...] = column[0].finish()
     qv_out[...] = column[1].finish()
     sums.own(norm)
+    for copy in leave:
+        copy.wait()
     sums.finish()
     plane.sent()
     plane.finish()
@@ -1073,7 +1094,7 @@
         if count >= LANES:
             return value.reshape(-1, LANES)
         places = LANES // count
-        spread = jnp.tile(value.reshape(-1, count), (1, places))
+        spread = jnp.concatenate([value.reshape(-1, count)] * places, axis=1)
         return jnp.where((jnp.arange(LANES) // count)[None] == index % places, spread, 0)
 
     me = row * n + i
@@ -1119,7 +1140,7 @@
                         pltpu.VMEM((n, size, units), BF), pltpu.VMEM((n, size, depth), BF),
                         pltpu.VMEM((depth, units), BF), pltpu.VMEM((units, depth), BF)] + sums +
                        [dma((2, n, LineGather.PIECES)), dma((n, LineGather.PIECES)), dma((n, pieces)), dma((n + 1, pieces)), dma((2,)), dma, dma,
-                        dma((n,)), dma((n,)), dma((n,)), pltpu.VMEM((n, size, depth), BF), dma((n,))],
+                        dma((n,)), dma((n,)), dma((n,)), pltpu.VMEM((n, size, depth), BF), dma((n,)), pltpu.VMEM((2, size, units), F32)],
         compiler_params=params(2), name="hidden",
     )(mlp_own, residual, cot_all, w_up, w_down, bias_up, vectors)
     mlp_in, hidden, grad_pre, cot_rows = [v.reshape(LEN, -1) for v in (mlp_in, hidden, grad_pre, cot_all)]
@@ -1135,8 +1156,9 @@
         functools.partial(branch_kernel, n, m, pieces),
         out_shape=(shape((n, size, depth), BF), shape((size, depth), BF), shape((units, depth // m), F32),
                    shape((depth // m, units), F32), shape((3, LEN, width), BF)),
-        in_specs=[VM] * 3 + [ANY] * 7, out_specs=(ANY, VM, VM, VM, ANY),
-        scratch_shapes=[pltpu.VMEM((depth // m, units), F32), dma((3,)), pltpu.VMEM((LEN, depth), BF), pltpu.VMEM((LEN, units), BF), pltpu.VMEM((width, depth), BF),
+        in_specs=[VM] * 3 + [ANY] * 7, out_specs=(ANY, VM, ANY, ANY, ANY),
+        scratch_shapes=[pltpu.VMEM((units, depth // m), F32), pltpu.VMEM((depth // m, units), F32),
+                        pltpu.VMEM((depth // m, units), F32), dma((5,)), pltpu.VMEM((LEN, depth), BF), pltpu.VMEM((LEN, units), BF), pltpu.VMEM((width, depth), BF),
                         pltpu.VMEM((width // HD, LEN, HD), F32), pltpu.VMEM((width // HD, LEN, HD), F32)] + sums +
                        [pltpu.VMEM((m // 2, depth // m, units), BF)] + plane_scratch(units) * 2 +
                        [pltpu.VMEM((RB, depth), F32), dma((2, n, LineGather.PIECES)), dma((n, LineGather.PIECES))] + sum_sems +
@@ -1151,8 +1173,9 @@
         functools.partial(input_kernel, n, m, pieces, (piece, up_piece, qv_piece)),
         out_shape=(shape((size, depth), BF), shape((3, depth // m, width), F32), shape((width, depth // m), F32),
                    shape((8, piece), F32), shape((8, up_piece), F32), shape((8, qv_piece), F32)),
-        in_specs=[VM, ANY, ANY, ANY, VM, VM, VM, ANY, ANY, ANY, ANY], out_specs=(VM,) * 6,
-        scratch_shapes=[pltpu.VMEM((depth // m, width), F32)] + [pltpu.VMEM((8, tiles[k]), F32) for k in (0, 0, 1, 2)] + [
+        in_specs=[VM, ANY, ANY, ANY, VM, VM, VM, ANY, ANY, ANY, ANY], out_specs=(VM, ANY, ANY, VM, VM, VM),
+        scratch_shapes=[pltpu.VMEM((3, depth // m, width), F32), pltpu.VMEM((width, depth // m), F32), dma((2,)),
+                        pltpu.VMEM((depth // m, width), F32)] + [pltpu.VMEM((8, tiles[k]), F32) for k in (0, 0, 1, 2)] + [
                         pltpu.VMEM((8, depth), F32), pltpu.VMEM((8, width), F32),
                         pltpu.VMEM((3, depth, width), BF), pltpu.VMEM((LEN, depth), BF), pltpu.VMEM((LEN, depth), BF),
                         pltpu.VMEM((LEN, width), BF), pltpu.VMEM((LEN, depth), BF), pltpu.VMEM((size, depth), BF),

time: 519 us -> 523 us (level)
  no operation moved by 1% of the time
where the time goes in v12:
time: 523 us; the launch traced here: 522 us
  Pallas kernels  505 us (97%)
  local copies, waits for them, and re-layouts  14.2 us (3%)
    pallas_call x1, Pallas kernels, body(): pl.pallas_call(functools.partial(hidden_kernel, n, pieces), out_shape=(sh...  130 us
    pallas_call x1, Pallas kernels, body(): pl.pallas_call(functools.partial(branch_kernel, n, m, pieces), out_shape=...  105 us
    pallas_call x1, Pallas kernels, body(): pl.pallas_call(functools.partial(attend_kernel, n, m, pieces), out_shape=...  101 us
    pallas_call x1, Pallas kernels, body(): pl.pallas_call(functools.partial(tokens_kernel, n, m, (piece, qv_piece, u...  85.2 us
    pallas_call x1, Pallas kernels, body(): pl.pallas_call(functools.partial(input_kernel, n, m, pieces, (piece, up_p...  83 us

profile of v12, /device:TPU:0, one launch (start us, length us, event | category | flops | bytes accessed | tf_op | source)
XLA Modules:
  0.0 521.7 jit_solution(11698075482632946314)
XLA Ops:
  0.7 0.8 broadcast_select_fusion
  1.5 0.8 stack.27
  2.3 0.1 maximum_select_fusion
  2.3 1.3 fusion.4.pack_ref
  3.6 85.2 %gather_tokens.1 = (bf16[1024,2048]{1,0:T(8,128)(2,1)}, bf16[1024,2048]{1,0:T(8,128)(2,1)}, f32[8,2048]{1,0:T(8,128)}, f32[8,512]{1,0:T(8,128)}, f32[8,2048]{1,0...) custom-call(bf16[16,128]{1,0:T(8,128)(2,1)} %fusion.4.pack_ref, bf16[256,2048]{1,0:T(8,128)(2,1)} %x_hbm.1, ...), custom_call_target="tpu_custom_call" | custom-call | tf_op jit(solution)/shard_map/gather_tokens/pallas_call | solution.py:1108
  88.8 101.0 %attend.1 = (bf16[3,1024,512]{2,1,0:T(8,128)(2,1)}, bf16[1024,512]{1,0:T(8,128)(2,1)}, f32[256,2048]{1,0:T(8,128)}, bf16[256,2048]{1,0:T(8,128)(2,1)}, bf16[4,25...) custom-call(bf16[1024,2048]{1,0:T(8,128)(2,1)} %get-tuple-element.47.a_hbm, ...), custom_call_target="tpu_custom_call" | custom-call | tf_op jit(solution)/shard_map/attend/pallas_call | solution.py:1121
  189.8 130.4 %hidden.1 = (bf16[4,256,2048]{2,1,0:T(8,128)(2,1)}, bf16[4,256,2048]{2,1,0:T(8,128)(2,1)}, bf16[4,256,2048]{2,1,0:T(8,128)(2,1)}, bf16[4,256,2048]{2,1,0:T(8,128...) custom-call(bf16[256,2048]{1,0:T(8,128)(2,1)} %get-tuple-element.52.c_ref, ...), custom_call_target="tpu_custom_call" | custom-call | tf_op jit(solution)/shard_map/hidden/pallas_call | solution.py:1133
  320.2 105.1 %branch.1 = (bf16[4,256,2048]{2,1,0:T(8,128)(2,1)}, bf16[256,2048]{1,0:T(8,128)(2,1)}, f32[2048,256]{1,0:T(8,128)}, f32[256,2048]{1,0:T(8,128)}, bf16[3,1024,512]{2,1,0:T(8,128)(2,1)}) custom-call(bf16[256,2048]{1,0:T(8,128)(2,1)} %get-tuple-element.58.db_ref, f32[256,2048]{1,0:T(8,128)} %get-tuple-element.53.h_ref, f32[8,2048]{1,0:T(8,128)} %get-tuple-element.51.vec, ...), custom_call_target="tpu_custom_call" | custom-call | tf_op jit(solution)/shard_map/branch/pallas_call | solution.py:1155
  425.3 83.0 %input.1 = (bf16[256,2048]{1,0:T(8,128)(2,1)}, f32[3,256,512]{2,1,0:T(8,128)}, f32[512,256]{1,0:T(8,128)}, f32[8,64]{1,0:T(8,128)}, f32[8,256]{1,0:T(8,128)}, /*index=5*/f32[8,64]{1,0:T(8,128)}) custom-call(bf16[3,1024,512]{2,1,0:T(8,128)(2,1)} %get-tuple-element.65.dqkv_ref, bf16[3,2048,512]{2,1,0:T(8,128)(2,1)} %get-tuple-element.48.wq_hbm, ...), custom_call_target="tpu_custom_call" | custom-call | tf_op jit(solution)/shard_map/input/pallas_call | solution.py:1172
  508.2 0.0 copy-start.2
  508.3 0.0 copy-start.3
  508.3 1.4 slice.26
  509.7 1.3 slice.30
  510.9 1.4 slice_bitcast_fusion
  512.4 0.0 copy-start.1
  512.4 2.5 copy.34
  514.8 2.3 copy.35
  517.1 0.0 copy-done.2
  517.1 0.0 copy-start
  517.1 1.1 copy.36
  518.3 0.0 copy-done.3
  518.3 0.8 copy.37
  519.1 0.0 copy-done.1
  519.1 1.3 copy.38
  520.4 0.0 copy-done
  520.4 1.3 copy.39
  (2 shorter events, 0.0 us)
Async XLA Ops:
  508.2 8.9 %copy-start.2 = (f32[3,256,512]{2,1,0:T(8,128)S(1)}, f32[3,256,512]{2,1,0:T(8,128)}, u32[]{:S(2)}) copy-start(f32[3,256,512]{2,1,0:T(8,128)} %get-tuple-element.104) | copy-start | bytes 4718596
  508.3 10.0 %copy-start.3 = (f32[512,256]{1,0:T(8,128)S(1)}, f32[512,256]{1,0:T(8,128)}, u32[]{:S(2)}) copy-start(f32[512,256]{1,0:T(8,128)} %get-tuple-element.106) | copy-start | bytes 1572868
  512.4 6.7 %copy-start.1 = (f32[256,2048]{1,0:T(8,128)S(1)}, f32[256,2048]{1,0:T(8,128)}, u32[]{:S(2)}) copy-start(f32[256,2048]{1,0:T(8,128)} %get-tuple-element.110) | copy-start | bytes 6291460
  517.1 3.3 copy-start

commit v13 on v11

--- a/solution.py
+++ b/solution.py
@@ -935,9 +935,9 @@
 
 
 def input_kernel(n, m, pieces, widths, dqkv_ref, wq_hbm, x_hbm, dh_hbm, vec, early_ref, up_ref, a_hbm, db_hbm, o_hbm,
-                 n_hbm, gt_ref, gqkv_ref, gout_t, vec_out, up_out, qv_out, gout_ref, early_acc, late_acc, up_acc, qv_acc, vec_ref, qv_ref, wq, a_ref, db_ref,
-                 o_ref, n_ref, x_ref, dh_ref, part, land, out_p, terms, land_p, half_p, acc, early_land, late_land, up_land, qv_land, s_send,
-                 s_recv, in_sem, p_send, p_recv, h_send, h_recv, e_send, e_recv, l_send, l_recv, u_send, u_recv, q_send,
+                 n_hbm, gt_ref, gqkv_ref, gout_t, vec_out, up_out, qv_out, gout_ref, late_acc, up_acc, qv_acc, vec_ref, qv_ref, wq, a_ref, db_ref,
+                 o_ref, n_ref, x_ref, dh_ref, part, land, out_p, terms, land_p, half_p, acc, late_land, up_land, qv_land, s_send,
+                 s_recv, in_sem, p_send, p_recv, h_send, h_recv, l_send, l_recv, u_send, u_recv, q_send,
                  q_recv):
     i, row = lax.axis_index("tensor"), lax.axis_index("dp")
     me, total_devices = row * n + i, m * n
@@ -950,16 +950,14 @@
     loads[0].start()
     loads[4].start()
     greet_all(me, n, total_devices)
-    every = [VectorSum(me, total_devices, lambda g: {"dp": g // n, "tensor": g % n}, early_ref, piece, early_land, early_acc,
-                       e_send, e_recv),
-             VectorSum(me, total_devices, lambda g: {"dp": g // n, "tensor": g % n}, vec_ref, piece, late_land, late_acc,
-                       l_send, l_recv)]
+    every = VectorSum(me, total_devices, lambda g: {"dp": g // n, "tensor": g % n}, vec_ref, piece, late_land, late_acc,
+                      l_send, l_recv)
     column = [VectorSum(row, m, lambda g: {"dp": g}, up_ref, up_piece, up_land, up_acc, u_send, u_recv),
               VectorSum(row, m, lambda g: {"dp": g}, qv_ref, qv_piece, qv_land, qv_acc, q_send, q_recv)]
-    every[0].start()
     column[0].start()
     sums = LineSum(i, n, part, land, s_send, s_recv, pieces)
     vec_ref[...] = jnp.zeros_like(vec_ref)
+    vec_ref[2:6, :] = early_ref[0:4, :]
     qv_ref[...] = jnp.zeros_like(qv_ref)
     loads[0].wait()
     loads[4].wait()
@@ -990,7 +988,7 @@
             qv_ref[p : p + 1, :] += jnp.sum(dqkv_ref[2 * p, here, :].astype(F32), axis=0, keepdims=True)
 
     loop(n, term)
-    every[1].start()
+    every.start()
     column[1].start()
     loop(n - 1, lambda t: sums.launch(jnp.where(i < n // 2, n - 2 - t, t + 1)))
     for k in (1, 2, 3, 5, 6):
@@ -1036,8 +1034,8 @@
             plane.take(stage, out)
         stage += 1
     gout_t[...] = gout_ref[...].T
-    early, late = every[0].finish(), every[1].finish()
-    for k, (rows, at) in enumerate([(late, 0), (late, 1), (early, 2), (early, 0), (early, 1), (early, 3)]):
+    rows = every.finish()
+    for k, at in enumerate([0, 1, 4, 2, 3, 5]):
         vec_out[k : k + 1, :] = rows[at : at + 1, :]
     up_out[...] = column[0].finish()
     qv_out[...] = column[1].finish()
@@ -1152,7 +1150,7 @@
         out_shape=(shape((size, depth), BF), shape((3, depth // m, width), F32), shape((width, depth // m), F32),
                    shape((8, piece), F32), shape((8, up_piece), F32), shape((8, qv_piece), F32)),
         in_specs=[VM, ANY, ANY, ANY, VM, VM, VM, ANY, ANY, ANY, ANY], out_specs=(VM,) * 6,
-        scratch_shapes=[pltpu.VMEM((depth // m, width), F32)] + [pltpu.VMEM((8, tiles[k]), F32) for k in (0, 0, 1, 2)] + [
+        scratch_shapes=[pltpu.VMEM((depth // m, width), F32)] + [pltpu.VMEM((8, tiles[k]), F32) for k in (0, 1, 2)] + [
                         pltpu.VMEM((8, depth), F32), pltpu.VMEM((8, width), F32),
                         pltpu.VMEM((3, depth, width), BF), pltpu.VMEM((LEN, depth), BF), pltpu.VMEM((LEN, depth), BF),
                         pltpu.VMEM((LEN, width), BF), pltpu.VMEM((LEN, depth), BF), pltpu.VMEM((size, depth), BF),
@@ -1160,10 +1158,10 @@
                        [pltpu.VMEM((m // 2, depth // m, 4 * width), BF)] +
                        plane_scratch(4 * width) +
                        [pltpu.VMEM((RB, depth), F32), pltpu.VMEM((total, 8, tiles[0]), F32),
-                        pltpu.VMEM((total, 8, tiles[0]), F32), pltpu.VMEM((m, 8, tiles[1]), F32),
+                        pltpu.VMEM((m, 8, tiles[1]), F32),
                         pltpu.VMEM((m, 8, tiles[2]), F32)] + sum_sems +
                        [dma((7,)), dma((m // 2,)), dma((m // 2,)), dma((2, m // 2 - 1)), dma((2, m // 2 - 1))] +
-                       [dma((total,))] * 4 + [dma((m,))] * 4,
+                       [dma((total,))] * 2 + [dma((m,))] * 4,
         compiler_params=params(5), name="input",
     )(grad_qkv, w_qkv, tokens, grad_resid, vectors, vec_two, grad_up_b, attn_in, attn_cot, mixture, normal_one)
 

time: 519 us -> 518 us (level)
  no operation moved by 1% of the time
where the time goes in v13:
time: 518 us; the launch traced here: 516 us
  Pallas kernels  499 us (96%)
  local copies, waits for them, and re-layouts  15 us (3%)
    pallas_call x1, Pallas kernels, body(): pl.pallas_call(functools.partial(hidden_kernel, n, pieces), out_shape=(sh...  126 us
    pallas_call x1, Pallas kernels, body(): pl.pallas_call(functools.partial(branch_kernel, n, m, pieces), out_shape=...  105 us
    pallas_call x1, Pallas kernels, body(): pl.pallas_call(functools.partial(attend_kernel, n, m, pieces), out_shape=...  101 us
    pallas_call x1, Pallas kernels, body(): pl.pallas_call(functools.partial(tokens_kernel, n, m, (piece, qv_piece, u...  85.2 us
    pallas_call x1, Pallas kernels, body(): pl.pallas_call(functools.partial(input_kernel, n, m, pieces, (piece, up_p...  81.6 us

profile of v13, /device:TPU:0, one launch (start us, length us, event | category | flops | bytes accessed | tf_op | source)
XLA Modules:
  0.0 516.0 jit_solution(4582190025786358590)
XLA Ops:
  0.7 0.7 tile.20
  1.4 0.1 tile.21
  1.4 0.8 stack.27
  2.2 0.1 tile.9
  2.3 1.3 fusion.4.pack_ref
  3.6 85.2 %gather_tokens.1 = (bf16[1024,2048]{1,0:T(8,128)(2,1)}, bf16[1024,2048]{1,0:T(8,128)(2,1)}, f32[8,2048]{1,0:T(8,128)}, f32[8,512]{1,0:T(8,128)}, f32[8,2048]{1,0...) custom-call(bf16[16,128]{1,0:T(8,128)(2,1)} %fusion.4.pack_ref, bf16[256,2048]{1,0:T(8,128)(2,1)} %x_hbm.1, ...), custom_call_target="tpu_custom_call" | custom-call | tf_op jit(solution)/shard_map/gather_tokens/pallas_call | solution.py:1085
  88.8 101.0 %attend.1 = (bf16[3,1024,512]{2,1,0:T(8,128)(2,1)}, bf16[1024,512]{1,0:T(8,128)(2,1)}, f32[256,2048]{1,0:T(8,128)}, bf16[256,2048]{1,0:T(8,128)(2,1)}, bf16[4,25...) custom-call(bf16[1024,2048]{1,0:T(8,128)(2,1)} %get-tuple-element.47.a_hbm, ...), custom_call_target="tpu_custom_call" | custom-call | tf_op jit(solution)/shard_map/attend/pallas_call | solution.py:1098
  189.8 125.8 %hidden.1 = (bf16[4,256,2048]{2,1,0:T(8,128)(2,1)}, bf16[4,256,2048]{2,1,0:T(8,128)(2,1)}, bf16[4,256,2048]{2,1,0:T(8,128)(2,1)}, bf16[4,256,2048]{2,1,0:T(8,128...) custom-call(bf16[256,2048]{1,0:T(8,128)(2,1)} %get-tuple-element.52.c_ref, ...), custom_call_target="tpu_custom_call" | custom-call | tf_op jit(solution)/shard_map/hidden/pallas_call | solution.py:1110
  315.6 105.3 %branch.1 = (bf16[4,256,2048]{2,1,0:T(8,128)(2,1)}, bf16[256,2048]{1,0:T(8,128)(2,1)}, f32[2048,256]{1,0:T(8,128)}, f32[256,2048]{1,0:T(8,128)}, bf16[3,1024,512]{2,1,0:T(8,128)(2,1)}) custom-call(bf16[256,2048]{1,0:T(8,128)(2,1)} %get-tuple-element.58.db_ref, f32[256,2048]{1,0:T(8,128)} %get-tuple-element.53.h_ref, f32[8,2048]{1,0:T(8,128)} %get-tuple-element.51.vec, ...), custom_call_target="tpu_custom_call" | custom-call | tf_op jit(solution)/shard_map/branch/pallas_call | solution.py:1132
  420.9 81.6 %input.1 = (bf16[256,2048]{1,0:T(8,128)(2,1)}, f32[3,256,512]{2,1,0:T(8,128)}, f32[512,256]{1,0:T(8,128)}, f32[8,64]{1,0:T(8,128)}, f32[8,256]{1,0:T(8,128)}, /*index=5*/f32[8,64]{1,0:T(8,128)}) custom-call(bf16[3,1024,512]{2,1,0:T(8,128)(2,1)} %get-tuple-element.65.dqkv_ref, bf16[3,2048,512]{2,1,0:T(8,128)(2,1)} %get-tuple-element.48.wq_hbm, ...), custom_call_target="tpu_custom_call" | custom-call | tf_op jit(solution)/shard_map/input/pallas_call | solution.py:1148
  502.5 0.0 copy-start.2
  502.5 0.0 copy-start.3
  502.5 1.4 slice.26
  503.9 1.3 slice.30
  505.2 1.4 slice_bitcast_fusion
  506.6 0.0 copy-start.1
  506.6 2.5 copy.34
  509.1 2.3 copy.35
  511.4 0.0 copy-done.2
  511.4 0.0 copy-start
  511.4 1.1 copy.36
  512.5 0.0 copy-done.3
  512.5 0.8 copy.37
  513.3 0.0 copy-done.1
  513.3 1.3 copy.38
  514.6 0.0 copy-done
  514.7 1.3 copy.39
  (5 shorter events, 0.0 us)
Async XLA Ops:
  502.5 8.9 %copy-start.2 = (f32[3,256,512]{2,1,0:T(8,128)S(1)}, f32[3,256,512]{2,1,0:T(8,128)}, u32[]{:S(2)}) copy-start(f32[3,256,512]{2,1,0:T(8,128)} %get-tuple-element.104) | copy-start | bytes 4718596
  502.5 10.0 %copy-start.3 = (f32[512,256]{1,0:T(8,128)S(1)}, f32[512,256]{1,0:T(8,128)}, u32[]{:S(2)}) copy-start(f32[512,256]{1,0:T(8,128)} %get-tuple-element.106) | copy-start | bytes 1572868
  506.6 6.7 %copy-start.1 = (f32[256,2048]{1,0:T(8,128)S(1)}, f32[256,2048]{1,0:T(8,128)}, u32[]{:S(2)}) copy-start(f32[256,2048]{1,0:T(8,128)} %get-tuple-element.110) | copy-start | bytes 6291460
  511.4 3.3 copy-start
